TPU v7x, 32 devices: a whole 2x2x4 slice. The times are simulated.
32 devices in a mesh: tp: 8 (over z, y), cp: 4 (over x, core).
Axes of the slice: x: 2, y: 2, z: 4, core: 2. Of those that a mesh axis runs over, the one named last changes fastest.
Arguments:
- x_in: bfloat16 [4, 512, 2048], P(None, 'cp')
- d_y: bfloat16 [4, 512, 2048], P(None, 'cp')
- key_mask: int32 [4, 512], P(None, 'cp')
- rel_bias: float32 [32, 32], P(None, 'tp')
- g_attn: float32 [2, 2048], replicated
- g_mlp: float32 [2, 2048], replicated
- w_q: bfloat16 [2, 2048, 2048], P(None, None, 'tp')
- w_k: bfloat16 [2, 2048, 2048], P(None, None, 'tp')
- w_v: bfloat16 [2, 2048, 2048], P(None, None, 'tp')
- w_o: bfloat16 [2, 2048, 2048], P(None, 'tp')
- w_gate: bfloat16 [2, 2048, 5120], P(None, None, 'tp')
- w_lin: bfloat16 [2, 2048, 5120], P(None, None, 'tp')
- w_out: bfloat16 [2, 5120, 2048], P(None, 'tp')
Outputs:
- output 1: bfloat16 [4, 512, 2048], P(None, 'cp')
- output 2: float32 [32, 32], P(None, 'tp')
- output 3: float32 [2, 2048], replicated
- output 4: float32 [2, 2048], replicated
- output 5: bfloat16 [2, 2048, 2048], P(None, None, 'tp')
- output 6: bfloat16 [2, 2048, 2048], P(None, None, 'tp')
- output 7: bfloat16 [2, 2048, 2048], P(None, None, 'tp')
- output 8: bfloat16 [2, 2048, 2048], P(None, 'tp')
- output 9: bfloat16 [2, 2048, 5120], P(None, None, 'tp')
- output 10: bfloat16 [2, 2048, 5120], P(None, None, 'tp')
- output 11: bfloat16 [2, 5120, 2048], P(None, 'tp')
All inputs are finite; a program needn't handle non-finite values.
Results may differ from a plain program's by a relative error of at most 0.02.
Values are sent between devices in bfloat16 or wider.
A program may use at most 1 GiB of HBM per device.

v0:
```python
import jax
import jax.numpy as jnp
from jax import lax
from jax.sharding import PartitionSpec as P

NORM_EPS = 1e-6
MASK_NEG = -1e9


def rel_bucket(rel_pos):
    distance = jnp.minimum(jnp.abs(rel_pos), 128)
    distance_sq = distance * distance
    log_part = 8 + sum((distance_sq >= 64 * 2 ** power).astype(jnp.int32) for power in range(1, 8))
    return jnp.where(distance < 8, distance, log_part) + 16 * (rel_pos > 0).astype(jnp.int32)


def pair_bias(bias_table, q_block, k_block, blk_len):
    offsets = jnp.arange(blk_len)
    rel_pos = (k_block - q_block) * blk_len + offsets[None, :] - offsets[:, None]
    buckets = rel_bucket(rel_pos)
    return buckets, jnp.take(bias_table, buckets, axis=1)


def pair_scores(queries, key_blk, bias, key_add):
    scores = jnp.einsum('bqhd,bkhd->bhqk', queries, key_blk, preferred_element_type=jnp.float32)
    return scores + bias[None] + key_add[:, None, None, :]


def softmax_fold(state, queries, key_blk, val_blk, bias, key_add):
    run_max, run_sum, out_acc = state
    scores = pair_scores(queries, key_blk, bias, key_add)
    new_max = jnp.maximum(run_max, jnp.max(scores, axis=-1))
    rescale = jnp.exp(run_max - new_max)
    probs = jnp.exp(scores - new_max[..., None])
    new_sum = run_sum * rescale + jnp.sum(probs, axis=-1)
    weighted = jnp.einsum('bhqk,bkhd->bqhd', probs.astype(jnp.bfloat16), val_blk, preferred_element_type=jnp.float32)
    return new_max, new_sum, out_acc * jnp.transpose(rescale, (0, 2, 1))[..., None] + weighted


def pair_grads(queries, key_blk, val_blk, d_out, log_norm, row_dot, bias_table, key_add_all, q_block, k_block):
    batch, blk_len, heads, _ = queries.shape
    buckets, bias = pair_bias(bias_table, q_block, k_block, blk_len)
    key_add = lax.dynamic_slice_in_dim(key_add_all, k_block * blk_len, blk_len, axis=1)
    probs = jnp.exp(pair_scores(queries, key_blk, bias, key_add) - log_norm[..., None])
    d_probs = jnp.einsum('bqhd,bkhd->bhqk', d_out, val_blk, preferred_element_type=jnp.float32)
    d_scores = probs * (d_probs - row_dot[..., None])
    ds_low = d_scores.astype(jnp.bfloat16)
    dq_part = jnp.einsum('bhqk,bkhd->bqhd', ds_low, key_blk, preferred_element_type=jnp.float32)
    dk_part = jnp.einsum('bhqk,bqhd->bkhd', ds_low, queries, preferred_element_type=jnp.float32)
    dv_part = jnp.einsum('bhqk,bqhd->bkhd', probs.astype(jnp.bfloat16), d_out, preferred_element_type=jnp.float32)
    seg_ids = buckets.reshape(-1)
    n_buckets = bias_table.shape[1]
    bias_part = jax.vmap(lambda score_row: jax.ops.segment_sum(score_row, seg_ids, num_segments=n_buckets))(jnp.sum(d_scores, axis=0).reshape(heads, -1))
    return dq_part, dk_part, dv_part, bias_part


def attn_forward(queries, key_own, val_own, bias_table, key_add_all, cp_index, cp_size):
    batch, blk_len, heads, _ = queries.shape
    shift_pairs = [(device_pos, (device_pos + 1) % cp_size) for device_pos in range(cp_size)]

    def fold_from(state, key_blk, val_blk, k_block):
        _, bias = pair_bias(bias_table, cp_index, k_block, blk_len)
        key_add = lax.dynamic_slice_in_dim(key_add_all, k_block * blk_len, blk_len, axis=1)
        return softmax_fold(state, queries, key_blk, val_blk, bias, key_add)

    start_state = (jnp.full((batch, heads, blk_len), -jnp.inf, jnp.float32), jnp.zeros((batch, heads, blk_len), jnp.float32), jnp.zeros(queries.shape, jnp.float32))
    state = fold_from(start_state, key_own, val_own, cp_index)

    def step_body(step, carry):
        state, key_blk, val_blk = carry
        key_blk = lax.ppermute(key_blk, 'cp', shift_pairs)
        val_blk = lax.ppermute(val_blk, 'cp', shift_pairs)
        state = fold_from(state, key_blk, val_blk, (cp_index - step) % cp_size)
        return state, key_blk, val_blk

    state, _, _ = lax.fori_loop(1, cp_size, step_body, (state, key_own, val_own))
    run_max, run_sum, out_acc = state
    attn_out = out_acc / jnp.transpose(run_sum, (0, 2, 1))[..., None]
    return attn_out.astype(jnp.bfloat16), run_max + jnp.log(run_sum)


def attn_backward(queries, key_own, val_own, attn_out, d_out, log_norm, bias_table, key_add_all, cp_index, cp_size):
    shift_pairs = [(device_pos, (device_pos + 1) % cp_size) for device_pos in range(cp_size)]
    row_dot = jnp.einsum('bqhd,bqhd->bhq', d_out, attn_out, preferred_element_type=jnp.float32)

    def grads_from(key_blk, val_blk, k_block):
        return pair_grads(queries, key_blk, val_blk, d_out, log_norm, row_dot, bias_table, key_add_all, cp_index, k_block)

    dq_acc, dk_acc, dv_acc, bias_acc = grads_from(key_own, val_own, cp_index)

    def step_body(step, carry):
        dq_acc, bias_acc, key_blk, val_blk, dk_acc, dv_acc = carry
        key_blk = lax.ppermute(key_blk, 'cp', shift_pairs)
        val_blk = lax.ppermute(val_blk, 'cp', shift_pairs)
        dk_acc = lax.ppermute(dk_acc, 'cp', shift_pairs)
        dv_acc = lax.ppermute(dv_acc, 'cp', shift_pairs)
        dq_part, dk_part, dv_part, bias_part = grads_from(key_blk, val_blk, (cp_index - step) % cp_size)
        return dq_acc + dq_part, bias_acc + bias_part, key_blk, val_blk, dk_acc + dk_part, dv_acc + dv_part

    dq_acc, bias_acc, _, _, dk_acc, dv_acc = lax.fori_loop(1, cp_size, step_body, (dq_acc, bias_acc, key_own, val_own, dk_acc, dv_acc))
    dk_home = lax.ppermute(dk_acc, 'cp', shift_pairs)
    dv_home = lax.ppermute(dv_acc, 'cp', shift_pairs)
    return dq_acc.astype(jnp.bfloat16), dk_home.astype(jnp.bfloat16), dv_home.astype(jnp.bfloat16), bias_acc


def rms_parts(x_f, gain):
    inv_rms = lax.rsqrt(jnp.mean(x_f * x_f, axis=-1, keepdims=True) + NORM_EPS)
    return inv_rms, (x_f * inv_rms * gain).astype(jnp.bfloat16)


def rms_backward(d_norm, x_f, inv_rms, gain):
    normed = x_f * inv_rms
    d_gain = jnp.sum(d_norm * normed, axis=(0, 1))
    d_normed = d_norm * gain
    d_x = inv_rms * (d_normed - normed * jnp.mean(d_normed * normed, axis=-1, keepdims=True))
    return d_x, d_gain


def layer_forward(x_in, weights, bias_table, key_add_all, cp_index, cp_size):
    g_attn, g_mlp, w_q, w_k, w_v, w_o, w_gate, w_lin, w_out = weights
    batch, blk_len, _ = x_in.shape
    head_shape = (batch, blk_len, bias_table.shape[0], -1)
    x_f = x_in.astype(jnp.float32)
    inv_attn, h_attn = rms_parts(x_f, g_attn)
    queries = jnp.dot(h_attn, w_q, preferred_element_type=jnp.float32).astype(jnp.bfloat16).reshape(head_shape)
    key_own = jnp.dot(h_attn, w_k, preferred_element_type=jnp.float32).astype(jnp.bfloat16).reshape(head_shape)
    val_own = jnp.dot(h_attn, w_v, preferred_element_type=jnp.float32).astype(jnp.bfloat16).reshape(head_shape)
    attn_out, log_norm = attn_forward(queries, key_own, val_own, bias_table, key_add_all, cp_index, cp_size)
    attn_flat = attn_out.reshape(batch, blk_len, -1)
    after_attn = (x_f + lax.psum(jnp.dot(attn_flat, w_o, preferred_element_type=jnp.float32), 'tp')).astype(jnp.bfloat16)
    after_f = after_attn.astype(jnp.float32)
    inv_mlp, h_mlp = rms_parts(after_f, g_mlp)
    gate_pre = jnp.dot(h_mlp, w_gate, preferred_element_type=jnp.float32)
    lin_pre = jnp.dot(h_mlp, w_lin, preferred_element_type=jnp.float32)
    gated = (jax.nn.gelu(gate_pre, approximate=True) * lin_pre).astype(jnp.bfloat16)
    layer_out = (after_f + lax.psum(jnp.dot(gated, w_out, preferred_element_type=jnp.float32), 'tp')).astype(jnp.bfloat16)
    saved = (x_in, inv_attn, h_attn, queries, key_own, val_own, attn_out, log_norm, after_attn, inv_mlp, h_mlp, gate_pre, lin_pre, gated)
    return layer_out, saved


def layer_backward(d_layer, saved, weights, bias_table, key_add_all, cp_index, cp_size):
    g_attn, g_mlp, w_q, w_k, w_v, w_o, w_gate, w_lin, w_out = weights
    x_in, inv_attn, h_attn, queries, key_own, val_own, attn_out, log_norm, after_attn, inv_mlp, h_mlp, gate_pre, lin_pre, gated = saved
    batch, blk_len, _ = x_in.shape
    d_low = d_layer.astype(jnp.bfloat16)
    d_w_out = jnp.einsum('bsf,bsd->fd', gated, d_low, preferred_element_type=jnp.float32)
    d_gated = jnp.einsum('bsd,fd->bsf', d_low, w_out, preferred_element_type=jnp.float32)
    gelu_val, gelu_pull = jax.vjp(lambda gate_in: jax.nn.gelu(gate_in, approximate=True), gate_pre)
    d_lin = (d_gated * gelu_val).astype(jnp.bfloat16)
    d_gate = gelu_pull(d_gated * lin_pre)[0].astype(jnp.bfloat16)
    d_w_gate = jnp.einsum('bsd,bsf->df', h_mlp, d_gate, preferred_element_type=jnp.float32)
    d_w_lin = jnp.einsum('bsd,bsf->df', h_mlp, d_lin, preferred_element_type=jnp.float32)
    d_h_mlp = (jnp.einsum('bsf,df->bsd', d_gate, w_gate, preferred_element_type=jnp.float32)
               + jnp.einsum('bsf,df->bsd', d_lin, w_lin, preferred_element_type=jnp.float32))
    d_mid, d_g_mlp = rms_backward(lax.psum(d_h_mlp, 'tp'), after_attn.astype(jnp.float32), inv_mlp, g_mlp)
    d_mid = d_mid + d_layer
    d_mid_low = d_mid.astype(jnp.bfloat16)
    attn_flat = attn_out.reshape(batch, blk_len, -1)
    d_w_o = jnp.einsum('bsn,bsd->nd', attn_flat, d_mid_low, preferred_element_type=jnp.float32)
    d_out = jnp.einsum('bsd,nd->bsn', d_mid_low, w_o, preferred_element_type=jnp.float32).astype(jnp.bfloat16).reshape(attn_out.shape)
    d_q, d_k, d_v, d_bias = attn_backward(queries, key_own, val_own, attn_out, d_out, log_norm, bias_table, key_add_all, cp_index, cp_size)
    flat_shape = (batch, blk_len, -1)
    d_q = d_q.reshape(flat_shape)
    d_k = d_k.reshape(flat_shape)
    d_v = d_v.reshape(flat_shape)
    d_w_q = jnp.einsum('bsd,bsn->dn', h_attn, d_q, preferred_element_type=jnp.float32)
    d_w_k = jnp.einsum('bsd,bsn->dn', h_attn, d_k, preferred_element_type=jnp.float32)
    d_w_v = jnp.einsum('bsd,bsn->dn', h_attn, d_v, preferred_element_type=jnp.float32)
    d_h_attn = (jnp.einsum('bsn,dn->bsd', d_q, w_q, preferred_element_type=jnp.float32)
                + jnp.einsum('bsn,dn->bsd', d_k, w_k, preferred_element_type=jnp.float32)
                + jnp.einsum('bsn,dn->bsd', d_v, w_v, preferred_element_type=jnp.float32))
    d_x, d_g_attn = rms_backward(lax.psum(d_h_attn, 'tp'), x_in.astype(jnp.float32), inv_attn, g_attn)
    grads = (d_g_attn, d_g_mlp, d_w_q, d_w_k, d_w_v, d_w_o, d_w_gate, d_w_lin, d_w_out)
    return d_x + d_mid, grads, d_bias


def solution(mesh):
    cp_size = mesh.shape['cp']
    seq_spec = P(None, 'cp', None)
    col_spec = P(None, None, 'tp')
    row_spec = P(None, 'tp', None)
    weight_specs = (P(), P(), col_spec, col_spec, col_spec, row_spec, col_spec, col_spec, row_spec)

    def local_program(x_in, d_y, key_mask, rel_bias, g_attn, g_mlp, w_q, w_k, w_v, w_o, w_gate, w_lin, w_out):
        cp_index = lax.axis_index('cp')
        mask_all = lax.all_gather(key_mask, 'cp', axis=1, tiled=True)
        key_add_all = jnp.where(mask_all > 0, 0.0, MASK_NEG).astype(jnp.float32)
        bias_table = rel_bias.T
        stacks = (g_attn, g_mlp, w_q, w_k, w_v, w_o, w_gate, w_lin, w_out)
        layer_weights = [tuple(stack[layer] for stack in stacks) for layer in range(w_q.shape[0])]
        hidden = x_in
        saved_all = []
        for weights in layer_weights:
            hidden, saved = layer_forward(hidden, weights, bias_table, key_add_all, cp_index, cp_size)
            saved_all.append(saved)
        grad = d_y.astype(jnp.float32)
        bias_grad = jnp.zeros(bias_table.shape, jnp.float32)
        layer_grads = []
        for layer in reversed(range(len(layer_weights))):
            grad, grads, d_bias = layer_backward(grad, saved_all[layer], layer_weights[layer], bias_table, key_add_all, cp_index, cp_size)
            layer_grads.insert(0, grads)
            bias_grad = bias_grad + d_bias
        summed = [lax.psum(jnp.stack([grads[which] for grads in layer_grads]), 'cp') for which in range(len(stacks))]
        return tuple([grad.astype(jnp.bfloat16), lax.psum(bias_grad, 'cp').T, summed[0], summed[1]] + [part.astype(jnp.bfloat16) for part in summed[2:]])

    return jax.shard_map(local_program, mesh=mesh, in_specs=(seq_spec, seq_spec, P(None, 'cp'), P(None, 'tp')) + weight_specs, out_specs=(seq_spec, P(None, 'tp')) + weight_specs, check_vma=False)
```

profile of v0, /device:TPU:0, one launch (start us, length us, event | category | flops | bytes accessed | tf_op | source)
XLA Modules:
  0.0 3872.4 jit_solution(7080688984718601813)
XLA Ops:
  9.7 6.2 all_gather.3
  27.8 54.8 %gather_fusion.4 = f32[16384,4]{1,0:T(8,128)} fusion(f32[4,32]{0,1:T(8,128)S(1)} %bitcast.503, s32[16384]{0:T(1024)S(1)} %bitcast_clamp_fusion.4), kind=kCustom, calls=%fused_computation.4.clone | custom fusion | bytes 589824 | tf_op jit(solution)/shard_map/jit(_take)/gather | solution.py:21
  82.5 6.6 copy.226
  91.8 202.6 %while.96 = (s32[]{:T(128)}, f32[4,4,128]{2,1,0:T(4,128)S(1)}, f32[4,4,128]{2,1,0:T(4,128)S(1)}, f32[4,128,4,64]{1,3,2,0:T(8,128)S(1)}, bf16[4,128,4,64]{1,3,2,0...) while((s32[]{:T(128)}, f32[4,4,128]{2,1,0:T(4,128)S(1)}, ...), condition=%wide.region_6.8_spmd, body=%wide.region_3.0_spmd.sunk | while | flops 70424720 | bytes 10297260 | solution.py:76
  94.4 54.8 %gather_fusion = f32[16384,4]{1,0:T(8,128)} fusion(f32[4,32]{0,1:T(8,128)S(1)} %get-tuple-element.1768, s32[16384]{0:T(1024)S(1)} %bitcast_clamp_fusion.9), kind=kCustom, calls=%fused_computation.clone.clone.1 | custom fusion | bytes 589824 | tf_op jit(solution)/shard_map/while/body/eval_jaxpr/jit(_take)/gather | solution.py:21
  149.1 6.6 copy.347
  160.8 54.8 %gather_fusion = f32[16384,4]{1,0:T(8,128)} fusion(f32[4,32]{0,1:T(8,128)S(1)} %get-tuple-element.1768, s32[16384]{0:T(1024)S(1)} %bitcast_clamp_fusion.9), kind=kCustom, calls=%fused_computation.clone.clone.1 | custom fusion | bytes 589824 | tf_op jit(solution)/shard_map/while/body/eval_jaxpr/jit(_take)/gather | solution.py:21
  215.6 6.6 copy.347
  228.8 54.8 %gather_fusion = f32[16384,4]{1,0:T(8,128)} fusion(f32[4,32]{0,1:T(8,128)S(1)} %get-tuple-element.1768, s32[16384]{0:T(1024)S(1)} %bitcast_clamp_fusion.9), kind=kCustom, calls=%fused_computation.clone.clone.1 | custom fusion | bytes 589824 | tf_op jit(solution)/shard_map/while/body/eval_jaxpr/jit(_take)/gather | solution.py:21
  283.5 6.6 copy.347
  299.7 155.4 %all-reduce.10.cloned.1.call-done = f32[4,128,2048]{2,1,0:T(8,128)} async-done(((f32[4,128,2048]{2,1,0:T(8,128)}), f32[4,128,2048]{2,1,0:T(8,128)}) %all-reduce.10.cloned.1.call-update) | async-done | bytes 4194320 | tf_op jit(solution)/shard_map/psum | solution.py:130
  458.2 4.4 fusion.142
  470.4 154.5 %all-reduce.12.cloned.1.call-done = f32[4,128,2048]{2,1,0:T(8,128)} async-done(((f32[4,128,2048]{2,1,0:T(8,128)}), f32[4,128,2048]{2,1,0:T(8,128)}) %all-reduce.12.cloned.1.call-update) | async-done | bytes 4194320 | tf_op jit(solution)/shard_map/psum | solution.py:136
  636.7 192.2 %while.97 = (s32[]{:T(128)}, f32[4,4,128]{2,1,0:T(4,128)S(1)}, f32[4,4,128]{2,1,0:T(4,128)S(1)}, f32[4,128,4,64]{1,3,2,0:T(8,128)S(1)}, bf16[4,128,4,64]{1,3,2,0...) while((s32[]{:T(128)}, f32[4,4,128]{2,1,0:T(4,128)S(1)}, ...), condition=%wide.region_16.18_spmd, body=%wide.region_13.17_spmd.sunk | while | flops 70424720 | bytes 10297260 | solution.py:76
  638.7 54.8 %gather_fusion.1 = f32[16384,4]{1,0:T(8,128)} fusion(f32[4,32]{0,1:T(8,128)S(1)} %get-tuple-element.1816, s32[16384]{0:T(1024)S(1)} %bitcast_clamp_fusion.10), kind=kCustom, calls=%fused_computation.1.clone.clone.1 | custom fusion | bytes 589824 | tf_op jit(solution)/shard_map/while/body/eval_jaxpr/jit(_take)/gather | solution.py:21
  693.5 6.6 copy.349
  702.2 54.8 %gather_fusion.1 = f32[16384,4]{1,0:T(8,128)} fusion(f32[4,32]{0,1:T(8,128)S(1)} %get-tuple-element.1816, s32[16384]{0:T(1024)S(1)} %bitcast_clamp_fusion.10), kind=kCustom, calls=%fused_computation.1.clone.clone.1 | custom fusion | bytes 589824 | tf_op jit(solution)/shard_map/while/body/eval_jaxpr/jit(_take)/gather | solution.py:21
  757.0 6.6 copy.349
  766.6 54.8 %gather_fusion.1 = f32[16384,4]{1,0:T(8,128)} fusion(f32[4,32]{0,1:T(8,128)S(1)} %get-tuple-element.1816, s32[16384]{0:T(1024)S(1)} %bitcast_clamp_fusion.10), kind=kCustom, calls=%fused_computation.1.clone.clone.1 | custom fusion | bytes 589824 | tf_op jit(solution)/shard_map/while/body/eval_jaxpr/jit(_take)/gather | solution.py:21
  821.4 6.6 copy.349
  834.2 153.2 %all-reduce.14.cloned.1.call-done = f32[4,128,2048]{2,1,0:T(8,128)} async-done(((f32[4,128,2048]{2,1,0:T(8,128)}), f32[4,128,2048]{2,1,0:T(8,128)}) %all-reduce.14.cloned.1.call-update) | async-done | bytes 4194320 | tf_op jit(solution)/shard_map/psum | solution.py:130
  991.2 4.4 fusion.126
  1007.1 153.8 %all-reduce.16.cloned.1.call-done = f32[4,128,2048]{2,1,0:T(8,128)} async-done(((f32[4,128,2048]{2,1,0:T(8,128)}), f32[4,128,2048]{2,1,0:T(8,128)}) %all-reduce.16.cloned.1.call-update) | async-done | bytes 4194320 | tf_op jit(solution)/shard_map/psum | solution.py:155
  1160.9 4.8 fusion.97
  1177.6 5.1 copy.239
  1182.7 101.5 %scatter_custom_fusion.2 = f32[4,32]{0,1:T(8,128)S(1)} fusion(s32[16384]{0:T(1024)S(1)} %bitcast.622, f32[16384,4]{1,0:T(8,128)} %copy.239, f32[]{:T(128)} %constant.635.clone.1), kind=kCustom, calls=%fused_computation.435 | custom fusion | flops 65536 | bytes 1024 | tf_op jit(solution)/shard_map/vmap()/scatter-add | solution.py:53
  1284.2 563.7 %while.98 = (s32[]{:T(128)}, f32[4,128,4,64]{1,3,2,0:T(8,128)S(1)}, f32[4,32]{0,1:T(8,128)S(1)}, bf16[4,128,4,64]{1,3,2,0:T(8,128)(2,1)}, bf16[4,128,4,64]{1,3,2...) while((s32[]{:T(128)}, f32[4,128,4,64]{1,3,2,0:T(8,128)S(1)}, ...), condition=%wide.region_26.28_spmd, body=%wide.region_23.27_spmd.sunk | while | flops 171966608 | bytes 21029404 | solution.py:100
  1287.2 54.8 %gather_fusion.2 = f32[16384,4]{1,0:T(8,128)} fusion(f32[4,32]{0,1:T(8,128)S(1)} %get-tuple-element.1873, s32[16384]{0:T(1024)S(1)} %bitcast_clamp_fusion.11), kind=kCustom, calls=%fused_computation.2.clone.clone.1 | custom fusion | bytes 589824 | tf_op jit(solution)/shard_map/while/body/eval_jaxpr/jit(_take)/gather | solution.py:21
  1342.0 5.2 copy.351
  1348.3 4.7 copy.352
  1353.1 113.5 %scatter_fusion = f32[4,32]{0,1:T(8,128)S(1)} fusion(f32[4,32]{0,1:T(8,128)S(1)} %get-tuple-element.1846, s32[16384]{0:T(1024)S(1)} %bitcast.524, f32[16384,4]{1,0:T(8,128)} %bitcast.505), kind=kCustom, calls=%fused_computation.5.clone.1 | custom fusion | flops 65536 | bytes 851968 | tf_op jit(solution)/shard_map/while/body/eval_jaxpr/vmap()/scatter-add | solution.py:53
  1475.7 54.8 %gather_fusion.2 = f32[16384,4]{1,0:T(8,128)} fusion(f32[4,32]{0,1:T(8,128)S(1)} %get-tuple-element.1873, s32[16384]{0:T(1024)S(1)} %bitcast_clamp_fusion.11), kind=kCustom, calls=%fused_computation.2.clone.clone.1 | custom fusion | bytes 589824 | tf_op jit(solution)/shard_map/while/body/eval_jaxpr/jit(_take)/gather | solution.py:21
  1530.4 5.2 copy.351
  1536.8 4.7 copy.352
  1541.5 113.5 %scatter_fusion = f32[4,32]{0,1:T(8,128)S(1)} fusion(f32[4,32]{0,1:T(8,128)S(1)} %get-tuple-element.1846, s32[16384]{0:T(1024)S(1)} %bitcast.524, f32[16384,4]{1,0:T(8,128)} %bitcast.505), kind=kCustom, calls=%fused_computation.5.clone.1 | custom fusion | flops 65536 | bytes 851968 | tf_op jit(solution)/shard_map/while/body/eval_jaxpr/vmap()/scatter-add | solution.py:53
  1664.1 54.8 %gather_fusion.2 = f32[16384,4]{1,0:T(8,128)} fusion(f32[4,32]{0,1:T(8,128)S(1)} %get-tuple-element.1873, s32[16384]{0:T(1024)S(1)} %bitcast_clamp_fusion.11), kind=kCustom, calls=%fused_computation.2.clone.clone.1 | custom fusion | bytes 589824 | tf_op jit(solution)/shard_map/while/body/eval_jaxpr/jit(_take)/gather | solution.py:21
  1718.9 5.2 copy.351
  1725.3 4.7 copy.352
  1730.0 111.8 %scatter_fusion = f32[4,32]{0,1:T(8,128)S(1)} fusion(f32[4,32]{0,1:T(8,128)S(1)} %get-tuple-element.1846, s32[16384]{0:T(1024)S(1)} %bitcast.524, f32[16384,4]{1,0:T(8,128)} %bitcast.505), kind=kCustom, calls=%fused_computation.5.clone.1 | custom fusion | flops 65536 | bytes 851968 | tf_op jit(solution)/shard_map/while/body/eval_jaxpr/vmap()/scatter-add | solution.py:53
  1862.0 153.3 %all-reduce.18.cloned.1.call-done = f32[4,128,2048]{2,1,0:T(8,128)} async-done(((f32[4,128,2048]{2,1,0:T(8,128)}), f32[4,128,2048]{2,1,0:T(8,128)}) %all-reduce.18.cloned.1.call-update) | async-done | bytes 4194320 | tf_op jit(solution)/shard_map/psum | solution.py:172
  2015.4 4.2 fusion.121
  2034.8 6.0 convolution_bitcast_fusion.10
  2040.9 4.3 convolution_bitcast_fusion.12
  2062.1 4.9 pad_maximum_fusion.2
  2066.9 121.4 %all-reduce.20.cloned.1.call-done = f32[4,128,2048]{2,1,0:T(8,128)} async-done(((f32[4,128,2048]{2,1,0:T(8,128)}), f32[4,128,2048]{2,1,0:T(8,128)}) %all-reduce.20.cloned.1.call-update) | async-done | bytes 4194320 | tf_op jit(solution)/shard_map/psum | solution.py:155
  2204.4 5.1 copy.249
  2209.5 101.3 %scatter_custom_fusion.3 = f32[4,32]{0,1:T(8,128)S(1)} fusion(s32[16384]{0:T(1024)} %bitcast.623, f32[16384,4]{1,0:T(8,128)} %copy.249, f32[]{:T(128)} %constant.635.clone.1), kind=kCustom, calls=%fused_computation.433 | custom fusion | flops 65536 | bytes 1024 | tf_op jit(solution)/shard_map/vmap()/scatter-add | solution.py:53
  2310.9 563.8 %while.99 = (s32[]{:T(128)}, f32[4,128,4,64]{1,3,2,0:T(8,128)S(1)}, f32[4,32]{0,1:T(8,128)S(1)}, bf16[4,128,4,64]{1,3,2,0:T(8,128)(2,1)}, bf16[4,128,4,64]{1,3,2...) while((s32[]{:T(128)}, f32[4,128,4,64]{1,3,2,0:T(8,128)S(1)}, ...), condition=%wide.region_36.38_spmd, body=%wide.region_33.37_spmd.sunk | while | flops 171966608 | bytes 21029404 | solution.py:100
  2313.9 54.8 %gather_fusion.3 = f32[16384,4]{1,0:T(8,128)} fusion(f32[4,32]{0,1:T(8,128)S(1)} %get-tuple-element.1933, s32[16384]{0:T(1024)S(1)} %bitcast_clamp_fusion.12), kind=kCustom, calls=%fused_computation.3.clone.clone.1 | custom fusion | bytes 589824 | tf_op jit(solution)/shard_map/while/body/eval_jaxpr/jit(_take)/gather | solution.py:21
  2368.7 5.2 copy.353
  2375.0 4.7 copy.354
  2379.8 113.5 %scatter_fusion.1 = f32[4,32]{0,1:T(8,128)S(1)} fusion(f32[4,32]{0,1:T(8,128)S(1)} %get-tuple-element.1906, s32[16384]{0:T(1024)S(1)} %bitcast.525, f32[16384,4]{1,0:T(8,128)} %bitcast.506), kind=kCustom, calls=%fused_computation.6.clone.1 | custom fusion | flops 65536 | bytes 851968 | tf_op jit(solution)/shard_map/while/body/eval_jaxpr/vmap()/scatter-add | solution.py:53
  2502.4 54.8 %gather_fusion.3 = f32[16384,4]{1,0:T(8,128)} fusion(f32[4,32]{0,1:T(8,128)S(1)} %get-tuple-element.1933, s32[16384]{0:T(1024)S(1)} %bitcast_clamp_fusion.12), kind=kCustom, calls=%fused_computation.3.clone.clone.1 | custom fusion | bytes 589824 | tf_op jit(solution)/shard_map/while/body/eval_jaxpr/jit(_take)/gather | solution.py:21
  2557.2 5.2 copy.353
  2563.5 4.7 copy.354
  2568.3 113.5 %scatter_fusion.1 = f32[4,32]{0,1:T(8,128)S(1)} fusion(f32[4,32]{0,1:T(8,128)S(1)} %get-tuple-element.1906, s32[16384]{0:T(1024)S(1)} %bitcast.525, f32[16384,4]{1,0:T(8,128)} %bitcast.506), kind=kCustom, calls=%fused_computation.6.clone.1 | custom fusion | flops 65536 | bytes 851968 | tf_op jit(solution)/shard_map/while/body/eval_jaxpr/vmap()/scatter-add | solution.py:53
  2690.9 54.8 %gather_fusion.3 = f32[16384,4]{1,0:T(8,128)} fusion(f32[4,32]{0,1:T(8,128)S(1)} %get-tuple-element.1933, s32[16384]{0:T(1024)S(1)} %bitcast_clamp_fusion.12), kind=kCustom, calls=%fused_computation.3.clone.clone.1 | custom fusion | bytes 589824 | tf_op jit(solution)/shard_map/while/body/eval_jaxpr/jit(_take)/gather | solution.py:21
  2745.7 5.2 copy.353
  2752.0 4.7 copy.354
  2756.8 111.8 %scatter_fusion.1 = f32[4,32]{0,1:T(8,128)S(1)} fusion(f32[4,32]{0,1:T(8,128)S(1)} %get-tuple-element.1906, s32[16384]{0:T(1024)S(1)} %bitcast.525, f32[16384,4]{1,0:T(8,128)} %bitcast.506), kind=kCustom, calls=%fused_computation.6.clone.1 | custom fusion | flops 65536 | bytes 851968 | tf_op jit(solution)/shard_map/while/body/eval_jaxpr/vmap()/scatter-add | solution.py:53
  2894.8 8.0 pad_maximum_fusion
  2917.7 124.6 %all-reduce.22.cloned.1.call-done = f32[4,128,2048]{2,1,0:T(8,128)} async-done(((f32[4,128,2048]{2,1,0:T(8,128)}), f32[4,128,2048]{2,1,0:T(8,128)}) %all-reduce.22.cloned.1.call-update) | async-done | bytes 4194320 | tf_op jit(solution)/shard_map/psum | solution.py:172
  3045.8 813.4 %all-reduce.23 = (f32[32,4]{0,1:T(4,128)}, f32[2,2048]{1,0:T(2,128)}, f32[2,2048]{1,0:T(2,128)}, bf16[2,2048,256]{2,1,0:T(8,128)(2,1)}, bf16[2,2048,256]{2,1,0:T...) all-reduce(f32[32,4]{0,1:T(4,128)S(1)} %add_bitcast_fusion, ...), channel_id=1, replica_groups=mesh['tp'=8,'cp'=4] {'cp'}, use_global_device_ids=true, to_apply=%region_39.41 | all-reduce | flops 12066944 | bytes 72418304 | tf_op jit(solution)/shard_map/psum | solution.py:204
  3859.2 5.9 fusion.104
  (603 shorter events, 264.0 us)
Async XLA Ops:
  7.2 447.9 %all-reduce.10.cloned.1.call-start = ((), (), s32[]{:S(2)}) async-start(), calls=%async_computation | async-start | bytes 8388608 | tf_op jit(solution)/shard_map/psum | solution.py:130
  7.4 12.9 copy-start.10
  9.7 15.2 copy-start.74
  27.0 62.7 %copy-start.31 = (bf16[4,128,256]{1,2,0:T(8,128)(2,1)}, bf16[4,128,256]{1,2,0:T(8,128)(2,1)S(1)}, u32[]{:S(2)}) copy-start(bf16[4,128,256]{1,2,0:T(8,128)(2,1)S(1)} %copy.222) | copy-start | bytes 786436
  91.8 67.2 %collective-permute-start.1 = (bf16[4,128,4,64]{1,3,2,0:T(8,128)(2,1)}, bf16[4,128,4,64]{1,3,2,0:T(8,128)(2,1)S(1)}, u32[]{:S(2)}, u32[]{:S(2)}) collective-permute-start(bf16[4,128,4,64]{1,3,2,0:T(8,128)(2,1)} %get-tuple-element.1749), channel_id=1, source_target_pairs={{0,1},{1,2},{2,3},{3,0},{4,5},{5,6},{6,7},{7,4},{8,9},{9,10},{10,1... | collective-permute-start | bytes 786440 | tf_op jit(solution)/shard_map/while/body/eval_jaxpr/ppermute | solution.py:72
  92.2 63.5 %collective-permute-start = (bf16[4,128,4,64]{1,3,2,0:T(8,128)(2,1)}, bf16[4,128,4,64]{1,3,2,0:T(8,128)(2,1)}, u32[]{:S(2)}, u32[]{:S(2)}) collective-permute-start(bf16[4,128,4,64]{1,3,2,0:T(8,128)(2,1)} %get-tuple-element.1748), channel_id=1, source_target_pairs={{0,1},{1,2},{2,3},{3,0},{4,5},{5,6},{6,7},{7,4},{8,9},{9,10},{10,1... | collective-permute-start | bytes 786440 | tf_op jit(solution)/shard_map/while/body/eval_jaxpr/ppermute | solution.py:71
  160.0 65.4 %collective-permute-start.1 = (bf16[4,128,4,64]{1,3,2,0:T(8,128)(2,1)}, bf16[4,128,4,64]{1,3,2,0:T(8,128)(2,1)S(1)}, u32[]{:S(2)}, u32[]{:S(2)}) collective-permute-start(bf16[4,128,4,64]{1,3,2,0:T(8,128)(2,1)} %get-tuple-element.1749), channel_id=1, source_target_pairs={{0,1},{1,2},{2,3},{3,0},{4,5},{5,6},{6,7},{7,4},{8,9},{9,10},{10,1... | collective-permute-start | bytes 786440 | tf_op jit(solution)/shard_map/while/body/eval_jaxpr/ppermute | solution.py:72
  160.4 61.8 %collective-permute-start = (bf16[4,128,4,64]{1,3,2,0:T(8,128)(2,1)}, bf16[4,128,4,64]{1,3,2,0:T(8,128)(2,1)}, u32[]{:S(2)}, u32[]{:S(2)}) collective-permute-start(bf16[4,128,4,64]{1,3,2,0:T(8,128)(2,1)} %get-tuple-element.1748), channel_id=1, source_target_pairs={{0,1},{1,2},{2,3},{3,0},{4,5},{5,6},{6,7},{7,4},{8,9},{9,10},{10,1... | collective-permute-start | bytes 786440 | tf_op jit(solution)/shard_map/while/body/eval_jaxpr/ppermute | solution.py:71
  226.5 66.9 %collective-permute-start.1 = (bf16[4,128,4,64]{1,3,2,0:T(8,128)(2,1)}, bf16[4,128,4,64]{1,3,2,0:T(8,128)(2,1)S(1)}, u32[]{:S(2)}, u32[]{:S(2)}) collective-permute-start(bf16[4,128,4,64]{1,3,2,0:T(8,128)(2,1)} %get-tuple-element.1749), channel_id=1, source_target_pairs={{0,1},{1,2},{2,3},{3,0},{4,5},{5,6},{6,7},{7,4},{8,9},{9,10},{10,1... | collective-permute-start | bytes 786440 | tf_op jit(solution)/shard_map/while/body/eval_jaxpr/ppermute | solution.py:72
  226.6 63.5 %collective-permute-start = (bf16[4,128,4,64]{1,3,2,0:T(8,128)(2,1)}, bf16[4,128,4,64]{1,3,2,0:T(8,128)(2,1)}, u32[]{:S(2)}, u32[]{:S(2)}) collective-permute-start(bf16[4,128,4,64]{1,3,2,0:T(8,128)(2,1)} %get-tuple-element.1748), channel_id=1, source_target_pairs={{0,1},{1,2},{2,3},{3,0},{4,5},{5,6},{6,7},{7,4},{8,9},{9,10},{10,1... | collective-permute-start | bytes 786440 | tf_op jit(solution)/shard_map/while/body/eval_jaxpr/ppermute | solution.py:71
  294.4 168.1 %copy-start.57 = (f32[4,4,128]{2,1,0:T(4,128)}, f32[4,4,128]{2,1,0:T(4,128)S(1)}, u32[]{:S(2)}) copy-start(f32[4,4,128]{2,1,0:T(4,128)S(1)} %get-tuple-element.1171) | copy-start | bytes 24580
  299.4 325.5 %all-reduce.12.cloned.1.call-start = ((), (), s32[]{:S(2)}) async-start(), calls=%async_computation.1 | async-start | bytes 8388608 | tf_op jit(solution)/shard_map/psum | solution.py:136
  299.7 162.9 %copy-start.69 = (f32[1,2048]{1,0:T(1,128)}, f32[1,2048]{1,0:T(1,128)S(1)}, u32[]{:S(2)}) copy-start(f32[1,2048]{1,0:T(1,128)S(1)} %get-tuple-element.1373) | copy-start | bytes 24580
  466.5 158.4 %copy-start.13 = (bf16[4,128,2048]{2,1,0:T(8,128)(2,1)S(1)}, bf16[4,128,2048]{2,1,0:T(8,128)(2,1)}, u32[]{:S(2)}) copy-start(bf16[4,128,2048]{2,1,0:T(8,128)(2,1)} %copy-done.12) | copy-start | bytes 6291460
  470.4 517.0 %all-reduce.14.cloned.1.call-start = ((), (), s32[]{:S(2)}) async-start(), calls=%async_computation.2 | async-start | bytes 8388608 | tf_op jit(solution)/shard_map/psum | solution.py:130
  636.7 64.0 %collective-permute-start.3 = (bf16[4,128,4,64]{1,3,2,0:T(8,128)(2,1)S(1)}, bf16[4,128,4,64]{1,3,2,0:T(8,128)(2,1)S(1)}, u32[]{:S(2)}, u32[]{:S(2)}) collective-permute-start(bf16[4,128,4,64]{1,3,2,0:T(8,128)(2,1)S(1)} %get-tuple-element.1797), channel_id=1, source_target_pairs={{0,1},{1,2},{2,3},{3,0},{4,5},{5,6},{6,7},{7,4},{8,9},{9,10},{10,1... | collective-permute-start | bytes 786440 | tf_op jit(solution)/shard_map/while/body/eval_jaxpr/ppermute | solution.py:72
  636.8 63.3 %collective-permute-start.2 = (bf16[4,128,4,64]{1,3,2,0:T(8,128)(2,1)S(1)}, bf16[4,128,4,64]{1,3,2,0:T(8,128)(2,1)S(1)}, u32[]{:S(2)}, u32[]{:S(2)}) collective-permute-start(bf16[4,128,4,64]{1,3,2,0:T(8,128)(2,1)S(1)} %get-tuple-element.1796), channel_id=1, source_target_pairs={{0,1},{1,2},{2,3},{3,0},{4,5},{5,6},{6,7},{7,4},{8,9},{9,10},{10,1... | collective-permute-start | bytes 786440 | tf_op jit(solution)/shard_map/while/body/eval_jaxpr/ppermute | solution.py:71
  701.1 63.1 %collective-permute-start.3 = (bf16[4,128,4,64]{1,3,2,0:T(8,128)(2,1)S(1)}, bf16[4,128,4,64]{1,3,2,0:T(8,128)(2,1)S(1)}, u32[]{:S(2)}, u32[]{:S(2)}) collective-permute-start(bf16[4,128,4,64]{1,3,2,0:T(8,128)(2,1)S(1)} %get-tuple-element.1797), channel_id=1, source_target_pairs={{0,1},{1,2},{2,3},{3,0},{4,5},{5,6},{6,7},{7,4},{8,9},{9,10},{10,1... | collective-permute-start | bytes 786440 | tf_op jit(solution)/shard_map/while/body/eval_jaxpr/ppermute | solution.py:72
  701.2 62.3 %collective-permute-start.2 = (bf16[4,128,4,64]{1,3,2,0:T(8,128)(2,1)S(1)}, bf16[4,128,4,64]{1,3,2,0:T(8,128)(2,1)S(1)}, u32[]{:S(2)}, u32[]{:S(2)}) collective-permute-start(bf16[4,128,4,64]{1,3,2,0:T(8,128)(2,1)S(1)} %get-tuple-element.1796), channel_id=1, source_target_pairs={{0,1},{1,2},{2,3},{3,0},{4,5},{5,6},{6,7},{7,4},{8,9},{9,10},{10,1... | collective-permute-start | bytes 786440 | tf_op jit(solution)/shard_map/while/body/eval_jaxpr/ppermute | solution.py:71
  764.6 64.0 %collective-permute-start.3 = (bf16[4,128,4,64]{1,3,2,0:T(8,128)(2,1)S(1)}, bf16[4,128,4,64]{1,3,2,0:T(8,128)(2,1)S(1)}, u32[]{:S(2)}, u32[]{:S(2)}) collective-permute-start(bf16[4,128,4,64]{1,3,2,0:T(8,128)(2,1)S(1)} %get-tuple-element.1797), channel_id=1, source_target_pairs={{0,1},{1,2},{2,3},{3,0},{4,5},{5,6},{6,7},{7,4},{8,9},{9,10},{10,1... | collective-permute-start | bytes 786440 | tf_op jit(solution)/shard_map/while/body/eval_jaxpr/ppermute | solution.py:72
  764.7 63.3 %collective-permute-start.2 = (bf16[4,128,4,64]{1,3,2,0:T(8,128)(2,1)S(1)}, bf16[4,128,4,64]{1,3,2,0:T(8,128)(2,1)S(1)}, u32[]{:S(2)}, u32[]{:S(2)}) collective-permute-start(bf16[4,128,4,64]{1,3,2,0:T(8,128)(2,1)S(1)} %get-tuple-element.1796), channel_id=1, source_target_pairs={{0,1},{1,2},{2,3},{3,0},{4,5},{5,6},{6,7},{7,4},{8,9},{9,10},{10,1... | collective-permute-start | bytes 786440 | tf_op jit(solution)/shard_map/while/body/eval_jaxpr/ppermute | solution.py:71
  833.7 327.2 %all-reduce.16.cloned.1.call-start = ((), (), s32[]{:S(2)}) async-start(), calls=%async_computation.3 | async-start | bytes 8388608 | tf_op jit(solution)/shard_map/psum | solution.py:155
  1006.4 1009.0 %all-reduce.18.cloned.1.call-start = ((), (), s32[]{:S(2)}) async-start(), calls=%async_computation.4 | async-start | bytes 8388608 | tf_op jit(solution)/shard_map/psum | solution.py:172
  1007.1 175.6 %copy-start.71 = (s32[16384,1]{0,1:T(1,128)}, s32[16384,1]{0,1:T(1,128)S(1)}, u32[]{:S(2)}) copy-start(s32[16384,1]{0,1:T(1,128)S(1)} %fusion.255) | copy-start | bytes 196612
  1284.2 63.6 %collective-permute-start.5 = (bf16[4,128,4,64]{1,3,2,0:T(8,128)(2,1)}, bf16[4,128,4,64]{1,3,2,0:T(8,128)(2,1)S(1)}, u32[]{:S(2)}, u32[]{:S(2)}) collective-permute-start(bf16[4,128,4,64]{1,3,2,0:T(8,128)(2,1)} %get-tuple-element.1848), channel_id=1, source_target_pairs={{0,1},{1,2},{2,3},{3,0},{4,5},{5,6},{6,7},{7,4},{8,9},{9,10},{10,1... | collective-permute-start | bytes 786440 | tf_op jit(solution)/shard_map/while/body/eval_jaxpr/ppermute | solution.py:94
  1284.3 63.0 %collective-permute-start.4 = (bf16[4,128,4,64]{1,3,2,0:T(8,128)(2,1)}, bf16[4,128,4,64]{1,3,2,0:T(8,128)(2,1)S(1)}, u32[]{:S(2)}, u32[]{:S(2)}) collective-permute-start(bf16[4,128,4,64]{1,3,2,0:T(8,128)(2,1)} %get-tuple-element.1847), channel_id=1, source_target_pairs={{0,1},{1,2},{2,3},{3,0},{4,5},{5,6},{6,7},{7,4},{8,9},{9,10},{10,1... | collective-permute-start | bytes 786440 | tf_op jit(solution)/shard_map/while/body/eval_jaxpr/ppermute | solution.py:93
  1285.8 182.6 %collective-permute-start.7 = (f32[4,128,4,64]{1,3,2,0:T(8,128)}, f32[4,128,4,64]{1,3,2,0:T(8,128)}, u32[]{:S(2)}, u32[]{:S(2)}) collective-permute-start(f32[4,128,4,64]{1,3,2,0:T(8,128)} %get-tuple-element.1850), channel_id=1, source_target_pairs={{0,1},{1,2},{2,3},{3,0},{4,5},{5,6},{6,7},{7,4},{8,9},{9,10},{10,1... | collective-permute-start | bytes 1572872 | tf_op jit(solution)/shard_map/while/body/eval_jaxpr/ppermute | solution.py:96
  1285.9 184.7 %collective-permute-start.6 = (f32[4,128,4,64]{1,3,2,0:T(8,128)}, f32[4,128,4,64]{1,3,2,0:T(8,128)}, u32[]{:S(2)}, u32[]{:S(2)}) collective-permute-start(f32[4,128,4,64]{1,3,2,0:T(8,128)} %get-tuple-element.1849), channel_id=1, source_target_pairs={{0,1},{1,2},{2,3},{3,0},{4,5},{5,6},{6,7},{7,4},{8,9},{9,10},{10,1... | collective-permute-start | bytes 1572872 | tf_op jit(solution)/shard_map/while/body/eval_jaxpr/ppermute | solution.py:95
  1472.7 63.5 %collective-permute-start.5 = (bf16[4,128,4,64]{1,3,2,0:T(8,128)(2,1)}, bf16[4,128,4,64]{1,3,2,0:T(8,128)(2,1)S(1)}, u32[]{:S(2)}, u32[]{:S(2)}) collective-permute-start(bf16[4,128,4,64]{1,3,2,0:T(8,128)(2,1)} %get-tuple-element.1848), channel_id=1, source_target_pairs={{0,1},{1,2},{2,3},{3,0},{4,5},{5,6},{6,7},{7,4},{8,9},{9,10},{10,1... | collective-permute-start | bytes 786440 | tf_op jit(solution)/shard_map/while/body/eval_jaxpr/ppermute | solution.py:94
  1472.7 63.0 %collective-permute-start.4 = (bf16[4,128,4,64]{1,3,2,0:T(8,128)(2,1)}, bf16[4,128,4,64]{1,3,2,0:T(8,128)(2,1)S(1)}, u32[]{:S(2)}, u32[]{:S(2)}) collective-permute-start(bf16[4,128,4,64]{1,3,2,0:T(8,128)(2,1)} %get-tuple-element.1847), channel_id=1, source_target_pairs={{0,1},{1,2},{2,3},{3,0},{4,5},{5,6},{6,7},{7,4},{8,9},{9,10},{10,1... | collective-permute-start | bytes 786440 | tf_op jit(solution)/shard_map/while/body/eval_jaxpr/ppermute | solution.py:93
  1472.7 184.2 %collective-permute-start.7 = (f32[4,128,4,64]{1,3,2,0:T(8,128)}, f32[4,128,4,64]{1,3,2,0:T(8,128)}, u32[]{:S(2)}, u32[]{:S(2)}) collective-permute-start(f32[4,128,4,64]{1,3,2,0:T(8,128)} %get-tuple-element.1850), channel_id=1, source_target_pairs={{0,1},{1,2},{2,3},{3,0},{4,5},{5,6},{6,7},{7,4},{8,9},{9,10},{10,1... | collective-permute-start | bytes 1572872 | tf_op jit(solution)/shard_map/while/body/eval_jaxpr/ppermute | solution.py:96
  1472.7 186.3 %collective-permute-start.6 = (f32[4,128,4,64]{1,3,2,0:T(8,128)}, f32[4,128,4,64]{1,3,2,0:T(8,128)}, u32[]{:S(2)}, u32[]{:S(2)}) collective-permute-start(f32[4,128,4,64]{1,3,2,0:T(8,128)} %get-tuple-element.1849), channel_id=1, source_target_pairs={{0,1},{1,2},{2,3},{3,0},{4,5},{5,6},{6,7},{7,4},{8,9},{9,10},{10,1... | collective-permute-start | bytes 1572872 | tf_op jit(solution)/shard_map/while/body/eval_jaxpr/ppermute | solution.py:95
  1661.2 63.5 %collective-permute-start.5 = (bf16[4,128,4,64]{1,3,2,0:T(8,128)(2,1)}, bf16[4,128,4,64]{1,3,2,0:T(8,128)(2,1)S(1)}, u32[]{:S(2)}, u32[]{:S(2)}) collective-permute-start(bf16[4,128,4,64]{1,3,2,0:T(8,128)(2,1)} %get-tuple-element.1848), channel_id=1, source_target_pairs={{0,1},{1,2},{2,3},{3,0},{4,5},{5,6},{6,7},{7,4},{8,9},{9,10},{10,1... | collective-permute-start | bytes 786440 | tf_op jit(solution)/shard_map/while/body/eval_jaxpr/ppermute | solution.py:94
  1661.2 63.0 %collective-permute-start.4 = (bf16[4,128,4,64]{1,3,2,0:T(8,128)(2,1)}, bf16[4,128,4,64]{1,3,2,0:T(8,128)(2,1)S(1)}, u32[]{:S(2)}, u32[]{:S(2)}) collective-permute-start(bf16[4,128,4,64]{1,3,2,0:T(8,128)(2,1)} %get-tuple-element.1847), channel_id=1, source_target_pairs={{0,1},{1,2},{2,3},{3,0},{4,5},{5,6},{6,7},{7,4},{8,9},{9,10},{10,1... | collective-permute-start | bytes 786440 | tf_op jit(solution)/shard_map/while/body/eval_jaxpr/ppermute | solution.py:93
  1661.2 182.4 %collective-permute-start.7 = (f32[4,128,4,64]{1,3,2,0:T(8,128)}, f32[4,128,4,64]{1,3,2,0:T(8,128)}, u32[]{:S(2)}, u32[]{:S(2)}) collective-permute-start(f32[4,128,4,64]{1,3,2,0:T(8,128)} %get-tuple-element.1850), channel_id=1, source_target_pairs={{0,1},{1,2},{2,3},{3,0},{4,5},{5,6},{6,7},{7,4},{8,9},{9,10},{10,1... | collective-permute-start | bytes 1572872 | tf_op jit(solution)/shard_map/while/body/eval_jaxpr/ppermute | solution.py:96
  1661.2 184.5 %collective-permute-start.6 = (f32[4,128,4,64]{1,3,2,0:T(8,128)}, f32[4,128,4,64]{1,3,2,0:T(8,128)}, u32[]{:S(2)}, u32[]{:S(2)}) collective-permute-start(f32[4,128,4,64]{1,3,2,0:T(8,128)} %get-tuple-element.1849), channel_id=1, source_target_pairs={{0,1},{1,2},{2,3},{3,0},{4,5},{5,6},{6,7},{7,4},{8,9},{9,10},{10,1... | collective-permute-start | bytes 1572872 | tf_op jit(solution)/shard_map/while/body/eval_jaxpr/ppermute | solution.py:95
  1850.3 5.8 collective-permute-start.12
  1850.3 8.6 collective-permute-start.13
  1850.4 8.5 copy-start.45
  1861.7 153.7 %copy-start.17 = (bf16[4,128,2048]{2,1,0:T(8,128)(2,1)S(1)}, bf16[4,128,2048]{2,1,0:T(8,128)(2,1)}, u32[]{:S(2)}) copy-start(bf16[4,128,2048]{2,1,0:T(8,128)(2,1)} %copy-done.16) | copy-start | bytes 6291460
  1861.7 326.6 %all-reduce.20.cloned.1.call-start = ((), (), s32[]{:S(2)}) async-start(), calls=%async_computation.5 | async-start | bytes 8388608 | tf_op jit(solution)/shard_map/psum | solution.py:155
  2019.6 10.2 slice-start.10
  2033.7 1008.6 %all-reduce.22.cloned.1.call-start = ((), (), s32[]{:S(2)}) async-start(), calls=%async_computation.6 | async-start | bytes 8388608 | tf_op jit(solution)/shard_map/psum | solution.py:172
  2062.1 126.2 %copy-start.14 = (bf16[4,128,2048]{2,1,0:T(8,128)(2,1)S(1)}, bf16[4,128,2048]{2,1,0:T(8,128)(2,1)}, u32[]{:S(2)}) copy-start(bf16[4,128,2048]{2,1,0:T(8,128)(2,1)} %copy-done.12) | copy-start | bytes 6291460
  2062.1 126.2 %copy-start.70 = (f32[1,2048]{1,0:T(1,128)S(1)}, f32[1,2048]{1,0:T(1,128)}, u32[]{:S(2)}) copy-start(f32[1,2048]{1,0:T(1,128)} %copy-done.69) | copy-start | bytes 24580
  2062.1 126.2 %copy-start.77 = (f32[4,128]{1,0:T(4,128)S(1)}, f32[4,128]{1,0:T(4,128)}, u32[]{:S(2)}) copy-start(f32[4,128]{1,0:T(4,128)} %copy-done.76) | copy-start | bytes 6148
  2310.9 63.6 %collective-permute-start.9 = (bf16[4,128,4,64]{1,3,2,0:T(8,128)(2,1)}, bf16[4,128,4,64]{1,3,2,0:T(8,128)(2,1)S(1)}, u32[]{:S(2)}, u32[]{:S(2)}) collective-permute-start(bf16[4,128,4,64]{1,3,2,0:T(8,128)(2,1)} %get-tuple-element.1908), channel_id=1, source_target_pairs={{0,1},{1,2},{2,3},{3,0},{4,5},{5,6},{6,7},{7,4},{8,9},{9,10},{10,1... | collective-permute-start | bytes 786440 | tf_op jit(solution)/shard_map/while/body/eval_jaxpr/ppermute | solution.py:94
  2310.9 63.0 %collective-permute-start.8 = (bf16[4,128,4,64]{1,3,2,0:T(8,128)(2,1)}, bf16[4,128,4,64]{1,3,2,0:T(8,128)(2,1)S(1)}, u32[]{:S(2)}, u32[]{:S(2)}) collective-permute-start(bf16[4,128,4,64]{1,3,2,0:T(8,128)(2,1)} %get-tuple-element.1907), channel_id=1, source_target_pairs={{0,1},{1,2},{2,3},{3,0},{4,5},{5,6},{6,7},{7,4},{8,9},{9,10},{10,1... | collective-permute-start | bytes 786440 | tf_op jit(solution)/shard_map/while/body/eval_jaxpr/ppermute | solution.py:93
  2312.5 182.7 %collective-permute-start.11 = (f32[4,128,4,64]{1,3,2,0:T(8,128)}, f32[4,128,4,64]{1,3,2,0:T(8,128)}, u32[]{:S(2)}, u32[]{:S(2)}) collective-permute-start(f32[4,128,4,64]{1,3,2,0:T(8,128)} %get-tuple-element.1910), channel_id=1, source_target_pairs={{0,1},{1,2},{2,3},{3,0},{4,5},{5,6},{6,7},{7,4},{8,9},{9,10},{10,1... | collective-permute-start | bytes 1572872 | tf_op jit(solution)/shard_map/while/body/eval_jaxpr/ppermute | solution.py:96
  2312.6 184.7 %collective-permute-start.10 = (f32[4,128,4,64]{1,3,2,0:T(8,128)}, f32[4,128,4,64]{1,3,2,0:T(8,128)}, u32[]{:S(2)}, u32[]{:S(2)}) collective-permute-start(f32[4,128,4,64]{1,3,2,0:T(8,128)} %get-tuple-element.1909), channel_id=1, source_target_pairs={{0,1},{1,2},{2,3},{3,0},{4,5},{5,6},{6,7},{7,4},{8,9},{9,10},{10,1... | collective-permute-start | bytes 1572872 | tf_op jit(solution)/shard_map/while/body/eval_jaxpr/ppermute | solution.py:95
  2499.4 63.6 %collective-permute-start.9 = (bf16[4,128,4,64]{1,3,2,0:T(8,128)(2,1)}, bf16[4,128,4,64]{1,3,2,0:T(8,128)(2,1)S(1)}, u32[]{:S(2)}, u32[]{:S(2)}) collective-permute-start(bf16[4,128,4,64]{1,3,2,0:T(8,128)(2,1)} %get-tuple-element.1908), channel_id=1, source_target_pairs={{0,1},{1,2},{2,3},{3,0},{4,5},{5,6},{6,7},{7,4},{8,9},{9,10},{10,1... | collective-permute-start | bytes 786440 | tf_op jit(solution)/shard_map/while/body/eval_jaxpr/ppermute | solution.py:94
  2499.4 63.0 %collective-permute-start.8 = (bf16[4,128,4,64]{1,3,2,0:T(8,128)(2,1)}, bf16[4,128,4,64]{1,3,2,0:T(8,128)(2,1)S(1)}, u32[]{:S(2)}, u32[]{:S(2)}) collective-permute-start(bf16[4,128,4,64]{1,3,2,0:T(8,128)(2,1)} %get-tuple-element.1907), channel_id=1, source_target_pairs={{0,1},{1,2},{2,3},{3,0},{4,5},{5,6},{6,7},{7,4},{8,9},{9,10},{10,1... | collective-permute-start | bytes 786440 | tf_op jit(solution)/shard_map/while/body/eval_jaxpr/ppermute | solution.py:93
  2499.4 184.2 %collective-permute-start.11 = (f32[4,128,4,64]{1,3,2,0:T(8,128)}, f32[4,128,4,64]{1,3,2,0:T(8,128)}, u32[]{:S(2)}, u32[]{:S(2)}) collective-permute-start(f32[4,128,4,64]{1,3,2,0:T(8,128)} %get-tuple-element.1910), channel_id=1, source_target_pairs={{0,1},{1,2},{2,3},{3,0},{4,5},{5,6},{6,7},{7,4},{8,9},{9,10},{10,1... | collective-permute-start | bytes 1572872 | tf_op jit(solution)/shard_map/while/body/eval_jaxpr/ppermute | solution.py:96
  2499.4 186.4 %collective-permute-start.10 = (f32[4,128,4,64]{1,3,2,0:T(8,128)}, f32[4,128,4,64]{1,3,2,0:T(8,128)}, u32[]{:S(2)}, u32[]{:S(2)}) collective-permute-start(f32[4,128,4,64]{1,3,2,0:T(8,128)} %get-tuple-element.1909), channel_id=1, source_target_pairs={{0,1},{1,2},{2,3},{3,0},{4,5},{5,6},{6,7},{7,4},{8,9},{9,10},{10,1... | collective-permute-start | bytes 1572872 | tf_op jit(solution)/shard_map/while/body/eval_jaxpr/ppermute | solution.py:95
  2687.9 63.6 %collective-permute-start.9 = (bf16[4,128,4,64]{1,3,2,0:T(8,128)(2,1)}, bf16[4,128,4,64]{1,3,2,0:T(8,128)(2,1)S(1)}, u32[]{:S(2)}, u32[]{:S(2)}) collective-permute-start(bf16[4,128,4,64]{1,3,2,0:T(8,128)(2,1)} %get-tuple-element.1908), channel_id=1, source_target_pairs={{0,1},{1,2},{2,3},{3,0},{4,5},{5,6},{6,7},{7,4},{8,9},{9,10},{10,1... | collective-permute-start | bytes 786440 | tf_op jit(solution)/shard_map/while/body/eval_jaxpr/ppermute | solution.py:94
  2687.9 63.0 %collective-permute-start.8 = (bf16[4,128,4,64]{1,3,2,0:T(8,128)(2,1)}, bf16[4,128,4,64]{1,3,2,0:T(8,128)(2,1)S(1)}, u32[]{:S(2)}, u32[]{:S(2)}) collective-permute-start(bf16[4,128,4,64]{1,3,2,0:T(8,128)(2,1)} %get-tuple-element.1907), channel_id=1, source_target_pairs={{0,1},{1,2},{2,3},{3,0},{4,5},{5,6},{6,7},{7,4},{8,9},{9,10},{10,1... | collective-permute-start | bytes 786440 | tf_op jit(solution)/shard_map/while/body/eval_jaxpr/ppermute | solution.py:93
  2688.0 182.5 %collective-permute-start.11 = (f32[4,128,4,64]{1,3,2,0:T(8,128)}, f32[4,128,4,64]{1,3,2,0:T(8,128)}, u32[]{:S(2)}, u32[]{:S(2)}) collective-permute-start(f32[4,128,4,64]{1,3,2,0:T(8,128)} %get-tuple-element.1910), channel_id=1, source_target_pairs={{0,1},{1,2},{2,3},{3,0},{4,5},{5,6},{6,7},{7,4},{8,9},{9,10},{10,1... | collective-permute-start | bytes 1572872 | tf_op jit(solution)/shard_map/while/body/eval_jaxpr/ppermute | solution.py:96
  2688.0 184.6 %collective-permute-start.10 = (f32[4,128,4,64]{1,3,2,0:T(8,128)}, f32[4,128,4,64]{1,3,2,0:T(8,128)}, u32[]{:S(2)}, u32[]{:S(2)}) collective-permute-start(f32[4,128,4,64]{1,3,2,0:T(8,128)} %get-tuple-element.1909), channel_id=1, source_target_pairs={{0,1},{1,2},{2,3},{3,0},{4,5},{5,6},{6,7},{7,4},{8,9},{9,10},{10,1... | collective-permute-start | bytes 1572872 | tf_op jit(solution)/shard_map/while/body/eval_jaxpr/ppermute | solution.py:95
  2874.7 8.4 copy-start.42
  2877.0 6.1 collective-permute-start.14
  2877.3 8.6 collective-permute-start.15
  2877.4 8.5 copy-start.46
  2917.7 128.1 %copy-start.72 = (f32[2048]{0:T(1024)S(1)}, f32[2048]{0:T(1024)}, u32[]{:S(2)}) copy-start(f32[2048]{0:T(1024)} %get-tuple-element.1234) | copy-start | bytes 24580
  2917.7 128.1 %copy-start.73 = (f32[2048]{0:T(1024)S(1)}, f32[2048]{0:T(1024)}, u32[]{:S(2)}) copy-start(f32[2048]{0:T(1024)} %get-tuple-element.1238) | copy-start | bytes 24580
  (90 other events, 323.0 us)
Sparse Core Ops, SparseCore 0:
  299.5 155.5 all-reduce.9
  470.5 154.3 all-reduce.11
  833.9 153.5 all-reduce.13
  1006.5 154.3 all-reduce.15
  1861.8 153.4 all-reduce.17
  2033.8 154.3 all-reduce.19
  2888.8 153.4 all-reduce.21
where the time goes:
time: 3880 us; the launch traced here: 3870 us
  waiting for transfers between devices  1030 us (27%)
  other arithmetic  959 us (25%)
  local copies, waits for them, and re-layouts  871 us (22%)
  blocking collectives  820 us (21%)
  matrix products  154 us (4%)
    scatter-add x8, other arithmetic, pair_grads(): jax.ops.segment_sum(score_row, seg_ids, num_segments=n_buckets)  880 us
    psum x1, blocking collectives, local_program(): lax.psum(bias_grad, 'cp')  813 us
    gather x26, local copies, waits for them, and re-layouts, pair_bias(): return (buckets, jnp.take(bias_table, buckets, axis=1))  789 us
    psum x2, waiting for transfers between devices, layer_forward(): lax.psum(jnp.dot(attn_flat, w_o, preferred_element_type=jnp.float32), 'tp')  309 us
    psum x2, waiting for transfers between devices, layer_backward(): lax.psum(d_h_attn, 'tp')  278 us
    psum x2, waiting for transfers between devices, layer_backward(): lax.psum(d_h_mlp, 'tp')  275 us
    psum x1, waiting for transfers between devices, layer_forward(): lax.psum(jnp.dot(gated, w_out, preferred_element_type=jnp.float32), 'tp')  154 us
  transfers between devices with their start and end apart: 47, of which 11 were waited for; matrix products, arithmetic and copies ran while one was open for 40% of the time, Pallas kernels for 0%

commit v1 on v0

v1 whole, which is shorter than its diff:
```python
import functools

import jax
import jax.numpy as jnp
from jax import lax
from jax.experimental import pallas as pl
from jax.experimental.pallas import tpu as pltpu
from jax.sharding import PartitionSpec as P

NORM_EPS = 1e-6
MASK_NEG = -1e9
BF16 = jnp.bfloat16
F32 = jnp.float32
VMEM = pltpu.VMEM
MESH = pl.DeviceIdType.MESH
HEAD_DIM = 64
VMEM_SPEC = pl.BlockSpec(memory_space=pltpu.VMEM)
SMEM_SPEC = pl.BlockSpec(memory_space=pltpu.SMEM)


def rel_bucket(rel_pos):
    distance = jnp.minimum(jnp.abs(rel_pos), 128)
    distance_sq = distance * distance
    log_part = 8 + sum((distance_sq >= 64 * 2 ** power).astype(jnp.int32) for power in range(1, 8))
    return jnp.where(distance < 8, distance, log_part) + 16 * (rel_pos > 0).astype(jnp.int32)


def dot_nt(a, b):
    return lax.dot_general(a, b, (((1,), (1,)), ((), ())), preferred_element_type=F32)


def dot_nn(a, b):
    return lax.dot_general(a, b, (((1,), (0,)), ((), ())), preferred_element_type=F32)


def dot_tn(a, b):
    return lax.dot_general(a, b, (((0,), (0,)), ((), ())), preferred_element_type=F32)


def stack_heads(block, heads):
    wide = block.astype(F32)
    lane_head = lax.broadcasted_iota(jnp.int32, block.shape, 1) // HEAD_DIM
    return jnp.concatenate([jnp.where(lane_head == h, wide, 0.0).astype(BF16) for h in range(heads)], axis=0)


def pick_heads(stacked, heads, rows):
    lane_head = lax.broadcasted_iota(jnp.int32, (rows, stacked.shape[1]), 1) // HEAD_DIM
    out = stacked[:rows]
    for h in range(1, heads):
        out = jnp.where(lane_head == h, stacked[h * rows:(h + 1) * rows], out)
    return out


def cp_places():
    me = lax.axis_index('cp')
    mate = me + 1 - 2 * lax.rem(me, 2)
    across = lax.rem(me + 2, 4)
    diagonal = lax.rem(mate + 2, 4)
    return me, mate, across, diagonal


def entry_barrier(axis, peers):
    barrier = pltpu.get_barrier_semaphore()
    for peer in peers:
        pl.semaphore_signal(barrier, inc=1, device_id={axis: peer}, device_id_type=MESH)
    pl.semaphore_wait(barrier, len(peers))


def attn_fwd_kernel(heads, q_ref, kv_ref, bias_ref, mask_ref, o_ref, all_ref, send, recv):
    batch, rows, width = q_ref.shape
    me, mate, across, _ = cp_places()
    entry_barrier('cp', (mate, across))

    def to_mate(b):
        return pltpu.make_async_remote_copy(src_ref=kv_ref.at[b], dst_ref=all_ref.at[b, me], send_sem=send.at[0, b], recv_sem=recv.at[0, b], device_id={'cp': mate}, device_id_type=MESH)

    def to_across(b):
        return pltpu.make_async_remote_copy(src_ref=kv_ref.at[b], dst_ref=all_ref.at[b, me], send_sem=send.at[1, b], recv_sem=recv.at[1, b], device_id={'cp': across}, device_id_type=MESH)

    def forward(b):
        return pltpu.make_async_remote_copy(src_ref=all_ref.at[b, across], dst_ref=all_ref.at[b, across], send_sem=send.at[2, b], recv_sem=recv.at[2, b], device_id={'cp': mate}, device_id_type=MESH)

    for b in range(batch):
        to_across(b).start()
        to_mate(b).start()

    def step(b, carry):
        to_across(b).wait_recv()
        forward(b).start()
        all_ref[b, me] = kv_ref[b]
        to_mate(b).wait_recv()
        forward(b).wait_recv()
        kv = all_ref[b].reshape(-1, 2 * width)
        stacked = stack_heads(q_ref[b], heads)
        scores = dot_nt(stacked, kv[:, :width]) + bias_ref[...] + mask_ref[b]
        top = jnp.max(scores, axis=1, keepdims=True)
        probs = jnp.exp(scores - top)
        total = jnp.sum(probs, axis=1, keepdims=True)
        out = dot_nn(probs.astype(BF16), kv[:, width:]) / total
        o_ref[b] = pick_heads(out, heads, rows).astype(BF16)
        return carry

    lax.fori_loop(0, batch, step, 0)

    def finish(b, carry):
        to_across(b).wait_send()
        to_mate(b).wait_send()
        forward(b).wait_send()
        return carry

    lax.fori_loop(0, batch, finish, 0)


def attn_fwd(q, kv, bias_rows, mask_rows, cp_size, cid):
    batch, rows, width = q.shape
    heads = width // HEAD_DIM
    return pl.pallas_call(
        functools.partial(attn_fwd_kernel, heads),
        out_shape=(jax.ShapeDtypeStruct(q.shape, BF16), jax.ShapeDtypeStruct((batch, cp_size, rows, 2 * width), BF16)),
        in_specs=[VMEM_SPEC] * 4,
        out_specs=(VMEM_SPEC, VMEM_SPEC),
        scratch_shapes=[pltpu.SemaphoreType.DMA((3, batch)), pltpu.SemaphoreType.DMA((3, batch))],
        compiler_params=pltpu.CompilerParams(collective_id=cid, has_side_effects=True, vmem_limit_bytes=32 * 2 ** 20),
        cost_estimate=pl.CostEstimate(flops=4 * 10 ** 9, bytes_accessed=6 * 10 ** 6, transcendentals=10 ** 6),
        name='attn_fwd',
    )(q, kv, bias_rows, mask_rows)


def attn_bwd_kernel(heads, qdo_ref, kv_ref, bias_r_ref, bias_c_ref, mask_r_ref, mask_c_ref, dq_ref, dkv_ref, ds_ref, all_ref, own_stats, all_stats, send, recv, send_st, recv_st):
    batch, rows, wide = qdo_ref.shape
    width = wide // 2
    n_blocks = kv_ref.shape[1]
    me, mate, across, diagonal = cp_places()
    entry_barrier('cp', (mate, across, diagonal))

    def to_mate(b):
        return pltpu.make_async_remote_copy(src_ref=qdo_ref.at[b], dst_ref=all_ref.at[b, me], send_sem=send.at[0, b], recv_sem=recv.at[0, b], device_id={'cp': mate}, device_id_type=MESH)

    def to_across(b):
        return pltpu.make_async_remote_copy(src_ref=qdo_ref.at[b], dst_ref=all_ref.at[b, me], send_sem=send.at[1, b], recv_sem=recv.at[1, b], device_id={'cp': across}, device_id_type=MESH)

    def forward(b):
        return pltpu.make_async_remote_copy(src_ref=all_ref.at[b, across], dst_ref=all_ref.at[b, across], send_sem=send.at[2, b], recv_sem=recv.at[2, b], device_id={'cp': mate}, device_id_type=MESH)

    def stats_to(which, b):
        peer = (mate, across, diagonal)[which]
        return pltpu.make_async_remote_copy(src_ref=own_stats.at[b], dst_ref=all_stats.at[b, me], send_sem=send_st.at[which, b], recv_sem=recv_st.at[which, b], device_id={'cp': peer}, device_id_type=MESH)

    for b in range(batch):
        to_across(b).start()
        to_mate(b).start()

    ds_ref[...] = jnp.zeros_like(ds_ref)

    def row_step(b, carry):
        kv = kv_ref[b].reshape(-1, wide)
        keys, vals = kv[:, :width], kv[:, width:]
        qdo = qdo_ref[b]
        all_ref[b, me] = qdo
        scores = dot_nt(stack_heads(qdo[:, :width], heads), keys) + bias_r_ref[...] + mask_r_ref[b]
        top = jnp.max(scores, axis=1, keepdims=True)
        unnorm = jnp.exp(scores - top)
        total = jnp.sum(unnorm, axis=1, keepdims=True)
        log_norm = top + jnp.log(total)
        probs = unnorm * (1.0 / total)
        d_probs = dot_nt(stack_heads(qdo[:, width:], heads), vals)
        row_dot = jnp.sum(probs * d_probs, axis=1, keepdims=True)
        lane = lax.broadcasted_iota(jnp.int32, (rows, rows), 1)
        table = jnp.zeros((rows, rows), F32)
        for h in range(heads):
            table = jnp.where(lane == h, log_norm[h * rows:(h + 1) * rows], table)
            table = jnp.where(lane == heads + h, row_dot[h * rows:(h + 1) * rows], table)
        stats = jnp.transpose(table)[:2 * heads]
        own_stats[b] = stats
        all_stats[b, me] = stats
        d_scores = probs * (d_probs - row_dot)
        ds_ref[...] += d_scores
        d_q = dot_nn(d_scores.astype(BF16), keys)
        dq_ref[b] = pick_heads(d_q, heads, rows).astype(BF16)
        for which in range(3):
            stats_to(which, b).start()
        to_across(b).wait_recv()
        forward(b).start()
        return carry

    lax.fori_loop(0, batch, row_step, 0)

    def col_step(b, carry):
        to_mate(b).wait_recv()
        forward(b).wait_recv()
        for which in range(3):
            stats_to(which, b).wait_recv()
        own = kv_ref[b, me]
        keys, vals = own[:, :width], own[:, width:]
        mask_col = mask_c_ref[b]

        def block(src, acc):
            d_k, d_v = acc
            qdo = all_ref[b, src]
            stats = all_stats[b, src]
            log_norm = jnp.concatenate([stats[h:h + 1] for h in range(heads)], axis=1)
            row_dot = jnp.concatenate([stats[heads + h:heads + h + 1] for h in range(heads)], axis=1)
            q_st = stack_heads(qdo[:, :width], heads)
            do_st = stack_heads(qdo[:, width:], heads)
            scores = dot_nt(keys, q_st) + bias_c_ref[src] + mask_col
            probs = jnp.exp(scores - log_norm)
            d_scores = probs * (dot_nt(vals, do_st) - row_dot)
            d_k = d_k + dot_nn(d_scores.astype(BF16), q_st)
            d_v = d_v + dot_nn(probs.astype(BF16), do_st)
            return d_k, d_v

        zero = jnp.zeros((rows, width), F32)
        d_k, d_v = lax.fori_loop(0, n_blocks, block, (zero, zero))
        dkv_ref[b] = jnp.concatenate([d_k, d_v], axis=1).astype(BF16)
        return carry

    lax.fori_loop(0, batch, col_step, 0)

    def finish(b, carry):
        to_across(b).wait_send()
        to_mate(b).wait_send()
        forward(b).wait_send()
        for which in range(3):
            stats_to(which, b).wait_send()
        return carry

    lax.fori_loop(0, batch, finish, 0)


def attn_bwd(qdo, kv_all, bias_rows, bias_cols, mask_rows, mask_cols, cid):
    batch, rows, wide = qdo.shape
    width = wide // 2
    heads = width // HEAD_DIM
    n_blocks = kv_all.shape[1]
    return pl.pallas_call(
        functools.partial(attn_bwd_kernel, heads),
        out_shape=(jax.ShapeDtypeStruct((batch, rows, width), BF16), jax.ShapeDtypeStruct((batch, rows, wide), BF16), jax.ShapeDtypeStruct((heads * rows, n_blocks * rows), F32)),
        in_specs=[VMEM_SPEC] * 6,
        out_specs=(VMEM_SPEC,) * 3,
        scratch_shapes=[
            pltpu.VMEM((batch, n_blocks, rows, wide), BF16),
            pltpu.VMEM((batch, 2 * heads, rows), F32),
            pltpu.VMEM((batch, n_blocks, 2 * heads, rows), F32),
            pltpu.SemaphoreType.DMA((3, batch)),
            pltpu.SemaphoreType.DMA((3, batch)),
            pltpu.SemaphoreType.DMA((3, batch)),
            pltpu.SemaphoreType.DMA((3, batch)),
        ],
        compiler_params=pltpu.CompilerParams(collective_id=cid, has_side_effects=True, vmem_limit_bytes=40 * 2 ** 20),
        cost_estimate=pl.CostEstimate(flops=10 * 10 ** 9, bytes_accessed=10 ** 7, transcendentals=2 * 10 ** 6),
        name='attn_bwd',
    )(qdo, kv_all, bias_rows, bias_cols, mask_rows, mask_cols)


def bias_grad_kernel(heads, n_buckets, pos_ref, ds0_ref, ds1_ref, out_ref):
    rows = ds0_ref.shape[0] // heads
    cols = ds0_ref.shape[1]
    rel = lax.broadcasted_iota(jnp.int32, (rows, cols), 1) - lax.broadcasted_iota(jnp.int32, (rows, cols), 0) - pos_ref[0]
    buckets = rel_bucket(rel)
    sums = [ds0_ref[h * rows:(h + 1) * rows] + ds1_ref[h * rows:(h + 1) * rows] for h in range(heads)]

    def step(k, carry):
        hit = buckets == k
        out_ref[k] = jnp.concatenate([jnp.sum(jnp.where(hit, part, 0.0), axis=0, keepdims=True) for part in sums], axis=0)
        return carry

    lax.fori_loop(0, n_buckets, step, 0)


def bias_grad(ds0, ds1, start, heads, n_buckets):
    out = pl.pallas_call(
        functools.partial(bias_grad_kernel, heads, n_buckets),
        out_shape=jax.ShapeDtypeStruct((n_buckets, heads, ds0.shape[1]), F32),
        in_specs=[SMEM_SPEC, VMEM_SPEC, VMEM_SPEC],
        out_specs=VMEM_SPEC,
        compiler_params=pltpu.CompilerParams(vmem_limit_bytes=16 * 2 ** 20),
        name='bias_grad',
    )(start.reshape(1), ds0, ds1)
    return jnp.sum(out, axis=-1)


def bias_from(rel_bias, rel):
    buckets = rel_bucket(rel)
    table = rel_bias.T
    shape = (table.shape[0],) + rel.shape
    out = jnp.zeros(shape, F32)
    for k in range(table.shape[1]):
        out = jnp.where((buckets == k)[None], table[:, k].reshape((-1,) + (1,) * rel.ndim), out)
    return out


def rms_parts(x_f, gain):
    inv_rms = lax.rsqrt(jnp.mean(x_f * x_f, axis=-1, keepdims=True) + NORM_EPS)
    return (x_f * inv_rms * gain).astype(BF16)


def rms_backward(d_norm, x_f, gain):
    inv_rms = lax.rsqrt(jnp.mean(x_f * x_f, axis=-1, keepdims=True) + NORM_EPS)
    normed = x_f * inv_rms
    d_gain = jnp.sum(d_norm * normed, axis=0)
    d_normed = d_norm * gain
    d_x = inv_rms * (d_normed - normed * jnp.mean(d_normed * normed, axis=-1, keepdims=True))
    return d_x, d_gain


def reduce_rows(partial):
    return lax.psum_scatter(partial, 'tp', scatter_dimension=0, tiled=True)


def gather_rows(shard):
    return lax.all_gather(shard, 'tp', axis=0, tiled=True)


def cp_sum(partial):
    own = lax.psum_scatter(partial, 'cp', scatter_dimension=0, tiled=True).astype(BF16)
    return lax.all_gather(own, 'cp', axis=0, tiled=True)


def solution(mesh):
    cp_size = mesh.shape['cp']
    tp_size = mesh.shape['tp']
    seq_spec = P(None, 'cp', None)
    col_spec = P(None, None, 'tp')
    row_spec = P(None, 'tp', None)
    weight_specs = (P(), P(), col_spec, col_spec, col_spec, row_spec, col_spec, col_spec, row_spec)

    def local_program(x_in, d_y, key_mask, rel_bias, g_attn, g_mlp, w_q, w_k, w_v, w_o, w_gate, w_lin, w_out):
        batch, rows, d_model = x_in.shape
        tokens = batch * rows
        n_layers = w_q.shape[0]
        n_buckets, heads = rel_bias.shape
        width = heads * HEAD_DIM
        cp_index = lax.axis_index('cp')
        tp_index = lax.axis_index('tp')
        seq = cp_size * rows
        start = (cp_index * rows).astype(jnp.int32)

        mask_all = lax.all_gather(key_mask, 'cp', axis=1, tiled=True)
        mask_rows = jnp.where(mask_all > 0, 0.0, MASK_NEG).astype(F32)[:, None, :]
        mask_cols = jnp.where(key_mask > 0, 0.0, MASK_NEG).astype(F32)[:, :, None]
        pos = jnp.arange(rows)
        bias_rows = bias_from(rel_bias, jnp.arange(seq)[None, :] - start - pos[:, None]).reshape(heads * rows, seq)
        rel_cols = start + pos[None, :, None] - (jnp.arange(cp_size) * rows)[:, None, None] - pos[None, None, :]
        bias_cols = jnp.transpose(bias_from(rel_bias, rel_cols), (1, 2, 0, 3)).reshape(cp_size, rows, heads * rows)

        def own_rows(full):
            return lax.dynamic_slice_in_dim(full, tp_index * (tokens // tp_size), tokens // tp_size, axis=0)

        x = x_in.reshape(tokens, d_model)
        x_s = own_rows(x)
        saved = []
        for l in range(n_layers):
            h = rms_parts(x.astype(F32), g_attn[l])
            q = jnp.dot(h, w_q[l], preferred_element_type=F32).astype(BF16)
            k = jnp.dot(h, w_k[l], preferred_element_type=F32).astype(BF16)
            v = jnp.dot(h, w_v[l], preferred_element_type=F32).astype(BF16)
            kv = jnp.concatenate([k, v], axis=1).reshape(batch, rows, 2 * width)
            o, kv_all = attn_fwd(q.reshape(batch, rows, width), kv, bias_rows, mask_rows, cp_size, 2 * l)
            o = o.reshape(tokens, width)
            x1_s = (x_s.astype(F32) + reduce_rows(jnp.dot(o, w_o[l], preferred_element_type=F32))).astype(BF16)
            x1 = gather_rows(x1_s)
            h2 = rms_parts(x1.astype(F32), g_mlp[l])
            gate = jnp.dot(h2, w_gate[l], preferred_element_type=F32)
            lin = jnp.dot(h2, w_lin[l], preferred_element_type=F32)
            u = (jax.nn.gelu(gate, approximate=True) * lin).astype(BF16)
            saved.append((x_s, h, q, kv_all, o, x1_s, h2, gate, lin, u))
            if l + 1 < n_layers:
                x_s = (x1_s.astype(F32) + reduce_rows(jnp.dot(u, w_out[l], preferred_element_type=F32))).astype(BF16)
                x = gather_rows(x_s)

        d = d_y.reshape(tokens, d_model)
        d_s = own_rows(d)
        big = [[None] * n_layers for _ in range(7)]
        gains = [[None] * n_layers for _ in range(2)]
        ds_all = []
        for l in reversed(range(n_layers)):
            x_s, h, q, kv_all, o, x1_s, h2, gate, lin, u = saved[l]
            big[6][l] = cp_sum(dot_tn(u, d))
            d_u = dot_nt(d, w_out[l]).astype(BF16).astype(F32)
            gelu_val, gelu_pull = jax.vjp(lambda g: jax.nn.gelu(g, approximate=True), gate)
            d_lin = (d_u * gelu_val).astype(BF16)
            d_gate = gelu_pull(d_u * lin)[0].astype(BF16)
            big[4][l] = cp_sum(dot_tn(h2, d_gate))
            big[5][l] = cp_sum(dot_tn(h2, d_lin))
            dh2_s = reduce_rows(dot_nt(d_gate, w_gate[l]) + dot_nt(d_lin, w_lin[l]))
            d_mid, gains[1][l] = rms_backward(dh2_s, x1_s.astype(F32), g_mlp[l])
            dm_s = (d_mid + d_s.astype(F32)).astype(BF16)
            dm = gather_rows(dm_s)
            big[3][l] = cp_sum(dot_tn(o, dm))
            d_o = dot_nt(dm, w_o[l]).astype(BF16)
            qdo = jnp.concatenate([q, d_o], axis=1).reshape(batch, rows, 2 * width)
            d_q, d_kv, ds = attn_bwd(qdo, kv_all, bias_rows, bias_cols, mask_rows, mask_cols, 2 * l + 1)
            ds_all.append(ds)
            d_q = d_q.reshape(tokens, width)
            d_kv = d_kv.reshape(tokens, 2 * width)
            d_k, d_v = d_kv[:, :width], d_kv[:, width:]
            big[0][l] = cp_sum(dot_tn(h, d_q))
            big[1][l] = cp_sum(dot_tn(h, d_k))
            big[2][l] = cp_sum(dot_tn(h, d_v))
            dh_s = reduce_rows(dot_nt(d_q, w_q[l]) + dot_nt(d_k, w_k[l]) + dot_nt(d_v, w_v[l]))
            d_x, gains[0][l] = rms_backward(dh_s, x_s.astype(F32), g_attn[l])
            d_s = (d_x + dm_s.astype(F32)).astype(BF16)
            d = gather_rows(d_s)

        d_bias = bias_grad(ds_all[0], ds_all[1], start, heads, n_buckets)
        slots = jnp.zeros((tp_size, n_buckets * heads), F32)
        slots = lax.dynamic_update_slice(slots, d_bias.reshape(1, -1), (tp_index, jnp.int32(0)))
        small = lax.psum(jnp.concatenate([jnp.stack(gains[0]).reshape(-1), jnp.stack(gains[1]).reshape(-1), slots.reshape(-1)]), ('tp', 'cp'))
        n_gain = n_layers * d_model
        d_g_attn = small[:n_gain].reshape(n_layers, d_model)
        d_g_mlp = small[n_gain:2 * n_gain].reshape(n_layers, d_model)
        d_rel = lax.dynamic_slice(small[2 * n_gain:].reshape(tp_size, -1), (tp_index, jnp.int32(0)), (1, n_buckets * heads)).reshape(n_buckets, heads)
        return (d.reshape(batch, rows, d_model), d_rel, d_g_attn, d_g_mlp) + tuple(jnp.stack(parts) for parts in big)

    return jax.shard_map(local_program, mesh=mesh, in_specs=(seq_spec, seq_spec, P(None, 'cp'), P(None, 'tp')) + weight_specs, out_specs=(seq_spec, P(None, 'tp')) + weight_specs, check_vma=False)
```

time: 3880 us -> 2070 us (0.53)
  other arithmetic: 959 us -> 105 us
  local copies, waits for them, and re-layouts: 871 us -> 78.6 us
  blocking collectives: 820 us -> 46.8 us
  waiting for transfers between devices: 1030 us -> 1590 us
  Pallas kernels: 0 us -> 82.8 us
    reduce_scatter x0 -> x21, waiting for transfers between devices: none -> 1110 us  [the longest x7 616 us: reduce_rows(): return lax.psum_scatter(partial, 'tp', scatter_dimension=0, tiled=True)]
    psum x7 -> x0, waiting for transfers between devices: 1020 us -> none  [the longest x2 309 us: layer_forward(): lax.psum(jnp.dot(attn_flat, w_o, preferred_element_type=jnp.float32), 'tp')]
    scatter-add x8 -> x0, other arithmetic: 880 us -> none  [pair_grads(): jax.ops.segment_sum(score_row, seg_ids, num_segments=n_buckets)]
    gather x26 -> x0, local copies, waits for them, and re-layouts: 789 us -> none  [pair_bias(): return (buckets, jnp.take(bias_table, buckets, axis=1))]
    psum x1, blocking collectives: 813 us -> 40.5 us  [local_program(): lax.psum(jnp.concatenate([jnp.stack(gains[0]).reshape(-1), jnp.stack(gain...]
    all_gather x0 -> x21, waiting for transfers between devices: none -> 477 us  [the longest x14 274 us: cp_sum(): return lax.all_gather(own, 'cp', axis=0, tiled=True)]
    pallas_call x0 -> x5, Pallas kernels: none -> 82.8 us  [the longest x2 46.3 us: attn_bwd(): pl.pallas_call(functools.partial(attn_bwd_kernel, heads), out_shape=(jax....]
    broadcast_in_dim x0 -> x83, local copies, waits for them, and re-layouts: none -> 50.9 us  [the longest x80 50 us: bias_from(): jnp.where((buckets == k)[None], table[:, k].reshape((-1,) + (1,) * rel.nd...]
  transfers between devices with their start and end apart: 47 -> 42, of which waited for: 11 -> 40; matrix products, arithmetic and copies ran while one was open for 40% -> 10% of each run, Pallas kernels for 0% -> 1%
where the time goes in v1:
time: 2070 us
  waiting for transfers between devices  1590 us (77%)
  matrix products  140 us (7%)
  other arithmetic  105 us (5%)
  Pallas kernels  82.8 us (4%)
  local copies, waits for them, and re-layouts  78.6 us (4%)
  blocking collectives  46.8 us (2%)
    reduce_scatter x7, waiting for transfers between devices, reduce_rows(): return lax.psum_scatter(partial, 'tp', scatter_dimension=0, tiled=True)  616 us
    reduce_scatter x14, waiting for transfers between devices, cp_sum(): lax.psum_scatter(partial, 'cp', scatter_dimension=0, tiled=True)  499 us
    all_gather x14, waiting for transfers between devices, cp_sum(): return lax.all_gather(own, 'cp', axis=0, tiled=True)  274 us
    all_gather x7, waiting for transfers between devices, gather_rows(): return lax.all_gather(shard, 'tp', axis=0, tiled=True)  203 us
    dot_general x14, matrix products, dot_tn(): lax.dot_general(a, b, (((0,), (0,)), ((), ())), preferred_element_type=F32)  66.2 us
    broadcast_in_dim x80, local copies, waits for them, and re-layouts, bias_from(): jnp.where((buckets == k)[None], table[:, k].reshape((-1,) + (1,) * rel.nd...  50 us
    pallas_call x2, Pallas kernels, attn_bwd(): pl.pallas_call(functools.partial(attn_bwd_kernel, heads), out_shape=(jax....  46.3 us
  transfers between devices with their start and end apart: 42, of which 40 were waited for; matrix products, arithmetic and copies ran while one was open for 10% of the time, Pallas kernels for 1%

profile of v1, /device:TPU:0, one launch (start us, length us, event | category | flops | bytes accessed | tf_op | source)
XLA Modules:
  0.0 2065.2 jit_solution(11902165566031584780)
XLA Ops:
  22.0 6.3 all_gather.66
  29.5 5.4 select_select_fusion.1.bias_ref.bias_r_ref
  34.9 16.5 attn_fwd.2
  56.6 90.1 %reduce-scatter.22.cloned.1.call-done = f32[64,2048]{1,0:T(8,128)} async-done(((f32[512,2048]{1,0:T(8,128)}), f32[64,2048]{1,0:T(8,128)}) %reduce-scatter.22.cloned.1.call-update) | async-done | bytes 524304 | tf_op jit(solution)/shard_map/reduce_scatter | solution.py:307
  149.6 48.5 %all-gather.22.cloned.1.call-done = bf16[512,2048]{1,0:T(8,128)(2,1)} async-done(((bf16[64,2048]{1,0:T(8,128)(2,1)}), bf16[512,2048]{1,0:T(8,128)(2,1)}) %all-gather.22.cloned.1.call-update) | async-done | bytes 2097168 | tf_op jit(solution)/shard_map/all_gather | solution.py:311
  200.3 4.4 fusion.30
  212.6 87.3 %reduce-scatter.24.cloned.1.call-done = f32[64,2048]{1,0:T(8,128)} async-done(((f32[512,2048]{1,0:T(8,128)}), f32[64,2048]{1,0:T(8,128)}) %reduce-scatter.24.cloned.1.call-update) | async-done | bytes 524304 | tf_op jit(solution)/shard_map/reduce_scatter | solution.py:307
  302.4 48.8 %all-gather.24.cloned.1.call-done = bf16[512,2048]{1,0:T(8,128)(2,1)} async-done(((bf16[64,2048]{1,0:T(8,128)(2,1)}), bf16[512,2048]{1,0:T(8,128)(2,1)}) %all-gather.24.cloned.1.call-update) | async-done | bytes 2097168 | tf_op jit(solution)/shard_map/all_gather | solution.py:311
  359.6 16.1 attn_fwd.3
  379.9 87.1 %reduce-scatter.26.cloned.1.call-done = f32[64,2048]{1,0:T(8,128)} async-done(((f32[512,2048]{1,0:T(8,128)}), f32[64,2048]{1,0:T(8,128)}) %reduce-scatter.26.cloned.1.call-update) | async-done | bytes 524304 | tf_op jit(solution)/shard_map/reduce_scatter | solution.py:307
  469.4 4.2 fusion.46
  473.6 44.1 %all-gather.26.cloned.1.call-done = bf16[512,2048]{1,0:T(8,128)(2,1)} async-done(((bf16[64,2048]{1,0:T(8,128)(2,1)}), bf16[512,2048]{1,0:T(8,128)(2,1)}) %all-gather.26.cloned.1.call-update) | async-done | bytes 2097168 | tf_op jit(solution)/shard_map/all_gather | solution.py:311
  523.9 4.8 fusion.64
  534.6 87.3 %reduce-scatter.28.cloned.1.call-done = f32[64,2048]{1,0:T(8,128)} async-done(((f32[512,2048]{1,0:T(8,128)}), f32[64,2048]{1,0:T(8,128)}) %reduce-scatter.28.cloned.1.call-update) | async-done | bytes 524304 | tf_op jit(solution)/shard_map/reduce_scatter | solution.py:307
  679.2 7.3 select_select_fusion.bias_c_ref
  689.4 23.1 %attn_bwd.2 = (bf16[4,128,256]{2,1,0:T(8,128)(2,1)S(1)}, bf16[4,128,512]{2,1,0:T(8,128)(2,1)S(1)}, f32[512,512]{1,0:T(8,128)S(1)}) custom-call(bf16[4,128,512]{2,1,0:T(8,128)(2,1)S(1)} %bitcast.293, bf16[4,4,128,512]{3,2,1,0:T(8,128)(2,1)S(1)} %copy-done.18, f32[512,512]{1,0:T(8,128)S(1)} %select_select_fusion.1.bias_ref.bias_r_ref, ...), custom_call_target="tpu_custom_call" | custom-call | flops 10000000000 | bytes 10000000 | tf_op jit(solution)/shard_map/attn_bwd/pallas_call | solution.py:235
  719.4 87.5 %reduce-scatter.30.cloned.1.call-done = f32[64,2048]{1,0:T(8,128)} async-done(((f32[512,2048]{1,0:T(8,128)}), f32[64,2048]{1,0:T(8,128)}) %reduce-scatter.30.cloned.1.call-update) | async-done | bytes 524304 | tf_op jit(solution)/shard_map/reduce_scatter | solution.py:307
  810.5 48.8 %all-gather.30.cloned.1.call-done = bf16[512,2048]{1,0:T(8,128)(2,1)} async-done(((bf16[64,2048]{1,0:T(8,128)(2,1)}), bf16[512,2048]{1,0:T(8,128)(2,1)}) %all-gather.30.cloned.1.call-update) | async-done | bytes 2097168 | tf_op jit(solution)/shard_map/all_gather | solution.py:311
  859.2 5.6 fusion.57
  864.8 4.1 fusion.28
  868.9 5.7 convolution_add_fusion
  875.3 86.8 %reduce-scatter.32.cloned.1.call-done = f32[64,2048]{1,0:T(8,128)} async-done(((f32[512,2048]{1,0:T(8,128)}), f32[64,2048]{1,0:T(8,128)}) %reduce-scatter.32.cloned.1.call-update) | async-done | bytes 524304 | tf_op jit(solution)/shard_map/reduce_scatter | solution.py:307
  965.7 6.0 fusion.192
  972.4 6.0 fusion.197
  978.5 6.7 fusion.188
  985.3 6.6 fusion.185
  991.9 6.4 fusion.115
  998.4 5.7 fusion.216
  1009.0 5.5 all-gather.32.cloned.1.call-done
  1017.3 23.1 %attn_bwd.3 = (bf16[4,128,256]{2,1,0:T(8,128)(2,1)S(1)}, bf16[4,128,512]{2,1,0:T(8,128)(2,1)S(1)}, f32[512,512]{1,0:T(8,128)S(1)}) custom-call(bf16[4,128,512]{2,1,0:T(8,128)(2,1)S(1)} %bitcast.292, bf16[4,4,128,512]{3,2,1,0:T(8,128)(2,1)S(1)} %copy-done.16, f32[512,512]{1,0:T(8,128)S(1)} %select_select_fusion.1.bias_ref.bias_r_ref, ...), custom_call_target="tpu_custom_call" | custom-call | flops 10000000000 | bytes 10000000 | tf_op jit(solution)/shard_map/attn_bwd/pallas_call | solution.py:235
  1080.0 40.3 %reduce-scatter.52.cloned.1.call-done = f32[512,640]{1,0:T(8,128)} async-done(((f32[2048,640]{1,0:T(8,128)}), f32[512,640]{1,0:T(8,128)}) %reduce-scatter.52.cloned.1.call-update) | async-done | bytes 1310736 | tf_op jit(solution)/shard_map/reduce_scatter | solution.py:315
  1122.6 51.1 %reduce-scatter.58.cloned.1.call-done = f32[512,640]{1,0:T(8,128)} async-done(((f32[2048,640]{1,0:T(8,128)}), f32[512,640]{1,0:T(8,128)}) %reduce-scatter.58.cloned.1.call-update) | async-done | bytes 1310736 | tf_op jit(solution)/shard_map/reduce_scatter | solution.py:315
  1176.0 50.4 %reduce-scatter.56.cloned.1.call-done = f32[512,640]{1,0:T(8,128)} async-done(((f32[2048,640]{1,0:T(8,128)}), f32[512,640]{1,0:T(8,128)}) %reduce-scatter.56.cloned.1.call-update) | async-done | bytes 1310736 | tf_op jit(solution)/shard_map/reduce_scatter | solution.py:315
  1228.8 50.5 %reduce-scatter.62.cloned.1.call-done = f32[160,2048]{1,0:T(8,128)} async-done(((f32[640,2048]{1,0:T(8,128)}), f32[160,2048]{1,0:T(8,128)}) %reduce-scatter.62.cloned.1.call-update) | async-done | bytes 1310736 | tf_op jit(solution)/shard_map/reduce_scatter | solution.py:315
  1281.5 50.5 %reduce-scatter.60.cloned.1.call-done = f32[160,2048]{1,0:T(8,128)} async-done(((f32[640,2048]{1,0:T(8,128)}), f32[160,2048]{1,0:T(8,128)}) %reduce-scatter.60.cloned.1.call-update) | async-done | bytes 1310736 | tf_op jit(solution)/shard_map/reduce_scatter | solution.py:315
  1334.3 31.8 %reduce-scatter.38.cloned.1.call-done = f32[512,256]{1,0:T(8,128)} async-done(((f32[2048,256]{1,0:T(8,128)}), f32[512,256]{1,0:T(8,128)}) %reduce-scatter.38.cloned.1.call-update) | async-done | bytes 524304 | tf_op jit(solution)/shard_map/reduce_scatter | solution.py:315
  1368.0 32.2 %reduce-scatter.36.cloned.1.call-done = f32[512,256]{1,0:T(8,128)} async-done(((f32[2048,256]{1,0:T(8,128)}), f32[512,256]{1,0:T(8,128)}) %reduce-scatter.36.cloned.1.call-update) | async-done | bytes 524304 | tf_op jit(solution)/shard_map/reduce_scatter | solution.py:315
  1402.1 32.4 %reduce-scatter.42.cloned.1.call-done = f32[512,256]{1,0:T(8,128)} async-done(((f32[2048,256]{1,0:T(8,128)}), f32[512,256]{1,0:T(8,128)}) %reduce-scatter.42.cloned.1.call-update) | async-done | bytes 524304 | tf_op jit(solution)/shard_map/reduce_scatter | solution.py:315
  1436.3 32.4 %reduce-scatter.40.cloned.1.call-done = f32[512,256]{1,0:T(8,128)} async-done(((f32[2048,256]{1,0:T(8,128)}), f32[512,256]{1,0:T(8,128)}) %reduce-scatter.40.cloned.1.call-update) | async-done | bytes 524304 | tf_op jit(solution)/shard_map/reduce_scatter | solution.py:315
  1470.5 32.4 %reduce-scatter.46.cloned.1.call-done = f32[512,256]{1,0:T(8,128)} async-done(((f32[2048,256]{1,0:T(8,128)}), f32[512,256]{1,0:T(8,128)}) %reduce-scatter.46.cloned.1.call-update) | async-done | bytes 524304 | tf_op jit(solution)/shard_map/reduce_scatter | solution.py:315
  1504.9 31.4 %reduce-scatter.44.cloned.1.call-done = f32[512,256]{1,0:T(8,128)} async-done(((f32[2048,256]{1,0:T(8,128)}), f32[512,256]{1,0:T(8,128)}) %reduce-scatter.44.cloned.1.call-update) | async-done | bytes 524304 | tf_op jit(solution)/shard_map/reduce_scatter | solution.py:315
  1538.2 31.8 %reduce-scatter.50.cloned.1.call-done = f32[64,2048]{1,0:T(8,128)} async-done(((f32[256,2048]{1,0:T(8,128)}), f32[64,2048]{1,0:T(8,128)}) %reduce-scatter.50.cloned.1.call-update) | async-done | bytes 524304 | tf_op jit(solution)/shard_map/reduce_scatter | solution.py:315
  1571.8 31.6 %reduce-scatter.48.cloned.1.call-done = f32[64,2048]{1,0:T(8,128)} async-done(((f32[256,2048]{1,0:T(8,128)}), f32[64,2048]{1,0:T(8,128)}) %reduce-scatter.48.cloned.1.call-update) | async-done | bytes 524304 | tf_op jit(solution)/shard_map/reduce_scatter | solution.py:315
  1605.3 90.1 %reduce-scatter.34.cloned.1.call-done = f32[64,2048]{1,0:T(8,128)} async-done(((f32[512,2048]{1,0:T(8,128)}), f32[64,2048]{1,0:T(8,128)}) %reduce-scatter.34.cloned.1.call-update) | async-done | bytes 524304 | tf_op jit(solution)/shard_map/reduce_scatter | solution.py:307
  1698.9 4.0 bias_grad.1
  1703.1 19.0 all-gather.54.cloned.1.call-done
  1722.2 27.4 %all-gather.52.cloned.1.call-done = bf16[2048,640]{1,0:T(8,128)(2,1)} async-done(((bf16[512,640]{1,0:T(8,128)(2,1)}), bf16[2048,640]{1,0:T(8,128)(2,1)}) %all-gather.52.cloned.1.call-update) | async-done | bytes 2621456 | tf_op jit(solution)/shard_map/all_gather | solution.py:316
  1749.5 5.4 pad_maximum_fusion
  1755.0 21.2 %all-gather.58.cloned.1.call-done = bf16[2048,640]{1,0:T(8,128)(2,1)} async-done(((bf16[512,640]{1,0:T(8,128)(2,1)}), bf16[2048,640]{1,0:T(8,128)(2,1)}) %all-gather.58.cloned.1.call-update) | async-done | bytes 2621456 | tf_op jit(solution)/shard_map/all_gather | solution.py:316
  1776.2 26.8 %all-gather.56.cloned.1.call-done = bf16[2048,640]{1,0:T(8,128)(2,1)} async-done(((bf16[512,640]{1,0:T(8,128)(2,1)}), bf16[2048,640]{1,0:T(8,128)(2,1)}) %all-gather.56.cloned.1.call-update) | async-done | bytes 2621456 | tf_op jit(solution)/shard_map/all_gather | solution.py:316
  1803.0 5.4 pad_maximum_fusion.1
  1808.4 21.4 %all-gather.62.cloned.1.call-done = bf16[640,2048]{1,0:T(8,128)(2,1)} async-done(((bf16[160,2048]{1,0:T(8,128)(2,1)}), bf16[640,2048]{1,0:T(8,128)(2,1)}) %all-gather.62.cloned.1.call-update) | async-done | bytes 2621456 | tf_op jit(solution)/shard_map/all_gather | solution.py:316
  1829.8 26.6 %all-gather.60.cloned.1.call-done = bf16[640,2048]{1,0:T(8,128)(2,1)} async-done(((bf16[160,2048]{1,0:T(8,128)(2,1)}), bf16[640,2048]{1,0:T(8,128)(2,1)}) %all-gather.60.cloned.1.call-update) | async-done | bytes 2621456 | tf_op jit(solution)/shard_map/all_gather | solution.py:316
  1856.4 5.4 pad_maximum_fusion.2
  1861.8 13.3 all-gather.38.cloned.1.call-done
  1875.1 18.7 all-gather.36.cloned.1.call-done
  1896.8 15.5 all-gather.42.cloned.1.call-done
  1912.3 17.9 all-gather.40.cloned.1.call-done
  1933.3 15.0 all-gather.46.cloned.1.call-done
  1948.3 17.9 all-gather.44.cloned.1.call-done
  1969.3 15.0 all-gather.50.cloned.1.call-done
  1984.4 18.1 all-gather.48.cloned.1.call-done
  2005.6 40.5 %psum.7 = f32[9216]{0:T(1024)S(1)} all-reduce(f32[9216]{0:T(1024)S(1)} %pad_maximum_fusion.11), channel_id=1, replica_groups=mesh['tp'=8,'cp'=4] {'tp','cp'}, use_global_device_ids=true, to_apply=%region_24.25 | all-reduce | flops 9216 | bytes 73728 | tf_op jit(solution)/shard_map/psum | solution.py:408
  2048.1 7.1 all-gather.34.cloned.1.call-done
  (564 shorter events, 232.2 us)
Async XLA Ops:
  7.2 139.5 %reduce-scatter.22.cloned.1.call-start = ((), (), s32[]{:S(2)}) async-start(), calls=%async_computation.21 | async-start | bytes 4718592 | tf_op jit(solution)/shard_map/reduce_scatter | solution.py:307
  28.4 23.0 %copy-start.54 = (f32[512]{0:T(512)}, f32[512]{0:T(512)S(1)}, u32[]{:S(2)}) copy-start(f32[512]{0:T(512)S(1)} %get-tuple-element.178) | copy-start | bytes 6148
  28.4 23.0 %copy-start.56 = (f32[512]{0:T(512)}, f32[512]{0:T(512)S(1)}, u32[]{:S(2)}) copy-start(f32[512]{0:T(512)S(1)} %get-tuple-element.179) | copy-start | bytes 6148
  28.5 22.9 %copy-start.58 = (f32[512]{0:T(512)}, f32[512]{0:T(512)S(1)}, u32[]{:S(2)}) copy-start(f32[512]{0:T(512)S(1)} %get-tuple-element.180) | copy-start | bytes 6148
  28.5 22.9 %copy-start.60 = (f32[512]{0:T(512)}, f32[512]{0:T(512)S(1)}, u32[]{:S(2)}) copy-start(f32[512]{0:T(512)S(1)} %get-tuple-element.181) | copy-start | bytes 6148
  28.6 22.9 %copy-start.62 = (f32[512]{0:T(512)}, f32[512]{0:T(512)S(1)}, u32[]{:S(2)}) copy-start(f32[512]{0:T(512)S(1)} %get-tuple-element.182) | copy-start | bytes 6148
  28.6 22.9 %copy-start.64 = (f32[512]{0:T(512)}, f32[512]{0:T(512)S(1)}, u32[]{:S(2)}) copy-start(f32[512]{0:T(512)S(1)} %get-tuple-element.183) | copy-start | bytes 6148
  56.5 93.0 %copy-start.118 = (f32[2,2048]{1,0:T(2,128)S(1)}, f32[2,2048]{1,0:T(2,128)}, u32[]{:S(2)}) copy-start(f32[2,2048]{1,0:T(2,128)} %param.18) | copy-start | bytes 49156
  56.5 141.5 %all-gather.22.cloned.1.call-start = ((), (), s32[]{:S(2)}) async-start(), calls=%async_computation.22 | async-start | bytes 2359296 | tf_op jit(solution)/shard_map/all_gather | solution.py:311
  149.2 150.7 %reduce-scatter.24.cloned.1.call-start = ((), (), s32[]{:S(2)}) async-start(), calls=%async_computation.23 | async-start | bytes 4718592 | tf_op jit(solution)/shard_map/reduce_scatter | solution.py:307
  149.5 55.2 %copy-start.49 = (f32[1,2048]{1,0:T(1,128)}, f32[1,2048]{1,0:T(1,128)S(1)}, u32[]{:S(2)}) copy-start(f32[1,2048]{1,0:T(1,128)S(1)} %get-tuple-element.103) | copy-start | bytes 24580
  149.6 474.2 %copy-start.51 = (f32[1,2048]{1,0:T(1,128)}, f32[1,2048]{1,0:T(1,128)S(1)}, u32[]{:S(2)}) copy-start(f32[1,2048]{1,0:T(1,128)S(1)} %get-tuple-element.102) | copy-start | bytes 24580
  212.5 87.4 %copy-start.20 = (bf16[64,2048]{1,0:T(8,128)(2,1)S(1)}, bf16[64,2048]{1,0:T(8,128)(2,1)}, u32[]{:S(2)}) copy-start(bf16[64,2048]{1,0:T(8,128)(2,1)} %get-tuple-element.94) | copy-start | bytes 786436
  212.5 138.7 %all-gather.24.cloned.1.call-start = ((), (), s32[]{:S(2)}) async-start(), calls=%async_computation.24 | async-start | bytes 2359296 | tf_op jit(solution)/shard_map/all_gather | solution.py:311
  302.4 164.6 %reduce-scatter.26.cloned.1.call-start = ((), (), s32[]{:S(2)}) async-start(), calls=%async_computation.25 | async-start | bytes 4718592 | tf_op jit(solution)/shard_map/reduce_scatter | solution.py:307
  379.8 87.2 %copy-start.21 = (bf16[64,2048]{1,0:T(8,128)(2,1)S(1)}, bf16[64,2048]{1,0:T(8,128)(2,1)}, u32[]{:S(2)}) copy-start(bf16[64,2048]{1,0:T(8,128)(2,1)} %get-tuple-element.96) | copy-start | bytes 786436
  379.8 137.9 %all-gather.26.cloned.1.call-start = ((), (), s32[]{:S(2)}) async-start(), calls=%async_computation.26 | async-start | bytes 2359296 | tf_op jit(solution)/shard_map/all_gather | solution.py:311
  469.0 153.0 %reduce-scatter.28.cloned.1.call-start = ((), (), s32[]{:S(2)}) async-start(), calls=%async_computation.27 | async-start | bytes 4718592 | tf_op jit(solution)/shard_map/reduce_scatter | solution.py:307
  473.6 56.9 %copy-start.45 = (bf16[512,640]{1,0:T(8,128)(2,1)}, bf16[512,640]{1,0:T(8,128)(2,1)S(1)}, u32[]{:S(2)}) copy-start(bf16[512,640]{1,0:T(8,128)(2,1)S(1)} %fusion.46) | copy-start | bytes 1966084
  534.6 87.4 %copy-start.23 = (bf16[64,2048]{1,0:T(8,128)(2,1)S(1)}, bf16[64,2048]{1,0:T(8,128)(2,1)}, u32[]{:S(2)}) copy-start(bf16[64,2048]{1,0:T(8,128)(2,1)} %get-tuple-element.98) | copy-start | bytes 786436
  534.6 151.9 %all-gather.28.cloned.1.call-start = ((), (), s32[]{:S(2)}) async-start(), calls=%async_computation.28 | async-start | bytes 2359296 | tf_op jit(solution)/shard_map/all_gather | solution.py:311
  625.8 181.0 %reduce-scatter.30.cloned.1.call-start = ((), (), s32[]{:S(2)}) async-start(), calls=%async_computation.29 | async-start | bytes 4718592 | tf_op jit(solution)/shard_map/reduce_scatter | solution.py:307
  689.4 23.2 %copy-start.36 = (bf16[2,2048,256]{2,1,0:T(8,128)(2,1)S(1)}, bf16[2,2048,256]{2,1,0:T(8,128)(2,1)}, u32[]{:S(2)}) copy-start(bf16[2,2048,256]{2,1,0:T(8,128)(2,1)} %param.19) | copy-start | bytes 6291460
  718.8 140.4 %all-gather.30.cloned.1.call-start = ((), (), s32[]{:S(2)}) async-start(), calls=%async_computation.30 | async-start | bytes 2359296 | tf_op jit(solution)/shard_map/all_gather | solution.py:311
  810.4 151.7 %reduce-scatter.32.cloned.1.call-start = ((), (), s32[]{:S(2)}) async-start(), calls=%async_computation.31 | async-start | bytes 4718592 | tf_op jit(solution)/shard_map/reduce_scatter | solution.py:307
  874.7 87.4 %copy-start.50 = (f32[1,2048]{1,0:T(1,128)S(1)}, f32[1,2048]{1,0:T(1,128)}, u32[]{:S(2)}) copy-start(f32[1,2048]{1,0:T(1,128)} %copy-done.49) | copy-start | bytes 24580
  874.7 91.0 %copy-start.52 = (f32[1,2048]{1,0:T(1,128)S(1)}, f32[1,2048]{1,0:T(1,128)}, u32[]{:S(2)}) copy-start(f32[1,2048]{1,0:T(1,128)} %copy-done.51) | copy-start | bytes 24580
  874.7 91.0 %copy-start.127 = (f32[512]{0:T(512)S(1)}, f32[512]{0:T(512)}, u32[]{:S(2)}) copy-start(f32[512]{0:T(512)} %copy-done.126) | copy-start | bytes 6148
  874.7 139.8 %all-gather.32.cloned.1.call-start = ((), (), s32[]{:S(2)}) async-start(), calls=%async_computation.32 | async-start | bytes 2359296 | tf_op jit(solution)/shard_map/all_gather | solution.py:311
  965.7 112.1 %reduce-scatter.54.cloned.1.call-start = ((), (), s32[]{:S(2)}) async-start(), calls=%async_computation.53 | async-start | bytes 6553600 | tf_op jit(solution)/shard_map/reduce_scatter | solution.py:315
  971.8 148.5 %reduce-scatter.52.cloned.1.call-start = ((), (), s32[]{:S(2)}) async-start(), calls=%async_computation.51 | async-start | bytes 6553600 | tf_op jit(solution)/shard_map/reduce_scatter | solution.py:315
  978.5 195.2 %reduce-scatter.58.cloned.1.call-start = ((), (), s32[]{:S(2)}) async-start(), calls=%async_computation.57 | async-start | bytes 6553600 | tf_op jit(solution)/shard_map/reduce_scatter | solution.py:315
  985.2 241.2 %reduce-scatter.56.cloned.1.call-start = ((), (), s32[]{:S(2)}) async-start(), calls=%async_computation.55 | async-start | bytes 6553600 | tf_op jit(solution)/shard_map/reduce_scatter | solution.py:315
  991.9 287.3 %reduce-scatter.62.cloned.1.call-start = ((), (), s32[]{:S(2)}) async-start(), calls=%async_computation.61 | async-start | bytes 6553600 | tf_op jit(solution)/shard_map/reduce_scatter | solution.py:315
  998.4 333.6 %reduce-scatter.60.cloned.1.call-start = ((), (), s32[]{:S(2)}) async-start(), calls=%async_computation.59 | async-start | bytes 6553600 | tf_op jit(solution)/shard_map/reduce_scatter | solution.py:315
  1004.2 362.0 %reduce-scatter.38.cloned.1.call-start = ((), (), s32[]{:S(2)}) async-start(), calls=%async_computation.37 | async-start | bytes 2621440 | tf_op jit(solution)/shard_map/reduce_scatter | solution.py:315
  1008.7 391.5 %reduce-scatter.36.cloned.1.call-start = ((), (), s32[]{:S(2)}) async-start(), calls=%async_computation.35 | async-start | bytes 2621440 | tf_op jit(solution)/shard_map/reduce_scatter | solution.py:315
  1017.3 25.6 %copy-start.29 = (bf16[4,128,2048]{2,1,0:T(8,128)(2,1)S(1)}, bf16[4,128,2048]{2,1,0:T(8,128)(2,1)}, u32[]{:S(2)}) copy-start(bf16[4,128,2048]{2,1,0:T(8,128)(2,1)} %copy-done.28) | copy-start | bytes 6291460
  1045.0 389.4 %reduce-scatter.42.cloned.1.call-start = ((), (), s32[]{:S(2)}) async-start(), calls=%async_computation.41 | async-start | bytes 2621440 | tf_op jit(solution)/shard_map/reduce_scatter | solution.py:315
  1050.0 418.7 %reduce-scatter.40.cloned.1.call-start = ((), (), s32[]{:S(2)}) async-start(), calls=%async_computation.39 | async-start | bytes 2621440 | tf_op jit(solution)/shard_map/reduce_scatter | solution.py:315
  1054.9 448.0 %reduce-scatter.46.cloned.1.call-start = ((), (), s32[]{:S(2)}) async-start(), calls=%async_computation.45 | async-start | bytes 2621440 | tf_op jit(solution)/shard_map/reduce_scatter | solution.py:315
  1058.8 477.5 %reduce-scatter.44.cloned.1.call-start = ((), (), s32[]{:S(2)}) async-start(), calls=%async_computation.43 | async-start | bytes 2621440 | tf_op jit(solution)/shard_map/reduce_scatter | solution.py:315
  1062.8 507.2 %reduce-scatter.50.cloned.1.call-start = ((), (), s32[]{:S(2)}) async-start(), calls=%async_computation.49 | async-start | bytes 2621440 | tf_op jit(solution)/shard_map/reduce_scatter | solution.py:315
  1066.5 536.9 %reduce-scatter.48.cloned.1.call-start = ((), (), s32[]{:S(2)}) async-start(), calls=%async_computation.47 | async-start | bytes 2621440 | tf_op jit(solution)/shard_map/reduce_scatter | solution.py:315
  1071.1 624.2 %reduce-scatter.34.cloned.1.call-start = ((), (), s32[]{:S(2)}) async-start(), calls=%async_computation.33 | async-start | bytes 4718592 | tf_op jit(solution)/shard_map/reduce_scatter | solution.py:307
  1077.6 644.5 %all-gather.54.cloned.1.call-start = ((), (), s32[]{:S(2)}) async-start(), calls=%async_computation.54 | async-start | bytes 3276800 | tf_op jit(solution)/shard_map/all_gather | solution.py:316
  1080.0 669.6 %all-gather.52.cloned.1.call-start = ((), (), s32[]{:S(2)}) async-start(), calls=%async_computation.52 | async-start | bytes 3276800 | tf_op jit(solution)/shard_map/all_gather | solution.py:316
  1122.6 653.6 %all-gather.58.cloned.1.call-start = ((), (), s32[]{:S(2)}) async-start(), calls=%async_computation.58 | async-start | bytes 3276800 | tf_op jit(solution)/shard_map/all_gather | solution.py:316
  1176.0 627.0 %all-gather.56.cloned.1.call-start = ((), (), s32[]{:S(2)}) async-start(), calls=%async_computation.56 | async-start | bytes 3276800 | tf_op jit(solution)/shard_map/all_gather | solution.py:316
  1228.7 601.1 %all-gather.62.cloned.1.call-start = ((), (), s32[]{:S(2)}) async-start(), calls=%async_computation.62 | async-start | bytes 3276800 | tf_op jit(solution)/shard_map/all_gather | solution.py:316
  1281.5 575.0 %all-gather.60.cloned.1.call-start = ((), (), s32[]{:S(2)}) async-start(), calls=%async_computation.60 | async-start | bytes 3276800 | tf_op jit(solution)/shard_map/all_gather | solution.py:316
  1334.3 540.8 %all-gather.38.cloned.1.call-start = ((), (), s32[]{:S(2)}) async-start(), calls=%async_computation.38 | async-start | bytes 1310720 | tf_op jit(solution)/shard_map/all_gather | solution.py:316
  1368.0 525.8 %all-gather.36.cloned.1.call-start = ((), (), s32[]{:S(2)}) async-start(), calls=%async_computation.36 | async-start | bytes 1310720 | tf_op jit(solution)/shard_map/all_gather | solution.py:316
  1402.0 510.3 %all-gather.42.cloned.1.call-start = ((), (), s32[]{:S(2)}) async-start(), calls=%async_computation.42 | async-start | bytes 1310720 | tf_op jit(solution)/shard_map/all_gather | solution.py:316
  1436.2 494.0 %all-gather.40.cloned.1.call-start = ((), (), s32[]{:S(2)}) async-start(), calls=%async_computation.40 | async-start | bytes 1310720 | tf_op jit(solution)/shard_map/all_gather | solution.py:316
  1470.4 134.9 %copy-start.128 = (f32[64]{0:T(128)S(1)}, f32[64]{0:T(128)}, u32[]{:S(2)}) copy-start(f32[64]{0:T(128)} %get-tuple-element.99) | copy-start | bytes 772
  1470.4 477.9 %all-gather.46.cloned.1.call-start = ((), (), s32[]{:S(2)}) async-start(), calls=%async_computation.46 | async-start | bytes 1310720 | tf_op jit(solution)/shard_map/all_gather | solution.py:316
  1504.6 192.2 %copy-start.24 = (bf16[64,2048]{1,0:T(8,128)(2,1)S(1)}, bf16[64,2048]{1,0:T(8,128)(2,1)}, u32[]{:S(2)}) copy-start(bf16[64,2048]{1,0:T(8,128)(2,1)} %fusion.135) | copy-start | bytes 786436
  1504.6 461.6 %all-gather.44.cloned.1.call-start = ((), (), s32[]{:S(2)}) async-start(), calls=%async_computation.44 | async-start | bytes 1310720 | tf_op jit(solution)/shard_map/all_gather | solution.py:316
  1538.1 160.7 %copy-start.53 = (f32[2048]{0:T(1024)S(1)}, f32[2048]{0:T(1024)}, u32[]{:S(2)}) copy-start(f32[2048]{0:T(1024)} %get-tuple-element.59) | copy-start | bytes 24580
  1538.1 446.3 %all-gather.50.cloned.1.call-start = ((), (), s32[]{:S(2)}) async-start(), calls=%async_computation.50 | async-start | bytes 1310720 | tf_op jit(solution)/shard_map/all_gather | solution.py:316
  1571.7 127.1 %copy-start.1 = (f32[512,512]{1,0:T(8,128)S(1)}, f32[512,512]{1,0:T(8,128)}, u32[]{:S(2)}) copy-start(f32[512,512]{1,0:T(8,128)} %copy-done) | copy-start | bytes 3145732
  1571.8 430.7 %all-gather.48.cloned.1.call-start = ((), (), s32[]{:S(2)}) async-start(), calls=%async_computation.48 | async-start | bytes 1310720 | tf_op jit(solution)/shard_map/all_gather | solution.py:316
  1605.2 450.0 %all-gather.34.cloned.1.call-start = ((), (), s32[]{:S(2)}) async-start(), calls=%async_computation.34 | async-start | bytes 2359296 | tf_op jit(solution)/shard_map/all_gather | solution.py:311
  (119 other events, 1025.1 us)
Sparse Core Ops, SparseCore 0:
  56.6 89.9 reduce-scatter.21
  149.4 48.6 all-gather.21
  212.6 87.2 reduce-scatter.23
  302.5 48.6 all-gather.23
  380.0 86.9 reduce-scatter.25
  469.1 48.6 all-gather.25
  534.7 87.2 reduce-scatter.27
  626.0 48.6 all-gather.27
  718.9 87.9 reduce-scatter.29
  810.5 48.6 all-gather.29
  874.8 87.2 reduce-scatter.31
  965.8 48.6 all-gather.31
  1017.6 49.3 reduce-scatter.53
  1069.9 50.3 reduce-scatter.51
  1123.3 50.3 reduce-scatter.57
  1176.1 50.3 reduce-scatter.55
  1228.8 50.3 reduce-scatter.61
  1281.6 50.3 reduce-scatter.59
  1335.1 31.0 reduce-scatter.37
  1369.1 31.0 reduce-scatter.35
  1403.3 31.0 reduce-scatter.41
  1437.5 31.0 reduce-scatter.39
  1471.7 31.0 reduce-scatter.45
  1505.2 31.0 reduce-scatter.43
  1538.8 31.0 reduce-scatter.49
  1572.3 31.0 reduce-scatter.47
  1606.9 88.4 reduce-scatter.33
  1697.5 24.6 all-gather.53
  1724.3 25.1 all-gather.51
  1750.9 25.1 all-gather.57
  1777.8 25.1 all-gather.55
  1804.6 25.1 all-gather.61
  1831.2 25.1 all-gather.59
  1858.6 16.4 all-gather.37
  1877.3 16.4 all-gather.35
  1895.8 16.4 all-gather.41
  1913.7 16.4 all-gather.39
  1931.8 16.4 all-gather.45
  1949.8 16.4 all-gather.43
  1967.9 16.4 all-gather.49
  1985.9 16.4 all-gather.47
  2005.2 49.9 all-gather.33

commit v2 on v1

--- a/solution.py
+++ b/solution.py
@@ -303,17 +303,198 @@
     return d_x, d_gain
 
 
-def reduce_rows(partial):
-    return lax.psum_scatter(partial, 'tp', scatter_dimension=0, tiled=True)
-
-
-def gather_rows(shard):
-    return lax.all_gather(shard, 'tp', axis=0, tiled=True)
-
-
-def cp_sum(partial):
-    own = lax.psum_scatter(partial, 'cp', scatter_dimension=0, tiled=True).astype(BF16)
-    return lax.all_gather(own, 'cp', axis=0, tiled=True)
+def tp_places():
+    me = lax.axis_index('tp')
+    z, y = me // 2, lax.rem(me, 2)
+    return me, z, y
+
+
+def rsag_kernel(cfg, *refs):
+    n_mat, trans, layer, is_rms, n_big, n_small = cfg
+    it = iter(refs)
+    take = lambda n: [next(it) for _ in range(n)]
+    acts, weights = take(n_mat), take(n_mat)
+    res_ref = next(it)
+    xs_ref, gain_ref = take(2) if is_rms else (None, None)
+    bigs, smalls = take(n_big), take(n_small)
+    shard_ref, full_ref = take(2)
+    dgain_ref = next(it) if is_rms else None
+    bigs_g, smalls_g = take(n_big), take(n_small)
+    w_bufs = take(n_mat)
+    part, from_y, from_z, w_sem, ry_s, ry_r, rz_s, rz_r, gz_s, gz_r, gy_s, gy_r, x_s, x_r = take(14)
+    batch, _, _, seg, d_model = part.shape
+    half = d_model // 2
+    me, z, y = tp_places()
+    my_seg = y * 4 + z
+    pair = me + 1 - 2 * y
+    z_peer = [2 * lax.rem(z + j, 4) + y for j in range(4)]
+    cp_me, mate, across, diagonal = cp_places()
+    core = lax.rem(cp_me, 2)
+
+    loads = [pltpu.make_async_copy(w.at[layer], buf, w_sem.at[i]) for i, (w, buf) in enumerate(zip(weights, w_bufs))]
+    for load in loads:
+        load.start()
+
+    barrier = pltpu.get_barrier_semaphore()
+    for peer in [pair] + z_peer[1:]:
+        pl.semaphore_signal(barrier, inc=1, device_id={'tp': peer}, device_id_type=MESH)
+    n_peers = 4
+    if n_big + n_small:
+        n_peers = 7
+        for peer in (mate, across, diagonal):
+            pl.semaphore_signal(barrier, inc=1, device_id={'cp': peer}, device_id_type=MESH)
+    pl.semaphore_wait(barrier, n_peers)
+
+    def remote(src, dst, send, recv, axis, peer):
+        return pltpu.make_async_remote_copy(src_ref=src, dst_ref=dst, send_sem=send, recv_sem=recv, device_id={axis: peer}, device_id_type=MESH)
+
+    def big_copy(i, r):
+        peer = (mate, across, diagonal)[r]
+        want = core if r == 1 else 1 - core
+        src = bigs[i].at[:, pl.ds(pl.multiple_of(want * half, half), half)]
+        return remote(src, bigs_g[i].at[r], x_s.at[i, r], x_r.at[i, r], 'cp', peer)
+
+    def small_copy(i, r):
+        src = smalls[i] if r < 2 else smalls_g[i].at[1]
+        peer = across if r == 1 else mate
+        k = n_big + i
+        return remote(src, smalls_g[i].at[r], x_s.at[k, r], x_r.at[k, r], 'cp', peer)
+
+    for i in range(n_small):
+        small_copy(i, 1).start()
+        small_copy(i, 0).start()
+    for i in range(n_big):
+        for r in (1, 2, 0):
+            big_copy(i, r).start()
+    for load in loads:
+        load.wait()
+    if is_rms:
+        dgain_ref[...] = jnp.zeros_like(dgain_ref)
+
+    def y_sum(b):
+        return remote(part.at[b, 1 - y], from_y.at[b], ry_s.at[b], ry_r.at[b], 'tp', pair)
+
+    def z_sum(b, j):
+        return remote(part.at[b, y, lax.rem(z + j, 4)], from_z.at[b, j - 1], rz_s.at[b, j - 1], rz_r.at[b, j - 1], 'tp', z_peer[j])
+
+    def z_gather(b, j):
+        return remote(full_ref.at[b, my_seg], full_ref.at[b, my_seg], gz_s.at[b, j - 1], gz_r.at[b, j - 1], 'tp', z_peer[j])
+
+    def y_gather(b, j):
+        seg_j = y * 4 + lax.rem(z - j + 4, 4)
+        return remote(full_ref.at[b, seg_j], full_ref.at[b, seg_j], gy_s.at[b, j], gy_r.at[b, j], 'tp', pair)
+
+    def stage0(b):
+        total = None
+        for a, w, t in zip(acts, w_bufs, trans):
+            prod = dot_nt(a[b], w[...]) if t else dot_nn(a[b], w[...])
+            total = prod if total is None else total + prod
+        part[b] = total.reshape(2, 4, seg, d_model)
+        y_sum(b).start()
+
+    def stage1(b):
+        y_sum(b).wait_recv()
+        part[b, y] = part[b, y] + from_y[b]
+        for j in (2, 1, 3):
+            z_sum(b, j).start()
+
+    def stage2(b):
+        for j in (1, 2, 3):
+            z_sum(b, j).wait_recv()
+        total = part[b, y, z] + from_z[b, 0] + from_z[b, 1] + from_z[b, 2]
+        res = res_ref[b].astype(F32)
+        if is_rms:
+            d_norm = total.astype(BF16).astype(F32)
+            x_f = xs_ref[b].astype(F32)
+            inv_rms = lax.rsqrt(jnp.mean(x_f * x_f, axis=-1, keepdims=True) + NORM_EPS)
+            normed = x_f * inv_rms
+            dgain_ref[...] += jnp.sum(d_norm * normed, axis=0, keepdims=True)
+            d_normed = d_norm * gain_ref[...]
+            total = inv_rms * (d_normed - normed * jnp.mean(d_normed * normed, axis=-1, keepdims=True))
+        out = (res + total).astype(BF16)
+        full_ref[b, my_seg] = out
+        shard_ref[b] = out
+        for j in (2, 1, 3):
+            z_gather(b, j).start()
+        y_gather(b, 0).start()
+
+    def stage3(b):
+        for j in (1, 2, 3):
+            z_gather(b, j).wait_recv()
+            y_gather(b, j).start()
+
+    def slot_step(slot, carry):
+        for k, stage in enumerate((stage0, stage1, stage2, stage3)):
+            @pl.when(jnp.logical_and(slot >= k, slot < batch + k))
+            def _():
+                stage(slot - k)
+        return carry
+
+    lax.fori_loop(0, batch + 3, slot_step, 0)
+
+    for i in range(n_small):
+        small_copy(i, 1).wait_recv()
+        small_copy(i, 2).start()
+
+    def finish(b, carry):
+        for j in range(4):
+            y_gather(b, j).wait_recv()
+            y_gather(b, j).wait_send()
+        y_sum(b).wait_send()
+        for j in (1, 2, 3):
+            z_sum(b, j).wait_send()
+            z_gather(b, j).wait_send()
+        return carry
+
+    lax.fori_loop(0, batch, finish, 0)
+    for i in range(n_small):
+        small_copy(i, 0).wait_recv()
+        small_copy(i, 2).wait_recv()
+        for r in range(3):
+            small_copy(i, r).wait_send()
+    for i in range(n_big):
+        for r in range(3):
+            big_copy(i, r).wait()
+
+
+def rsag(acts, weights, trans, layer, res, cid, rms=None, bigs=(), smalls=()):
+    batch, rows, _ = acts[0].shape
+    seg, d_model = res.shape[1:]
+    n_tp = rows // seg
+    is_rms = rms is not None
+    any_spec = pl.BlockSpec(memory_space=pl.ANY)
+    dma = pltpu.SemaphoreType.DMA
+    outs = [jax.ShapeDtypeStruct(res.shape, BF16), jax.ShapeDtypeStruct((batch, n_tp, seg, d_model), BF16)]
+    if is_rms:
+        outs.append(jax.ShapeDtypeStruct((1, d_model), F32))
+    n_vmem = len(outs)
+    outs += [jax.ShapeDtypeStruct((3, a.shape[0], a.shape[1] // 2), BF16) for a in bigs]
+    outs += [jax.ShapeDtypeStruct((3,) + a.shape, BF16) for a in smalls]
+    n_x = len(bigs) + len(smalls)
+    result = pl.pallas_call(
+        functools.partial(rsag_kernel, (len(acts), trans, layer, is_rms, len(bigs), len(smalls))),
+        out_shape=tuple(outs),
+        in_specs=[VMEM_SPEC] * len(acts) + [any_spec] * len(weights) + [VMEM_SPEC] * (3 if is_rms else 1) + [any_spec] * n_x,
+        out_specs=tuple([VMEM_SPEC] * n_vmem + [any_spec] * n_x),
+        scratch_shapes=[pltpu.VMEM(w.shape[1:], BF16) for w in weights] + [
+            pltpu.VMEM((batch, 2, 4, seg, d_model), F32),
+            pltpu.VMEM((batch, 4, seg, d_model), F32),
+            pltpu.VMEM((batch, 3, seg, d_model), F32),
+            dma((len(acts),)),
+            dma((batch,)), dma((batch,)),
+            dma((batch, 3)), dma((batch, 3)),
+            dma((batch, 3)), dma((batch, 3)),
+            dma((batch, 4)), dma((batch, 4)),
+            dma((max(n_x, 1), 3)), dma((max(n_x, 1), 3)),
+        ],
+        compiler_params=pltpu.CompilerParams(collective_id=cid, has_side_effects=True, vmem_limit_bytes=40 * 2 ** 20),
+        cost_estimate=pl.CostEstimate(flops=4 * 10 ** 10, bytes_accessed=10 ** 7, transcendentals=0),
+        name='rsag',
+    )(*acts, *weights, res, *(rms or ()), *bigs, *smalls)
+    shard, full = result[:2]
+    full = full.reshape(batch * rows, d_model)
+    d_gain = result[2][0] if is_rms else None
+    return shard, full, d_gain, list(result[n_vmem:n_vmem + len(bigs)]), list(result[n_vmem + len(bigs):])
 
 
 def solution(mesh):
@@ -332,6 +513,10 @@
         width = heads * HEAD_DIM
         cp_index = lax.axis_index('cp')
         tp_index = lax.axis_index('tp')
+        core = lax.rem(cp_index, 2)
+        half = d_model // 2
+        seg = rows // tp_size
+        my_seg = lax.rem(tp_index, 2) * 4 + tp_index // 2
         seq = cp_size * rows
         start = (cp_index * rows).astype(jnp.int32)
 
@@ -344,72 +529,109 @@
         bias_cols = jnp.transpose(bias_from(rel_bias, rel_cols), (1, 2, 0, 3)).reshape(cp_size, rows, heads * rows)
 
         def own_rows(full):
-            return lax.dynamic_slice_in_dim(full, tp_index * (tokens // tp_size), tokens // tp_size, axis=0)
-
-        x = x_in.reshape(tokens, d_model)
-        x_s = own_rows(x)
-        saved = []
-        for l in range(n_layers):
-            h = rms_parts(x.astype(F32), g_attn[l])
+            return lax.dynamic_slice_in_dim(full, my_seg * seg, seg, axis=1)
+
+        def rows3(flat):
+            return flat.reshape(batch, rows, -1)
+
+        def own_half(flat):
+            return lax.dynamic_slice_in_dim(flat, core * half, half, axis=1)
+
+        def wide_rows(big, small):
+            (own, others), (s_own, s_others) = big, small
+            return (dot_tn(own_half(own), s_own) + dot_tn(others.reshape(-1, half), s_others.reshape(-1, s_own.shape[1]))).astype(BF16)
+
+        def wide_cols(small, big):
+            (own, others), (s_own, s_others) = big, small
+            return (dot_tn(s_own, own_half(own)) + dot_tn(s_others.reshape(-1, s_own.shape[1]), others.reshape(-1, half))).astype(BF16)
+
+        cores = [[0, 1], [2, 3]]
+
+        def join_rows(part):
+            return lax.all_gather(part, 'cp', axis=0, tiled=True, axis_index_groups=cores)
+
+        def join_cols(part):
+            both = lax.all_gather(part, 'cp', axis=0, tiled=False, axis_index_groups=cores)
+            return jnp.transpose(both, (1, 0, 2)).reshape(part.shape[0], 2 * part.shape[1])
+
+        def norm(flat, gain):
+            return rms_parts(flat.astype(F32), gain)
+
+        def project(h, l):
             q = jnp.dot(h, w_q[l], preferred_element_type=F32).astype(BF16)
             k = jnp.dot(h, w_k[l], preferred_element_type=F32).astype(BF16)
             v = jnp.dot(h, w_v[l], preferred_element_type=F32).astype(BF16)
-            kv = jnp.concatenate([k, v], axis=1).reshape(batch, rows, 2 * width)
-            o, kv_all = attn_fwd(q.reshape(batch, rows, width), kv, bias_rows, mask_rows, cp_size, 2 * l)
-            o = o.reshape(tokens, width)
-            x1_s = (x_s.astype(F32) + reduce_rows(jnp.dot(o, w_o[l], preferred_element_type=F32))).astype(BF16)
-            x1 = gather_rows(x1_s)
-            h2 = rms_parts(x1.astype(F32), g_mlp[l])
+            return q, rows3(jnp.concatenate([k, v], axis=1))
+
+        def mlp(h2, l):
             gate = jnp.dot(h2, w_gate[l], preferred_element_type=F32)
             lin = jnp.dot(h2, w_lin[l], preferred_element_type=F32)
-            u = (jax.nn.gelu(gate, approximate=True) * lin).astype(BF16)
-            saved.append((x_s, h, q, kv_all, o, x1_s, h2, gate, lin, u))
-            if l + 1 < n_layers:
-                x_s = (x1_s.astype(F32) + reduce_rows(jnp.dot(u, w_out[l], preferred_element_type=F32))).astype(BF16)
-                x = gather_rows(x_s)
-
-        d = d_y.reshape(tokens, d_model)
-        d_s = own_rows(d)
-        big = [[None] * n_layers for _ in range(7)]
-        gains = [[None] * n_layers for _ in range(2)]
-        ds_all = []
-        for l in reversed(range(n_layers)):
-            x_s, h, q, kv_all, o, x1_s, h2, gate, lin, u = saved[l]
-            big[6][l] = cp_sum(dot_tn(u, d))
+            return gate, lin, (jax.nn.gelu(gate, approximate=True) * lin).astype(BF16)
+
+        def mlp_grads(d, gate, lin, l):
             d_u = dot_nt(d, w_out[l]).astype(BF16).astype(F32)
             gelu_val, gelu_pull = jax.vjp(lambda g: jax.nn.gelu(g, approximate=True), gate)
-            d_lin = (d_u * gelu_val).astype(BF16)
-            d_gate = gelu_pull(d_u * lin)[0].astype(BF16)
-            big[4][l] = cp_sum(dot_tn(h2, d_gate))
-            big[5][l] = cp_sum(dot_tn(h2, d_lin))
-            dh2_s = reduce_rows(dot_nt(d_gate, w_gate[l]) + dot_nt(d_lin, w_lin[l]))
-            d_mid, gains[1][l] = rms_backward(dh2_s, x1_s.astype(F32), g_mlp[l])
-            dm_s = (d_mid + d_s.astype(F32)).astype(BF16)
-            dm = gather_rows(dm_s)
-            big[3][l] = cp_sum(dot_tn(o, dm))
+            return gelu_pull(d_u * lin)[0].astype(BF16), (d_u * gelu_val).astype(BF16)
+
+        def mlp_back(d_gate, d_lin, x1_s, d_s, l, cid, bigs, smalls):
+            return rsag([rows3(d_gate), rows3(d_lin)], [w_gate, w_lin], (True, True), l, d_s, cid, (x1_s, g_mlp[l][None]), bigs, smalls)
+
+        def attn_grads(q, kv_all, dm, l, cid):
             d_o = dot_nt(dm, w_o[l]).astype(BF16)
-            qdo = jnp.concatenate([q, d_o], axis=1).reshape(batch, rows, 2 * width)
-            d_q, d_kv, ds = attn_bwd(qdo, kv_all, bias_rows, bias_cols, mask_rows, mask_cols, 2 * l + 1)
-            ds_all.append(ds)
-            d_q = d_q.reshape(tokens, width)
-            d_kv = d_kv.reshape(tokens, 2 * width)
-            d_k, d_v = d_kv[:, :width], d_kv[:, width:]
-            big[0][l] = cp_sum(dot_tn(h, d_q))
-            big[1][l] = cp_sum(dot_tn(h, d_k))
-            big[2][l] = cp_sum(dot_tn(h, d_v))
-            dh_s = reduce_rows(dot_nt(d_q, w_q[l]) + dot_nt(d_k, w_k[l]) + dot_nt(d_v, w_v[l]))
-            d_x, gains[0][l] = rms_backward(dh_s, x_s.astype(F32), g_attn[l])
-            d_s = (d_x + dm_s.astype(F32)).astype(BF16)
-            d = gather_rows(d_s)
-
-        d_bias = bias_grad(ds_all[0], ds_all[1], start, heads, n_buckets)
+            d_q, d_kv, ds = attn_bwd(rows3(jnp.concatenate([q, d_o], axis=1)), kv_all, bias_rows, bias_cols, mask_rows, mask_cols, cid)
+            d_k, d_v = d_kv[:, :, :width], d_kv[:, :, width:]
+            d_qkv = jnp.concatenate([d_q, d_kv], axis=2).reshape(tokens, 3 * width)
+            return [d_q, d_k, d_v], d_qkv, ds
+
+        x = x_in.reshape(tokens, d_model)
+        d1 = d_y.reshape(tokens, d_model)
+        xs0 = own_rows(x_in)
+        ds1 = own_rows(d_y)
+
+        h0 = norm(x, g_attn[0])
+        q0, kv = project(h0, 0)
+        o0, kva0 = attn_fwd(rows3(q0), kv, bias_rows, mask_rows, cp_size, 0)
+        x1s0, x1, _, (h0_g,), _ = rsag([o0], [w_o], (False,), 0, xs0, 1, bigs=[h0])
+        h20 = norm(x1, g_mlp[0])
+        gate0, lin0, u0 = mlp(h20, 0)
+        o0 = o0.reshape(tokens, width)
+        xs1, x, _, (h20_g,), (o0_g, u0_g) = rsag([rows3(u0)], [w_out], (False,), 0, x1s0, 2, bigs=[h20], smalls=[o0, u0])
+
+        h1 = norm(x, g_attn[1])
+        q1, kv = project(h1, 1)
+        o1, kva1 = attn_fwd(rows3(q1), kv, bias_rows, mask_rows, cp_size, 3)
+        x1s1, x1, _, (h1_g, d1_g), _ = rsag([o1], [w_o], (False,), 1, xs1, 4, bigs=[h1, d1])
+        o1 = o1.reshape(tokens, width)
+        h21 = norm(x1, g_mlp[1])
+        gate1, lin1, u1 = mlp(h21, 1)
+        dg1, dl1 = mlp_grads(d1, gate1, lin1, 1)
+        dms1, dm1, dgm1, (h21_g,), (o1_g, u1_g, dg1_g, dl1_g) = mlp_back(dg1, dl1, x1s1, ds1, 1, 5, [h21], [o1, u1, dg1, dl1])
+        dqkv, dqkv1, score_grad1 = attn_grads(q1, kva1, dm1, 1, 6)
+        ds0, d0, dga1, (dm1_g,), (dqkv1_g,) = rsag(dqkv, [w_q, w_k, w_v], (True,) * 3, 1, dms1, 7, (xs1, g_attn[1][None]), [dm1], [dqkv1])
+
+        dg0, dl0 = mlp_grads(d0, gate0, lin0, 0)
+        dms0, dm0, dgm0, (d0_g,), (dg0_g, dl0_g) = mlp_back(dg0, dl0, x1s0, ds0, 0, 8, [d0], [dg0, dl0])
+        dqkv, dqkv0, score_grad0 = attn_grads(q0, kva0, dm0, 0, 9)
+        _, d_x, dga0, (dm0_g,), (dqkv0_g,) = rsag(dqkv, [w_q, w_k, w_v], (True,) * 3, 0, dms0, 10, (xs0, g_attn[0][None]), [dm0], [dqkv0])
+
+        big = []
+        for h, h_g, dqkv, dqkv_g in ((h0, h0_g, dqkv0, dqkv0_g), (h1, h1_g, dqkv1, dqkv1_g)):
+            part = wide_rows((h, h_g), (dqkv, dqkv_g))
+            big.append([join_rows(part[:, i * width:(i + 1) * width]) for i in range(3)])
+        w_o_grads = [join_cols(wide_cols((o, o_g), (dm, dm_g))) for o, o_g, dm, dm_g in ((o0, o0_g, dm0, dm0_g), (o1, o1_g, dm1, dm1_g))]
+        gate_grads = [join_rows(wide_rows((h, h_g), (d, d_g))) for h, h_g, d, d_g in ((h20, h20_g, dg0, dg0_g), (h21, h21_g, dg1, dg1_g))]
+        lin_grads = [join_rows(wide_rows((h, h_g), (d, d_g))) for h, h_g, d, d_g in ((h20, h20_g, dl0, dl0_g), (h21, h21_g, dl1, dl1_g))]
+        out_grads = [join_cols(wide_cols((u, u_g), (d, d_g))) for u, u_g, d, d_g in ((u0, u0_g, d0, d0_g), (u1, u1_g, d1, d1_g))]
+        grads = [jnp.stack([big[0][i], big[1][i]]) for i in range(3)] + [jnp.stack(p) for p in (w_o_grads, gate_grads, lin_grads, out_grads)]
+
+        d_bias = bias_grad(score_grad0, score_grad1, start, heads, n_buckets)
         slots = jnp.zeros((tp_size, n_buckets * heads), F32)
         slots = lax.dynamic_update_slice(slots, d_bias.reshape(1, -1), (tp_index, jnp.int32(0)))
-        small = lax.psum(jnp.concatenate([jnp.stack(gains[0]).reshape(-1), jnp.stack(gains[1]).reshape(-1), slots.reshape(-1)]), ('tp', 'cp'))
+        small = lax.psum(jnp.concatenate([dga0, dga1, dgm0, dgm1, slots.reshape(-1)]), ('tp', 'cp'))
         n_gain = n_layers * d_model
         d_g_attn = small[:n_gain].reshape(n_layers, d_model)
         d_g_mlp = small[n_gain:2 * n_gain].reshape(n_layers, d_model)
         d_rel = lax.dynamic_slice(small[2 * n_gain:].reshape(tp_size, -1), (tp_index, jnp.int32(0)), (1, n_buckets * heads)).reshape(n_buckets, heads)
-        return (d.reshape(batch, rows, d_model), d_rel, d_g_attn, d_g_mlp) + tuple(jnp.stack(parts) for parts in big)
+        return (d_x.reshape(batch, rows, d_model), d_rel, d_g_attn, d_g_mlp) + tuple(grads)
 
     return jax.shard_map(local_program, mesh=mesh, in_specs=(seq_spec, seq_spec, P(None, 'cp'), P(None, 'tp')) + weight_specs, out_specs=(seq_spec, P(None, 'tp')) + weight_specs, check_vma=False)

time: 2070 us -> 1180 us (0.57)
  waiting for transfers between devices: 1590 us -> 18.7 us
  Pallas kernels: 82.8 us -> 736 us
  local copies, waits for them, and re-layouts: 78.6 us -> 202 us
  other arithmetic: 105 us -> 54.4 us
  matrix products: 140 us -> 90 us
    reduce_scatter x21 -> x0, waiting for transfers between devices: 1110 us -> none  [the longest x7 616 us: reduce_rows(): return lax.psum_scatter(partial, 'tp', scatter_dimension=0, tiled=True)]
    pallas_call x0 -> x7, Pallas kernels: none -> 652 us  [rsag(): pl.pallas_call(functools.partial(rsag_kernel, (len(acts), trans, layer, i...]
    all_gather x21 -> x14, waiting for transfers between devices: 477 us -> 16.1 us  [the longest x10 16.1 us: join_rows(): lax.all_gather(part, 'cp', axis=0, tiled=True, axis_index_groups=cores)]
    broadcast_in_dim x80, local copies, waits for them, and re-layouts: 50 us -> 117 us  [bias_from(): jnp.where((buckets == k)[None], table[:, k].reshape((-1,) + (1,) * rel.nd...]
    convert_element_type x18 -> x0, other arithmetic: 35.9 us -> none  [the longest x14 27.6 us: cp_sum(): lax.psum_scatter(partial, 'cp', scatter_dimension=0, tiled=True)]
    dot_general x14 -> x4, matrix products: 40.6 us -> 12 us  [dot_nt(): lax.dot_general(a, b, (((1,), (1,)), ((), ())), preferred_element_type=F32)]
    unnamed x286 -> x416, local copies, waits for them, and re-layouts: 21.6 us -> 44.6 us
    dot_general x14 -> x20, matrix products: 66.2 us -> 56.9 us  [dot_tn(): lax.dot_general(a, b, (((0,), (0,)), ((), ())), preferred_element_type=F32)]
  transfers between devices with their start and end apart: 42 -> 14, of which waited for: 40 -> 2; matrix products, arithmetic and copies ran while one was open for 10% -> 9% of each run, Pallas kernels for 1% -> 18%
where the time goes in v2:
time: 1180 us; the launch traced here: 1170 us
  Pallas kernels  736 us (62%)
  local copies, waits for them, and re-layouts  202 us (17%)
  matrix products  90 us (8%)
  other arithmetic  54.4 us (5%)
  blocking collectives  46.3 us (4%)
  waiting for transfers between devices  18.7 us (2%)
  between operations  16.8 us (1%)
    pallas_call x7, Pallas kernels, rsag(): pl.pallas_call(functools.partial(rsag_kernel, (len(acts), trans, layer, i...  652 us
    broadcast_in_dim x80, local copies, waits for them, and re-layouts, bias_from(): jnp.where((buckets == k)[None], table[:, k].reshape((-1,) + (1,) * rel.nd...  117 us
    dot_general x20, matrix products, dot_tn(): lax.dot_general(a, b, (((0,), (0,)), ((), ())), preferred_element_type=F32)  56.9 us
    pallas_call x2, Pallas kernels, attn_bwd(): pl.pallas_call(functools.partial(attn_bwd_kernel, heads), out_shape=(jax....  46.5 us
    unnamed x416, local copies, waits for them, and re-layouts  44.6 us
    psum x1, blocking collectives, local_program(): lax.psum(jnp.concatenate([dga0, dga1, dgm0, dgm1, slots.reshape(-1)]), ('...  40.2 us
    pallas_call x2, Pallas kernels, attn_fwd(): pl.pallas_call(functools.partial(attn_fwd_kernel, heads), out_shape=(jax....  33.5 us
  transfers between devices with their start and end apart: 14, of which 2 were waited for; matrix products, arithmetic and copies ran while one was open for 9% of the time, Pallas kernels for 18%

profile of v2, /device:TPU:0, one launch (start us, length us, event | category | flops | bytes accessed | tf_op | source)
XLA Modules:
  0.0 1165.4 jit_solution(17118758061548395449)
XLA Ops:
  9.1 6.1 all_gather.57
  15.3 2.1 slice_reduce_fusion.30
  17.4 2.4 slice_reduce_fusion.31
  19.8 2.1 multiply_reduce_fusion.3
  30.5 2.5 broadcast_compare_fusion.60
  36.2 6.8 select_select_fusion.1.bias_ref.bias_r_ref
  43.4 16.4 %attn_fwd.2 = (bf16[4,128,256]{2,1,0:T(8,128)(2,1)S(1)}, bf16[4,4,128,512]{3,2,1,0:T(8,128)(2,1)S(1)}) custom-call(bf16[4,128,256]{2,1,0:T(8,128)(2,1)S(1)} %bitcast.374, bf16[4,128,512]{2,1,0:T(8,128)(2,1)S(1)} %bitcast.366, f32[512,512]{1,0:T(8,128)S(1)} %select_select_fusion.1.bias_ref.bias_r_ref, f32[4,1,512]{2,1,0:T(1,128)S(1)} %broadcast_in_dim.1271.mask_ref.mask_r_ref), custom_call_target="tpu_custom_call" | custom-call | flops 4000000000 | bytes 6000000 | tf_op jit(solution)/shard_map/attn_fwd/pallas_call | solution.py:117
  61.2 91.0 %rsag.7 = (bf16[4,16,2048]{2,1,0:T(8,128)(2,1)S(1)}, bf16[4,8,16,2048]{3,2,1,0:T(8,128)(2,1)S(1)}, bf16[3,512,1024]{2,1,0:T(8,128)(2,1)S(1)}) custom-call(bf16[4,128,256]{2,1,0:T(8,128)(2,1)S(1)} %get-tuple-element.56.refs_0_, bf16[2,256,2048]{2,1,0:T(8,128)(2,1)S(1)} %copy-done.44, bf16[4,16,2048]{2,1,0:T(8,128)(2,1)S(1)} %get-tuple-element.277.refs_2_.refs_7_, ...), custom_call_target="tpu_custom_call" | custom-call | flops 40000000000 | bytes 10000000 | tf_op jit(solution)/shard_map/rsag/pallas_call | solution.py:474
  156.3 4.6 fusion.26
  160.9 2.9 multiply_convert_fusion.5
  163.8 90.6 %rsag.8 = (bf16[4,16,2048]{2,1,0:T(8,128)(2,1)S(1)}, bf16[4,8,16,2048]{3,2,1,0:T(8,128)(2,1)S(1)}, bf16[3,512,1024]{2,1,0:T(8,128)(2,1)S(1)}, bf16[3,512,256]{2,1,0:T(8,128)(2,1)S(1)}, bf16[3,512,640]{2,1,0:T(8,128)(2,1)S(1)}) custom-call(bf16[4,128,640]{2,1,0:T(8,128)(2,1)S(1)} %bitcast.349, bf16[2,640,2048]{2,1,0:T(8,128)(2,1)} %refs_1_.4, ...), custom_call_target="tpu_custom_call" | custom-call | flops 40000000000 | bytes 10000000 | tf_op jit(solution)/shard_map/rsag/pallas_call | solution.py:474
  266.8 5.0 fusion.34
  271.9 2.6 broadcast_compare_fusion.30
  297.4 1.9 broadcast_in_dim.1291
  314.0 2.0 broadcast_in_dim.1305
  326.9 1.9 broadcast_in_dim.1315
  334.2 1.9 broadcast_in_dim.1321
  348.8 1.9 broadcast_in_dim.1333
  374.4 1.9 broadcast_in_dim.1354
  385.4 1.9 broadcast_in_dim.1363
  393.0 17.0 %attn_fwd.3 = (bf16[4,128,256]{2,1,0:T(8,128)(2,1)S(1)}, bf16[4,4,128,512]{3,2,1,0:T(8,128)(2,1)S(1)}) custom-call(bf16[4,128,256]{2,1,0:T(8,128)(2,1)S(1)} %bitcast.375, bf16[4,128,512]{2,1,0:T(8,128)(2,1)S(1)} %bitcast.369, f32[512,512]{1,0:T(8,128)S(1)} %select_select_fusion.1.bias_ref.bias_r_ref, f32[4,1,512]{2,1,0:T(1,128)S(1)} %broadcast_in_dim.1271.mask_ref.mask_r_ref), custom_call_target="tpu_custom_call" | custom-call | flops 4000000000 | bytes 6000000 | tf_op jit(solution)/shard_map/attn_fwd/pallas_call | solution.py:117
  411.4 95.5 %rsag.9 = (bf16[4,16,2048]{2,1,0:T(8,128)(2,1)S(1)}, bf16[4,8,16,2048]{3,2,1,0:T(8,128)(2,1)S(1)}, bf16[3,512,1024]{2,1,0:T(8,128)(2,1)S(1)}, bf16[3,512,1024]{2,1,0:T(8,128)(2,1)}) custom-call(bf16[4,128,256]{2,1,0:T(8,128)(2,1)S(1)} %get-tuple-element.60.refs_0_, bf16[2,256,2048]{2,1,0:T(8,128)(2,1)S(1)} %copy-done.45, ...), custom_call_target="tpu_custom_call" | custom-call | flops 40000000000 | bytes 10000000 | tf_op jit(solution)/shard_map/rsag/pallas_call | solution.py:474
  511.1 4.4 fusion.18
  515.6 2.6 multiply_convert_fusion.4
  518.4 97.3 %rsag.10 = (bf16[4,16,2048]{2,1,0:T(8,128)(2,1)S(1)}, bf16[4,8,16,2048]{3,2,1,0:T(8,128)(2,1)S(1)}, f32[1,2048]{1,0:T(1,128)S(1)}, bf16[3,512,1024]{2,1,0:T(8,12...) custom-call(bf16[4,128,640]{2,1,0:T(8,128)(2,1)S(1)} %bitcast.389, ...), custom_call_target="tpu_custom_call" | custom-call | flops 40000000000 | bytes 10000000 | tf_op jit(solution)/shard_map/rsag/pallas_call | solution.py:474
  622.4 5.1 select_select_fusion.bias_c_ref
  627.5 23.4 %attn_bwd.2 = (bf16[4,128,256]{2,1,0:T(8,128)(2,1)S(1)}, bf16[4,128,512]{2,1,0:T(8,128)(2,1)S(1)}, f32[512,512]{1,0:T(8,128)S(1)}) custom-call(bf16[4,128,512]{2,1,0:T(8,128)(2,1)S(1)} %bitcast.367, bf16[4,4,128,512]{3,2,1,0:T(8,128)(2,1)S(1)} %copy-done.85, f32[512,512]{1,0:T(8,128)S(1)} %select_select_fusion.1.bias_ref.bias_r_ref, ...), custom_call_target="tpu_custom_call" | custom-call | flops 10000000000 | bytes 10000000 | tf_op jit(solution)/shard_map/attn_bwd/pallas_call | solution.py:235
  659.6 89.9 %rsag.11 = (bf16[4,16,2048]{2,1,0:T(8,128)(2,1)S(1)}, bf16[4,8,16,2048]{3,2,1,0:T(8,128)(2,1)S(1)}, f32[1,2048]{1,0:T(1,128)S(1)}, bf16[3,512,1024]{2,1,0:T(8,128)(2,1)}, bf16[3,512,768]{2,1,0:T(8,128)(2,1)}) custom-call(bf16[4,128,256]{2,1,0:T(8,128)(2,1)S(1)} %get-tuple-element.66.refs_0_, bf16[4,128,256]{2,1,0:T(8,128)(2,1)S(1)} %get-tuple-element.169.refs_1_, ...), custom_call_target="tpu_custom_call" | custom-call | flops 40000000000 | bytes 10000000 | tf_op jit(solution)/shard_map/rsag/pallas_call | solution.py:474
  749.5 3.7 convolution_bitcast_fusion
  754.7 5.4 fusion.41
  760.2 95.1 %rsag.12 = (bf16[4,16,2048]{2,1,0:T(8,128)(2,1)S(1)}, bf16[4,8,16,2048]{3,2,1,0:T(8,128)(2,1)S(1)}, f32[1,2048]{1,0:T(1,128)S(1)}, bf16[3,512,1024]{2,1,0:T(8,12...) custom-call(bf16[4,128,640]{2,1,0:T(8,128)(2,1)S(1)} %bitcast.391, ...), custom_call_target="tpu_custom_call" | custom-call | flops 40000000000 | bytes 10000000 | tf_op jit(solution)/shard_map/rsag/pallas_call | solution.py:474
  860.3 23.2 %attn_bwd.3 = (bf16[4,128,256]{2,1,0:T(8,128)(2,1)S(1)}, bf16[4,128,512]{2,1,0:T(8,128)(2,1)S(1)}, f32[512,512]{1,0:T(8,128)S(1)}) custom-call(bf16[4,128,512]{2,1,0:T(8,128)(2,1)S(1)} %bitcast.368, bf16[4,4,128,512]{3,2,1,0:T(8,128)(2,1)S(1)} %copy-done.83, f32[512,512]{1,0:T(8,128)S(1)} %copy-done.14, f32[4,128,512]{2,1,0:T(8,128)S(1)} %copy-done.16, ...), custom_call_target="tpu_custom_call" | custom-call | flops 10000000000 | bytes 10000000 | tf_op jit(solution)/shard_map/attn_bwd/pallas_call | solution.py:235
  885.8 93.1 %rsag.13 = (bf16[4,16,2048]{2,1,0:T(8,128)(2,1)}, bf16[4,8,16,2048]{3,2,1,0:T(8,128)(2,1)S(1)}, f32[1,2048]{1,0:T(1,128)S(1)}, bf16[3,512,1024]{2,1,0:T(8,128)(2,1)}, bf16[3,512,768]{2,1,0:T(8,128)(2,1)}) custom-call(bf16[4,128,256]{2,1,0:T(8,128)(2,1)S(1)} %get-tuple-element.73.refs_0_, bf16[4,128,256]{2,1,0:T(8,128)(2,1)S(1)} %get-tuple-element.167.refs_1_, ...), custom_call_target="tpu_custom_call" | custom-call | flops 40000000000 | bytes 10000000 | tf_op jit(solution)/shard_map/rsag/pallas_call | solution.py:474
  979.0 3.7 convolution_bitcast_fusion.1
  984.0 2.6 fusion.72
  987.2 2.8 fusion.8
  991.7 2.6 fusion.74
  994.9 2.8 fusion.9
  1001.7 2.4 fusion.66
  1004.1 5.3 fusion.10
  1009.5 2.4 fusion.68
  1011.9 3.5 fusion.11
  1015.7 2.6 fusion.86
  1018.6 3.8 fusion.14
  1025.0 3.8 fusion.15
  1029.0 2.4 fusion.84
  1031.7 3.9 fusion.12
  1038.2 3.8 fusion.13
  1042.1 4.0 bias_grad.1
  1046.4 40.2 %psum.7 = f32[9216]{0:T(1024)S(1)} all-reduce(f32[9216]{0:T(1024)S(1)} %constant_dynamic-update-slice_fusion), channel_id=1, replica_groups=mesh['tp'=8,'cp'=4] {'tp','cp'}, use_global_device_ids=true, to_apply=%region_5.6 | all-reduce | flops 9216 | bytes 73728 | tf_op jit(solution)/shard_map/psum | solution.py:630
  1088.7 2.3 copy.54
  1091.8 2.3 copy.52
  1095.0 3.1 pad_maximum_fusion.5
  1098.1 3.1 pad_maximum_fusion.4
  1101.1 3.1 pad_maximum_fusion.3
  1105.7 5.9 copy.62
  1111.6 4.3 stack_reshape.15
  1115.9 5.9 copy.60
  1121.9 5.5 stack_reshape.14
  1127.3 5.4 pad_maximum_fusion
  1132.8 2.0 all-gather.37.cloned.1.call-done
  1134.7 14.1 %all-gather.35.cloned.1.call-done = bf16[2048,640]{1,0:T(8,128)(2,1)} async-done(((bf16[1024,640]{1,0:T(8,128)(2,1)}), bf16[2048,640]{1,0:T(8,128)(2,1)}) %all-gather.35.cloned.1.call-update) | async-done | bytes 2621456 | tf_op jit(solution)/shard_map/all_gather | solution.py:551
  1148.8 5.6 pad_maximum_fusion.1
  1154.4 2.8 pad_maximum_fusion.2
  (598 shorter events, 186.3 us)
Async XLA Ops:
  7.2 15.4 %copy-start.96 = (bf16[4,128,2048]{2,1,0:T(8,128)(2,1)S(1)}, bf16[4,128,2048]{2,1,0:T(8,128)(2,1)}, u32[]{:S(2)}) copy-start(bf16[4,128,2048]{2,1,0:T(8,128)(2,1)} %param.13) | copy-start | bytes 6291460
  7.2 14.7 %copy-start.168 = (f32[2,2048]{1,0:T(2,128)S(1)}, f32[2,2048]{1,0:T(2,128)}, u32[]{:S(2)}) copy-start(f32[2,2048]{1,0:T(2,128)} %param.17) | copy-start | bytes 49156
  7.2 14.7 %copy-start.169 = (f32[2,2048]{1,0:T(2,128)S(1)}, f32[2,2048]{1,0:T(2,128)}, u32[]{:S(2)}) copy-start(f32[2,2048]{1,0:T(2,128)} %param.18) | copy-start | bytes 49156
  7.2 1081.5 %all-gather.41.cloned.1.call-start = ((), (), s32[]{:S(2)}) async-start(), calls=%async_computation.11 | async-start | bytes 1572864 | tf_op jit(solution)/shard_map/all_gather | solution.py:554
  27.6 15.8 %copy-start.34 = (bf16[512,256]{1,0:T(8,128)(2,1)}, bf16[512,256]{1,0:T(8,128)(2,1)S(1)}, u32[]{:S(2)}) copy-start(bf16[512,256]{1,0:T(8,128)(2,1)S(1)} %convolution_convert_fusion.7) | copy-start | bytes 786436
  33.1 9.9 copy-start.131
  33.1 9.9 copy-start.133
  33.2 9.8 copy-start.135
  33.2 9.8 copy-start.137
  33.3 9.8 copy-start.139
  33.3 9.8 copy-start.141
  33.4 9.7 copy-start.142
  33.4 9.7 copy-start.143
  33.5 9.6 copy-start.144
  33.5 9.6 copy-start.145
  33.6 9.6 copy-start.147
  36.2 25.0 %copy-start.36 = (bf16[4,16,2048]{2,1,0:T(8,128)(2,1)}, bf16[4,16,2048]{2,1,0:T(8,128)(2,1)S(1)}, u32[]{:S(2)}) copy-start(bf16[4,16,2048]{2,1,0:T(8,128)(2,1)S(1)} %get-tuple-element.277.refs_2_.refs_7_) | copy-start | bytes 786436
  43.3 584.1 %copy-start.13 = (f32[512,512]{1,0:T(8,128)}, f32[512,512]{1,0:T(8,128)S(1)}, u32[]{:S(2)}) copy-start(f32[512,512]{1,0:T(8,128)S(1)} %select_select_fusion.1.bias_ref.bias_r_ref) | copy-start | bytes 3145732
  43.4 17.8 %copy-start.2 = (bf16[512,2048]{1,0:T(8,128)(2,1)S(1)}, bf16[512,2048]{1,0:T(8,128)(2,1)}, u32[]{:S(2)}) copy-start(bf16[512,2048]{1,0:T(8,128)(2,1)} %fusion.7.refs_3_) | copy-start | bytes 6291460
  43.4 17.8 %copy-start.44 = (bf16[2,256,2048]{2,1,0:T(8,128)(2,1)S(1)}, bf16[2,256,2048]{2,1,0:T(8,128)(2,1)}, u32[]{:S(2)}) copy-start(bf16[2,256,2048]{2,1,0:T(8,128)(2,1)} %refs_1_.5) | copy-start | bytes 6291460
  163.8 90.6 %copy-start.21 = (bf16[512,640]{1,0:T(8,128)(2,1)}, bf16[512,640]{1,0:T(8,128)(2,1)S(1)}, u32[]{:S(2)}) copy-start(bf16[512,640]{1,0:T(8,128)(2,1)S(1)} %get-tuple-element.242.refs_5_) | copy-start | bytes 1966084
  392.9 18.4 %copy-start.6 = (bf16[512,2048]{1,0:T(8,128)(2,1)S(1)}, bf16[512,2048]{1,0:T(8,128)(2,1)}, u32[]{:S(2)}) copy-start(bf16[512,2048]{1,0:T(8,128)(2,1)} %fusion.3.refs_3_) | copy-start | bytes 6291460
  392.9 18.4 %copy-start.23 = (bf16[4,128,2048]{2,1,0:T(8,128)(2,1)S(1)}, bf16[4,128,2048]{2,1,0:T(8,128)(2,1)}, u32[]{:S(2)}) copy-start(bf16[4,128,2048]{2,1,0:T(8,128)(2,1)} %param.14) | copy-start | bytes 6291460
  393.0 18.4 %copy-start.45 = (bf16[2,256,2048]{2,1,0:T(8,128)(2,1)S(1)}, bf16[2,256,2048]{2,1,0:T(8,128)(2,1)}, u32[]{:S(2)}) copy-start(bf16[2,256,2048]{2,1,0:T(8,128)(2,1)} %refs_1_.5) | copy-start | bytes 6291460
  393.0 18.4 %copy-start.94 = (bf16[4,16,2048]{2,1,0:T(8,128)(2,1)S(1)}, bf16[4,16,2048]{2,1,0:T(8,128)(2,1)}, u32[]{:S(2)}) copy-start(bf16[4,16,2048]{2,1,0:T(8,128)(2,1)} %copy-done.93) | copy-start | bytes 786436
  411.3 95.6 %copy-start.30 = (bf16[4,128,256]{2,1,0:T(8,128)(2,1)}, bf16[4,128,256]{2,1,0:T(8,128)(2,1)S(1)}, u32[]{:S(2)}) copy-start(bf16[4,128,256]{2,1,0:T(8,128)(2,1)S(1)} %get-tuple-element.60.refs_0_) | copy-start | bytes 786436
  518.2 97.5 %copy-start.22 = (bf16[512,640]{1,0:T(8,128)(2,1)}, bf16[512,640]{1,0:T(8,128)(2,1)S(1)}, u32[]{:S(2)}) copy-start(bf16[512,640]{1,0:T(8,128)(2,1)S(1)} %get-tuple-element.155.refs_9_) | copy-start | bytes 1966084
  518.2 97.5 %copy-start.60 = (bf16[512,640]{1,0:T(8,128)(2,1)}, bf16[512,640]{1,0:T(8,128)(2,1)S(1)}, u32[]{:S(2)}) copy-start(bf16[512,640]{1,0:T(8,128)(2,1)S(1)} %get-tuple-element.157.refs_11_) | copy-start | bytes 1966084
  518.2 97.5 %copy-start.62 = (bf16[512,640]{1,0:T(8,128)(2,1)}, bf16[512,640]{1,0:T(8,128)(2,1)S(1)}, u32[]{:S(2)}) copy-start(bf16[512,640]{1,0:T(8,128)(2,1)S(1)} %get-tuple-element.156.refs_10_) | copy-start | bytes 1966084
  518.3 100.1 %copy-start.46 = (bf16[2,256,2048]{2,1,0:T(8,128)(2,1)S(1)}, bf16[2,256,2048]{2,1,0:T(8,128)(2,1)}, u32[]{:S(2)}) copy-start(bf16[2,256,2048]{2,1,0:T(8,128)(2,1)} %refs_1_.5) | copy-start | bytes 6291460
  518.3 102.2 %copy-start.117 = (pred[4,128,512]{2,1,0:T(8,128)(4,1)S(1)}, pred[4,128,512]{2,1,0:T(8,128)(4,1)}, u32[]{:S(2)}) copy-start(pred[4,128,512]{2,1,0:T(8,128)(4,1)} %broadcast_in_dim.1330) | copy-start | bytes 786436
  518.3 102.2 %copy-start.118 = (pred[4,128,512]{2,1,0:T(8,128)(4,1)S(1)}, pred[4,128,512]{2,1,0:T(8,128)(4,1)}, u32[]{:S(2)}) copy-start(pred[4,128,512]{2,1,0:T(8,128)(4,1)} %broadcast_in_dim.1333) | copy-start | bytes 786436
  518.3 102.2 %copy-start.119 = (pred[4,128,512]{2,1,0:T(8,128)(4,1)S(1)}, pred[4,128,512]{2,1,0:T(8,128)(4,1)}, u32[]{:S(2)}) copy-start(pred[4,128,512]{2,1,0:T(8,128)(4,1)} %broadcast_in_dim.1336) | copy-start | bytes 786436
  518.3 102.2 %copy-start.120 = (pred[4,128,512]{2,1,0:T(8,128)(4,1)S(1)}, pred[4,128,512]{2,1,0:T(8,128)(4,1)}, u32[]{:S(2)}) copy-start(pred[4,128,512]{2,1,0:T(8,128)(4,1)} %broadcast_in_dim.1339) | copy-start | bytes 786436
  518.4 102.2 %copy-start.121 = (pred[4,128,512]{2,1,0:T(8,128)(4,1)S(1)}, pred[4,128,512]{2,1,0:T(8,128)(4,1)}, u32[]{:S(2)}) copy-start(pred[4,128,512]{2,1,0:T(8,128)(4,1)} %broadcast_in_dim.1342) | copy-start | bytes 786436
  518.4 102.2 %copy-start.122 = (pred[4,128,512]{2,1,0:T(8,128)(4,1)S(1)}, pred[4,128,512]{2,1,0:T(8,128)(4,1)}, u32[]{:S(2)}) copy-start(pred[4,128,512]{2,1,0:T(8,128)(4,1)} %broadcast_in_dim.1345) | copy-start | bytes 786436
  518.4 102.2 %copy-start.123 = (pred[4,128,512]{2,1,0:T(8,128)(4,1)S(1)}, pred[4,128,512]{2,1,0:T(8,128)(4,1)}, u32[]{:S(2)}) copy-start(pred[4,128,512]{2,1,0:T(8,128)(4,1)} %broadcast_in_dim.1348) | copy-start | bytes 786436
  518.4 102.2 %copy-start.124 = (pred[4,128,512]{2,1,0:T(8,128)(4,1)S(1)}, pred[4,128,512]{2,1,0:T(8,128)(4,1)}, u32[]{:S(2)}) copy-start(pred[4,128,512]{2,1,0:T(8,128)(4,1)} %broadcast_in_dim.1351) | copy-start | bytes 786436
  518.4 102.2 %copy-start.125 = (pred[4,128,512]{2,1,0:T(8,128)(4,1)S(1)}, pred[4,128,512]{2,1,0:T(8,128)(4,1)}, u32[]{:S(2)}) copy-start(pred[4,128,512]{2,1,0:T(8,128)(4,1)} %broadcast_in_dim.1354) | copy-start | bytes 786436
  518.4 102.2 %copy-start.126 = (pred[4,128,512]{2,1,0:T(8,128)(4,1)S(1)}, pred[4,128,512]{2,1,0:T(8,128)(4,1)}, u32[]{:S(2)}) copy-start(pred[4,128,512]{2,1,0:T(8,128)(4,1)} %broadcast_in_dim.1357) | copy-start | bytes 786436
  518.4 102.2 %copy-start.127 = (pred[4,128,512]{2,1,0:T(8,128)(4,1)S(1)}, pred[4,128,512]{2,1,0:T(8,128)(4,1)}, u32[]{:S(2)}) copy-start(pred[4,128,512]{2,1,0:T(8,128)(4,1)} %broadcast_in_dim.1360) | copy-start | bytes 786436
  518.4 102.2 %copy-start.128 = (pred[4,128,512]{2,1,0:T(8,128)(4,1)S(1)}, pred[4,128,512]{2,1,0:T(8,128)(4,1)}, u32[]{:S(2)}) copy-start(pred[4,128,512]{2,1,0:T(8,128)(4,1)} %broadcast_in_dim.1363) | copy-start | bytes 786436
  627.4 23.4 %copy-start.15 = (f32[4,128,512]{2,1,0:T(8,128)}, f32[4,128,512]{2,1,0:T(8,128)S(1)}, u32[]{:S(2)}) copy-start(f32[4,128,512]{2,1,0:T(8,128)S(1)} %select_select_fusion.bias_c_ref) | copy-start | bytes 3145732
  651.9 97.5 %copy-start.24 = (bf16[4,128,768]{2,1,0:T(8,128)(2,1)}, bf16[4,128,768]{2,1,0:T(8,128)(2,1)S(1)}, u32[]{:S(2)}) copy-start(bf16[4,128,768]{2,1,0:T(8,128)(2,1)S(1)} %pad_maximum_fusion.7) | copy-start | bytes 2359300
  754.6 337.2 %all-gather.39.cloned.1.call-start = ((), (), s32[]{:S(2)}) async-start(), calls=%async_computation.10 | async-start | bytes 1572864 | tf_op jit(solution)/shard_map/all_gather | solution.py:554
  760.1 95.1 %copy-start.63 = (bf16[512,640]{1,0:T(8,128)(2,1)}, bf16[512,640]{1,0:T(8,128)(2,1)S(1)}, u32[]{:S(2)}) copy-start(bf16[512,640]{1,0:T(8,128)(2,1)S(1)} %get-tuple-element.158.refs_9_) | copy-start | bytes 1966084
  760.1 95.1 %copy-start.65 = (bf16[512,640]{1,0:T(8,128)(2,1)}, bf16[512,640]{1,0:T(8,128)(2,1)S(1)}, u32[]{:S(2)}) copy-start(bf16[512,640]{1,0:T(8,128)(2,1)S(1)} %get-tuple-element.159.refs_8_) | copy-start | bytes 1966084
  760.1 97.8 %copy-start.47 = (bf16[2,256,2048]{2,1,0:T(8,128)(2,1)S(1)}, bf16[2,256,2048]{2,1,0:T(8,128)(2,1)}, u32[]{:S(2)}) copy-start(bf16[2,256,2048]{2,1,0:T(8,128)(2,1)} %refs_1_.5) | copy-start | bytes 6291460
  860.3 24.2 %copy-start.55 = (bf16[2,2048,256]{2,1,0:T(8,128)(2,1)S(1)}, bf16[2,2048,256]{2,1,0:T(8,128)(2,1)}, u32[]{:S(2)}) copy-start(bf16[2,2048,256]{2,1,0:T(8,128)(2,1)} %refs_5_.3) | copy-start | bytes 6291460
  860.3 24.2 %copy-start.59 = (bf16[2,2048,256]{2,1,0:T(8,128)(2,1)S(1)}, bf16[2,2048,256]{2,1,0:T(8,128)(2,1)}, u32[]{:S(2)}) copy-start(bf16[2,2048,256]{2,1,0:T(8,128)(2,1)} %refs_4_.3) | copy-start | bytes 6291460
  883.6 95.3 %copy-start.25 = (bf16[4,128,768]{2,1,0:T(8,128)(2,1)}, bf16[4,128,768]{2,1,0:T(8,128)(2,1)S(1)}, u32[]{:S(2)}) copy-start(bf16[4,128,768]{2,1,0:T(8,128)(2,1)S(1)} %pad_maximum_fusion.8) | copy-start | bytes 2359300
  885.8 93.1 %copy-start.12 = (bf16[3,512,256]{2,1,0:T(8,128)(2,1)S(1)}, bf16[3,512,256]{2,1,0:T(8,128)(2,1)}, u32[]{:S(2)}) copy-start(bf16[3,512,256]{2,1,0:T(8,128)(2,1)} %copy-done.11) | copy-start | bytes 2359300
  984.0 111.0 %all-gather.29.cloned.1.call-start = ((), (), s32[]{:S(2)}) async-start(), calls=%async_computation.5 | async-start | bytes 1572864 | tf_op jit(solution)/shard_map/all_gather | solution.py:551
  991.2 103.8 %all-gather.27.cloned.1.call-start = ((), (), s32[]{:S(2)}) async-start(), calls=%async_computation.4 | async-start | bytes 1572864 | tf_op jit(solution)/shard_map/all_gather | solution.py:551
  998.9 99.1 %all-gather.25.cloned.1.call-start = ((), (), s32[]{:S(2)}) async-start(), calls=%async_computation.3 | async-start | bytes 1572864 | tf_op jit(solution)/shard_map/all_gather | solution.py:551
  999.5 98.6 %all-gather.23.cloned.1.call-start = ((), (), s32[]{:S(2)}) async-start(), calls=%async_computation.2 | async-start | bytes 1572864 | tf_op jit(solution)/shard_map/all_gather | solution.py:551
  1000.1 101.0 %all-gather.21.cloned.1.call-start = ((), (), s32[]{:S(2)}) async-start(), calls=%async_computation.1 | async-start | bytes 1572864 | tf_op jit(solution)/shard_map/all_gather | solution.py:551
  1000.8 100.3 %all-gather.19.cloned.1.call-start = ((), (), s32[]{:S(2)}) async-start(), calls=%async_computation | async-start | bytes 1572864 | tf_op jit(solution)/shard_map/all_gather | solution.py:551
  1001.6 104.1 %all-gather.45.cloned.1.call-start = ((), (), s32[]{:S(2)}) async-start(), calls=%async_computation.13 | async-start | bytes 3932160 | tf_op jit(solution)/shard_map/all_gather | solution.py:554
  1009.4 106.5 %all-gather.43.cloned.1.call-start = ((), (), s32[]{:S(2)}) async-start(), calls=%async_computation.12 | async-start | bytes 3932160 | tf_op jit(solution)/shard_map/all_gather | solution.py:554
  1015.4 111.9 %all-gather.33.cloned.1.call-start = ((), (), s32[]{:S(2)}) async-start(), calls=%async_computation.7 | async-start | bytes 3932160 | tf_op jit(solution)/shard_map/all_gather | solution.py:551
  1022.5 104.9 %all-gather.31.cloned.1.call-start = ((), (), s32[]{:S(2)}) async-start(), calls=%async_computation.6 | async-start | bytes 3932160 | tf_op jit(solution)/shard_map/all_gather | solution.py:551
  1028.9 105.9 %all-gather.37.cloned.1.call-start = ((), (), s32[]{:S(2)}) async-start(), calls=%async_computation.9 | async-start | bytes 3932160 | tf_op jit(solution)/shard_map/all_gather | solution.py:551
  1035.7 113.1 %all-gather.35.cloned.1.call-start = ((), (), s32[]{:S(2)}) async-start(), calls=%async_computation.8 | async-start | bytes 3932160 | tf_op jit(solution)/shard_map/all_gather | solution.py:551
  (155 other events, 574.4 us)
Sparse Core Ops, SparseCore 0:
  754.7 10.7 all-gather.40
  984.1 8.2 all-gather.38
  994.5 10.0 all-gather.28
  1006.5 10.0 all-gather.26
  1018.0 10.0 all-gather.24
  1029.5 10.0 all-gather.22
  1041.1 10.0 all-gather.20
  1052.8 10.0 all-gather.18
  1065.0 12.6 all-gather.44
  1079.0 12.6 all-gather.42
  1093.8 12.6 all-gather.32
  1107.9 12.6 all-gather.30
  1122.1 12.6 all-gather.36
  1136.1 12.6 all-gather.34

commit v3 on v1

--- a/solution.py
+++ b/solution.py
@@ -13,6 +13,7 @@
 F32 = jnp.float32
 VMEM = pltpu.VMEM
 MESH = pl.DeviceIdType.MESH
+MIB = 2 ** 20
 HEAD_DIM = 64
 VMEM_SPEC = pl.BlockSpec(memory_space=pltpu.VMEM)
 SMEM_SPEC = pl.BlockSpec(memory_space=pltpu.SMEM)
@@ -23,6 +24,14 @@
     distance_sq = distance * distance
     log_part = 8 + sum((distance_sq >= 64 * 2 ** power).astype(jnp.int32) for power in range(1, 8))
     return jnp.where(distance < 8, distance, log_part) + 16 * (rel_pos > 0).astype(jnp.int32)
+
+
+def comm_params(cid, mib):
+    return pltpu.CompilerParams(collective_id=cid, has_side_effects=True, vmem_limit_bytes=mib * MIB)
+
+
+def cost(gflops):
+    return pl.CostEstimate(flops=gflops * 1000 * MIB, bytes_accessed=8 * MIB, transcendentals=MIB)
 
 
 def dot_nt(a, b):
@@ -64,6 +73,10 @@
     for peer in peers:
         pl.semaphore_signal(barrier, inc=1, device_id={axis: peer}, device_id_type=MESH)
     pl.semaphore_wait(barrier, len(peers))
+
+
+def mask_row(mask_ref, b):
+    return jnp.concatenate([mask_ref[c, b] for c in range(mask_ref.shape[0])], axis=1)
 
 
 def attn_fwd_kernel(heads, q_ref, kv_ref, bias_ref, mask_ref, o_ref, all_ref, send, recv):
@@ -92,7 +105,7 @@
         forward(b).wait_recv()
         kv = all_ref[b].reshape(-1, 2 * width)
         stacked = stack_heads(q_ref[b], heads)
-        scores = dot_nt(stacked, kv[:, :width]) + bias_ref[...] + mask_ref[b]
+        scores = dot_nt(stacked, kv[:, :width]) + bias_ref[:] + mask_row(mask_ref, b)
         top = jnp.max(scores, axis=1, keepdims=True)
         probs = jnp.exp(scores - top)
         total = jnp.sum(probs, axis=1, keepdims=True)
@@ -120,8 +133,8 @@
         in_specs=[VMEM_SPEC] * 4,
         out_specs=(VMEM_SPEC, VMEM_SPEC),
         scratch_shapes=[pltpu.SemaphoreType.DMA((3, batch)), pltpu.SemaphoreType.DMA((3, batch))],
-        compiler_params=pltpu.CompilerParams(collective_id=cid, has_side_effects=True, vmem_limit_bytes=32 * 2 ** 20),
-        cost_estimate=pl.CostEstimate(flops=4 * 10 ** 9, bytes_accessed=6 * 10 ** 6, transcendentals=10 ** 6),
+        compiler_params=comm_params(cid, 32),
+        cost_estimate=cost(4),
         name='attn_fwd',
     )(q, kv, bias_rows, mask_rows)
 
@@ -150,14 +163,14 @@
         to_across(b).start()
         to_mate(b).start()
 
-    ds_ref[...] = jnp.zeros_like(ds_ref)
+    ds_ref[:] = jnp.zeros_like(ds_ref)
 
     def row_step(b, carry):
         kv = kv_ref[b].reshape(-1, wide)
         keys, vals = kv[:, :width], kv[:, width:]
         qdo = qdo_ref[b]
         all_ref[b, me] = qdo
-        scores = dot_nt(stack_heads(qdo[:, :width], heads), keys) + bias_r_ref[...] + mask_r_ref[b]
+        scores = dot_nt(stack_heads(qdo[:, :width], heads), keys) + bias_r_ref[:] + mask_row(mask_r_ref, b)
         top = jnp.max(scores, axis=1, keepdims=True)
         unnorm = jnp.exp(scores - top)
         total = jnp.sum(unnorm, axis=1, keepdims=True)
@@ -174,7 +187,7 @@
         own_stats[b] = stats
         all_stats[b, me] = stats
         d_scores = probs * (d_probs - row_dot)
-        ds_ref[...] += d_scores
+        ds_ref[:] += d_scores
         d_q = dot_nn(d_scores.astype(BF16), keys)
         dq_ref[b] = pick_heads(d_q, heads, rows).astype(BF16)
         for which in range(3):
@@ -246,8 +259,8 @@
             pltpu.SemaphoreType.DMA((3, batch)),
             pltpu.SemaphoreType.DMA((3, batch)),
         ],
-        compiler_params=pltpu.CompilerParams(collective_id=cid, has_side_effects=True, vmem_limit_bytes=40 * 2 ** 20),
-        cost_estimate=pl.CostEstimate(flops=10 * 10 ** 9, bytes_accessed=10 ** 7, transcendentals=2 * 10 ** 6),
+        compiler_params=comm_params(cid, 40),
+        cost_estimate=cost(10),
         name='attn_bwd',
     )(qdo, kv_all, bias_rows, bias_cols, mask_rows, mask_cols)
 
@@ -273,47 +286,447 @@
         out_shape=jax.ShapeDtypeStruct((n_buckets, heads, ds0.shape[1]), F32),
         in_specs=[SMEM_SPEC, VMEM_SPEC, VMEM_SPEC],
         out_specs=VMEM_SPEC,
-        compiler_params=pltpu.CompilerParams(vmem_limit_bytes=16 * 2 ** 20),
+        compiler_params=pltpu.CompilerParams(vmem_limit_bytes=16 * MIB),
         name='bias_grad',
     )(start.reshape(1), ds0, ds1)
     return jnp.sum(out, axis=-1)
 
 
-def bias_from(rel_bias, rel):
-    buckets = rel_bucket(rel)
-    table = rel_bias.T
-    shape = (table.shape[0],) + rel.shape
-    out = jnp.zeros(shape, F32)
-    for k in range(table.shape[1]):
-        out = jnp.where((buckets == k)[None], table[:, k].reshape((-1,) + (1,) * rel.ndim), out)
-    return out
-
-
 def rms_parts(x_f, gain):
     inv_rms = lax.rsqrt(jnp.mean(x_f * x_f, axis=-1, keepdims=True) + NORM_EPS)
     return (x_f * inv_rms * gain).astype(BF16)
 
 
-def rms_backward(d_norm, x_f, gain):
+GELU_C = 0.7978845608028654
+GELU_A = 0.044715
+
+
+def gelu_parts(x):
+    t = jnp.tanh(GELU_C * (x + GELU_A * x * x * x))
+    cdf = 0.5 * (1.0 + t)
+    return x * cdf, cdf + 0.5 * x * (1.0 - t * t) * GELU_C * (1.0 + 3.0 * GELU_A * x * x)
+
+
+def remote(src, dst, send, recv, axis, peer):
+    return pltpu.make_async_remote_copy(src_ref=src, dst_ref=dst, send_sem=send, recv_sem=recv, device_id={axis: peer}, device_id_type=MESH)
+
+
+def tp_places():
+    me = lax.axis_index('tp')
+    z, y = me // 2, lax.rem(me, 2)
+    return me, z, y
+
+
+def meet(tp_peers, cp_peers):
+    barrier = pltpu.get_barrier_semaphore()
+    for axis, peers in (('tp', tp_peers), ('cp', cp_peers)):
+        for peer in peers:
+            pl.semaphore_signal(barrier, inc=1, device_id={axis: peer}, device_id_type=MESH)
+    pl.semaphore_wait(barrier, len(tp_peers) + len(cp_peers))
+
+
+class Ring:
+    def __init__(self, part, from_y, from_z, full, sems):
+        self.part, self.from_y, self.from_z, self.full = part, from_y, from_z, full
+        self.sems = sems
+        me, self.z, self.y = tp_places()
+        self.pair = me + 1 - 2 * self.y
+        self.z_peer = [2 * lax.rem(self.z + j, 4) + self.y for j in range(4)]
+        self.seg = self.y * 4 + self.z
+
+    @staticmethod
+    def scratch(batch, seg, d_model):
+        dma = pltpu.SemaphoreType.DMA
+        return [
+            pltpu.VMEM((batch, 2, 4, seg, d_model), F32),
+            pltpu.VMEM((batch, 4, seg, d_model), F32),
+            pltpu.VMEM((batch, 3, seg, d_model), F32),
+            dma((2, batch)), dma((2, batch, 3)), dma((2, batch, 3)), dma((2, batch, 4)),
+        ]
+
+    def y_sum(self, b):
+        s = self.sems[0]
+        return remote(self.part.at[b, 1 - self.y], self.from_y.at[b], s.at[0, b], s.at[1, b], 'tp', self.pair)
+
+    def z_sum(self, b, j):
+        s = self.sems[1]
+        return remote(self.part.at[b, self.y, lax.rem(self.z + j, 4)], self.from_z.at[b, j - 1], s.at[0, b, j - 1], s.at[1, b, j - 1], 'tp', self.z_peer[j])
+
+    def z_gather(self, b, j):
+        s = self.sems[2]
+        ref = self.full.at[b, self.seg]
+        return remote(ref, ref, s.at[0, b, j - 1], s.at[1, b, j - 1], 'tp', self.z_peer[j])
+
+    def y_gather(self, b, j):
+        s = self.sems[3]
+        ref = self.full.at[b, self.y * 4 + lax.rem(self.z - j + 4, 4)]
+        return remote(ref, ref, s.at[0, b, j], s.at[1, b, j], 'tp', self.pair)
+
+    def send_partial(self, b, partial):
+        self.part[b] = partial.reshape(self.part.shape[1:])
+        self.y_sum(b).start()
+
+    def reduce_pair(self, b):
+        self.y_sum(b).wait_recv()
+        self.part[b, self.y] = self.part[b, self.y] + self.from_y[b]
+        for j in (2, 1, 3):
+            self.z_sum(b, j).start()
+
+    def reduced(self, b):
+        for j in (1, 2, 3):
+            self.z_sum(b, j).wait_recv()
+        return self.part[b, self.y, self.z] + self.from_z[b, 0] + self.from_z[b, 1] + self.from_z[b, 2]
+
+    def publish(self, b, out):
+        self.full[b, self.seg] = out
+        for j in (2, 1, 3):
+            self.z_gather(b, j).start()
+        self.y_gather(b, 0).start()
+
+    def forward(self, b):
+        for j in (1, 2, 3):
+            self.z_gather(b, j).wait_recv()
+            self.y_gather(b, j).start()
+
+    def rows(self, b):
+        for j in range(4):
+            self.y_gather(b, j).wait_recv()
+        return self.full[b].reshape(-1, self.full.shape[-1])
+
+    def drain(self, b):
+        self.y_sum(b).wait_send()
+        for j in range(4):
+            self.y_gather(b, j).wait_send()
+        for j in (1, 2, 3):
+            self.z_sum(b, j).wait_send()
+            self.z_gather(b, j).wait_send()
+
+
+class Exchange:
+    def __init__(self, wide, late, narrow, send, recv):
+        self.wide, self.late, self.narrow, self.send, self.recv = wide, late, narrow, send, recv
+        me, self.mate, self.across, self.diagonal = cp_places()
+        self.core = lax.rem(me, 2)
+
+    def columns(self, r, n):
+        want = self.core if r == 1 else 1 - self.core
+        return pl.ds(pl.multiple_of(want * n, n), n)
+
+    def wide_copy(self, i, r):
+        src, dst = self.wide[i]
+        n = dst.shape[-1]
+        return remote(src.at[:, :, self.columns(r, n)], dst.at[r], self.send.at[i, r, 0], self.recv.at[i, r, 0], 'cp', (self.mate, self.across, self.diagonal)[r])
+
+    def late_copy(self, i, r, b):
+        src, dst = self.late[i]
+        k = len(self.wide) + i
+        n = dst.shape[-1]
+        return remote(src.at[b].at[..., self.columns(r, n)], dst.at[r, b], self.send.at[k, r, b], self.recv.at[k, r, b], 'cp', (self.mate, self.across, self.diagonal)[r])
+
+    def narrow_copy(self, i, r):
+        src, dst = self.narrow[i]
+        k = len(self.wide) + len(self.late) + i
+        return remote(src if r < 2 else dst.at[1], dst.at[r], self.send.at[k, r, 0], self.recv.at[k, r, 0], 'cp', self.across if r == 1 else self.mate)
+
+    def start(self):
+        for i in range(len(self.narrow)):
+            self.narrow_copy(i, 1).start()
+            self.narrow_copy(i, 0).start()
+        for i in range(len(self.wide)):
+            for r in (1, 2, 0):
+                self.wide_copy(i, r).start()
+
+    def start_late(self, i, b):
+        for r in (1, 2, 0):
+            self.late_copy(i, r, b).start()
+
+    def pass_on(self):
+        for i in range(len(self.narrow)):
+            self.narrow_copy(i, 1).wait_recv()
+            self.narrow_copy(i, 2).start()
+
+    def finish(self, batch):
+        for i in range(len(self.narrow)):
+            self.narrow_copy(i, 0).wait_recv()
+            self.narrow_copy(i, 2).wait_recv()
+            for r in range(3):
+                self.narrow_copy(i, r).wait_send()
+        for i in range(len(self.wide)):
+            for r in range(3):
+                self.wide_copy(i, r).wait()
+        if self.late:
+            def each(b, carry):
+                for i in range(len(self.late)):
+                    for r in range(3):
+                        self.late_copy(i, r, b).wait()
+                return carry
+
+            lax.fori_loop(0, batch, each, 0)
+
+
+def run_slots(batch, stages):
+    def slot_step(slot, carry):
+        for k, stage in enumerate(stages):
+            @pl.when(jnp.logical_and(slot >= k, slot < batch + k))
+            def _():
+                stage(slot - k)
+        return carry
+
+    lax.fori_loop(0, batch + len(stages) - 1, slot_step, 0)
+
+
+def norm_rows(rows, gain):
+    return rms_parts(rows.astype(F32), gain)
+
+
+def rms_pull(total, x_shard, gain, res, d_gain_ref):
+    d_norm = total.astype(BF16).astype(F32)
+    x_f = x_shard.astype(F32)
     inv_rms = lax.rsqrt(jnp.mean(x_f * x_f, axis=-1, keepdims=True) + NORM_EPS)
     normed = x_f * inv_rms
-    d_gain = jnp.sum(d_norm * normed, axis=0)
+    d_gain_ref[:] += jnp.sum(d_norm * normed, axis=0, keepdims=True)
     d_normed = d_norm * gain
     d_x = inv_rms * (d_normed - normed * jnp.mean(d_normed * normed, axis=-1, keepdims=True))
-    return d_x, d_gain
-
-
-def reduce_rows(partial):
-    return lax.psum_scatter(partial, 'tp', scatter_dimension=0, tiled=True)
-
-
-def gather_rows(shard):
-    return lax.all_gather(shard, 'tp', axis=0, tiled=True)
-
-
-def cp_sum(partial):
-    own = lax.psum_scatter(partial, 'cp', scatter_dimension=0, tiled=True).astype(BF16)
-    return lax.all_gather(own, 'cp', axis=0, tiled=True)
+    return (res.astype(F32) + d_x).astype(BF16)
+
+
+class Refs:
+    pass
+
+
+def chain(name, cid, ins, outs, loads, n_rings, wide, late, narrow, body, geometry):
+    batch, seg, d_model = geometry
+    any_spec = pl.BlockSpec(memory_space=pl.ANY)
+    dma = pltpu.SemaphoreType.DMA
+    shapes = {k: v[0].shape for k, v in ins.items()}
+    shapes.update({k: v[0] for k, v in outs.items()})
+    outs = dict(outs)
+    x_names = []
+    for group, halved in ((wide, True), (late, True), (narrow, False)):
+        for src, dst in group:
+            shape = shapes[src]
+            outs[dst] = ((3,) + shape[:-1] + (shape[-1] // 2 if halved else shape[-1],), BF16)
+            x_names.append(dst)
+    n_x = len(x_names)
+    in_names, out_names, load_names = list(ins), list(outs), list(loads)
+    ring_parts = len(Ring.scratch(batch, seg, d_model))
+    n_loads = sum(len(parts) for _, parts in loads.values())
+
+    def kernel(*refs):
+        it = iter(refs)
+        r = Refs()
+        for key in in_names + out_names + load_names:
+            setattr(r, key, next(it))
+        rings = []
+        for i in range(n_rings):
+            pieces = [next(it) for _ in range(ring_parts)]
+            rings.append((pieces[:3], pieces[3:]))
+        load_sem, x_send, x_recv = next(it), next(it), next(it)
+        copies = []
+        for buf, (_, parts) in loads.items():
+            for src, layer, col in parts:
+                array = getattr(r, src).at[layer]
+                dst = getattr(r, buf)
+                if array.shape[-1] != dst.shape[-1]:
+                    dst = dst.at[:, pl.ds(col, array.shape[-1])]
+                copies.append(pltpu.make_async_copy(array, dst, load_sem.at[len(copies)]))
+        for copy in copies:
+            copy.start()
+        r.rings = [Ring(*pieces, getattr(r, 'full_%d' % i), sems) for i, (pieces, sems) in enumerate(rings)]
+        pairs = [[(getattr(r, s), getattr(r, d)) for s, d in group] for group in (wide, late, narrow)]
+        r.exchange = Exchange(*pairs, x_send, x_recv)
+        first = r.rings[0]
+        others = [r.exchange.mate, r.exchange.across, r.exchange.diagonal] if n_x else []
+        meet([first.pair] + first.z_peer[1:], others)
+        r.exchange.start()
+        for copy in copies:
+            copy.wait()
+        run_slots(batch, body(r))
+        r.exchange.pass_on()
+
+        def finish(b, carry):
+            for ring in r.rings:
+                ring.drain(b)
+            return carry
+
+        lax.fori_loop(0, batch, finish, 0)
+        r.exchange.finish(batch)
+
+    scratch = [pltpu.VMEM(shape, BF16) for shape, _ in loads.values()]
+    for _ in range(n_rings):
+        scratch += Ring.scratch(batch, seg, d_model)
+    scratch += [dma((max(n_loads, 1),)), dma((max(n_x, 1), 3, batch)), dma((max(n_x, 1), 3, batch))]
+    result = pl.pallas_call(
+        kernel,
+        out_shape=tuple(jax.ShapeDtypeStruct(*outs[k]) for k in out_names),
+        in_specs=[VMEM_SPEC if ins[k][1] else any_spec for k in in_names],
+        out_specs=tuple(any_spec if k in x_names else VMEM_SPEC for k in out_names),
+        scratch_shapes=scratch,
+        compiler_params=comm_params(cid, 58),
+        cost_estimate=cost(80),
+        name=name,
+    )(*[ins[k][0] for k in in_names])
+    named = Refs()
+    for key, value in zip(out_names, result):
+        setattr(named, key, value)
+    return named
+
+
+def block_stages(ring, start, epilogue):
+    return [start, ring.reduce_pair, lambda b: ring.publish(b, epilogue(b, ring.reduced(b))), ring.forward]
+
+
+def mlp_rows(r, b, rows, gain, ff):
+    h2 = norm_rows(rows, gain)
+    r.h2[b] = h2
+    both = dot_nn(h2, r.wgl[:])
+    return both[:, :ff], both[:, ff:]
+
+
+def prep_kernel(mask_ref, table_ref, all_ref, rows_ref, cols_ref, send, recv):
+    me, mate, across, diagonal = cp_places()
+    n_buckets, heads = table_ref.shape
+    rows = rows_ref.shape[0] // heads
+    seq = rows_ref.shape[1]
+    peers = (mate, across, diagonal)
+    meet([], peers)
+
+    def copy(i):
+        return remote(mask_ref, all_ref.at[me], send.at[i], recv.at[i], 'cp', peers[i])
+
+    for i in range(3):
+        copy(i).start()
+    all_ref[me] = mask_ref[:]
+
+    def strip(i, carry):
+        first = pl.multiple_of(i * 8, 8)
+        rel = lax.broadcasted_iota(jnp.int32, (8, seq), 1) - lax.broadcasted_iota(jnp.int32, (8, seq), 0) - me * rows - first
+        for is_col in (False, True):
+            buckets = rel_bucket(-rel if is_col else rel)
+            vals = [jnp.zeros((8, seq), F32) for _ in range(heads)]
+            for k in range(n_buckets):
+                hit = buckets == k
+                vals = [jnp.where(hit, table_ref[k, h], v) for h, v in enumerate(vals)]
+            for h, v in enumerate(vals):
+                if is_col:
+                    for q in range(seq // rows):
+                        cols_ref[q, pl.ds(first, 8), h * rows:(h + 1) * rows] = v[:, q * rows:(q + 1) * rows]
+                else:
+                    rows_ref[pl.ds(pl.multiple_of(h * rows + first, 8), 8), :] = v
+        return carry
+
+    lax.fori_loop(0, rows // 8, strip, 0)
+    for i in range(3):
+        copy(i).wait()
+
+
+def prep(key_add, rel_bias, cp_size, cid):
+    batch, rows = key_add.shape
+    heads = rel_bias.shape[1]
+    dma = pltpu.SemaphoreType.DMA
+    return pl.pallas_call(
+        prep_kernel,
+        out_shape=(jax.ShapeDtypeStruct((cp_size, batch, 1, rows), F32), jax.ShapeDtypeStruct((heads * rows, cp_size * rows), F32), jax.ShapeDtypeStruct((cp_size, rows, heads * rows), F32)),
+        in_specs=[VMEM_SPEC, SMEM_SPEC],
+        out_specs=(VMEM_SPEC,) * 3,
+        scratch_shapes=[dma((3,)), dma((3,))],
+        compiler_params=comm_params(cid, 16),
+        cost_estimate=cost(1),
+        name='prep',
+    )(key_add.reshape(batch, 1, rows), rel_bias)
+
+
+def swap_kernel(n, *refs):
+    halves, small, mates, total = refs[:n], refs[n], refs[n + 1:2 * n + 1], refs[2 * n + 1]
+    stage, by_z, send, recv, s_send, s_recv = refs[2 * n + 2:]
+    me, z, y = tp_places()
+    pair = me + 1 - 2 * y
+    z_peer = [2 * lax.rem(z + j, 4) + y for j in range(4)]
+    _, mate, across, _ = cp_places()
+    meet([pair] + z_peer[1:], [mate, across])
+
+    def half(i):
+        return remote(halves[i], mates[i], send.at[i], recv.at[i], 'cp', mate)
+
+    for i in range(n):
+        half(i).start()
+    mine = small
+    for k, (axis, peer) in enumerate((('cp', mate), ('cp', across), ('tp', pair))):
+        copy = remote(mine, stage.at[2 * k], s_send.at[k], s_recv.at[k], axis, peer)
+        copy.start()
+        copy.wait()
+        if k < 2:
+            stage[2 * k + 1] = mine[:] + stage[2 * k]
+            mine = stage.at[2 * k + 1]
+        else:
+            by_z[z] = mine[:] + stage[2 * k]
+    copies = [remote(by_z.at[z], by_z.at[z], s_send.at[2 + j], s_recv.at[2 + j], 'tp', z_peer[j]) for j in (1, 2, 3)]
+    for copy in copies:
+        copy.start()
+    for copy in copies:
+        copy.wait()
+    total[:] = by_z[0] + by_z[1] + by_z[2] + by_z[3]
+    for i in range(n):
+        half(i).wait()
+
+
+def swap(halves, small, cid):
+    n = len(halves)
+    any_spec = pl.BlockSpec(memory_space=pl.ANY)
+    dma = pltpu.SemaphoreType.DMA
+    result = pl.pallas_call(
+        functools.partial(swap_kernel, n),
+        out_shape=tuple(jax.ShapeDtypeStruct(h.shape, h.dtype) for h in halves) + (jax.ShapeDtypeStruct(small.shape, F32),),
+        in_specs=[any_spec] * n + [VMEM_SPEC],
+        out_specs=tuple([any_spec] * n + [VMEM_SPEC]),
+        scratch_shapes=[pltpu.VMEM((5,) + small.shape, F32), pltpu.VMEM((4,) + small.shape, F32), dma((n,)), dma((n,)), dma((6,)), dma((6,))],
+        compiler_params=comm_params(cid, 8),
+        cost_estimate=cost(10),
+        name='swap',
+    )(*halves, small)
+    return list(result[:n]), result[n]
+
+
+def place_kernel(plan, n_out, *refs):
+    n = len(plan)
+    owns, mates, outs = refs[:n], refs[n:2 * n], refs[2 * n:2 * n + n_out]
+    bufs, in_sem, out_sem = refs[2 * n + n_out:4 * n + n_out], refs[4 * n + n_out], refs[4 * n + n_out + 1]
+    core = lax.rem(lax.axis_index('cp'), 2)
+    loads = [pltpu.make_async_copy(src, buf, in_sem.at[i]) for i, (src, buf) in enumerate(zip(owns + mates, bufs))]
+    for load in loads:
+        load.start()
+    stores = []
+    for i, load in enumerate(loads):
+        layer, by_rows, first_out, n_pieces = plan[i % n]
+        which = core if i < n else 1 - core
+        buf = bufs[i]
+        load.wait()
+        width = buf.shape[1] // n_pieces
+        for p in range(n_pieces):
+            src = buf if n_pieces == 1 else buf.at[:, pl.ds(p * width, width)]
+            size = buf.shape[0] if by_rows else width
+            window = pl.ds(pl.multiple_of(which * size, size), size)
+            out = outs[first_out + p].at[layer]
+            dst = out.at[window, :] if by_rows else out.at[:, window]
+            stores.append(pltpu.make_async_copy(src, dst, out_sem.at[len(stores)]))
+            stores[-1].start()
+    for store in stores:
+        store.wait()
+
+
+def place(plan, owns, mates, out_shapes):
+    n = len(plan)
+    any_spec = pl.BlockSpec(memory_space=pl.ANY)
+    n_stores = 2 * sum(p[3] for p in plan)
+    return pl.pallas_call(
+        functools.partial(place_kernel, plan, len(out_shapes)),
+        out_shape=tuple(jax.ShapeDtypeStruct(s, BF16) for s in out_shapes),
+        in_specs=[any_spec] * (2 * n),
+        out_specs=tuple([any_spec] * len(out_shapes)),
+        scratch_shapes=[pltpu.VMEM(a.shape, BF16) for a in list(owns) + list(mates)] + [pltpu.SemaphoreType.DMA((2 * n,)), pltpu.SemaphoreType.DMA((n_stores,))],
+        compiler_params=pltpu.CompilerParams(vmem_limit_bytes=40 * MIB),
+        name='place',
+    )(*owns, *mates)
 
 
 def solution(mesh):
@@ -328,88 +741,224 @@
         batch, rows, d_model = x_in.shape
         tokens = batch * rows
         n_layers = w_q.shape[0]
+        ff = w_gate.shape[2]
         n_buckets, heads = rel_bias.shape
         width = heads * HEAD_DIM
         cp_index = lax.axis_index('cp')
         tp_index = lax.axis_index('tp')
-        seq = cp_size * rows
+        core = lax.rem(cp_index, 2)
+        half = d_model // 2
+        seg = rows // tp_size
+        my_seg = lax.rem(tp_index, 2) * 4 + tp_index // 2
         start = (cp_index * rows).astype(jnp.int32)
-
-        mask_all = lax.all_gather(key_mask, 'cp', axis=1, tiled=True)
-        mask_rows = jnp.where(mask_all > 0, 0.0, MASK_NEG).astype(F32)[:, None, :]
-        mask_cols = jnp.where(key_mask > 0, 0.0, MASK_NEG).astype(F32)[:, :, None]
-        pos = jnp.arange(rows)
-        bias_rows = bias_from(rel_bias, jnp.arange(seq)[None, :] - start - pos[:, None]).reshape(heads * rows, seq)
-        rel_cols = start + pos[None, :, None] - (jnp.arange(cp_size) * rows)[:, None, None] - pos[None, None, :]
-        bias_cols = jnp.transpose(bias_from(rel_bias, rel_cols), (1, 2, 0, 3)).reshape(cp_size, rows, heads * rows)
-
-        def own_rows(full):
-            return lax.dynamic_slice_in_dim(full, tp_index * (tokens // tp_size), tokens // tp_size, axis=0)
-
-        x = x_in.reshape(tokens, d_model)
-        x_s = own_rows(x)
-        saved = []
-        for l in range(n_layers):
-            h = rms_parts(x.astype(F32), g_attn[l])
-            q = jnp.dot(h, w_q[l], preferred_element_type=F32).astype(BF16)
-            k = jnp.dot(h, w_k[l], preferred_element_type=F32).astype(BF16)
-            v = jnp.dot(h, w_v[l], preferred_element_type=F32).astype(BF16)
-            kv = jnp.concatenate([k, v], axis=1).reshape(batch, rows, 2 * width)
-            o, kv_all = attn_fwd(q.reshape(batch, rows, width), kv, bias_rows, mask_rows, cp_size, 2 * l)
-            o = o.reshape(tokens, width)
-            x1_s = (x_s.astype(F32) + reduce_rows(jnp.dot(o, w_o[l], preferred_element_type=F32))).astype(BF16)
-            x1 = gather_rows(x1_s)
-            h2 = rms_parts(x1.astype(F32), g_mlp[l])
-            gate = jnp.dot(h2, w_gate[l], preferred_element_type=F32)
-            lin = jnp.dot(h2, w_lin[l], preferred_element_type=F32)
-            u = (jax.nn.gelu(gate, approximate=True) * lin).astype(BF16)
-            saved.append((x_s, h, q, kv_all, o, x1_s, h2, gate, lin, u))
-            if l + 1 < n_layers:
-                x_s = (x1_s.astype(F32) + reduce_rows(jnp.dot(u, w_out[l], preferred_element_type=F32))).astype(BF16)
-                x = gather_rows(x_s)
-
-        d = d_y.reshape(tokens, d_model)
-        d_s = own_rows(d)
-        big = [[None] * n_layers for _ in range(7)]
-        gains = [[None] * n_layers for _ in range(2)]
-        ds_all = []
-        for l in reversed(range(n_layers)):
-            x_s, h, q, kv_all, o, x1_s, h2, gate, lin, u = saved[l]
-            big[6][l] = cp_sum(dot_tn(u, d))
-            d_u = dot_nt(d, w_out[l]).astype(BF16).astype(F32)
-            gelu_val, gelu_pull = jax.vjp(lambda g: jax.nn.gelu(g, approximate=True), gate)
-            d_lin = (d_u * gelu_val).astype(BF16)
-            d_gate = gelu_pull(d_u * lin)[0].astype(BF16)
-            big[4][l] = cp_sum(dot_tn(h2, d_gate))
-            big[5][l] = cp_sum(dot_tn(h2, d_lin))
-            dh2_s = reduce_rows(dot_nt(d_gate, w_gate[l]) + dot_nt(d_lin, w_lin[l]))
-            d_mid, gains[1][l] = rms_backward(dh2_s, x1_s.astype(F32), g_mlp[l])
-            dm_s = (d_mid + d_s.astype(F32)).astype(BF16)
-            dm = gather_rows(dm_s)
-            big[3][l] = cp_sum(dot_tn(o, dm))
-            d_o = dot_nt(dm, w_o[l]).astype(BF16)
-            qdo = jnp.concatenate([q, d_o], axis=1).reshape(batch, rows, 2 * width)
-            d_q, d_kv, ds = attn_bwd(qdo, kv_all, bias_rows, bias_cols, mask_rows, mask_cols, 2 * l + 1)
-            ds_all.append(ds)
-            d_q = d_q.reshape(tokens, width)
-            d_kv = d_kv.reshape(tokens, 2 * width)
-            d_k, d_v = d_kv[:, :width], d_kv[:, width:]
-            big[0][l] = cp_sum(dot_tn(h, d_q))
-            big[1][l] = cp_sum(dot_tn(h, d_k))
-            big[2][l] = cp_sum(dot_tn(h, d_v))
-            dh_s = reduce_rows(dot_nt(d_q, w_q[l]) + dot_nt(d_k, w_k[l]) + dot_nt(d_v, w_v[l]))
-            d_x, gains[0][l] = rms_backward(dh_s, x_s.astype(F32), g_attn[l])
-            d_s = (d_x + dm_s.astype(F32)).astype(BF16)
-            d = gather_rows(d_s)
-
-        d_bias = bias_grad(ds_all[0], ds_all[1], start, heads, n_buckets)
+        geometry = (batch, seg, d_model)
+        shard = ((batch, seg, d_model), BF16)
+        whole = ((batch, rows, d_model), BF16)
+        full = ((batch, tp_size, seg, d_model), BF16)
+        gain_row = ((1, d_model), F32)
+
+        key_add = jnp.where(key_mask > 0, 0.0, MASK_NEG).astype(F32)
+        mask_rows, bias_rows, bias_cols = prep(key_add, rel_bias, cp_size, 0)
+        mask_cols = key_add[:, :, None]
+
+        def own_rows(array):
+            return lax.dynamic_slice_in_dim(array, my_seg * seg, seg, axis=1)
+
+        def mlp_pull(d_u, gate, lin):
+            d_u = d_u.astype(BF16).astype(F32)
+            value, slope = gelu_parts(gate)
+            return jnp.concatenate([(d_u * lin * slope).astype(BF16), (d_u * value).astype(BF16)], axis=1)
+
+        wgl = lambda l: ((d_model, 2 * ff), [('w_gate', l, 0), ('w_lin', l, ff)])
+        wqkv = lambda l: ((d_model, 3 * width), [('w_q', l, 0), ('w_k', l, width), ('w_v', l, 2 * width)])
+        wo = lambda l: ((width, d_model), [('w_o', l, 0)])
+        wout = lambda l: ((ff, d_model), [('w_out', l, 0)])
+        qkv_in = dict(w_q=(w_q, False), w_k=(w_k, False), w_v=(w_v, False))
+        mlp_in = dict(w_gate=(w_gate, False), w_lin=(w_lin, False), w_out=(w_out, False))
+        vm = lambda array: (array, True)
+        hbm = lambda array: (array, False)
+
+        x0 = x_in.reshape(tokens, d_model)
+        h0 = norm_rows(x0, g_attn[0])
+        q0, k0, v0 = [jnp.dot(h0, w[0], preferred_element_type=F32).astype(BF16) for w in (w_q, w_k, w_v)]
+        h0 = h0.reshape(batch, rows, d_model)
+        q0 = q0.reshape(batch, rows, width)
+        kv0 = jnp.concatenate([k0, v0], axis=1).reshape(batch, rows, 2 * width)
+        o0, kva0 = attn_fwd(q0, kv0, bias_rows, mask_rows, cp_size, 1)
+
+        def body_f0(r):
+            ring_a, ring_b = r.rings
+
+            def add_a(b, total):
+                out = (r.xs[b].astype(F32) + total).astype(BF16)
+                r.x1s[b] = out
+                return out
+
+            def middle(b):
+                gate, lin = mlp_rows(r, b, ring_a.rows(b), r.gain_m[:], ff)
+                r.exchange.start_late(0, b)
+                r.gate[b] = gate
+                r.lin[b] = lin
+                u = (gelu_parts(gate)[0] * lin).astype(BF16)
+                r.u[b] = u
+                ring_b.send_partial(b, dot_nn(u, r.wout[:]))
+
+            def add_b(b, total):
+                out = (r.x1s[b].astype(F32) + total).astype(BF16)
+                r.xs1[b] = out
+                return out
+
+            def last(b):
+                h = norm_rows(ring_b.rows(b), r.gain_a[:])
+                r.h1[b] = h
+                qkv = dot_nn(h, r.wqkv[:]).astype(BF16)
+                r.q1[b] = qkv[:, :width]
+                r.kv1[b] = qkv[:, width:]
+
+            return block_stages(ring_a, lambda b: ring_a.send_partial(b, dot_nn(r.o[b], r.wo[:])), add_a) + block_stages(ring_b, middle, add_b) + [last]
+
+        f0 = chain('fwd_0', 2,
+                   dict(o=vm(o0), xs=vm(own_rows(x_in)), gain_m=vm(g_mlp[0][None]), gain_a=vm(g_attn[1][None]), h0=hbm(h0), w_o=hbm(w_o), **mlp_in, **qkv_in),
+                   dict(x1s=shard, h2=whole, gate=((batch, rows, ff), F32), lin=((batch, rows, ff), F32), u=((batch, rows, ff), BF16), xs1=shard, h1=whole,
+                        q1=((batch, rows, width), BF16), kv1=((batch, rows, 2 * width), BF16), full_0=full, full_1=full),
+                   dict(wo=wo(0), wgl=wgl(0), wout=wout(0), wqkv=wqkv(1)), 2,
+                   [('h0', 'h0_g')], [('h2', 'h2_g')], [('o', 'o_g')], body_f0, geometry)
+
+        o1, kva1 = attn_fwd(f0.q1, f0.kv1, bias_rows, mask_rows, cp_size, 3)
+
+        def body_fb1(r):
+            ring_a, ring_b = r.rings
+            r.dgain_m[:] = jnp.zeros_like(r.dgain_m)
+
+            def add_a(b, total):
+                out = (r.xs[b].astype(F32) + total).astype(BF16)
+                r.x1s[b] = out
+                return out
+
+            def middle(b):
+                gate, lin = mlp_rows(r, b, ring_a.rows(b), r.gain_m[:], ff)
+                r.exchange.start_late(0, b)
+                r.u[b] = (gelu_parts(gate)[0] * lin).astype(BF16)
+                dgl = mlp_pull(dot_nt(r.d[b], r.wout[:]), gate, lin)
+                r.dgl[b] = dgl
+                ring_b.send_partial(b, dot_nt(dgl, r.wgl[:]))
+
+            def pull_b(b, total):
+                out = rms_pull(total, r.x1s[b], r.gain_m[:], r.ds[b], r.dgain_m)
+                r.dms[b] = out
+                return out
+
+            def last(b):
+                d_o = dot_nt(ring_b.rows(b), r.wo[:]).astype(BF16)
+                r.qdo[b] = jnp.concatenate([r.q[b], d_o], axis=1)
+
+            return block_stages(ring_a, lambda b: ring_a.send_partial(b, dot_nn(r.o[b], r.wo[:])), add_a) + block_stages(ring_b, middle, pull_b) + [last]
+
+        fb1 = chain('fwd_bwd_1', 4,
+                    dict(o=vm(o1), xs=vm(f0.xs1), gain_m=vm(g_mlp[1][None]), d=vm(d_y), ds=vm(own_rows(d_y)), q=vm(f0.q1), h1=hbm(f0.h1), u0=hbm(f0.u), w_o=hbm(w_o), **mlp_in),
+                    dict(x1s=shard, h2=whole, u=((batch, rows, ff), BF16), dgl=((batch, rows, 2 * ff), BF16), dms=shard, qdo=((batch, rows, 2 * width), BF16), dgain_m=gain_row, full_0=full, full_1=full),
+                    dict(wo=wo(1), wgl=wgl(1), wout=wout(1)), 2,
+                    [('h1', 'h1_g'), ('d', 'd_g')], [('h2', 'h2_g')], [('u0', 'u0_g'), ('o', 'o_g')], body_fb1, geometry)
+
+        dq1, dkv1, score_grad1 = attn_bwd(fb1.qdo, kva1, bias_rows, bias_cols, mask_rows, mask_cols, 5)
+
+        def start_qkv(r, ring):
+            return lambda b: ring.send_partial(b, dot_nt(jnp.concatenate([r.dq[b], r.dkv[b]], axis=1), r.wqkv[:]))
+
+        def body_bb(r):
+            ring_a, ring_b = r.rings
+            r.dgain_a[:] = jnp.zeros_like(r.dgain_a)
+            r.dgain_m[:] = jnp.zeros_like(r.dgain_m)
+
+            def pull_a(b, total):
+                out = rms_pull(total, r.xs[b], r.gain_a[:], r.dms_in[b], r.dgain_a)
+                r.ds[b] = out
+                return out
+
+            def middle(b):
+                d = ring_a.rows(b)
+                r.exchange.start_late(0, b)
+                dgl = mlp_pull(dot_nt(d, r.wout[:]), r.gate[b], r.lin[b])
+                r.dgl[b] = dgl
+                ring_b.send_partial(b, dot_nt(dgl, r.wgl[:]))
+
+            def pull_b(b, total):
+                out = rms_pull(total, r.x1s[b], r.gain_m[:], r.ds[b], r.dgain_m)
+                r.dms[b] = out
+                return out
+
+            def last(b):
+                d_o = dot_nt(ring_b.rows(b), r.wo[:]).astype(BF16)
+                r.qdo[b] = jnp.concatenate([r.q[b], d_o], axis=1)
+
+            return block_stages(ring_a, start_qkv(r, ring_a), pull_a) + block_stages(ring_b, middle, pull_b) + [last]
+
+        dm1 = fb1.full_1.reshape(whole[0])
+        bb = chain('bwd_1_0', 6,
+                   dict(dq=vm(dq1), dkv=vm(dkv1), xs=vm(f0.xs1), gain_a=vm(g_attn[1][None]), dms_in=vm(fb1.dms), gate=vm(f0.gate), lin=vm(f0.lin), x1s=vm(f0.x1s), gain_m=vm(g_mlp[0][None]), q=vm(q0),
+                        dm1=hbm(dm1), u1=hbm(fb1.u), dgl1=hbm(fb1.dgl), w_o=hbm(w_o), **mlp_in, **qkv_in),
+                   dict(ds=shard, dgl=((batch, rows, 2 * ff), BF16), dms=shard, qdo=((batch, rows, 2 * width), BF16), dgain_a=gain_row, dgain_m=gain_row, full_0=full, full_1=full),
+                   dict(wqkv=wqkv(1), wout=wout(0), wgl=wgl(0), wo=wo(0)), 2,
+                   [('dm1', 'dm1_g')], [('full_0', 'd_g')], [('u1', 'u1_g'), ('dgl1', 'dgl1_g'), ('dq', 'dq_g'), ('dkv', 'dkv_g')], body_bb, geometry)
+
+        dq0, dkv0, score_grad0 = attn_bwd(bb.qdo, kva0, bias_rows, bias_cols, mask_rows, mask_cols, 7)
+
+        def body_bf(r):
+            ring, = r.rings
+            r.dgain_a[:] = jnp.zeros_like(r.dgain_a)
+
+            def pull(b, total):
+                return rms_pull(total, r.xs[b], r.gain_a[:], r.dms_in[b], r.dgain_a)
+
+            def last(b):
+                for j in range(4):
+                    ring.y_gather(b, j).wait_recv()
+
+            return block_stages(ring, start_qkv(r, ring), pull) + [last]
+
+        dm0 = bb.full_1.reshape(whole[0])
+        bf = chain('bwd_0', 8,
+                   dict(dq=vm(dq0), dkv=vm(dkv0), xs=vm(own_rows(x_in)), gain_a=vm(g_attn[0][None]), dms_in=vm(bb.dms), dm0=hbm(dm0), dgl0=hbm(bb.dgl), **qkv_in),
+                   dict(dgain_a=gain_row, full_0=full), dict(wqkv=wqkv(0)), 1,
+                   [('dm0', 'dm0_g')], [], [('dgl0', 'dgl0_g'), ('dq', 'dq_g'), ('dkv', 'dkv_g')], body_bf, geometry)
+
+        def own_half(array):
+            return lax.dynamic_slice_in_dim(array.reshape(tokens, d_model), core * half, half, axis=1)
+
+        def flat(array, n):
+            return array.reshape(-1, n)
+
+        def grad(left, right, left_wide):
+            (a, a_g), (b, b_g) = left, right
+            a_n, b_n = a_g.shape[-1], b_g.shape[-1]
+            a = own_half(a) if left_wide else flat(a, a_n)
+            b = flat(b, b_n) if left_wide else own_half(b)
+            return (dot_tn(a, b) + dot_tn(flat(a_g, a_n), flat(b_g, b_n))).astype(BF16)
+
+        dqkv1 = (jnp.concatenate([dq1, dkv1], axis=2), jnp.concatenate([bb.dq_g, bb.dkv_g], axis=3))
+        dqkv0 = (jnp.concatenate([dq0, dkv0], axis=2), jnp.concatenate([bf.dq_g, bf.dkv_g], axis=3))
+        owns = [
+            grad((h0, f0.h0_g), dqkv0, True),
+            grad((f0.h1, fb1.h1_g), dqkv1, True),
+            grad((o0, f0.o_g), (dm0, bf.dm0_g), False),
+            grad((o1, fb1.o_g), (dm1, bb.dm1_g), False),
+            grad((f0.h2, f0.h2_g), (bb.dgl, bf.dgl0_g), True),
+            grad((fb1.h2, fb1.h2_g), (fb1.dgl, bb.dgl1_g), True),
+            grad((f0.u, fb1.u0_g), (bb.full_0, bb.d_g), False),
+            grad((fb1.u, bb.u1_g), (d_y, fb1.d_g), False),
+        ]
+
+        d_bias = bias_grad(score_grad0, score_grad1, start, heads, n_buckets)
         slots = jnp.zeros((tp_size, n_buckets * heads), F32)
         slots = lax.dynamic_update_slice(slots, d_bias.reshape(1, -1), (tp_index, jnp.int32(0)))
-        small = lax.psum(jnp.concatenate([jnp.stack(gains[0]).reshape(-1), jnp.stack(gains[1]).reshape(-1), slots.reshape(-1)]), ('tp', 'cp'))
-        n_gain = n_layers * d_model
+        small = jnp.concatenate([part.reshape(-1, 128) for part in (bf.dgain_a, bb.dgain_a, bb.dgain_m, fb1.dgain_m, slots)], axis=0)
+        mates, small = swap(owns, small, 9)
+        n_gain = n_layers * d_model // 128
         d_g_attn = small[:n_gain].reshape(n_layers, d_model)
         d_g_mlp = small[n_gain:2 * n_gain].reshape(n_layers, d_model)
         d_rel = lax.dynamic_slice(small[2 * n_gain:].reshape(tp_size, -1), (tp_index, jnp.int32(0)), (1, n_buckets * heads)).reshape(n_buckets, heads)
-        return (d.reshape(batch, rows, d_model), d_rel, d_g_attn, d_g_mlp) + tuple(jnp.stack(parts) for parts in big)
+        plan = tuple((layer, by_rows, first, n) for by_rows, first, n in ((True, 0, 3), (False, 3, 1), (True, 4, 2), (False, 6, 1)) for layer in range(n_layers))
+        grads = place(plan, owns, mates, [w.shape for w in (w_q, w_k, w_v, w_o, w_gate, w_lin, w_out)])
+        return (bf.full_0.reshape(batch, rows, d_model), d_rel, d_g_attn, d_g_mlp) + tuple(grads)
 
     return jax.shard_map(local_program, mesh=mesh, in_specs=(seq_spec, seq_spec, P(None, 'cp'), P(None, 'tp')) + weight_specs, out_specs=(seq_spec, P(None, 'tp')) + weight_specs, check_vma=False)

time: 2070 us -> 863 us (0.42)
  waiting for transfers between devices: 1590 us -> 0 us
  Pallas kernels: 82.8 us -> 780 us
  matrix products: 140 us -> 34.9 us
  other arithmetic: 105 us -> 4.76 us
  blocking collectives: 46.8 us -> 0 us
  local copies, waits for them, and re-layouts: 78.6 us -> 37.6 us
    reduce_scatter x21 -> x0, waiting for transfers between devices: 1110 us -> none  [the longest x7 616 us: reduce_rows(): return lax.psum_scatter(partial, 'tp', scatter_dimension=0, tiled=True)]
    pallas_call x0 -> x7, Pallas kernels: none -> 697 us  [the longest x4 643 us: chain(): pl.pallas_call(kernel, out_shape=tuple((jax.ShapeDtypeStruct(*outs[k]) fo...]
    all_gather x21 -> x0, waiting for transfers between devices: 477 us -> none  [the longest x14 274 us: cp_sum(): return lax.all_gather(own, 'cp', axis=0, tiled=True)]
    dot_general x27 -> x3, matrix products: 73.9 us -> 3.85 us  [local_program(): jnp.dot(h0, w[0], preferred_element_type=F32).astype(BF16)]
    broadcast_in_dim x82 -> x1, local copies, waits for them, and re-layouts: 50.9 us -> 0.14 us  [local_program(): mask_cols = key_add[:, :, None]]
    psum x1 -> x0, blocking collectives: 40.5 us -> none  [local_program(): lax.psum(jnp.concatenate([jnp.stack(gains[0]).reshape(-1), jnp.stack(gain...]
    convert_element_type x18 -> x1, other arithmetic: 35.9 us -> 0.65 us  [norm_rows(): return rms_parts(rows.astype(F32), gain)]
    dot_general x14 -> x16, matrix products: 66.2 us -> 31 us  [dot_tn(): lax.dot_general(a, b, (((0,), (0,)), ((), ())), preferred_element_type=F32)]
  transfers between devices with their start and end apart: 42 -> 0, of which waited for: 40 -> 0; matrix products, arithmetic and copies ran while one was open for 10% -> 0% of each run, Pallas kernels for 1% -> 0%
where the time goes in v3:
time: 863 us; the launch traced here: 860 us
  Pallas kernels  780 us (90%)
  local copies, waits for them, and re-layouts  37.6 us (4%)
  matrix products  34.9 us (4%)
    pallas_call x4, Pallas kernels, chain(): pl.pallas_call(kernel, out_shape=tuple((jax.ShapeDtypeStruct(*outs[k]) fo...  643 us
    pallas_call x2, Pallas kernels, attn_bwd(): pl.pallas_call(functools.partial(attn_bwd_kernel, heads), out_shape=(jax....  47.5 us
    pallas_call x2, Pallas kernels, attn_fwd(): pl.pallas_call(functools.partial(attn_fwd_kernel, heads), out_shape=(jax....  32.3 us
    unnamed x147, local copies, waits for them, and re-layouts  32.1 us
    pallas_call x1, Pallas kernels, swap(): pl.pallas_call(functools.partial(swap_kernel, n), out_shape=tuple((jax.Sh...  32 us
    dot_general x16, matrix products, dot_tn(): lax.dot_general(a, b, (((0,), (0,)), ((), ())), preferred_element_type=F32)  31 us

profile of v3, /device:TPU:0, one launch (start us, length us, event | category | flops | bytes accessed | tf_op | source)
XLA Modules:
  0.0 859.5 jit_solution(14241673988877413216)
XLA Ops:
  0.7 2.0 constant_dynamic-slice_fusion.1
  2.7 1.4 fusion.48
  4.1 2.1 multiply_reduce_fusion
  6.2 0.6 fusion.46
  7.8 0.8 convolution_convert_fusion
  8.6 1.3 copy-done.57
  9.8 0.8 convolution_convert_fusion.1
  10.9 0.6 copy-done.55
  11.4 2.3 convolution_convert_fusion.2
  13.8 0.6 fusion.45
  14.5 9.3 %prep.1 = (f32[4,4,1,128]{3,2,1,0:T(1,128)S(1)}, f32[512,512]{1,0:T(8,128)S(1)}, f32[4,128,512]{2,1,0:T(8,128)S(1)}) custom-call(f32[4,1,128]{2,1,0:T(1,128)S(1)} %bitcast.112, f32[32,4]{1,0:T(8,128)S(1)} %copy.36.table_ref), custom_call_target="tpu_custom_call" | custom-call | flops 1048576000 | bytes 8388608 | tf_op jit(solution)/shard_map/prep/pallas_call | solution.py:627
  23.8 16.2 %attn_fwd.2 = (bf16[4,128,256]{2,1,0:T(8,128)(2,1)S(1)}, bf16[4,4,128,512]{3,2,1,0:T(8,128)(2,1)S(1)}) custom-call(bf16[4,128,256]{2,1,0:T(8,128)(2,1)S(1)} %bitcast.113, bf16[4,128,512]{2,1,0:T(8,128)(2,1)S(1)} %bitcast.109, f32[512,512]{1,0:T(8,128)S(1)} %get-tuple-element.83.bias_ref.bias_r_ref, f32[4,4,1,128]{3,2,1,0:T(1,128)S(1)} %get-tuple-element.84.mask_ref.mask_r_ref), custom_call_target="tpu_custom_call" | custom-call | flops 4194304000 | bytes 8388608 | tf_op jit(solution)/shard_map/attn_fwd/pallas_call | solution.py:130
  40.0 0.7 copy-done.8
  40.7 1.3 copy-done.19
  42.0 181.3 %fwd_0.1 = (bf16[4,16,2048]{2,1,0:T(8,128)(2,1)}, bf16[4,128,2048]{2,1,0:T(8,128)(2,1)}, f32[4,128,640]{2,1,0:T(8,128)}, f32[4,128,640]{2,1,0:T(8,128)}, bf16[4,...) custom-call(bf16[4,128,256]{2,1,0:T(8,128)(2,1)} %copy-done.8, ...), custom_call_target="tpu_custom_call" | custom-call | flops 83886080000 | bytes 8388608 | tf_op jit(solution)/shard_map/fwd_0/pallas_call | solution.py:559
  223.3 1.0 copy-done.23
  224.4 0.9 copy-done.24
  225.3 16.1 %attn_fwd.3 = (bf16[4,128,256]{2,1,0:T(8,128)(2,1)S(1)}, bf16[4,4,128,512]{3,2,1,0:T(8,128)(2,1)S(1)}) custom-call(bf16[4,128,256]{2,1,0:T(8,128)(2,1)S(1)} %copy-done.24, bf16[4,128,512]{2,1,0:T(8,128)(2,1)S(1)} %copy-done.23, f32[512,512]{1,0:T(8,128)S(1)} %get-tuple-element.83.bias_ref.bias_r_ref, f32[4,4,1,128]{3,2,1,0:T(1,128)S(1)} %get-tuple-element.84.mask_ref.mask_r_ref), custom_call_target="tpu_custom_call" | custom-call | flops 4194304000 | bytes 8388608 | tf_op jit(solution)/shard_map/attn_fwd/pallas_call | solution.py:130
  241.5 0.7 copy-done.10
  242.2 1.3 copy-done.21
  243.5 179.6 %fwd_bwd_1.1 = (bf16[4,16,2048]{2,1,0:T(8,128)(2,1)}, bf16[4,128,2048]{2,1,0:T(8,128)(2,1)}, bf16[4,128,640]{2,1,0:T(8,128)(2,1)}, bf16[4,128,1280]{2,1,0:T(8,12...) custom-call(bf16[4,128,256]{2,1,0:T(8,128)(2,1)} %copy-done.10, ...), custom_call_target="tpu_custom_call" | custom-call | flops 83886080000 | bytes 8388608 | tf_op jit(solution)/shard_map/fwd_bwd_1/pallas_call | solution.py:559
  423.3 1.6 copy-done.22
  424.9 1.0 copy-done.26
  425.9 23.2 %attn_bwd.2 = (bf16[4,128,256]{2,1,0:T(8,128)(2,1)S(1)}, bf16[4,128,512]{2,1,0:T(8,128)(2,1)S(1)}, f32[512,512]{1,0:T(8,128)S(1)}) custom-call(bf16[4,128,512]{2,1,0:T(8,128)(2,1)S(1)} %copy-done.26, bf16[4,4,128,512]{3,2,1,0:T(8,128)(2,1)S(1)} %copy-done.22, f32[512,512]{1,0:T(8,128)S(1)} %get-tuple-element.83.bias_ref.bias_r_ref, ...), custom_call_target="tpu_custom_call" | custom-call | flops 10485760000 | bytes 8388608 | tf_op jit(solution)/shard_map/attn_bwd/pallas_call | solution.py:248
  449.1 0.8 copy-done.4
  449.9 0.7 copy-done.12
  450.6 180.1 %bwd_1_0.1 = (bf16[4,16,2048]{2,1,0:T(8,128)(2,1)}, bf16[4,128,1280]{2,1,0:T(8,128)(2,1)}, bf16[4,16,2048]{2,1,0:T(8,128)(2,1)}, bf16[4,128,512]{2,1,0:T(8,128)(...) custom-call(bf16[4,128,256]{2,1,0:T(8,128)(2,1)} %copy-done.12, ...), custom_call_target="tpu_custom_call" | custom-call | flops 83886080000 | bytes 8388608 | tf_op jit(solution)/shard_map/bwd_1_0/pallas_call | solution.py:559
  630.7 1.6 copy-done.20
  632.3 1.0 copy-done.25
  633.3 24.3 %attn_bwd.3 = (bf16[4,128,256]{2,1,0:T(8,128)(2,1)S(1)}, bf16[4,128,512]{2,1,0:T(8,128)(2,1)S(1)}, f32[512,512]{1,0:T(8,128)S(1)}) custom-call(bf16[4,128,512]{2,1,0:T(8,128)(2,1)S(1)} %copy-done.25, bf16[4,4,128,512]{3,2,1,0:T(8,128)(2,1)S(1)} %copy-done.20, f32[512,512]{1,0:T(8,128)S(1)} %get-tuple-element.83.bias_ref.bias_r_ref, ...), custom_call_target="tpu_custom_call" | custom-call | flops 10485760000 | bytes 8388608 | tf_op jit(solution)/shard_map/attn_bwd/pallas_call | solution.py:248
  657.7 0.8 copy-done.6
  658.4 0.7 copy-done.14
  659.1 102.3 %bwd_0.1 = (f32[1,2048]{1,0:T(1,128)}, bf16[4,8,16,2048]{3,2,1,0:T(8,128)(2,1)}, bf16[3,4,128,1024]{3,2,1,0:T(8,128)(2,1)}, bf16[3,4,128,1280]{3,2,1,0:T(8,128)(...) custom-call(bf16[4,128,256]{2,1,0:T(8,128)(2,1)} %copy-done.14, bf16[4,128,512]{2,1,0:T(8,128)(2,1)} %copy-done.6, ...), custom_call_target="tpu_custom_call" | custom-call | flops 83886080000 | bytes 8388608 | tf_op jit(solution)/shard_map/bwd_0/pallas_call | solution.py:559
  761.5 0.7 constant_dynamic-update-slice_fusion.4
  762.2 4.0 bias_grad.1
  766.7 2.5 fusion.23
  769.3 2.3 fusion.4.refs_7_
  771.8 2.3 fusion.52
  774.1 0.9 add_convert_fusion.refs_6_
  775.0 1.3 copy-done.66
  776.3 4.4 fusion.51
  780.8 1.6 fusion.refs_5_
  782.9 1.9 copy-done.68
  784.8 4.6 fusion.50
  789.5 1.6 fusion.1.refs_4_
  791.5 1.0 convolution_bitcast_fusion
  793.3 0.9 copy-done.31
  794.4 1.0 convolution_bitcast_fusion.1
  795.5 0.6 copy-done.43
  797.0 1.2 copy-done.61
  798.2 2.7 fusion.9
  801.0 1.1 fusion.2.refs_1_
  802.2 0.9 copy-done.60
  803.7 3.0 fusion.5
  806.8 0.7 bitcast_convert_fusion
  807.5 1.2 fusion.3.refs_0_
  808.7 32.0 %swap.1 = (bf16[1024,768]{1,0:T(8,128)(2,1)S(1)}, bf16[1024,768]{1,0:T(8,128)(2,1)S(1)}, bf16[256,1024]{1,0:T(8,128)(2,1)S(1)}, bf16[256,1024]{1,0:T(8,128)(2,1)...) custom-call(bf16[1024,768]{1,0:T(8,128)(2,1)S(1)} %fusion.3.refs_0_,, ...), custom_call_target="tpu_custom_call" | custom-call | flops 10485760000 | bytes 8388608 | tf_op jit(solution)/shard_map/swap/pallas_call | solution.py:677
  840.7 1.5 copy-done.2
  842.2 1.5 copy-done.3
  843.7 12.0 %place.1 = (bf16[2,2048,256]{2,1,0:T(8,128)(2,1)}, bf16[2,2048,256]{2,1,0:T(8,128)(2,1)}, bf16[2,2048,256]{2,1,0:T(8,128)(2,1)}, bf16[2,256,2048]{2,1,0:T(8,128)...) custom-call(bf16[1024,768]{1,0:T(8,128)(2,1)S(1)} %fusion.3.refs_0_, ...), custom_call_target="tpu_custom_call" | custom-call | tf_op jit(solution)/shard_map/place/pallas_call | solution.py:721
  855.7 0.6 reshape.218
  856.3 0.6 reshape.219
  857.0 0.7 copy.46
  857.7 1.3 copy.67
  (138 shorter events, 6.0 us)
Async XLA Ops:
  0.6 6.2 copy-start.27
  4.1 3.2 copy-start.46
  6.2 1.6 copy-start.56
  7.4 3.2 copy-start.33
  7.4 2.5 copy-start.57
  9.8 1.6 copy-start.55
  11.4 2.4 copy-start.53
  11.4 3.0 copy-start.54
  13.8 26.2 %copy-start.16 = (bf16[512,256]{1,0:T(8,128)(2,1)}, bf16[512,256]{1,0:T(8,128)(2,1)S(1)}, u32[]{:S(2)}) copy-start(bf16[512,256]{1,0:T(8,128)(2,1)S(1)} %convolution_convert_fusion.2) | copy-start | bytes 786436
  23.8 399.5 %copy-start.17 = (f32[4,128,512]{2,1,0:T(8,128)}, f32[4,128,512]{2,1,0:T(8,128)S(1)}, u32[]{:S(2)}) copy-start(f32[4,128,512]{2,1,0:T(8,128)S(1)} %get-tuple-element.94.bias_c_ref) | copy-start | bytes 3145732
  40.7 1.3 copy-start.19
  223.3 1.0 copy-start.23
  224.4 0.9 copy-start.24
  242.2 1.3 copy-start.21
  243.5 179.6 %copy-start.48 = (f32[4,128,1]{1,0,2:T(4,128)S(1)}, f32[4,128,1]{1,0,2:T(4,128)}, u32[]{:S(2)}) copy-start(f32[4,128,1]{1,0,2:T(4,128)} %get-tuple-element.185) | copy-start | bytes 6148
  423.3 1.6 copy-start.22
  424.9 1.0 copy-start.26
  449.1 0.8 copy-start.4
  450.6 180.1 %copy-start.18 = (f32[4,128,512]{2,1,0:T(8,128)S(1)}, f32[4,128,512]{2,1,0:T(8,128)}, u32[]{:S(2)}) copy-start(f32[4,128,512]{2,1,0:T(8,128)} %copy-done.17) | copy-start | bytes 3145732
  630.7 1.6 copy-start.20
  632.3 1.0 copy-start.25
  659.1 103.0 %copy-start.51 = (f32[1,2048]{1,0:T(1,128)S(1)}, f32[1,2048]{1,0:T(1,128)}, u32[]{:S(2)}) copy-start(f32[1,2048]{1,0:T(1,128)} %get-tuple-element.134) | copy-start | bytes 24580
  659.1 103.0 %copy-start.50 = (f32[1,2048]{1,0:T(1,128)S(1)}, f32[1,2048]{1,0:T(1,128)}, u32[]{:S(2)}) copy-start(f32[1,2048]{1,0:T(1,128)} %get-tuple-element.135) | copy-start | bytes 24580
  659.1 103.1 %copy-start.49 = (f32[1,2048]{1,0:T(1,128)S(1)}, f32[1,2048]{1,0:T(1,128)}, u32[]{:S(2)}) copy-start(f32[1,2048]{1,0:T(1,128)} %get-tuple-element.136) | copy-start | bytes 24580
  766.2 3.0 copy-start.34
  766.7 2.6 copy-start.29
  769.3 2.3 copy-start.58
  769.3 2.5 copy-start.59
  771.8 2.3 copy-start.39
  771.8 2.3 copy-start.45
  771.8 3.2 copy-start.69
  774.1 2.2 copy-start.66
  776.3 4.4 copy-start.35
  776.3 4.4 copy-start.42
  780.8 2.1 copy-start.67
  780.8 4.0 copy-start.68
  782.4 26.3 %copy-start = (bf16[1024,1280]{1,0:T(8,128)(2,1)}, bf16[1024,1280]{1,0:T(8,128)(2,1)S(1)}, u32[]{:S(2)}) copy-start(bf16[1024,1280]{1,0:T(8,128)(2,1)S(1)} %fusion.refs_5_) | copy-start | bytes 7864324
  784.8 4.6 copy-start.36
  784.8 4.6 copy-start.40
  789.5 1.9 copy-start.30
  789.5 2.1 copy-start.38
  789.5 3.2 copy-start.41
  791.1 17.6 %copy-start.1 = (bf16[1024,1280]{1,0:T(8,128)(2,1)}, bf16[1024,1280]{1,0:T(8,128)(2,1)S(1)}, u32[]{:S(2)}) copy-start(bf16[1024,1280]{1,0:T(8,128)(2,1)S(1)} %fusion.1.refs_4_) | copy-start | bytes 7864324
  791.5 1.3 copy-start.11
  791.5 2.7 copy-start.31
  792.5 1.9 copy-start.37
  794.4 1.0 copy-start.9
  794.4 1.7 copy-start.43
  794.4 2.6 copy-start.62
  794.4 2.6 copy-start.64
  795.4 1.4 copy-start.5
  795.4 1.5 copy-start.13
  795.4 2.8 copy-start.61
  798.2 2.7 copy-start.44
  800.9 1.2 copy-start.7
  800.9 1.2 copy-start.15
  801.0 2.1 copy-start.60
  801.0 2.6 copy-start.63
  801.0 2.8 copy-start.65
  803.7 3.0 copy-start.47
  803.7 3.1 copy-start.28
  840.7 1.5 copy-start.2
  842.2 1.5 copy-start.3
  843.7 14.0 %copy-start.32 = (bf16[4,8,16,2048]{3,2,1,0:T(8,128)(2,1)S(1)}, bf16[4,8,16,2048]{3,2,1,0:T(8,128)(2,1)}, u32[]{:S(2)}) copy-start(bf16[4,8,16,2048]{3,2,1,0:T(8,128)(2,1)} %get-tuple-element.111) | copy-start | bytes 6291460
  (6 other events, 4.3 us)

commit v4 on v0

v4 whole, which is shorter than its diff:
```python
import functools

import jax
import jax.numpy as jnp
from jax import lax
from jax.experimental import pallas as pl
from jax.experimental.pallas import tpu as pltpu
from jax.sharding import PartitionSpec as P

NORM_EPS = 1e-6
MASK_NEG = -1e9
BF16 = jnp.bfloat16
F32 = jnp.float32
VMEM = pltpu.VMEM
MESH = pl.DeviceIdType.MESH
MIB = 2 ** 20
HEAD_DIM = 64
VMEM_SPEC = pl.BlockSpec(memory_space=pltpu.VMEM)
SMEM_SPEC = pl.BlockSpec(memory_space=pltpu.SMEM)


def rel_bucket(rel_pos):
    distance = jnp.minimum(jnp.abs(rel_pos), 128)
    distance_sq = distance * distance
    log_part = 8 + sum((distance_sq >= 64 * 2 ** power).astype(jnp.int32) for power in range(1, 8))
    return jnp.where(distance < 8, distance, log_part) + 16 * (rel_pos > 0).astype(jnp.int32)


def comm_params(cid, mib):
    return pltpu.CompilerParams(collective_id=cid, has_side_effects=True, vmem_limit_bytes=mib * MIB)


def cost(gflops):
    return pl.CostEstimate(flops=gflops * 1000 * MIB, bytes_accessed=8 * MIB, transcendentals=MIB)


def dot_nt(a, b):
    return lax.dot_general(a, b, (((1,), (1,)), ((), ())), preferred_element_type=F32)


def dot_nn(a, b):
    return lax.dot_general(a, b, (((1,), (0,)), ((), ())), preferred_element_type=F32)


def dot_tn(a, b):
    return lax.dot_general(a, b, (((0,), (0,)), ((), ())), preferred_element_type=F32)


def stack_heads(block, heads):
    wide = block.astype(F32)
    lane_head = lax.broadcasted_iota(jnp.int32, block.shape, 1) // HEAD_DIM
    return jnp.concatenate([jnp.where(lane_head == h, wide, 0.0).astype(BF16) for h in range(heads)], axis=0)


def pick_heads(stacked, heads, rows):
    lane_head = lax.broadcasted_iota(jnp.int32, (rows, stacked.shape[1]), 1) // HEAD_DIM
    out = stacked[:rows]
    for h in range(1, heads):
        out = jnp.where(lane_head == h, stacked[h * rows:(h + 1) * rows], out)
    return out


def cp_places():
    me = lax.axis_index('cp')
    mate = me + 1 - 2 * lax.rem(me, 2)
    across = lax.rem(me + 2, 4)
    diagonal = lax.rem(mate + 2, 4)
    return me, mate, across, diagonal


def rms_parts(x_f, gain):
    inv_rms = lax.rsqrt(jnp.mean(x_f * x_f, axis=-1, keepdims=True) + NORM_EPS)
    return (x_f * inv_rms * gain).astype(BF16)


GELU_C = 0.7978845608028654
GELU_A = 0.044715


def gelu_parts(x):
    t = jnp.tanh(GELU_C * (x + GELU_A * x * x * x))
    cdf = 0.5 * (1.0 + t)
    return x * cdf, cdf + 0.5 * x * (1.0 - t * t) * GELU_C * (1.0 + 3.0 * GELU_A * x * x)


def remote(src, dst, send, recv, axis, peer):
    return pltpu.make_async_remote_copy(src_ref=src, dst_ref=dst, send_sem=send, recv_sem=recv, device_id={axis: peer}, device_id_type=MESH)


def tp_places():
    me = lax.axis_index('tp')
    z, y = me // 2, lax.rem(me, 2)
    pair = me + 1 - 2 * y
    return me, z, y, pair, [2 * lax.rem(z + j, 4) + y for j in range(4)]


def meet(tp_peers, cp_peers):
    barrier = pltpu.get_barrier_semaphore()
    for axis, peers in (('tp', tp_peers), ('cp', cp_peers)):
        for peer in peers:
            pl.semaphore_signal(barrier, inc=1, device_id={axis: peer}, device_id_type=MESH)
    pl.semaphore_wait(barrier, len(tp_peers) + len(cp_peers))


class Ring:
    def __init__(self, part, from_y, from_z, full, *sems):
        self.part, self.from_y, self.from_z, self.full, self.sems = part, from_y, from_z, full, sems
        _, self.z, self.y, self.pair, self.z_peer = tp_places()
        self.seg = self.y * 4 + self.z

    @staticmethod
    def scratch(batch, seg, d_model):
        dma = pltpu.SemaphoreType.DMA
        return [
            pltpu.VMEM((batch, 2, 4, seg, d_model), F32),
            pltpu.VMEM((batch, 4, seg, d_model), F32),
            pltpu.VMEM((batch, 3, seg, d_model), F32),
            pltpu.VMEM((batch, 8, seg, d_model), BF16),
            dma((2, batch)), dma((2, batch, 3)), dma((2, batch, 3)), dma((2, batch, 4)),
        ]

    def y_sum(self, b):
        s = self.sems[0]
        return remote(self.part.at[b, 1 - self.y], self.from_y.at[b], s.at[0, b], s.at[1, b], 'tp', self.pair)

    def z_sum(self, b, j):
        s = self.sems[1]
        return remote(self.part.at[b, self.y, lax.rem(self.z + j, 4)], self.from_z.at[b, j - 1], s.at[0, b, j - 1], s.at[1, b, j - 1], 'tp', self.z_peer[j])

    def z_gather(self, b, j):
        s = self.sems[2]
        ref = self.full.at[b, self.seg]
        return remote(ref, ref, s.at[0, b, j - 1], s.at[1, b, j - 1], 'tp', self.z_peer[j])

    def y_gather(self, b, j):
        s = self.sems[3]
        ref = self.full.at[b, self.y * 4 + lax.rem(self.z - j + 4, 4)]
        return remote(ref, ref, s.at[0, b, j], s.at[1, b, j], 'tp', self.pair)

    def send_partial(self, b, partial):
        self.part[b] = partial.reshape(self.part.shape[1:])
        self.y_sum(b).start()

    def reduce_pair(self, b):
        self.y_sum(b).wait_recv()
        self.part[b, self.y] = self.part[b, self.y] + self.from_y[b]
        for j in (2, 1, 3):
            self.z_sum(b, j).start()

    def reduced(self, b):
        for j in (1, 2, 3):
            self.z_sum(b, j).wait_recv()
        return self.part[b, self.y, self.z] + self.from_z[b, 0] + self.from_z[b, 1] + self.from_z[b, 2]

    def publish(self, b, out):
        self.full[b, self.seg] = out
        for j in (2, 1, 3):
            self.z_gather(b, j).start()
        self.y_gather(b, 0).start()

    def forward(self, b):
        for j in (1, 2, 3):
            self.z_gather(b, j).wait_recv()
            self.y_gather(b, j).start()

    def arrive(self, b):
        for j in range(4):
            self.y_gather(b, j).wait_recv()
        self.y_sum(b).wait_send()
        for j in range(4):
            self.y_gather(b, j).wait_send()
        for j in (1, 2, 3):
            self.z_sum(b, j).wait_send()
            self.z_gather(b, j).wait_send()

    def rows(self, b):
        return self.full[b].reshape(-1, self.full.shape[-1])


class Trade:
    def __init__(self, store, send, recv):
        self.store, self.send, self.recv = store, send, recv
        self.me, self.mate, self.across, self.diagonal = cp_places()

    def copy(self, b, r):
        ref = self.store.at[b, self.across if r == 2 else self.me]
        return remote(ref, ref, self.send.at[r, b], self.recv.at[r, b], 'cp', self.across if r == 1 else self.mate)

    def give(self, b):
        self.copy(b, 1).start()
        self.copy(b, 0).start()

    def pass_on(self, b):
        self.copy(b, 1).wait_recv()
        self.copy(b, 2).start()

    def take(self, b):
        self.copy(b, 0).wait_recv()
        self.copy(b, 2).wait_recv()

    def finish(self, b):
        for r in range(3):
            self.copy(b, r).wait_send()


class Wide:
    def __init__(self, src, dst, send, recv):
        self.src, self.dst, self.send, self.recv = src, dst, send, recv
        me, *self.peers = cp_places()
        mate, across, diagonal = self.peers
        self.peers = (mate, across, diagonal)
        self.core = lax.rem(me, 2)

    def copy(self, r, window):
        n = self.dst.shape[-1]
        want = self.core if r == 1 else 1 - self.core
        columns = pl.ds(pl.multiple_of(want * n, n), n)
        return remote(self.src.at[window].at[..., columns], self.dst.at[r].at[window], self.send.at[r], self.recv.at[r], 'cp', self.peers[r])

    def give(self, b):
        for r in (1, 2, 0):
            self.copy(r, pl.ds(b, 1)).start()

    def pass_on(self):
        pass

    def finish(self):
        for r in range(3):
            self.copy(r, pl.ds(0, self.src.shape[0])).wait()


class Narrow:
    def __init__(self, src, dst, send, recv):
        self.src, self.dst, self.send, self.recv = src, dst, send, recv
        _, self.mate, self.across, _ = cp_places()

    def copy(self, r, window):
        src = self.src if r < 2 else self.dst.at[1]
        return remote(src.at[window], self.dst.at[r].at[window], self.send.at[r], self.recv.at[r], 'cp', self.across if r == 1 else self.mate)

    def give(self, b):
        for r in (1, 0):
            self.copy(r, pl.ds(b, 1)).start()

    def pass_on(self):
        every = pl.ds(0, self.src.shape[0])
        self.copy(1, every).wait_recv()
        self.copy(2, every).start()

    def finish(self):
        every = pl.ds(0, self.src.shape[0])
        self.copy(0, every).wait()
        self.copy(1, every).wait_send()
        self.copy(2, every).wait()


class Spill:
    def __init__(self, slots, sem):
        self.slots, self.sem = slots, sem

    def copy(self, out, b):
        slot = lax.rem(b, 2)
        return pltpu.make_async_copy(self.slots.at[slot], out.at[b], self.sem.at[slot])

    def put(self, out, b, value):
        self.slots[lax.rem(b, 2)] = value
        self.copy(out, b).start()


def norm_rows(rows, gain):
    return rms_parts(rows.astype(F32), gain)


def rms_pull(total, x_shard, gain, res, d_gain_ref):
    d_norm = total.astype(BF16).astype(F32)
    x_f = x_shard.astype(F32)
    inv_rms = lax.rsqrt(jnp.mean(x_f * x_f, axis=-1, keepdims=True) + NORM_EPS)
    normed = x_f * inv_rms
    d_gain_ref[:] += jnp.sum(d_norm * normed, axis=0, keepdims=True)
    d_normed = d_norm * gain
    d_x = inv_rms * (d_normed - normed * jnp.mean(d_normed * normed, axis=-1, keepdims=True))
    return (res.astype(F32) + d_x).astype(BF16)


def mlp_pull(d_u, gate, lin):
    d_u = d_u.astype(BF16).astype(F32)
    value, slope = gelu_parts(gate)
    return jnp.concatenate([(d_u * lin * slope).astype(BF16), (d_u * value).astype(BF16)], axis=1)


def row_sum(x):
    return jnp.sum(x, axis=1, keepdims=True)


def row_max(x):
    return jnp.max(x, axis=1, keepdims=True)


def mask_row(mask_ref, b):
    return jnp.concatenate([mask_ref[c, b] for c in range(mask_ref.shape[0])], axis=1)


def attend(heads, q, kv, bias, mask):
    rows, width = q.shape
    scores = dot_nt(stack_heads(q, heads), kv[:, :width]) + bias + mask
    top = row_max(scores)
    probs = jnp.exp(scores - top)
    total = row_sum(probs)
    out = dot_nn(probs.astype(BF16), kv[:, width:]) / total
    return pick_heads(out, heads, rows).astype(BF16)


def attend_rows_back(heads, qdo, kv, bias, mask, ds_ref):
    rows, wide = qdo.shape
    width = wide // 2
    keys, vals = kv[:, :width], kv[:, width:]
    scores = dot_nt(stack_heads(qdo[:, :width], heads), keys) + bias + mask
    top = row_max(scores)
    unnorm = jnp.exp(scores - top)
    total = row_sum(unnorm)
    log_norm = top + jnp.log(total)
    probs = unnorm * (1.0 / total)
    d_probs = dot_nt(stack_heads(qdo[:, width:], heads), vals)
    row_dot = row_sum(probs * d_probs)
    lane = lax.broadcasted_iota(jnp.int32, (rows, rows), 1)
    table = jnp.zeros((rows, rows), F32)
    for h in range(heads):
        table = jnp.where(lane == h, log_norm[h * rows:(h + 1) * rows], table)
        table = jnp.where(lane == heads + h, row_dot[h * rows:(h + 1) * rows], table)
    d_scores = probs * (d_probs - row_dot)
    ds_ref[:] += d_scores
    d_q = dot_nn(d_scores.astype(BF16), keys)
    return pick_heads(d_q, heads, rows).astype(BF16), jnp.transpose(table)[:2 * heads]


def attend_cols_back(heads, own_kv, mask_col, bias_ref, qdo_of, stats_of):
    rows, wide = own_kv.shape
    width = wide // 2
    keys, vals = own_kv[:, :width], own_kv[:, width:]

    def block(src, acc):
        d_k, d_v = acc
        qdo, stats = qdo_of(src), stats_of(src)
        log_norm = jnp.concatenate([stats[h:h + 1] for h in range(heads)], axis=1)
        row_dot = jnp.concatenate([stats[heads + h:heads + h + 1] for h in range(heads)], axis=1)
        q_st = stack_heads(qdo[:, :width], heads)
        do_st = stack_heads(qdo[:, width:], heads)
        probs = jnp.exp(dot_nt(keys, q_st) + bias_ref[src] + mask_col - log_norm)
        d_scores = probs * (dot_nt(vals, do_st) - row_dot)
        return d_k + dot_nn(d_scores.astype(BF16), q_st), d_v + dot_nn(probs.astype(BF16), do_st)

    zero = jnp.zeros((rows, width), F32)
    d_k, d_v = lax.fori_loop(0, bias_ref.shape[0], block, (zero, zero))
    return jnp.concatenate([d_k, d_v], axis=1).astype(BF16)


def bias_tables(table_ref, me, rows_ref, cols_ref):
    n_buckets, heads = table_ref.shape
    rows = rows_ref.shape[0] // heads
    seq = rows_ref.shape[1]

    def strip(i, carry):
        first = pl.multiple_of(i * 8, 8)
        rel = lax.broadcasted_iota(jnp.int32, (8, seq), 1) - lax.broadcasted_iota(jnp.int32, (8, seq), 0) - me * rows - first
        for is_col in (False, True):
            buckets = rel_bucket(-rel if is_col else rel)
            vals = [jnp.zeros((8, seq), F32) for _ in range(heads)]
            for k in range(n_buckets):
                hit = buckets == k
                vals = [jnp.where(hit, table_ref[k, h], v) for h, v in enumerate(vals)]
            for h, v in enumerate(vals):
                if is_col:
                    for q in range(seq // rows):
                        cols_ref[q, pl.ds(first, 8), h * rows:(h + 1) * rows] = v[:, q * rows:(q + 1) * rows]
                else:
                    rows_ref[pl.ds(pl.multiple_of(h * rows + first, 8), 8), :] = v
        return carry

    lax.fori_loop(0, rows // 8, strip, 0)


def bucket_sums(ds_ref, me, out_ref):
    n_buckets, heads, seq = out_ref.shape
    rows = ds_ref.shape[0] // heads
    rel = lax.broadcasted_iota(jnp.int32, (rows, seq), 1) - lax.broadcasted_iota(jnp.int32, (rows, seq), 0) - me * rows

    def step(k, carry):
        hit = rel_bucket(rel) == k
        out_ref[k] = jnp.concatenate([jnp.sum(jnp.where(hit, ds_ref[h * rows:(h + 1) * rows], 0.0), axis=0, keepdims=True) for h in range(heads)], axis=0)
        return carry

    lax.fori_loop(0, n_buckets, step, 0)


class Refs:
    pass


WIDE = ('h0', 'h1', 'm0', 'm1', 'dy', 'd0')
NARROW = ('u0', 'u1', 'gl0', 'gl1', 'qkv0', 'qkv1')


def mega_kernel(names, heads, *refs):
    r = Refs()
    for key, ref in zip(names, refs):
        setattr(r, key, ref)
    batch, n_seg, seg, d_model = r.x.shape
    rows = n_seg * seg
    ff = r.w_out.shape[1]
    width = heads * HEAD_DIM
    ring = Ring(*[getattr(r, 'ring_%d' % i) for i in range(8)])
    me, mate, across, diagonal = cp_places()
    others = (mate, across, diagonal)

    def weight(buf, sem, sources, layer):
        out, col = [], 0
        for i, src in enumerate(sources):
            n = src.shape[-1]
            out.append(pltpu.make_async_copy(src.at[layer], buf.at[:, pl.ds(col, n)] if len(sources) > 1 else buf, sem.at[i]))
            col += n
        return out

    weights = dict(qkv=(r.wqkv, r.sem_qkv, (r.w_q, r.w_k, r.w_v)), o=(r.wo, r.sem_o, (r.w_o,)), gl=(r.wgl, r.sem_gl, (r.w_gate, r.w_lin)), out=(r.wout, r.sem_out, (r.w_out,)))

    def load(key, layer):
        def go():
            for copy in weight(*weights[key], layer):
                copy.start()
        return go

    def loaded(key, layer):
        def go():
            for copy in weight(*weights[key], layer):
                copy.wait()
        return go

    for key in ('qkv', 'o', 'gl', 'out'):
        load(key, 0)()
    rows_in = [pltpu.make_async_copy(r.x.at[b], ring.full.at[b], r.sem_in.at[b]) for b in range(batch)]
    shards_in = [pltpu.make_async_copy(src.at[:, ring.seg], dst, r.sem_in.at[batch + i]) for i, (src, dst) in enumerate(((r.x, r.xs0), (r.dy, r.ds1)))]
    for copy in rows_in + shards_in:
        copy.start()
    meet([ring.pair] + ring.z_peer[1:], others)
    masks = [remote(r.key_add, r.mask_all.at[me], r.sem_mask.at[0, i], r.sem_mask.at[1, i], 'cp', peer) for i, peer in enumerate(others)]
    for copy in masks:
        copy.start()
    r.mask_all[me] = r.key_add[:]
    for ref in (r.ds_sum, r.dga0, r.dga1, r.dgm0, r.dgm1):
        ref[:] = jnp.zeros_like(ref)
    for copy in rows_in + shards_in:
        copy.wait()
    loaded('qkv', 0)()

    hold = dict(h=Spill(r.hbuf, r.sem_h), u=Spill(r.ubuf, r.sem_u), gl=Spill(r.gbuf, r.sem_g), qkv=Spill(r.qbuf, r.sem_q), o=Spill(r.obuf, r.sem_ob))
    moves = {}
    for i, key in enumerate(WIDE):
        moves[key] = Wide(r.dy_rows if key == 'dy' else getattr(r, 'out_' + key), getattr(r, 'got_' + key), r.sem_wide.at[0, i], r.sem_wide.at[1, i])
    for i, key in enumerate(NARROW):
        moves[key] = Narrow(getattr(r, 'out_' + key), getattr(r, 'got_' + key), r.sem_narrow.at[0, i], r.sem_narrow.at[1, i])
    kv = [Trade(r.kv0, r.sem_kv.at[0, 0], r.sem_kv.at[1, 0]), Trade(r.kv1, r.sem_kv.at[0, 1], r.sem_kv.at[1, 1])]
    qdo = [Trade(r.qdo0, r.sem_qdo.at[0, 0], r.sem_qdo.at[1, 0]), Trade(r.qdo1, r.sem_qdo.at[0, 1], r.sem_qdo.at[1, 1])]
    q_own = (r.q0, r.q1)
    stats = (r.stats0, r.stats1)

    def send_stats(l, b, i):
        ref = stats[l].at[b, me]
        return remote(ref, ref, r.sem_stats.at[0, l, i, b], r.sem_stats.at[1, l, i, b], 'cp', others[i])

    def of(key, l):
        return getattr(r, '%s%d' % (key, l))

    def out(key, l):
        return getattr(r, 'out_%s%d' % (key, l))

    def project(l, b, flat):
        h = norm_rows(flat, r.g_attn[l])
        hold['h'].put(out('h', l), b, h)
        qkv = dot_nn(h, r.wqkv[:]).astype(BF16)
        q_own[l][b] = qkv[:, :width]
        kv[l].store[b, me] = qkv[:, width:]
        kv[l].give(b)

    def stage_first(b):
        project(0, b, ring.rows(b))

    def stage_attend(l):
        def go(b):
            kv[l].take(b)
            pairs = kv[l].store[b].reshape(-1, 2 * width)
            o = attend(heads, q_own[l][b], pairs, r.bias_rows[:], mask_row(r.mask_all, b))
            hold['o'].put(out('o', l), b, o)
            ring.send_partial(b, dot_nn(o, r.wo[:]))
        return go

    def add_stage(res, dst):
        def go(b):
            total = ring.reduced(b)
            value = (res[b].astype(F32) + total).astype(BF16)
            dst[b] = value
            ring.publish(b, value)
        return go

    def pull_stage(x_shard, gain, res, dst, d_gain):
        def go(b):
            value = rms_pull(ring.reduced(b), x_shard[b], gain[:], res[b], d_gain)
            if dst is not None:
                dst[b] = value
            ring.publish(b, value)
        return go

    def mlp_forward(l, b):
        ring.arrive(b)
        h2 = norm_rows(ring.rows(b), r.g_mlp[l])
        hold['h'].put(out('m', l), b, h2)
        both = dot_nn(h2, r.wgl[:])
        gate, lin = both[:, :ff], both[:, ff:]
        u = (gelu_parts(gate)[0] * lin).astype(BF16)
        hold['u'].put(out('u', l), b, u)
        return gate, lin, u

    def stage_mlp0(b):
        gate, lin, u = mlp_forward(0, b)
        r.gate[b] = gate
        r.lin[b] = lin
        ring.send_partial(b, dot_nn(u, r.wout[:]))

    def stage_next(b):
        ring.arrive(b)
        project(1, b, ring.rows(b))

    def dy_in(b):
        slot = lax.rem(b, 2)
        return pltpu.make_async_copy(r.dy_rows.at[b], r.dybuf.at[slot], r.sem_dy.at[slot])

    def mlp_backward(l, b, d, gate, lin):
        dgl = mlp_pull(dot_nt(d, r.wout[:]), gate, lin)
        hold['gl'].put(out('gl', l), b, dgl)
        ring.send_partial(b, dot_nt(dgl, r.wgl[:]))

    def stage_mlp1(b):
        gate, lin, _ = mlp_forward(1, b)
        dy_in(b).wait()
        mlp_backward(1, b, r.dybuf[lax.rem(b, 2)], gate, lin)

    def keep(dst, b):
        copy = pltpu.make_async_copy(ring.full.at[b], dst.at[b], r.sem_keep.at[b])
        copy.start()
        return copy

    def stage_rows_back(l, dst):
        def go(b):
            ring.arrive(b)
            copy = keep(dst, b)
            d_o = dot_nt(ring.rows(b), r.wo[:]).astype(BF16)
            both = jnp.concatenate([q_own[l][b], d_o], axis=1)
            qdo[l].store[b, me] = both
            qdo[l].give(b)
            pairs = kv[l].store[b].reshape(-1, 2 * width)
            d_q, table = attend_rows_back(heads, both, pairs, r.bias_rows[:], mask_row(r.mask_all, b), r.ds_sum)
            stats[l][b, me] = table
            r.dq[b] = d_q
            for i in range(3):
                send_stats(l, b, i).start()
            copy.wait()
        return go

    def stage_cols_back(l):
        def go(b):
            qdo[l].take(b)
            for i in range(3):
                send_stats(l, b, i).wait_recv()
            d_kv = attend_cols_back(heads, kv[l].store[b, me], r.mask_cols[b], r.bias_cols, lambda s: qdo[l].store[b, s], lambda s: stats[l][b, s])
            d_qkv = jnp.concatenate([r.dq[b], d_kv], axis=1)
            hold['qkv'].put(out('qkv', l), b, d_qkv)
            ring.send_partial(b, dot_nt(d_qkv, r.wqkv[:]))
        return go

    def stage_mlp_back0(b):
        ring.arrive(b)
        copy = keep(r.out_d0, b)
        mlp_backward(0, b, ring.rows(b), r.gate[b], r.lin[b])
        copy.wait()

    def stage_last(b):
        ring.arrive(b)
        keep(r.out_dx, b).wait()

    def kept(key, dst):
        return lambda b: hold[key].copy(dst, b).wait()

    def then(*parts):
        def go(b):
            for part in parts:
                part(b)
        return go

    def give(key):
        return lambda b: moves[key].give(b)

    stages = [
        stage_first,
        then(kv[0].pass_on, kept('h', r.out_h0)),
        stage_attend(0),
        then(ring.reduce_pair, kept('o', r.out_o0)),
        then(add_stage(r.xs0, r.x1s0), give('h0')),
        ring.forward,
        stage_mlp0,
        then(ring.reduce_pair, kept('h', r.out_m0), kept('u', r.out_u0), give('u0')),
        then(add_stage(r.x1s0, r.xs1), give('m0')),
        ring.forward,
        stage_next,
        then(kv[1].pass_on, kept('h', r.out_h1)),
        stage_attend(1),
        then(ring.reduce_pair, kept('o', r.out_o1)),
        then(add_stage(r.xs1, r.x1s1), give('h1')),
        then(lambda b: dy_in(b).start(), ring.forward),
        stage_mlp1,
        then(ring.reduce_pair, kept('h', r.out_m1), kept('u', r.out_u1), kept('gl', r.out_gl1), give('u1')),
        then(pull_stage(r.x1s1, r.g_mlp.at[1], r.ds1, r.dms1, r.dgm1), give('m1')),
        ring.forward,
        stage_rows_back(1, r.out_dm1),
        qdo[1].pass_on,
        stage_cols_back(1),
        then(ring.reduce_pair, kept('qkv', r.out_qkv1), give('gl1')),
        then(pull_stage(r.xs1, r.g_attn.at[1], r.dms1, r.ds0, r.dga1), give('dy')),
        then(ring.forward, give('qkv1')),
        stage_mlp_back0,
        then(ring.reduce_pair, kept('gl', r.out_gl0), give('d0')),
        pull_stage(r.x1s0, r.g_mlp.at[0], r.ds0, r.dms0, r.dgm0),
        ring.forward,
        stage_rows_back(0, r.out_dm0),
        qdo[0].pass_on,
        stage_cols_back(0),
        then(ring.reduce_pair, kept('qkv', r.out_qkv0), give('qkv0')),
        then(pull_stage(r.xs0, r.g_attn.at[0], r.dms0, None, r.dga0), give('gl0')),
        ring.forward,
        stage_last,
    ]

    def tables():
        bias_tables(r.rel_bias, me, r.bias_rows, r.bias_cols)
        for copy in masks:
            copy.wait()

    use = lambda k: k
    after = lambda k: k + batch
    hooks = [
        (use(2), tables), (use(2), loaded('o', 0)), (use(6), loaded('gl', 0)), (use(6), loaded('out', 0)),
        (after(0), load('qkv', 1)), (use(10), loaded('qkv', 1)),
        (after(2), load('o', 1)), (use(12), loaded('o', 1)),
        (after(6), load('gl', 1)), (after(6), load('out', 1)), (use(16), loaded('gl', 1)), (use(16), loaded('out', 1)),
        (after(16), load('gl', 0)), (after(16), load('out', 0)), (use(26), loaded('gl', 0)), (use(26), loaded('out', 0)),
        (after(20), load('o', 0)), (use(30), loaded('o', 0)),
        (after(22), load('qkv', 0)), (use(32), loaded('qkv', 0)),
        (after(20), moves['u0'].pass_on), (after(26), moves['u1'].pass_on), (after(30), moves['gl1'].pass_on), (after(32), moves['qkv1'].pass_on),
        (after(31), lambda: bucket_sums(r.ds_sum, me, r.bias_sum)),
    ]

    def slot_step(slot, carry):
        for at, work in hooks:
            pl.when(slot == at)(work)
        for k, stage in enumerate(stages):
            @pl.when(jnp.logical_and(slot >= k, slot < batch + k))
            def _():
                stage(slot - k)
        return carry

    lax.fori_loop(0, batch + len(stages) - 1, slot_step, 0)
    for key in ('gl0', 'qkv0'):
        moves[key].pass_on()

    def finish(b, carry):
        for l in range(2):
            kv[l].finish(b)
            qdo[l].finish(b)
            for i in range(3):
                send_stats(l, b, i).wait_send()
        return carry

    lax.fori_loop(0, batch, finish, 0)
    for key in WIDE + NARROW:
        moves[key].finish()


def mega(x, dy, key_add, rel_bias, g_attn, g_mlp, w_q, w_k, w_v, w_o, w_gate, w_lin, w_out, cid):
    batch, rows, d_model = x.shape
    heads = rel_bias.shape[1]
    width, ff = heads * HEAD_DIM, w_gate.shape[2]
    n_cp, n_tp = 4, 8
    seg = rows // n_tp
    dma = pltpu.SemaphoreType.DMA
    any_spec = pl.BlockSpec(memory_space=pl.ANY)
    by_seg = lambda a: a.reshape(batch, n_tp, seg, d_model)
    ins = dict(x=(by_seg(x), any_spec), dy=(by_seg(dy), any_spec), dy_rows=(dy, any_spec), key_add=(key_add[:, None, :], VMEM_SPEC), mask_cols=(key_add[:, :, None], VMEM_SPEC), rel_bias=(rel_bias, SMEM_SPEC),
               g_attn=(g_attn[:, None, :], VMEM_SPEC), g_mlp=(g_mlp[:, None, :], VMEM_SPEC), w_q=(w_q, any_spec), w_k=(w_k, any_spec), w_v=(w_v, any_spec), w_o=(w_o, any_spec),
               w_gate=(w_gate, any_spec), w_lin=(w_lin, any_spec), w_out=(w_out, any_spec))
    size = dict(h=d_model, m=d_model, u=ff, gl=2 * ff, qkv=3 * width, o=width)
    outs = {}
    for key, n in size.items():
        for l in range(2):
            outs['out_%s%d' % (key, l)] = ((batch, rows, n), BF16)
    for key in ('d0', 'dm0', 'dm1', 'dx'):
        outs['out_' + key] = ((batch, n_tp, seg, d_model), BF16)
    for key in WIDE:
        shape = outs['out_' + key][0] if key != 'dy' else x.shape
        outs['got_' + key] = ((3,) + shape[:-1] + (d_model // 2,), BF16)
    for key in NARROW:
        outs['got_' + key] = ((3,) + outs['out_' + key][0], BF16)
    n_any = len(outs)
    for key in ('dga0', 'dga1', 'dgm0', 'dgm1'):
        outs[key] = ((1, d_model), F32)
    outs['bias_sum'] = ((rel_bias.shape[0], heads, n_cp * rows), F32)
    shard = pltpu.VMEM((batch, seg, d_model), BF16)
    blocks = pltpu.VMEM((batch, n_cp, rows, 2 * width), BF16)
    table = pltpu.VMEM((batch, n_cp, 2 * heads, rows), F32)
    chunk_f32 = pltpu.VMEM((batch, rows, ff), F32)
    q_rows = pltpu.VMEM((batch, rows, width), BF16)
    two = lambda n: pltpu.VMEM((2, rows, n), BF16)
    scratch = dict(wqkv=pltpu.VMEM((d_model, 3 * width), BF16), wo=pltpu.VMEM((width, d_model), BF16), wgl=pltpu.VMEM((d_model, 2 * ff), BF16), wout=pltpu.VMEM((ff, d_model), BF16),
                   sem_qkv=dma((3,)), sem_o=dma((1,)), sem_gl=dma((2,)), sem_out=dma((1,)), sem_in=dma((batch + 2,)), sem_mask=dma((2, 3)), mask_all=pltpu.VMEM((n_cp, batch, 1, rows), F32),
                   bias_rows=pltpu.VMEM((heads * rows, n_cp * rows), F32), bias_cols=pltpu.VMEM((n_cp, rows, heads * rows), F32), ds_sum=pltpu.VMEM((heads * rows, n_cp * rows), F32),
                   xs0=shard, x1s0=shard, xs1=shard, x1s1=shard, ds1=shard, dms1=shard, ds0=shard, dms0=shard, kv0=blocks, kv1=blocks, qdo0=blocks, qdo1=blocks, stats0=table, stats1=table,
                   q0=q_rows, q1=q_rows, dq=q_rows, gate=chunk_f32, lin=chunk_f32, hbuf=two(d_model), ubuf=two(ff), gbuf=two(2 * ff), qbuf=two(3 * width), obuf=two(width), dybuf=two(d_model),
                   sem_h=dma((2,)), sem_u=dma((2,)), sem_g=dma((2,)), sem_q=dma((2,)), sem_ob=dma((2,)), sem_dy=dma((2,)), sem_keep=dma((batch,)),
                   sem_wide=dma((2, len(WIDE), 3)), sem_narrow=dma((2, len(NARROW), 3)), sem_kv=dma((2, 2, 3, batch)), sem_qdo=dma((2, 2, 3, batch)), sem_stats=dma((2, 2, 3, batch)))
    for i, piece in enumerate(Ring.scratch(batch, seg, d_model)):
        scratch['ring_%d' % i] = piece
    result = pl.pallas_call(
        functools.partial(mega_kernel, list(ins) + list(outs) + list(scratch), heads),
        out_shape=tuple(jax.ShapeDtypeStruct(*v) for v in outs.values()),
        in_specs=[v[1] for v in ins.values()],
        out_specs=tuple([any_spec] * n_any + [VMEM_SPEC] * (len(outs) - n_any)),
        scratch_shapes=list(scratch.values()),
        compiler_params=comm_params(cid, 62),
        cost_estimate=cost(300),
        name='mega',
    )(*[v[0] for v in ins.values()])
    return dict(zip(outs, result))


def swap_kernel(n, *refs):
    halves, wo_part, small, mates, wo_own, wo_mate, total = refs[:n], refs[n], refs[n + 1], refs[n + 2:2 * n + 2], refs[2 * n + 2], refs[2 * n + 3], refs[2 * n + 4]
    wo_in, wo_sum, wo_x, stage, by_z, send, recv, s_send, s_recv, w_send, w_recv = refs[2 * n + 5:]
    _, z, y, pair, z_peer = tp_places()
    me, mate, across, _ = cp_places()
    core, chip = lax.rem(me, 2), me // 2
    half = wo_in.shape[-1]
    meet([pair] + z_peer[1:], [mate, across])

    def columns(which):
        return pl.ds(pl.multiple_of(which * half, half), half)

    first = remote(wo_part.at[:, :, columns(1 - core)], wo_in, w_send.at[0], w_recv.at[0], 'cp', mate)
    first.start()
    swaps = [remote(halves[i], mates[i], send.at[i], recv.at[i], 'cp', mate) for i in range(n)]
    for copy in swaps:
        copy.start()
    first.wait()
    wo_sum[:] = wo_part[:, :, columns(core)] + wo_in[:]
    second = remote(wo_sum.at[1 - chip], wo_x, w_send.at[1], w_recv.at[1], 'cp', across)
    second.start()
    mine = small
    for k, (axis, peer) in enumerate((('cp', mate), ('cp', across), ('tp', pair))):
        copy = remote(mine, stage.at[2 * k], s_send.at[k], s_recv.at[k], axis, peer)
        copy.start()
        copy.wait()
        if k < 2:
            stage[2 * k + 1] = mine[:] + stage[2 * k]
            mine = stage.at[2 * k + 1]
        else:
            by_z[z] = mine[:] + stage[2 * k]
    copies = [remote(by_z.at[z], by_z.at[z], s_send.at[2 + j], s_recv.at[2 + j], 'tp', z_peer[j]) for j in (1, 2, 3)]
    for copy in copies:
        copy.start()
    second.wait()
    wo_own[chip] = (wo_sum[chip] + wo_x[:]).astype(BF16)
    third = remote(wo_own.at[chip], wo_own.at[chip], w_send.at[2], w_recv.at[2], 'cp', across)
    third.start()
    for copy in copies:
        copy.wait()
    total[:] = by_z[0] + by_z[1] + by_z[2] + by_z[3]
    third.wait()
    last = remote(wo_own, wo_mate, w_send.at[3], w_recv.at[3], 'cp', mate)
    last.start()
    for copy in swaps + [last]:
        copy.wait()


def swap(halves, wo_part, small, cid):
    n = len(halves)
    layers, width, d_model = wo_part.shape
    half = d_model // 2
    any_spec = pl.BlockSpec(memory_space=pl.ANY)
    dma = pltpu.SemaphoreType.DMA
    wo_shape = jax.ShapeDtypeStruct((layers, width, half), BF16)
    result = pl.pallas_call(
        functools.partial(swap_kernel, n),
        out_shape=tuple(jax.ShapeDtypeStruct(h.shape, h.dtype) for h in halves) + (wo_shape, wo_shape, jax.ShapeDtypeStruct(small.shape, F32)),
        in_specs=[any_spec] * n + [VMEM_SPEC] * 2,
        out_specs=tuple([any_spec] * n + [VMEM_SPEC] * 3),
        scratch_shapes=[pltpu.VMEM((layers, width, half), F32), pltpu.VMEM((layers, width, half), F32), pltpu.VMEM((width, half), F32),
                        pltpu.VMEM((5,) + small.shape, F32), pltpu.VMEM((4,) + small.shape, F32), dma((n,)), dma((n,)), dma((6,)), dma((6,)), dma((4,)), dma((4,))],
        compiler_params=comm_params(cid, 24),
        name='swap',
    )(*halves, wo_part, small)
    return list(result[:n]), result[n], result[n + 1], result[n + 2]


def place_kernel(plan, n_out, *refs):
    n = len(plan)
    owns, mates, outs = refs[:n], refs[n:2 * n], refs[2 * n:2 * n + n_out]
    bufs, in_sem, out_sem = refs[2 * n + n_out:4 * n + n_out], refs[4 * n + n_out], refs[4 * n + n_out + 1]
    core = lax.rem(lax.axis_index('cp'), 2)
    loads = [pltpu.make_async_copy(src, buf, in_sem.at[i]) for i, (src, buf) in enumerate(zip(owns + mates, bufs))]
    for load in loads:
        load.start()
    stores = []
    for i, load in enumerate(loads):
        layer, by_rows, first_out, n_pieces = plan[i % n]
        which = core if i < n else 1 - core
        buf = bufs[i]
        load.wait()
        width = buf.shape[1] // n_pieces
        for p in range(n_pieces):
            src = buf if n_pieces == 1 else buf.at[:, pl.ds(p * width, width)]
            size = buf.shape[0] if by_rows else width
            window = pl.ds(pl.multiple_of(which * size, size), size)
            out = outs[first_out + p].at[layer]
            dst = out.at[window, :] if by_rows else out.at[:, window]
            stores.append(pltpu.make_async_copy(src, dst, out_sem.at[len(stores)]))
            stores[-1].start()
    for store in stores:
        store.wait()


def place(plan, owns, mates, out_shapes):
    n = len(plan)
    any_spec = pl.BlockSpec(memory_space=pl.ANY)
    n_stores = 2 * sum(p[3] for p in plan)
    return pl.pallas_call(
        functools.partial(place_kernel, plan, len(out_shapes)),
        out_shape=tuple(jax.ShapeDtypeStruct(s, BF16) for s in out_shapes),
        in_specs=[any_spec] * (2 * n),
        out_specs=tuple([any_spec] * len(out_shapes)),
        scratch_shapes=[pltpu.VMEM(a.shape, BF16) for a in list(owns) + list(mates)] + [pltpu.SemaphoreType.DMA((2 * n,)), pltpu.SemaphoreType.DMA((n_stores,))],
        compiler_params=pltpu.CompilerParams(vmem_limit_bytes=40 * MIB),
        name='place',
    )(*owns, *mates)


def solution(mesh):
    seq_spec = P(None, 'cp', None)
    col_spec = P(None, None, 'tp')
    row_spec = P(None, 'tp', None)
    weight_specs = (P(), P(), col_spec, col_spec, col_spec, row_spec, col_spec, col_spec, row_spec)

    def local_program(x_in, d_y, key_mask, rel_bias, g_attn, g_mlp, w_q, w_k, w_v, w_o, w_gate, w_lin, w_out):
        batch, rows, d_model = x_in.shape
        tokens = batch * rows
        n_layers = w_q.shape[0]
        n_buckets, heads = rel_bias.shape
        tp_index = lax.axis_index('tp')
        core = lax.rem(lax.axis_index('cp'), 2)
        half = d_model // 2

        key_add = jnp.where(key_mask > 0, 0.0, MASK_NEG).astype(F32)
        m = mega(x_in, d_y, key_add, rel_bias, g_attn, g_mlp, w_q, w_k, w_v, w_o, w_gate, w_lin, w_out, 0)

        def flat(array):
            return array.reshape(-1, array.shape[-1])

        def own_half(array):
            return lax.dynamic_slice_in_dim(array.reshape(tokens, d_model), core * half, half, axis=1)

        def grad(left, right, left_wide):
            a, b = [d_y if key == 'dy' else m['out_' + key] for key in (left, right)]
            a_g, b_g = flat(m['got_' + left]), flat(m['got_' + right])
            a, b = (own_half(a), flat(b)) if left_wide else (flat(a), own_half(b))
            return (dot_tn(a, b) + dot_tn(a_g, b_g)).astype(BF16)

        owns = [grad('h0', 'qkv0', True), grad('h1', 'qkv1', True), grad('m0', 'gl0', True), grad('m1', 'gl1', True), grad('u0', 'd0', False), grad('u1', 'dy', False)]
        wo_part = jnp.stack([dot_tn(flat(m['out_o%d' % l]), m['out_dm%d' % l].reshape(tokens, d_model)) for l in range(n_layers)])
        slots = jnp.zeros((8, n_buckets * heads), F32)
        slots = lax.dynamic_update_slice(slots, jnp.sum(m['bias_sum'], axis=-1).reshape(1, -1), (tp_index, jnp.int32(0)))
        small = jnp.concatenate([part.reshape(-1, 128) for part in (m['dga0'], m['dga1'], m['dgm0'], m['dgm1'], slots)], axis=0)
        mates, wo_own, wo_mate, small = swap(owns, wo_part, small, 1)
        n_gain = n_layers * d_model // 128
        d_g_attn = small[:n_gain].reshape(n_layers, d_model)
        d_g_mlp = small[n_gain:2 * n_gain].reshape(n_layers, d_model)
        d_rel = lax.dynamic_slice(small[2 * n_gain:], (tp_index, jnp.int32(0)), (1, n_buckets * heads)).reshape(n_buckets, heads)
        plan = tuple((layer, by_rows, first, n) for by_rows, first, n in ((True, 0, 3), (True, 4, 2), (False, 6, 1), (False, 3, 1)) for layer in range(n_layers))
        wo_halves = [[w[l] for l in range(n_layers)] for w in (wo_own, wo_mate)]
        grads = place(plan, owns + wo_halves[0], mates + wo_halves[1], [w.shape for w in (w_q, w_k, w_v, w_o, w_gate, w_lin, w_out)])
        return (m['out_dx'].reshape(batch, rows, d_model), d_rel, d_g_attn, d_g_mlp) + tuple(grads)

    return jax.shard_map(local_program, mesh=mesh, in_specs=(seq_spec, seq_spec, P(None, 'cp'), P(None, 'tp')) + weight_specs, out_specs=(seq_spec, P(None, 'tp')) + weight_specs, check_vma=False)
```

time: 3880 us -> 743 us (0.19)
  waiting for transfers between devices: 1030 us -> 0 us
  other arithmetic: 959 us -> 2.81 us
  local copies, waits for them, and re-layouts: 871 us -> 24.6 us
  blocking collectives: 820 us -> 0 us
  Pallas kernels: 0 us -> 672 us
  matrix products: 154 us -> 30.1 us
    psum x7 -> x0, waiting for transfers between devices: 1020 us -> none  [the longest x2 309 us: layer_forward(): lax.psum(jnp.dot(attn_flat, w_o, preferred_element_type=jnp.float32), 'tp')]
    scatter-add x8 -> x0, other arithmetic: 880 us -> none  [pair_grads(): jax.ops.segment_sum(score_row, seg_ids, num_segments=n_buckets)]
    psum x1 -> x0, blocking collectives: 813 us -> none  [local_program(): lax.psum(bias_grad, 'cp')]
    gather x26 -> x0, local copies, waits for them, and re-layouts: 789 us -> none  [pair_bias(): return (buckets, jnp.take(bias_table, buckets, axis=1))]
    pallas_call x0 -> x3, Pallas kernels: none -> 672 us  [the longest x1 610 us: mega(): pl.pallas_call(functools.partial(mega_kernel, list(ins) + list(outs) + li...]
    dot_general x95 -> x14, matrix products: 154 us -> 30.1 us  [dot_tn(): lax.dot_general(a, b, (((0,), (0,)), ((), ())), preferred_element_type=F32)]
  transfers between devices with their start and end apart: 47 -> 0, of which waited for: 11 -> 0; matrix products, arithmetic and copies ran while one was open for 40% -> 0% of each run, Pallas kernels for 0% -> 0%
where the time goes in v4:
time: 743 us; the launch traced here: 731 us
  Pallas kernels  672 us (90%)
  matrix products  30.1 us (4%)
  local copies, waits for them, and re-layouts  24.6 us (3%)
    pallas_call x1, Pallas kernels, mega(): pl.pallas_call(functools.partial(mega_kernel, list(ins) + list(outs) + li...  610 us
    pallas_call x1, Pallas kernels, swap(): pl.pallas_call(functools.partial(swap_kernel, n), out_shape=tuple((jax.Sh...  50.3 us
    dot_general x14, matrix products, dot_tn(): lax.dot_general(a, b, (((0,), (0,)), ((), ())), preferred_element_type=F32)  30.1 us
    unnamed x73, local copies, waits for them, and re-layouts  19.3 us

profile of v4, /device:TPU:0, one launch (start us, length us, event | category | flops | bytes accessed | tf_op | source)
XLA Modules:
  0.0 730.8 jit_solution(4614279081372168610)
XLA Ops:
  0.7 1.3 fusion.21
  1.9 1.4 copy.33.refs_5_
  3.3 1.3 broadcast_in_dim.27.refs_6_
  4.6 1.3 broadcast_in_dim.28.refs_7_
  5.9 0.9 copy.32.refs_4_
  6.8 609.6 %mega.1 = (bf16[4,128,2048]{2,1,0:T(8,128)(2,1)}, bf16[4,128,2048]{2,1,0:T(8,128)(2,1)}, bf16[4,128,2048]{2,1,0:T(8,128)(2,1)}, bf16[4,128,2048]{2,1,0:T(8,128)(...) custom-call(bf16[4,8,16,2048]{3,2,1,0:T(8,128)(2,1)} %bitcast.111, ...), custom_call_target="tpu_custom_call" | custom-call | flops 314572800000 | bytes 8388608 | tf_op jit(solution)/shard_map/mega/pallas_call | solution.py:728
  616.4 1.1 reduce_sum.9
  617.4 0.1 reshape.144
  617.6 0.7 constant_dynamic-update-slice_fusion.4
  618.3 0.7 constant_dynamic-update-slice_fusion.3
  619.0 0.7 constant_dynamic-update-slice_fusion.2
  619.7 0.7 constant_dynamic-update-slice_fusion.1
  620.4 2.6 fusion.12
  623.0 0.0 copy-done.30
  623.0 0.5 copy-done.32
  623.6 2.8 fusion.3.refs_0_
  626.4 0.0 copy-done.9
  626.4 0.0 copy-done.20
  626.4 0.0 copy-start.8
  626.5 0.0 copy-start.19
  626.5 0.7 convolution_bitcast_fusion.1
  627.2 0.8 copy-done.8
  628.0 0.0 copy-done.19
  628.0 0.7 convolution_bitcast_fusion
  628.8 0.5 pad_maximum_fusion.refs_6_
  629.3 1.4 copy-done.21
  630.7 0.6 copy-done.23
  631.3 2.3 fusion.25
  633.6 0.0 copy-start.15
  633.6 0.9 add_convert_fusion.refs_4_
  634.5 0.2 copy-done.13
  634.6 0.7 copy-done.15
  635.4 0.9 fusion.5
  636.3 1.1 copy-done.6
  637.4 2.3 fusion.4.refs_5_
  639.8 1.0 fusion.10
  640.8 0.8 copy-done.29
  641.7 0.7 copy-done.31
  642.4 3.1 fusion.2.refs_1_
  645.5 4.5 fusion.23
  650.0 0.0 copy-done.12
  650.0 0.0 copy-done.17
  650.0 0.0 copy-start.25
  650.0 0.0 copy-start.27
  650.0 1.7 fusion.1.refs_2_
  651.8 0.4 copy-done.25
  652.1 1.0 copy-done.27
  653.1 4.5 fusion.24
  657.6 0.0 copy-done.11
  657.6 0.0 copy-done.16
  657.6 2.0 fusion.refs_3_
  659.6 50.3 %swap.1 = (bf16[1024,768]{1,0:T(8,128)(2,1)S(1)}, bf16[1024,768]{1,0:T(8,128)(2,1)S(1)}, bf16[1024,1280]{1,0:T(8,128)(2,1)S(1)}, bf16[1024,1280]{1,0:T(8,128)(2,...) custom-call(bf16[1024,768]{1,0:T(8,128)(2,1)S(1)} %fusion.3.refs_0_,, ...), custom_call_target="tpu_custom_call" | custom-call | tf_op jit(solution)/shard_map/swap/pallas_call | solution.py:796
  710.0 1.5 copy-done.3
  711.6 1.1 copy-done.4
  712.7 0.2 slice_bitcast_fusion
  712.9 1.2 copy-done.2
  714.2 0.9 copy-done.5
  715.1 12.0 %place.1 = (bf16[2,2048,256]{2,1,0:T(8,128)(2,1)}, bf16[2,2048,256]{2,1,0:T(8,128)(2,1)}, bf16[2,2048,256]{2,1,0:T(8,128)(2,1)}, bf16[2,256,2048]{2,1,0:T(8,128)...) custom-call(bf16[1024,768]{1,0:T(8,128)(2,1)S(1)} %fusion.3.refs_0_, ...), custom_call_target="tpu_custom_call" | custom-call | tf_op jit(solution)/shard_map/place/pallas_call | solution.py:840
  727.1 0.6 reshape.147
  727.7 0.1 reshape.145
  727.8 0.7 copy.39
  728.5 0.6 reshape.146
  729.1 0.0 copy-done.7
  729.1 1.3 copy.56
  (43 shorter events, 0.1 us)
Async XLA Ops:
  620.4 2.6 copy-start.30
  620.4 3.2 copy-start.32
  623.6 2.9 copy-start.9
  623.6 2.9 copy-start.20
  626.4 1.6 copy-start.8
  626.5 1.6 copy-start.19
  628.8 1.9 copy-start.21
  628.8 2.5 copy-start.23
  631.3 2.3 copy-start.14
  631.3 2.3 copy-start.18
  633.6 1.1 copy-start.13
  633.6 1.8 copy-start.15
  633.6 2.7 copy-start.10
  635.4 2.0 copy-start.6
  637.4 2.3 copy-start.22
  637.4 2.3 copy-start.24
  639.8 1.9 copy-start.29
  639.8 2.6 copy-start.31
  642.4 3.1 copy-start.26
  642.4 3.1 copy-start.28
  645.5 4.5 copy-start.12
  645.5 4.5 copy-start.17
  650.0 2.1 copy-start.25
  650.0 3.1 copy-start.27
  653.1 6.5 copy-start
  653.1 4.5 copy-start.11
  653.1 4.5 copy-start.16
  659.6 50.4 %copy-start.1 = (bf16[1024,1280]{1,0:T(8,128)(2,1)}, bf16[1024,1280]{1,0:T(8,128)(2,1)S(1)}, u32[]{:S(2)}) copy-start(bf16[1024,1280]{1,0:T(8,128)(2,1)S(1)} %fusion.refs_3_) | copy-start | bytes 7864324
  710.0 1.6 copy-start.3
  711.6 1.1 copy-start.4
  712.7 1.5 copy-start.2
  712.7 2.4 copy-start.5
  715.1 14.0 %copy-start.7 = (bf16[4,8,16,2048]{3,2,1,0:T(8,128)(2,1)S(1)}, bf16[4,8,16,2048]{3,2,1,0:T(8,128)(2,1)}, u32[]{:S(2)}) copy-start(bf16[4,8,16,2048]{3,2,1,0:T(8,128)(2,1)} %get-tuple-element.60) | copy-start | bytes 6291460

commit v5 on v4

--- a/solution.py
+++ b/solution.py
@@ -1,4 +1,6 @@
 import functools
+import itertools
+import string
 
 import jax
 import jax.numpy as jnp
@@ -83,8 +85,11 @@
     return x * cdf, cdf + 0.5 * x * (1.0 - t * t) * GELU_C * (1.0 + 3.0 * GELU_A * x * x)
 
 
-def remote(src, dst, send, recv, axis, peer):
-    return pltpu.make_async_remote_copy(src_ref=src, dst_ref=dst, send_sem=send, recv_sem=recv, device_id={axis: peer}, device_id_type=MESH)
+Z_STEPS = (2, 1, 3)
+
+
+def remote(src, dst, sem, at, axis, peer):
+    return pltpu.make_async_remote_copy(src_ref=src, dst_ref=dst, send_sem=sem.at[(0,) + at], recv_sem=sem.at[(1,) + at], device_id={axis: peer}, device_id_type=MESH)
 
 
 def tp_places():
@@ -104,7 +109,8 @@
 
 class Ring:
     def __init__(self, part, from_y, from_z, full, *sems):
-        self.part, self.from_y, self.from_z, self.full, self.sems = part, from_y, from_z, full, sems
+        self.part, self.from_y, self.from_z, self.full = part, from_y, from_z, full
+        self.sem_ys, self.sem_zs, self.sem_zg, self.sem_yg = sems
         _, self.z, self.y, self.pair, self.z_peer = tp_places()
         self.seg = self.y * 4 + self.z
 
@@ -120,22 +126,18 @@
         ]
 
     def y_sum(self, b):
-        s = self.sems[0]
-        return remote(self.part.at[b, 1 - self.y], self.from_y.at[b], s.at[0, b], s.at[1, b], 'tp', self.pair)
+        return remote(self.part.at[b, 1 - self.y], self.from_y.at[b], self.sem_ys, (b,), 'tp', self.pair)
 
     def z_sum(self, b, j):
-        s = self.sems[1]
-        return remote(self.part.at[b, self.y, lax.rem(self.z + j, 4)], self.from_z.at[b, j - 1], s.at[0, b, j - 1], s.at[1, b, j - 1], 'tp', self.z_peer[j])
+        return remote(self.part.at[b, self.y, lax.rem(self.z + j, 4)], self.from_z.at[b, j - 1], self.sem_zs, (b, j - 1), 'tp', self.z_peer[j])
 
     def z_gather(self, b, j):
-        s = self.sems[2]
         ref = self.full.at[b, self.seg]
-        return remote(ref, ref, s.at[0, b, j - 1], s.at[1, b, j - 1], 'tp', self.z_peer[j])
+        return remote(ref, ref, self.sem_zg, (b, j - 1), 'tp', self.z_peer[j])
 
     def y_gather(self, b, j):
-        s = self.sems[3]
         ref = self.full.at[b, self.y * 4 + lax.rem(self.z - j + 4, 4)]
-        return remote(ref, ref, s.at[0, b, j], s.at[1, b, j], 'tp', self.pair)
+        return remote(ref, ref, self.sem_yg, (b, j), 'tp', self.pair)
 
     def send_partial(self, b, partial):
         self.part[b] = partial.reshape(self.part.shape[1:])
@@ -144,22 +146,22 @@
     def reduce_pair(self, b):
         self.y_sum(b).wait_recv()
         self.part[b, self.y] = self.part[b, self.y] + self.from_y[b]
-        for j in (2, 1, 3):
+        for j in Z_STEPS:
             self.z_sum(b, j).start()
 
     def reduced(self, b):
-        for j in (1, 2, 3):
+        for j in Z_STEPS:
             self.z_sum(b, j).wait_recv()
         return self.part[b, self.y, self.z] + self.from_z[b, 0] + self.from_z[b, 1] + self.from_z[b, 2]
 
     def publish(self, b, out):
         self.full[b, self.seg] = out
-        for j in (2, 1, 3):
+        for j in Z_STEPS:
             self.z_gather(b, j).start()
         self.y_gather(b, 0).start()
 
     def forward(self, b):
-        for j in (1, 2, 3):
+        for j in Z_STEPS:
             self.z_gather(b, j).wait_recv()
             self.y_gather(b, j).start()
 
@@ -169,7 +171,7 @@
         self.y_sum(b).wait_send()
         for j in range(4):
             self.y_gather(b, j).wait_send()
-        for j in (1, 2, 3):
+        for j in Z_STEPS:
             self.z_sum(b, j).wait_send()
             self.z_gather(b, j).wait_send()
 
@@ -177,14 +179,50 @@
         return self.full[b].reshape(-1, self.full.shape[-1])
 
 
+class Columns:
+    def __init__(self, store, z_sem, y_sem):
+        self.store, self.z_sem, self.y_sem = store, z_sem, y_sem
+        self.me, self.z, self.y, self.pair, self.z_peer = tp_places()
+
+    def z_gather(self, b, j):
+        ref = self.store.at[b, self.me]
+        return remote(ref, ref, self.z_sem, (b, j - 1), 'tp', self.z_peer[j])
+
+    def y_gather(self, b, j):
+        ref = self.store.at[b, 2 * lax.rem(self.z - j + 4, 4) + self.y]
+        return remote(ref, ref, self.y_sem, (b, j), 'tp', self.pair)
+
+    def publish(self, b, out):
+        self.store[b, self.me] = out
+        for j in Z_STEPS:
+            self.z_gather(b, j).start()
+        self.y_gather(b, 0).start()
+
+    def forward(self, b):
+        for j in Z_STEPS:
+            self.z_gather(b, j).wait_recv()
+            self.y_gather(b, j).start()
+
+    def arrive(self, b):
+        for j in range(4):
+            self.y_gather(b, j).wait_recv()
+        for j in range(4):
+            self.y_gather(b, j).wait_send()
+        for j in Z_STEPS:
+            self.z_gather(b, j).wait_send()
+
+    def rows(self, b):
+        return jnp.concatenate([self.store[b, t] for t in range(self.store.shape[1])], axis=1)
+
+
 class Trade:
-    def __init__(self, store, send, recv):
-        self.store, self.send, self.recv = store, send, recv
+    def __init__(self, store, sem, layer):
+        self.store, self.sem, self.layer = store, sem, layer
         self.me, self.mate, self.across, self.diagonal = cp_places()
 
     def copy(self, b, r):
         ref = self.store.at[b, self.across if r == 2 else self.me]
-        return remote(ref, ref, self.send.at[r, b], self.recv.at[r, b], 'cp', self.across if r == 1 else self.mate)
+        return remote(ref, ref, self.sem, (self.layer, r, b), 'cp', self.across if r == 1 else self.mate)
 
     def give(self, b):
         self.copy(b, 1).start()
@@ -204,8 +242,8 @@
 
 
 class Wide:
-    def __init__(self, src, dst, send, recv):
-        self.src, self.dst, self.send, self.recv = src, dst, send, recv
+    def __init__(self, src, dst, sem, index):
+        self.src, self.dst, self.sem, self.index = src, dst, sem, index
         me, *self.peers = cp_places()
         mate, across, diagonal = self.peers
         self.peers = (mate, across, diagonal)
@@ -215,7 +253,7 @@
         n = self.dst.shape[-1]
         want = self.core if r == 1 else 1 - self.core
         columns = pl.ds(pl.multiple_of(want * n, n), n)
-        return remote(self.src.at[window].at[..., columns], self.dst.at[r].at[window], self.send.at[r], self.recv.at[r], 'cp', self.peers[r])
+        return remote(self.src.at[window].at[..., columns], self.dst.at[r].at[window], self.sem, (self.index, r), 'cp', self.peers[r])
 
     def give(self, b):
         for r in (1, 2, 0):
@@ -230,13 +268,13 @@
 
 
 class Narrow:
-    def __init__(self, src, dst, send, recv):
-        self.src, self.dst, self.send, self.recv = src, dst, send, recv
+    def __init__(self, src, dst, sem, index):
+        self.src, self.dst, self.sem, self.index = src, dst, sem, index
         _, self.mate, self.across, _ = cp_places()
 
     def copy(self, r, window):
         src = self.src if r < 2 else self.dst.at[1]
-        return remote(src.at[window], self.dst.at[r].at[window], self.send.at[r], self.recv.at[r], 'cp', self.across if r == 1 else self.mate)
+        return remote(src.at[window], self.dst.at[r].at[window], self.sem, (self.index, r), 'cp', self.across if r == 1 else self.mate)
 
     def give(self, b):
         for r in (1, 0):
@@ -398,6 +436,10 @@
 
 WIDE = ('h0', 'h1', 'm0', 'm1', 'dy', 'd0')
 NARROW = ('u0', 'u1', 'gl0', 'gl1', 'qkv0', 'qkv1')
+LETTERS = string.ascii_letters
+STEPS = '0212221212110211211110011010110101112'
+ORDER = 'jDAFnGlykdCKuHfIteqExvJhcbosapzgmiwrB'
+GIVES = tuple(zip(('h0', 'dy', 'm0', 'h1', 'u0', 'gl1', 'qkv1', 'm1', 'gl0', 'qkv0', 'u1', 'd0'), map(LETTERS.index, 'dhnuvBCEHIKK')))
 
 
 def mega_kernel(names, heads, *refs):
@@ -409,8 +451,12 @@
     ff = r.w_out.shape[1]
     width = heads * HEAD_DIM
     ring = Ring(*[getattr(r, 'ring_%d' % i) for i in range(8)])
+    gather_o = Columns(r.o_all, r.sem_oz, r.sem_oy)
+    gather_x = Columns(r.x_all, r.sem_xz, r.sem_xy)
     me, mate, across, diagonal = cp_places()
+    tp_me = gather_o.me
     others = (mate, across, diagonal)
+    my_columns = pl.ds(pl.multiple_of(tp_me * width, width), width)
 
     def weight(buf, sem, sources, layer):
         out, col = [], 0
@@ -434,17 +480,59 @@
                 copy.wait()
         return go
 
-    for key in ('qkv', 'o', 'gl', 'out'):
-        load(key, 0)()
+    for key, layer in (('qkv', 0), ('o', 1), ('gl', 0), ('out', 0)):
+        load(key, layer)()
     rows_in = [pltpu.make_async_copy(r.x.at[b], ring.full.at[b], r.sem_in.at[b]) for b in range(batch)]
-    shards_in = [pltpu.make_async_copy(src.at[:, ring.seg], dst, r.sem_in.at[batch + i]) for i, (src, dst) in enumerate(((r.x, r.xs0), (r.dy, r.ds1)))]
-    for copy in rows_in + shards_in:
+    shards_in = [(r.x.at[:, ring.seg], r.xs0), (r.dy.at[:, ring.seg], r.ds1), (r.x_rows.at[:, :, my_columns], r.x_col)]
+    shards_in = [pltpu.make_async_copy(src, dst, r.sem_in.at[batch + i]) for i, (src, dst) in enumerate(shards_in)]
+    deal_own = [pltpu.make_async_copy(r.w_deal.at[l, me, :, my_columns], r.w_cols.at[l, me, tp_me], r.sem_deal_in.at[l]) for l in range(2)]
+    for copy in rows_in + shards_in + deal_own:
         copy.start()
-    meet([ring.pair] + ring.z_peer[1:], others)
-    masks = [remote(r.key_add, r.mask_all.at[me], r.sem_mask.at[0, i], r.sem_mask.at[1, i], 'cp', peer) for i, peer in enumerate(others)]
+    r.key_add[:] = jnp.where(r.key_mask[:] > 0, 0.0, MASK_NEG).astype(F32)[:, None, :]
+    peers = [lax.rem(tp_me + j, n_seg) for j in range(n_seg)]
+    meet(peers[1:], others)
+    masks = [remote(r.key_add, r.mask_all.at[me], r.sem_mask, (i,), 'cp', peer) for i, peer in enumerate(others)]
     for copy in masks:
         copy.start()
     r.mask_all[me] = r.key_add[:]
+
+    def deal(l, j):
+        window = pl.ds(pl.multiple_of(peers[j] * width, width), width)
+        return remote(r.w_deal.at[l, me, :, window], r.w_cols.at[l, me, tp_me], r.sem_deal, (l, j), 'tp', peers[j])
+
+    def share(l, i):
+        ref = r.w_cols.at[l, across if i == 2 else me]
+        return remote(ref, ref, r.sem_share, (l, i), 'cp', across if i == 1 else mate)
+
+    for l in range(2):
+        for j in range(1, n_seg):
+            deal(l, j).start()
+
+    def share_start(l):
+        def go():
+            for j in range(1, n_seg):
+                deal(l, j).wait()
+            deal_own[l].wait()
+            share(l, 1).start()
+            share(l, 0).start()
+        return go
+
+    def share_pass(l):
+        def go():
+            share(l, 1).wait_recv()
+            share(l, 2).start()
+        return go
+
+    def shared(l):
+        def go():
+            share(l, 0).wait()
+            share(l, 1).wait_send()
+            share(l, 2).wait()
+            for c in range(r.w_cols.shape[1]):
+                for t in range(n_seg):
+                    r.w_now[t, c] = r.w_cols[l, c, t]
+        return go
+
     for ref in (r.ds_sum, r.dga0, r.dga1, r.dgm0, r.dgm1):
         ref[:] = jnp.zeros_like(ref)
     for copy in rows_in + shards_in:
@@ -454,26 +542,23 @@
     hold = dict(h=Spill(r.hbuf, r.sem_h), u=Spill(r.ubuf, r.sem_u), gl=Spill(r.gbuf, r.sem_g), qkv=Spill(r.qbuf, r.sem_q), o=Spill(r.obuf, r.sem_ob))
     moves = {}
     for i, key in enumerate(WIDE):
-        moves[key] = Wide(r.dy_rows if key == 'dy' else getattr(r, 'out_' + key), getattr(r, 'got_' + key), r.sem_wide.at[0, i], r.sem_wide.at[1, i])
+        moves[key] = Wide(r.dy_rows if key == 'dy' else getattr(r, 'out_' + key), getattr(r, 'got_' + key), r.sem_wide, i)
     for i, key in enumerate(NARROW):
-        moves[key] = Narrow(getattr(r, 'out_' + key), getattr(r, 'got_' + key), r.sem_narrow.at[0, i], r.sem_narrow.at[1, i])
-    kv = [Trade(r.kv0, r.sem_kv.at[0, 0], r.sem_kv.at[1, 0]), Trade(r.kv1, r.sem_kv.at[0, 1], r.sem_kv.at[1, 1])]
-    qdo = [Trade(r.qdo0, r.sem_qdo.at[0, 0], r.sem_qdo.at[1, 0]), Trade(r.qdo1, r.sem_qdo.at[0, 1], r.sem_qdo.at[1, 1])]
+        moves[key] = Narrow(getattr(r, 'out_' + key), getattr(r, 'got_' + key), r.sem_narrow, i)
+    kv = [Trade(store, r.sem_kv, l) for l, store in enumerate((r.kv0, r.kv1))]
+    qdo = [Trade(store, r.sem_qdo, l) for l, store in enumerate((r.qdo0, r.qdo1))]
     q_own = (r.q0, r.q1)
     stats = (r.stats0, r.stats1)
 
     def send_stats(l, b, i):
         ref = stats[l].at[b, me]
-        return remote(ref, ref, r.sem_stats.at[0, l, i, b], r.sem_stats.at[1, l, i, b], 'cp', others[i])
-
-    def of(key, l):
-        return getattr(r, '%s%d' % (key, l))
+        return remote(ref, ref, r.sem_stats, (l, i, b), 'cp', others[i])
 
     def out(key, l):
         return getattr(r, 'out_%s%d' % (key, l))
 
     def project(l, b, flat):
-        h = norm_rows(flat, r.g_attn[l])
+        h = norm_rows(flat, r.g_attn[l:l + 1])
         hold['h'].put(out('h', l), b, h)
         qkv = dot_nn(h, r.wqkv[:]).astype(BF16)
         q_own[l][b] = qkv[:, :width]
@@ -488,8 +573,15 @@
             kv[l].take(b)
             pairs = kv[l].store[b].reshape(-1, 2 * width)
             o = attend(heads, q_own[l][b], pairs, r.bias_rows[:], mask_row(r.mask_all, b))
+            gather_o.publish(b, o)
             hold['o'].put(out('o', l), b, o)
-            ring.send_partial(b, dot_nn(o, r.wo[:]))
+        return go
+
+    def stage_columns(l):
+        def go(b):
+            gather_o.arrive(b)
+            prod = dot_nn(gather_o.rows(b), r.w_now[:].reshape(d_model, width))
+            gather_x.publish(b, (r.x_col[b].astype(F32) + prod).astype(BF16))
         return go
 
     def add_stage(res, dst):
@@ -500,17 +592,19 @@
             ring.publish(b, value)
         return go
 
-    def pull_stage(x_shard, gain, res, dst, d_gain):
+    def pull_stage(x_shard, gain, l, res, dst, d_gain):
         def go(b):
-            value = rms_pull(ring.reduced(b), x_shard[b], gain[:], res[b], d_gain)
+            value = rms_pull(ring.reduced(b), x_shard[b], gain[l:l + 1], res[b], d_gain)
             if dst is not None:
                 dst[b] = value
             ring.publish(b, value)
         return go
 
-    def mlp_forward(l, b):
-        ring.arrive(b)
-        h2 = norm_rows(ring.rows(b), r.g_mlp[l])
+    def mlp_forward(l, b, shard):
+        gather_x.arrive(b)
+        window = pl.ds(pl.multiple_of(ring.seg * seg, seg), seg)
+        shard[b] = jnp.concatenate([r.x_all[b, t, window] for t in range(n_seg)], axis=1)
+        h2 = norm_rows(gather_x.rows(b), r.g_mlp[l:l + 1])
         hold['h'].put(out('m', l), b, h2)
         both = dot_nn(h2, r.wgl[:])
         gate, lin = both[:, :ff], both[:, ff:]
@@ -519,26 +613,29 @@
         return gate, lin, u
 
     def stage_mlp0(b):
-        gate, lin, u = mlp_forward(0, b)
+        gate, lin, u = mlp_forward(0, b, r.x1s0)
         r.gate[b] = gate
         r.lin[b] = lin
         ring.send_partial(b, dot_nn(u, r.wout[:]))
 
     def stage_next(b):
         ring.arrive(b)
+        r.x_col[b] = ring.full[b, :, :, my_columns].reshape(rows, width)
         project(1, b, ring.rows(b))
 
     def dy_in(b):
         slot = lax.rem(b, 2)
         return pltpu.make_async_copy(r.dy_rows.at[b], r.dybuf.at[slot], r.sem_dy.at[slot])
 
-    def mlp_backward(l, b, d, gate, lin):
+    def mlp_backward(l, b, d, gate, lin, copy=None):
         dgl = mlp_pull(dot_nt(d, r.wout[:]), gate, lin)
         hold['gl'].put(out('gl', l), b, dgl)
+        if copy is not None:
+            copy.wait()
         ring.send_partial(b, dot_nt(dgl, r.wgl[:]))
 
     def stage_mlp1(b):
-        gate, lin, _ = mlp_forward(1, b)
+        gate, lin, _ = mlp_forward(1, b, r.x1s1)
         dy_in(b).wait()
         mlp_backward(1, b, r.dybuf[lax.rem(b, 2)], gate, lin)
 
@@ -569,7 +666,8 @@
             qdo[l].take(b)
             for i in range(3):
                 send_stats(l, b, i).wait_recv()
-            d_kv = attend_cols_back(heads, kv[l].store[b, me], r.mask_cols[b], r.bias_cols, lambda s: qdo[l].store[b, s], lambda s: stats[l][b, s])
+            mask_col = jnp.transpose(jnp.broadcast_to(r.key_add[b], (rows, rows)))[:, :1]
+            d_kv = attend_cols_back(heads, kv[l].store[b, me], mask_col, r.bias_cols, lambda s: qdo[l].store[b, s], lambda s: stats[l][b, s])
             d_qkv = jnp.concatenate([r.dq[b], d_kv], axis=1)
             hold['qkv'].put(out('qkv', l), b, d_qkv)
             ring.send_partial(b, dot_nt(d_qkv, r.wqkv[:]))
@@ -578,96 +676,79 @@
     def stage_mlp_back0(b):
         ring.arrive(b)
         copy = keep(r.out_d0, b)
-        mlp_backward(0, b, ring.rows(b), r.gate[b], r.lin[b])
-        copy.wait()
+        mlp_backward(0, b, ring.rows(b), r.gate[b], r.lin[b], copy)
 
     def stage_last(b):
         ring.arrive(b)
         keep(r.out_dx, b).wait()
 
-    def kept(key, dst):
-        return lambda b: hold[key].copy(dst, b).wait()
-
-    def then(*parts):
-        def go(b):
-            for part in parts:
-                part(b)
-        return go
-
-    def give(key):
-        return lambda b: moves[key].give(b)
-
-    stages = [
-        stage_first,
-        then(kv[0].pass_on, kept('h', r.out_h0)),
-        stage_attend(0),
-        then(ring.reduce_pair, kept('o', r.out_o0)),
-        then(add_stage(r.xs0, r.x1s0), give('h0')),
-        ring.forward,
-        stage_mlp0,
-        then(ring.reduce_pair, kept('h', r.out_m0), kept('u', r.out_u0), give('u0')),
-        then(add_stage(r.x1s0, r.xs1), give('m0')),
-        ring.forward,
-        stage_next,
-        then(kv[1].pass_on, kept('h', r.out_h1)),
-        stage_attend(1),
-        then(ring.reduce_pair, kept('o', r.out_o1)),
-        then(add_stage(r.xs1, r.x1s1), give('h1')),
-        then(lambda b: dy_in(b).start(), ring.forward),
-        stage_mlp1,
-        then(ring.reduce_pair, kept('h', r.out_m1), kept('u', r.out_u1), kept('gl', r.out_gl1), give('u1')),
-        then(pull_stage(r.x1s1, r.g_mlp.at[1], r.ds1, r.dms1, r.dgm1), give('m1')),
-        ring.forward,
-        stage_rows_back(1, r.out_dm1),
-        qdo[1].pass_on,
-        stage_cols_back(1),
-        then(ring.reduce_pair, kept('qkv', r.out_qkv1), give('gl1')),
-        then(pull_stage(r.xs1, r.g_attn.at[1], r.dms1, r.ds0, r.dga1), give('dy')),
-        then(ring.forward, give('qkv1')),
-        stage_mlp_back0,
-        then(ring.reduce_pair, kept('gl', r.out_gl0), give('d0')),
-        pull_stage(r.x1s0, r.g_mlp.at[0], r.ds0, r.dms0, r.dgm0),
-        ring.forward,
-        stage_rows_back(0, r.out_dm0),
-        qdo[0].pass_on,
-        stage_cols_back(0),
-        then(ring.reduce_pair, kept('qkv', r.out_qkv0), give('qkv0')),
-        then(pull_stage(r.xs0, r.g_attn.at[0], r.dms0, None, r.dga0), give('gl0')),
-        ring.forward,
-        stage_last,
-    ]
+    def by_columns(tag, l):
+        return [('at' + tag, stage_attend(l)), ('', gather_o.forward), ('col' + tag, stage_columns(l)), ('', gather_x.forward)]
+
+    def by_sum(tag, start, finish):
+        return [(tag, start), ('', ring.reduce_pair), ('', finish), ('', ring.forward)]
+
+    stages = (
+        [('first', stage_first), ('', kv[0].pass_on)] + by_columns('0', 0)
+        + by_sum('mlp0', stage_mlp0, add_stage(r.x1s0, r.xs1))
+        + [('next', stage_next), ('', kv[1].pass_on)] + by_columns('1', 1)
+        + by_sum('mlp1', stage_mlp1, pull_stage(r.x1s1, r.g_mlp, 1, r.ds1, r.dms1, r.dgm1))
+        + [('rows1', stage_rows_back(1, r.out_dm1)), ('', qdo[1].pass_on)]
+        + by_sum('cols1', stage_cols_back(1), pull_stage(r.xs1, r.g_attn, 1, r.dms1, r.ds0, r.dga1))
+        + by_sum('back0', stage_mlp_back0, pull_stage(r.x1s0, r.g_mlp, 0, r.ds0, r.dms0, r.dgm0))
+        + [('rows0', stage_rows_back(0, r.out_dm0)), ('', qdo[0].pass_on)]
+        + by_sum('cols0', stage_cols_back(0), pull_stage(r.xs0, r.g_attn, 0, r.dms0, None, r.dga0))
+        + [('last', stage_last)])
+    lags = list(itertools.accumulate(int(step) for step in STEPS))
+    order = [LETTERS.index(letter) for letter in ORDER]
+    lag_of = {tag: lag for (tag, _), lag in zip(stages, lags)}
+    use = lambda tag: lag_of[tag]
+    after = lambda tag: lag_of[tag] + batch
 
     def tables():
         bias_tables(r.rel_bias, me, r.bias_rows, r.bias_cols)
         for copy in masks:
             copy.wait()
 
-    use = lambda k: k
-    after = lambda k: k + batch
-    hooks = [
-        (use(2), tables), (use(2), loaded('o', 0)), (use(6), loaded('gl', 0)), (use(6), loaded('out', 0)),
-        (after(0), load('qkv', 1)), (use(10), loaded('qkv', 1)),
-        (after(2), load('o', 1)), (use(12), loaded('o', 1)),
-        (after(6), load('gl', 1)), (after(6), load('out', 1)), (use(16), loaded('gl', 1)), (use(16), loaded('out', 1)),
-        (after(16), load('gl', 0)), (after(16), load('out', 0)), (use(26), loaded('gl', 0)), (use(26), loaded('out', 0)),
-        (after(20), load('o', 0)), (use(30), loaded('o', 0)),
-        (after(22), load('qkv', 0)), (use(32), loaded('qkv', 0)),
-        (after(20), moves['u0'].pass_on), (after(26), moves['u1'].pass_on), (after(30), moves['gl1'].pass_on), (after(32), moves['qkv1'].pass_on),
-        (after(31), lambda: bucket_sums(r.ds_sum, me, r.bias_sum)),
+    once = [
+        (use('at0'), tables), (use('mlp0'), loaded('gl', 0)), (use('mlp0'), loaded('out', 0)),
+        (2, share_start(0)), (3, share_pass(0)), (use('col0'), shared(0)), (use('col0'), share_start(1)), (after('col0'), share_pass(1)), (use('col1'), shared(1)),
+        (after('first'), load('qkv', 1)), (use('next'), loaded('qkv', 1)),
+        (after('mlp0'), load('gl', 1)), (after('mlp0'), load('out', 1)), (use('mlp1'), loaded('gl', 1)), (use('mlp1'), loaded('out', 1)),
+        (after('mlp1'), load('gl', 0)), (after('mlp1'), load('out', 0)), (use('back0'), loaded('gl', 0)), (use('back0'), loaded('out', 0)),
+        (use('rows1'), loaded('o', 1)), (after('rows1'), load('o', 0)), (use('rows0'), loaded('o', 0)),
+        (after('cols1'), load('qkv', 0)), (use('cols0'), loaded('qkv', 0)),
+        (after('rows0'), lambda: bucket_sums(r.ds_sum, me, r.bias_sum)),
     ]
+    early = [(use(tag) + 1, hold[key], ref) for tag, key, ref in (
+        ('first', 'h', r.out_h0), ('at0', 'o', r.out_o0), ('mlp0', 'h', r.out_m0), ('mlp0', 'u', r.out_u0), ('next', 'h', r.out_h1), ('at1', 'o', r.out_o1),
+        ('mlp1', 'h', r.out_m1), ('mlp1', 'u', r.out_u1), ('mlp1', 'gl', r.out_gl1), ('cols1', 'qkv', r.out_qkv1), ('back0', 'gl', r.out_gl0), ('cols0', 'qkv', r.out_qkv0))]
+    gives = dict(GIVES)
+    passes = [(gives[key] + 2 * batch, moves[key].pass_on) for key in NARROW]
+    n_slots = batch + lags[-1]
+
+    def chunk_at(slot, lag, work):
+        @pl.when(jnp.logical_and(slot >= lag, slot < batch + lag))
+        def _():
+            work(slot - lag)
 
     def slot_step(slot, carry):
-        for at, work in hooks:
-            pl.when(slot == at)(work)
-        for k, stage in enumerate(stages):
-            @pl.when(jnp.logical_and(slot >= k, slot < batch + k))
-            def _():
-                stage(slot - k)
+        for at, work in once + passes:
+            if at < n_slots:
+                pl.when(slot == at)(work)
+        for lag, spill, ref in early:
+            chunk_at(slot, lag, lambda b: spill.copy(ref, b).wait())
+        chunk_at(slot, use('mlp1') - 1, lambda b: dy_in(b).start())
+        for k in order:
+            chunk_at(slot, lags[k], stages[k][1])
+        for key, lag in GIVES:
+            chunk_at(slot, lag, moves[key].give)
         return carry
 
-    lax.fori_loop(0, batch + len(stages) - 1, slot_step, 0)
-    for key in ('gl0', 'qkv0'):
-        moves[key].pass_on()
+    lax.fori_loop(0, n_slots, slot_step, 0)
+    for at, work in passes:
+        if at >= n_slots:
+            work()
 
     def finish(b, carry):
         for l in range(2):
@@ -682,18 +763,19 @@
         moves[key].finish()
 
 
-def mega(x, dy, key_add, rel_bias, g_attn, g_mlp, w_q, w_k, w_v, w_o, w_gate, w_lin, w_out, cid):
+def mega(x, dy, key_mask, rel_bias, g_attn, g_mlp, w_q, w_k, w_v, w_o, w_gate, w_lin, w_out, cid):
     batch, rows, d_model = x.shape
     heads = rel_bias.shape[1]
     width, ff = heads * HEAD_DIM, w_gate.shape[2]
     n_cp, n_tp = 4, 8
     seg = rows // n_tp
+    quarter = width // n_cp
     dma = pltpu.SemaphoreType.DMA
     any_spec = pl.BlockSpec(memory_space=pl.ANY)
     by_seg = lambda a: a.reshape(batch, n_tp, seg, d_model)
-    ins = dict(x=(by_seg(x), any_spec), dy=(by_seg(dy), any_spec), dy_rows=(dy, any_spec), key_add=(key_add[:, None, :], VMEM_SPEC), mask_cols=(key_add[:, :, None], VMEM_SPEC), rel_bias=(rel_bias, SMEM_SPEC),
-               g_attn=(g_attn[:, None, :], VMEM_SPEC), g_mlp=(g_mlp[:, None, :], VMEM_SPEC), w_q=(w_q, any_spec), w_k=(w_k, any_spec), w_v=(w_v, any_spec), w_o=(w_o, any_spec),
-               w_gate=(w_gate, any_spec), w_lin=(w_lin, any_spec), w_out=(w_out, any_spec))
+    in_hbm = dict(x=by_seg(x), x_rows=x, dy=by_seg(dy), dy_rows=dy, w_q=w_q, w_k=w_k, w_v=w_v, w_o=w_o, w_deal=w_o.reshape(-1, n_cp, quarter, d_model), w_gate=w_gate, w_lin=w_lin, w_out=w_out)
+    ins = {key: (value, any_spec) for key, value in in_hbm.items()}
+    ins.update(key_mask=(key_mask, VMEM_SPEC), rel_bias=(rel_bias, SMEM_SPEC), g_attn=(g_attn, VMEM_SPEC), g_mlp=(g_mlp, VMEM_SPEC))
     size = dict(h=d_model, m=d_model, u=ff, gl=2 * ff, qkv=3 * width, o=width)
     outs = {}
     for key, n in size.items():
@@ -710,19 +792,30 @@
     for key in ('dga0', 'dga1', 'dgm0', 'dgm1'):
         outs[key] = ((1, d_model), F32)
     outs['bias_sum'] = ((rel_bias.shape[0], heads, n_cp * rows), F32)
-    shard = pltpu.VMEM((batch, seg, d_model), BF16)
-    blocks = pltpu.VMEM((batch, n_cp, rows, 2 * width), BF16)
-    table = pltpu.VMEM((batch, n_cp, 2 * heads, rows), F32)
-    chunk_f32 = pltpu.VMEM((batch, rows, ff), F32)
-    q_rows = pltpu.VMEM((batch, rows, width), BF16)
-    two = lambda n: pltpu.VMEM((2, rows, n), BF16)
-    scratch = dict(wqkv=pltpu.VMEM((d_model, 3 * width), BF16), wo=pltpu.VMEM((width, d_model), BF16), wgl=pltpu.VMEM((d_model, 2 * ff), BF16), wout=pltpu.VMEM((ff, d_model), BF16),
-                   sem_qkv=dma((3,)), sem_o=dma((1,)), sem_gl=dma((2,)), sem_out=dma((1,)), sem_in=dma((batch + 2,)), sem_mask=dma((2, 3)), mask_all=pltpu.VMEM((n_cp, batch, 1, rows), F32),
-                   bias_rows=pltpu.VMEM((heads * rows, n_cp * rows), F32), bias_cols=pltpu.VMEM((n_cp, rows, heads * rows), F32), ds_sum=pltpu.VMEM((heads * rows, n_cp * rows), F32),
-                   xs0=shard, x1s0=shard, xs1=shard, x1s1=shard, ds1=shard, dms1=shard, ds0=shard, dms0=shard, kv0=blocks, kv1=blocks, qdo0=blocks, qdo1=blocks, stats0=table, stats1=table,
-                   q0=q_rows, q1=q_rows, dq=q_rows, gate=chunk_f32, lin=chunk_f32, hbuf=two(d_model), ubuf=two(ff), gbuf=two(2 * ff), qbuf=two(3 * width), obuf=two(width), dybuf=two(d_model),
-                   sem_h=dma((2,)), sem_u=dma((2,)), sem_g=dma((2,)), sem_q=dma((2,)), sem_ob=dma((2,)), sem_dy=dma((2,)), sem_keep=dma((batch,)),
-                   sem_wide=dma((2, len(WIDE), 3)), sem_narrow=dma((2, len(NARROW), 3)), sem_kv=dma((2, 2, 3, batch)), sem_qdo=dma((2, 2, 3, batch)), sem_stats=dma((2, 2, 3, batch)))
+    vmem = lambda *shape: pltpu.VMEM(shape, BF16)
+    wide = lambda *shape: pltpu.VMEM(shape, F32)
+    scratch = dict(wqkv=vmem(d_model, 3 * width), wo=vmem(width, d_model), wgl=vmem(d_model, 2 * ff), wout=vmem(ff, d_model), w_cols=vmem(2, n_cp, n_tp, quarter, width), w_now=vmem(n_tp, n_cp, quarter, width),
+                   o_all=vmem(batch, n_tp, rows, width), x_all=vmem(batch, n_tp, rows, width), key_add=wide(batch, 1, rows), mask_all=wide(n_cp, batch, 1, rows),
+                   bias_rows=wide(heads * rows, n_cp * rows), bias_cols=wide(n_cp, rows, heads * rows), ds_sum=wide(heads * rows, n_cp * rows), gate=wide(batch, rows, ff), lin=wide(batch, rows, ff))
+    for key in ('xs0', 'x1s0', 'xs1', 'x1s1', 'ds1', 'dms1', 'ds0', 'dms0'):
+        scratch[key] = vmem(batch, seg, d_model)
+    for key in ('kv0', 'kv1', 'qdo0', 'qdo1'):
+        scratch[key] = vmem(batch, n_cp, rows, 2 * width)
+    for key in ('stats0', 'stats1'):
+        scratch[key] = wide(batch, n_cp, 2 * heads, rows)
+    for key in ('q0', 'q1', 'dq', 'x_col'):
+        scratch[key] = vmem(batch, rows, width)
+    for key, n in (('hbuf', d_model), ('ubuf', ff), ('gbuf', 2 * ff), ('qbuf', 3 * width), ('obuf', width), ('dybuf', d_model)):
+        scratch[key] = vmem(2, rows, n)
+    for key in ('o', 'out', 'gl', 'h', 'u', 'g', 'q', 'ob', 'dy', 'deal_in'):
+        scratch['sem_' + key] = dma((2,))
+    scratch.update(sem_qkv=dma((3,)), sem_in=dma((batch + 3,)), sem_keep=dma((batch,)), sem_mask=dma((2, 3)), sem_deal=dma((2, 2, n_tp)), sem_share=dma((2, 2, 3)),
+                   sem_wide=dma((2, len(WIDE), 3)), sem_narrow=dma((2, len(NARROW), 3)))
+    for key in ('kv', 'qdo', 'stats'):
+        scratch['sem_' + key] = dma((2, 2, 3, batch))
+    for key in ('o', 'x'):
+        scratch['sem_%sz' % key] = dma((2, batch, 3))
+        scratch['sem_%sy' % key] = dma((2, batch, 4))
     for i, piece in enumerate(Ring.scratch(batch, seg, d_model)):
         scratch['ring_%d' % i] = piece
     result = pl.pallas_call(
@@ -731,7 +824,7 @@
         in_specs=[v[1] for v in ins.values()],
         out_specs=tuple([any_spec] * n_any + [VMEM_SPEC] * (len(outs) - n_any)),
         scratch_shapes=list(scratch.values()),
-        compiler_params=comm_params(cid, 62),
+        compiler_params=comm_params(cid, 63),
         cost_estimate=cost(300),
         name='mega',
     )(*[v[0] for v in ins.values()])
@@ -740,7 +833,7 @@
 
 def swap_kernel(n, *refs):
     halves, wo_part, small, mates, wo_own, wo_mate, total = refs[:n], refs[n], refs[n + 1], refs[n + 2:2 * n + 2], refs[2 * n + 2], refs[2 * n + 3], refs[2 * n + 4]
-    wo_in, wo_sum, wo_x, stage, by_z, send, recv, s_send, s_recv, w_send, w_recv = refs[2 * n + 5:]
+    wo_in, wo_sum, wo_x, stage, by_z, sem, s_sem, w_sem = refs[2 * n + 5:]
     _, z, y, pair, z_peer = tp_places()
     me, mate, across, _ = cp_places()
     core, chip = lax.rem(me, 2), me // 2
@@ -750,18 +843,18 @@
     def columns(which):
         return pl.ds(pl.multiple_of(which * half, half), half)
 
-    first = remote(wo_part.at[:, :, columns(1 - core)], wo_in, w_send.at[0], w_recv.at[0], 'cp', mate)
+    first = remote(wo_part.at[:, :, columns(1 - core)], wo_in, w_sem, (0,), 'cp', mate)
     first.start()
-    swaps = [remote(halves[i], mates[i], send.at[i], recv.at[i], 'cp', mate) for i in range(n)]
+    swaps = [remote(halves[i], mates[i], sem, (i,), 'cp', mate) for i in range(n)]
     for copy in swaps:
         copy.start()
     first.wait()
     wo_sum[:] = wo_part[:, :, columns(core)] + wo_in[:]
-    second = remote(wo_sum.at[1 - chip], wo_x, w_send.at[1], w_recv.at[1], 'cp', across)
+    second = remote(wo_sum.at[1 - chip], wo_x, w_sem, (1,), 'cp', across)
     second.start()
     mine = small
     for k, (axis, peer) in enumerate((('cp', mate), ('cp', across), ('tp', pair))):
-        copy = remote(mine, stage.at[2 * k], s_send.at[k], s_recv.at[k], axis, peer)
+        copy = remote(mine, stage.at[2 * k], s_sem, (k,), axis, peer)
         copy.start()
         copy.wait()
         if k < 2:
@@ -769,18 +862,18 @@
             mine = stage.at[2 * k + 1]
         else:
             by_z[z] = mine[:] + stage[2 * k]
-    copies = [remote(by_z.at[z], by_z.at[z], s_send.at[2 + j], s_recv.at[2 + j], 'tp', z_peer[j]) for j in (1, 2, 3)]
+    copies = [remote(by_z.at[z], by_z.at[z], s_sem, (2 + j,), 'tp', z_peer[j]) for j in (1, 2, 3)]
     for copy in copies:
         copy.start()
     second.wait()
     wo_own[chip] = (wo_sum[chip] + wo_x[:]).astype(BF16)
-    third = remote(wo_own.at[chip], wo_own.at[chip], w_send.at[2], w_recv.at[2], 'cp', across)
+    third = remote(wo_own.at[chip], wo_own.at[chip], w_sem, (2,), 'cp', across)
     third.start()
     for copy in copies:
         copy.wait()
     total[:] = by_z[0] + by_z[1] + by_z[2] + by_z[3]
     third.wait()
-    last = remote(wo_own, wo_mate, w_send.at[3], w_recv.at[3], 'cp', mate)
+    last = remote(wo_own, wo_mate, w_sem, (3,), 'cp', mate)
     last.start()
     for copy in swaps + [last]:
         copy.wait()
@@ -799,7 +892,7 @@
         in_specs=[any_spec] * n + [VMEM_SPEC] * 2,
         out_specs=tuple([any_spec] * n + [VMEM_SPEC] * 3),
         scratch_shapes=[pltpu.VMEM((layers, width, half), F32), pltpu.VMEM((layers, width, half), F32), pltpu.VMEM((width, half), F32),
-                        pltpu.VMEM((5,) + small.shape, F32), pltpu.VMEM((4,) + small.shape, F32), dma((n,)), dma((n,)), dma((6,)), dma((6,)), dma((4,)), dma((4,))],
+                        pltpu.VMEM((5,) + small.shape, F32), pltpu.VMEM((4,) + small.shape, F32), dma((2, n)), dma((2, 6)), dma((2, 4))],
         compiler_params=comm_params(cid, 24),
         name='swap',
     )(*halves, wo_part, small)
@@ -863,8 +956,7 @@
         core = lax.rem(lax.axis_index('cp'), 2)
         half = d_model // 2
 
-        key_add = jnp.where(key_mask > 0, 0.0, MASK_NEG).astype(F32)
-        m = mega(x_in, d_y, key_add, rel_bias, g_attn, g_mlp, w_q, w_k, w_v, w_o, w_gate, w_lin, w_out, 0)
+        m = mega(x_in, d_y, key_mask, rel_bias, g_attn, g_mlp, w_q, w_k, w_v, w_o, w_gate, w_lin, w_out, 0)
 
         def flat(array):
             return array.reshape(-1, array.shape[-1])

time: 743 us -> 700 us (0.942)
  Pallas kernels: 672 us -> 633 us
    pallas_call x1, Pallas kernels: 610 us -> 566 us  [mega(): pl.pallas_call(functools.partial(mega_kernel, list(ins) + list(outs) + li...]
where the time goes in v5:
time: 700 us; the launch traced here: 687 us
  Pallas kernels  633 us (90%)
  matrix products  30 us (4%)
  local copies, waits for them, and re-layouts  21.1 us (3%)
    pallas_call x1, Pallas kernels, mega(): pl.pallas_call(functools.partial(mega_kernel, list(ins) + list(outs) + li...  566 us
    pallas_call x1, Pallas kernels, swap(): pl.pallas_call(functools.partial(swap_kernel, n), out_shape=tuple((jax.Sh...  55.5 us
    dot_general x14, matrix products, dot_tn(): lax.dot_general(a, b, (((0,), (0,)), ((), ())), preferred_element_type=F32)  30 us
    unnamed x73, local copies, waits for them, and re-layouts  19.3 us

profile of v5, /device:TPU:0, one launch (start us, length us, event | category | flops | bytes accessed | tf_op | source)
XLA Modules:
  0.0 687.4 jit_solution(16892030764209643791)
XLA Ops:
  0.7 1.4 copy.31.refs_13_
  2.0 565.7 %mega.1 = (bf16[4,128,2048]{2,1,0:T(8,128)(2,1)}, bf16[4,128,2048]{2,1,0:T(8,128)(2,1)}, bf16[4,128,2048]{2,1,0:T(8,128)(2,1)}, bf16[4,128,2048]{2,1,0:T(8,128)(...) custom-call(bf16[4,8,16,2048]{3,2,1,0:T(8,128)(2,1)} %bitcast.108, ...), custom_call_target="tpu_custom_call" | custom-call | flops 314572800000 | bytes 8388608 | tf_op jit(solution)/shard_map/mega/pallas_call | solution.py:821
  567.7 1.1 reduce_sum.9
  568.8 0.1 reshape.148
  569.0 0.7 constant_dynamic-update-slice_fusion.4
  569.7 0.7 constant_dynamic-update-slice_fusion.3
  570.4 0.7 constant_dynamic-update-slice_fusion.2
  571.1 0.7 constant_dynamic-update-slice_fusion.1
  571.8 2.6 fusion.12
  574.4 0.0 copy-done.30
  574.4 0.5 copy-done.32
  574.9 2.8 fusion.3.refs_0_
  577.8 0.0 copy-done.9
  577.8 0.0 copy-done.20
  577.8 0.0 copy-start.8
  577.8 0.0 copy-start.19
  577.8 0.7 convolution_bitcast_fusion.1
  578.5 0.8 copy-done.8
  579.4 0.0 copy-done.19
  579.4 0.7 convolution_bitcast_fusion
  580.1 0.0 copy-start.21
  580.1 0.0 copy-start.23
  580.1 0.5 pad_maximum_fusion.refs_6_
  580.6 1.4 copy-done.21
  582.0 0.6 copy-done.23
  582.6 2.3 fusion.24
  584.9 0.0 copy-done.14
  584.9 0.0 copy-done.18
  584.9 0.0 copy-start.13
  584.9 0.0 copy-start.15
  584.9 0.0 copy-start.10
  585.0 0.9 add_convert_fusion.refs_4_
  585.8 0.2 copy-done.13
  586.0 0.7 copy-done.15
  586.7 0.9 fusion.5
  587.6 0.0 copy-done.10
  587.6 1.1 copy-done.6
  588.8 2.3 fusion.4.refs_5_
  591.1 0.0 copy-done.22
  591.1 0.0 copy-done.24
  591.1 1.0 fusion.10
  592.2 0.8 copy-done.29
  593.0 0.7 copy-done.31
  593.7 3.1 fusion.2.refs_1_
  596.9 4.5 fusion.22
  601.4 1.7 fusion.1.refs_2_
  603.1 0.4 copy-done.25
  603.5 1.0 copy-done.27
  604.5 4.5 fusion.23
  609.0 2.0 fusion.refs_3_
  611.0 0.0 copy-done
  611.0 0.0 copy-start.1
  611.0 55.5 %swap.1 = (bf16[1024,768]{1,0:T(8,128)(2,1)S(1)}, bf16[1024,768]{1,0:T(8,128)(2,1)S(1)}, bf16[1024,1280]{1,0:T(8,128)(2,1)S(1)}, bf16[1024,1280]{1,0:T(8,128)(2,...) custom-call(bf16[1024,768]{1,0:T(8,128)(2,1)S(1)} %fusion.3.refs_0_,, ...), custom_call_target="tpu_custom_call" | custom-call | tf_op jit(solution)/shard_map/swap/pallas_call | solution.py:889
  666.5 1.6 copy-done.3
  668.1 1.1 copy-done.4
  669.2 0.2 slice_bitcast_fusion
  669.5 1.2 copy-done.2
  670.7 0.9 copy-done.5
  671.6 12.0 %place.1 = (bf16[2,2048,256]{2,1,0:T(8,128)(2,1)}, bf16[2,2048,256]{2,1,0:T(8,128)(2,1)}, bf16[2,2048,256]{2,1,0:T(8,128)(2,1)}, bf16[2,256,2048]{2,1,0:T(8,128)...) custom-call(bf16[1024,768]{1,0:T(8,128)(2,1)S(1)} %fusion.3.refs_0_, ...), custom_call_target="tpu_custom_call" | custom-call | tf_op jit(solution)/shard_map/place/pallas_call | solution.py:933
  683.6 0.6 reshape.151
  684.2 0.1 reshape.149
  684.3 0.7 copy.37
  685.0 0.6 reshape.150
  685.6 1.3 copy.54
  (39 shorter events, 0.1 us)
Async XLA Ops:
  571.8 2.6 copy-start.30
  571.8 3.2 copy-start.32
  574.9 2.9 copy-start.9
  574.9 2.9 copy-start.20
  577.8 1.6 copy-start.8
  577.8 1.6 copy-start.19
  580.1 1.9 copy-start.21
  580.1 2.5 copy-start.23
  582.6 2.3 copy-start.14
  582.6 2.3 copy-start.18
  584.9 1.1 copy-start.13
  584.9 1.8 copy-start.15
  584.9 2.7 copy-start.10
  586.7 2.0 copy-start.6
  588.8 2.3 copy-start.22
  588.8 2.3 copy-start.24
  591.1 1.9 copy-start.29
  591.1 2.6 copy-start.31
  593.7 3.1 copy-start.26
  593.7 3.1 copy-start.28
  596.8 4.5 copy-start.12
  596.9 4.5 copy-start.17
  601.4 2.1 copy-start.25
  601.4 3.1 copy-start.27
  604.5 6.5 copy-start
  604.5 4.5 copy-start.11
  604.5 4.5 copy-start.16
  611.0 55.5 %copy-start.1 = (bf16[1024,1280]{1,0:T(8,128)(2,1)}, bf16[1024,1280]{1,0:T(8,128)(2,1)S(1)}, u32[]{:S(2)}) copy-start(bf16[1024,1280]{1,0:T(8,128)(2,1)S(1)} %fusion.refs_3_) | copy-start | bytes 7864324
  666.5 1.6 copy-start.3
  668.1 1.1 copy-start.4
  669.2 1.5 copy-start.2
  669.2 2.4 copy-start.5
  671.6 14.0 %copy-start.7 = (bf16[4,8,16,2048]{3,2,1,0:T(8,128)(2,1)S(1)}, bf16[4,8,16,2048]{3,2,1,0:T(8,128)(2,1)}, u32[]{:S(2)}) copy-start(bf16[4,8,16,2048]{3,2,1,0:T(8,128)(2,1)} %get-tuple-element.60) | copy-start | bytes 6291460

commit v6 on v5

--- a/solution.py
+++ b/solution.py
@@ -417,17 +417,19 @@
     lax.fori_loop(0, rows // 8, strip, 0)
 
 
-def bucket_sums(ds_ref, me, out_ref):
-    n_buckets, heads, seq = out_ref.shape
-    rows = ds_ref.shape[0] // heads
+def bucket_sums(ds_ref, heads, n_buckets, me):
+    rows, seq = ds_ref.shape[0] // heads, ds_ref.shape[1]
     rel = lax.broadcasted_iota(jnp.int32, (rows, seq), 1) - lax.broadcasted_iota(jnp.int32, (rows, seq), 0) - me * rows
-
-    def step(k, carry):
+    lane = lax.broadcasted_iota(jnp.int32, (1, n_buckets * heads), 1)
+
+    def step(k, acc):
         hit = rel_bucket(rel) == k
-        out_ref[k] = jnp.concatenate([jnp.sum(jnp.where(hit, ds_ref[h * rows:(h + 1) * rows], 0.0), axis=0, keepdims=True) for h in range(heads)], axis=0)
-        return carry
-
-    lax.fori_loop(0, n_buckets, step, 0)
+        for h in range(heads):
+            total = jnp.sum(row_sum(jnp.where(hit, ds_ref[h * rows:(h + 1) * rows], 0.0)), axis=0, keepdims=True)
+            acc = jnp.where(lane == k * heads + h, total, acc)
+        return acc
+
+    return lax.fori_loop(0, n_buckets, step, jnp.zeros(lane.shape, F32))
 
 
 class Refs:
@@ -437,9 +439,10 @@
 WIDE = ('h0', 'h1', 'm0', 'm1', 'dy', 'd0')
 NARROW = ('u0', 'u1', 'gl0', 'gl1', 'qkv0', 'qkv1')
 LETTERS = string.ascii_letters
-STEPS = '0212221212110211211110011010110101112'
-ORDER = 'jDAFnGlykdCKuHfIteqExvJhcbosapzgmiwrB'
-GIVES = tuple(zip(('h0', 'dy', 'm0', 'h1', 'u0', 'gl1', 'qkv1', 'm1', 'gl0', 'qkv0', 'u1', 'd0'), map(LETTERS.index, 'dhnuvBCEHIKK')))
+STEPS = '0303221222210111101101010101101101123'
+ORDER = 'FaKGeCtbdqpHlkExvozmjiwshfuBJnDIcAgyr'
+PASS_FROM = 34
+GIVES = tuple(zip(('h0', 'dy', 'u0', 'm0', 'h1', 'u1', 'm1', 'gl1', 'd0', 'qkv1', 'gl0', 'qkv0'), map(LETTERS.index, 'ddmvxzABDHHJ')))
 
 
 def mega_kernel(names, heads, *refs):
@@ -480,6 +483,37 @@
                 copy.wait()
         return go
 
+    chip, core = me // 2, lax.rem(me, 2)
+    half = d_model // 2
+
+    def half_of(which):
+        return pl.ds(pl.multiple_of(which * half, half), half)
+
+    def wo_send(l, step):
+        src, dst, peer = (
+            (r.wo_acc.at[:, half_of(1 - core)], r.wo_in.at[l], mate),
+            (r.wo_in.at[l, pl.ds(pl.multiple_of((1 - chip) * (width // 2), 8), width // 2)], r.wo_x.at[l], across),
+            (r.wo_half.at[l, chip], r.wo_half.at[l, chip], across))[step]
+        return remote(src, dst, r.sem_wo, (l, step), 'cp', peer)
+
+    def wo_first(l):
+        return lambda: wo_send(l, 0).start()
+
+    def wo_second(l):
+        def go():
+            wo_send(l, 0).wait()
+            r.wo_in[l] = r.wo_in[l] + r.wo_acc[:, half_of(core)]
+            wo_send(l, 1).start()
+        return go
+
+    def wo_third(l):
+        def go():
+            wo_send(l, 1).wait()
+            mine = r.wo_in[l, pl.ds(pl.multiple_of(chip * (width // 2), 8), width // 2)]
+            r.wo_half[l, chip] = (mine + r.wo_x[l]).astype(BF16)
+            wo_send(l, 2).start()
+        return go
+
     for key, layer in (('qkv', 0), ('o', 1), ('gl', 0), ('out', 0)):
         load(key, layer)()
     rows_in = [pltpu.make_async_copy(r.x.at[b], ring.full.at[b], r.sem_in.at[b]) for b in range(batch)]
@@ -535,11 +569,12 @@
 
     for ref in (r.ds_sum, r.dga0, r.dga1, r.dgm0, r.dgm1):
         ref[:] = jnp.zeros_like(ref)
+    bias_tables(r.rel_bias, me, r.bias_rows, r.bias_cols)
     for copy in rows_in + shards_in:
         copy.wait()
     loaded('qkv', 0)()
 
-    hold = dict(h=Spill(r.hbuf, r.sem_h), u=Spill(r.ubuf, r.sem_u), gl=Spill(r.gbuf, r.sem_g), qkv=Spill(r.qbuf, r.sem_q), o=Spill(r.obuf, r.sem_ob))
+    hold = dict(h=Spill(r.hbuf, r.sem_h), u=Spill(r.ubuf, r.sem_u), gl=Spill(r.gbuf, r.sem_g), qkv=Spill(r.qbuf, r.sem_q))
     moves = {}
     for i, key in enumerate(WIDE):
         moves[key] = Wide(r.dy_rows if key == 'dy' else getattr(r, 'out_' + key), getattr(r, 'got_' + key), r.sem_wide, i)
@@ -574,7 +609,7 @@
             pairs = kv[l].store[b].reshape(-1, 2 * width)
             o = attend(heads, q_own[l][b], pairs, r.bias_rows[:], mask_row(r.mask_all, b))
             gather_o.publish(b, o)
-            hold['o'].put(out('o', l), b, o)
+            r.o_own[l, b] = o
         return go
 
     def stage_columns(l):
@@ -644,11 +679,11 @@
         copy.start()
         return copy
 
-    def stage_rows_back(l, dst):
+    def stage_rows_back(l):
         def go(b):
             ring.arrive(b)
-            copy = keep(dst, b)
-            d_o = dot_nt(ring.rows(b), r.wo[:]).astype(BF16)
+            d_mid = ring.rows(b)
+            d_o = dot_nt(d_mid, r.wo[:]).astype(BF16)
             both = jnp.concatenate([q_own[l][b], d_o], axis=1)
             qdo[l].store[b, me] = both
             qdo[l].give(b)
@@ -658,7 +693,15 @@
             r.dq[b] = d_q
             for i in range(3):
                 send_stats(l, b, i).start()
-            copy.wait()
+            d_wo = dot_tn(r.o_own[l, b], d_mid)
+
+            @pl.when(b == 0)
+            def _():
+                r.wo_acc[:] = d_wo
+
+            @pl.when(b > 0)
+            def _():
+                r.wo_acc[:] += d_wo
         return go
 
     def stage_cols_back(l):
@@ -693,10 +736,10 @@
         + by_sum('mlp0', stage_mlp0, add_stage(r.x1s0, r.xs1))
         + [('next', stage_next), ('', kv[1].pass_on)] + by_columns('1', 1)
         + by_sum('mlp1', stage_mlp1, pull_stage(r.x1s1, r.g_mlp, 1, r.ds1, r.dms1, r.dgm1))
-        + [('rows1', stage_rows_back(1, r.out_dm1)), ('', qdo[1].pass_on)]
+        + [('rows1', stage_rows_back(1)), ('', qdo[1].pass_on)]
         + by_sum('cols1', stage_cols_back(1), pull_stage(r.xs1, r.g_attn, 1, r.dms1, r.ds0, r.dga1))
         + by_sum('back0', stage_mlp_back0, pull_stage(r.x1s0, r.g_mlp, 0, r.ds0, r.dms0, r.dgm0))
-        + [('rows0', stage_rows_back(0, r.out_dm0)), ('', qdo[0].pass_on)]
+        + [('rows0', stage_rows_back(0)), ('', qdo[0].pass_on)]
         + by_sum('cols0', stage_cols_back(0), pull_stage(r.xs0, r.g_attn, 0, r.dms0, None, r.dga0))
         + [('last', stage_last)])
     lags = list(itertools.accumulate(int(step) for step in STEPS))
@@ -705,26 +748,29 @@
     use = lambda tag: lag_of[tag]
     after = lambda tag: lag_of[tag] + batch
 
-    def tables():
-        bias_tables(r.rel_bias, me, r.bias_rows, r.bias_cols)
+    def masked():
         for copy in masks:
             copy.wait()
 
+    def count_buckets():
+        r.small[-n_seg:] = jnp.where(lax.broadcasted_iota(jnp.int32, (n_seg, 128), 0) == tp_me, bucket_sums(r.ds_sum, heads, r.rel_bias.shape[0], me), 0.0)
+
     once = [
-        (use('at0'), tables), (use('mlp0'), loaded('gl', 0)), (use('mlp0'), loaded('out', 0)),
-        (2, share_start(0)), (3, share_pass(0)), (use('col0'), shared(0)), (use('col0'), share_start(1)), (after('col0'), share_pass(1)), (use('col1'), shared(1)),
+        (use('at0'), masked), (use('mlp0'), loaded('gl', 0)), (use('mlp0'), loaded('out', 0)),
+        (batch, share_start(0)), (batch + 1, share_pass(0)), (use('col0'), shared(0)), (batch, share_start(1)), (after('col0'), share_pass(1)), (use('col1'), shared(1)),
         (after('first'), load('qkv', 1)), (use('next'), loaded('qkv', 1)),
         (after('mlp0'), load('gl', 1)), (after('mlp0'), load('out', 1)), (use('mlp1'), loaded('gl', 1)), (use('mlp1'), loaded('out', 1)),
         (after('mlp1'), load('gl', 0)), (after('mlp1'), load('out', 0)), (use('back0'), loaded('gl', 0)), (use('back0'), loaded('out', 0)),
         (use('rows1'), loaded('o', 1)), (after('rows1'), load('o', 0)), (use('rows0'), loaded('o', 0)),
         (after('cols1'), load('qkv', 0)), (use('cols0'), loaded('qkv', 0)),
-        (after('rows0'), lambda: bucket_sums(r.ds_sum, me, r.bias_sum)),
+        (after('rows1'), wo_first(1)), (after('rows1') + 1, wo_second(1)), (after('rows1') + 4, wo_third(1)),
+        (after('rows0'), wo_first(0)), (after('rows0') + 1, wo_second(0)),
     ]
     early = [(use(tag) + 1, hold[key], ref) for tag, key, ref in (
-        ('first', 'h', r.out_h0), ('at0', 'o', r.out_o0), ('mlp0', 'h', r.out_m0), ('mlp0', 'u', r.out_u0), ('next', 'h', r.out_h1), ('at1', 'o', r.out_o1),
+        ('first', 'h', r.out_h0), ('mlp0', 'h', r.out_m0), ('mlp0', 'u', r.out_u0), ('next', 'h', r.out_h1),
         ('mlp1', 'h', r.out_m1), ('mlp1', 'u', r.out_u1), ('mlp1', 'gl', r.out_gl1), ('cols1', 'qkv', r.out_qkv1), ('back0', 'gl', r.out_gl0), ('cols0', 'qkv', r.out_qkv0))]
     gives = dict(GIVES)
-    passes = [(gives[key] + 2 * batch, moves[key].pass_on) for key in NARROW]
+    passes = [(max(gives[key] + 2 * batch, PASS_FROM), moves[key].pass_on) for key in NARROW]
     n_slots = batch + lags[-1]
 
     def chunk_at(slot, lag, work):
@@ -743,12 +789,18 @@
             chunk_at(slot, lags[k], stages[k][1])
         for key, lag in GIVES:
             chunk_at(slot, lag, moves[key].give)
+        pl.when(slot == n_slots - batch)(count_buckets)
         return carry
 
     lax.fori_loop(0, n_slots, slot_step, 0)
+    wo_third(0)()
     for at, work in passes:
         if at >= n_slots:
             work()
+    n_lines = d_model // 128
+    for i, ref in enumerate((r.dga0, r.dga1, r.dgm0, r.dgm1)):
+        for k in range(n_lines):
+            r.small[i * n_lines + k:i * n_lines + k + 1] = ref[:, k * 128:(k + 1) * 128]
 
     def finish(b, carry):
         for l in range(2):
@@ -761,6 +813,8 @@
     lax.fori_loop(0, batch, finish, 0)
     for key in WIDE + NARROW:
         moves[key].finish()
+    for l, _ in enumerate(kv):
+        wo_send(l, 2).wait()
 
 
 def mega(x, dy, key_mask, rel_bias, g_attn, g_mlp, w_q, w_k, w_v, w_o, w_gate, w_lin, w_out, cid):
@@ -776,12 +830,12 @@
     in_hbm = dict(x=by_seg(x), x_rows=x, dy=by_seg(dy), dy_rows=dy, w_q=w_q, w_k=w_k, w_v=w_v, w_o=w_o, w_deal=w_o.reshape(-1, n_cp, quarter, d_model), w_gate=w_gate, w_lin=w_lin, w_out=w_out)
     ins = {key: (value, any_spec) for key, value in in_hbm.items()}
     ins.update(key_mask=(key_mask, VMEM_SPEC), rel_bias=(rel_bias, SMEM_SPEC), g_attn=(g_attn, VMEM_SPEC), g_mlp=(g_mlp, VMEM_SPEC))
-    size = dict(h=d_model, m=d_model, u=ff, gl=2 * ff, qkv=3 * width, o=width)
+    size = dict(h=d_model, m=d_model, u=ff, gl=2 * ff, qkv=3 * width)
     outs = {}
     for key, n in size.items():
         for l in range(2):
             outs['out_%s%d' % (key, l)] = ((batch, rows, n), BF16)
-    for key in ('d0', 'dm0', 'dm1', 'dx'):
+    for key in ('d0', 'dx'):
         outs['out_' + key] = ((batch, n_tp, seg, d_model), BF16)
     for key in WIDE:
         shape = outs['out_' + key][0] if key != 'dy' else x.shape
@@ -789,9 +843,8 @@
     for key in NARROW:
         outs['got_' + key] = ((3,) + outs['out_' + key][0], BF16)
     n_any = len(outs)
-    for key in ('dga0', 'dga1', 'dgm0', 'dgm1'):
-        outs[key] = ((1, d_model), F32)
-    outs['bias_sum'] = ((rel_bias.shape[0], heads, n_cp * rows), F32)
+    outs['small'] = ((4 * d_model // 128 + n_tp, 128), F32)
+    outs['wo_half'] = ((2, 2, width // 2, d_model // 2), BF16)
     vmem = lambda *shape: pltpu.VMEM(shape, BF16)
     wide = lambda *shape: pltpu.VMEM(shape, F32)
     scratch = dict(wqkv=vmem(d_model, 3 * width), wo=vmem(width, d_model), wgl=vmem(d_model, 2 * ff), wout=vmem(ff, d_model), w_cols=vmem(2, n_cp, n_tp, quarter, width), w_now=vmem(n_tp, n_cp, quarter, width),
@@ -805,9 +858,12 @@
         scratch[key] = wide(batch, n_cp, 2 * heads, rows)
     for key in ('q0', 'q1', 'dq', 'x_col'):
         scratch[key] = vmem(batch, rows, width)
-    for key, n in (('hbuf', d_model), ('ubuf', ff), ('gbuf', 2 * ff), ('qbuf', 3 * width), ('obuf', width), ('dybuf', d_model)):
+    for key in ('dga0', 'dga1', 'dgm0', 'dgm1'):
+        scratch[key] = wide(1, d_model)
+    scratch.update(o_own=vmem(2, batch, rows, width), wo_acc=wide(width, d_model), wo_in=wide(2, width, d_model // 2), wo_x=wide(2, width // 2, d_model // 2), sem_wo=dma((2, 2, 3)))
+    for key, n in (('hbuf', d_model), ('ubuf', ff), ('gbuf', 2 * ff), ('qbuf', 3 * width), ('dybuf', d_model)):
         scratch[key] = vmem(2, rows, n)
-    for key in ('o', 'out', 'gl', 'h', 'u', 'g', 'q', 'ob', 'dy', 'deal_in'):
+    for key in ('o', 'out', 'gl', 'h', 'u', 'g', 'q', 'dy', 'deal_in'):
         scratch['sem_' + key] = dma((2,))
     scratch.update(sem_qkv=dma((3,)), sem_in=dma((batch + 3,)), sem_keep=dma((batch,)), sem_mask=dma((2, 3)), sem_deal=dma((2, 2, n_tp)), sem_share=dma((2, 2, 3)),
                    sem_wide=dma((2, len(WIDE), 3)), sem_narrow=dma((2, len(NARROW), 3)))
@@ -831,30 +887,13 @@
     return dict(zip(outs, result))
 
 
-def swap_kernel(n, *refs):
-    halves, wo_part, small, mates, wo_own, wo_mate, total = refs[:n], refs[n], refs[n + 1], refs[n + 2:2 * n + 2], refs[2 * n + 2], refs[2 * n + 3], refs[2 * n + 4]
-    wo_in, wo_sum, wo_x, stage, by_z, sem, s_sem, w_sem = refs[2 * n + 5:]
+def sums_kernel(small, g_attn, g_mlp, g_bias, stage, by_z, sem):
     _, z, y, pair, z_peer = tp_places()
-    me, mate, across, _ = cp_places()
-    core, chip = lax.rem(me, 2), me // 2
-    half = wo_in.shape[-1]
+    _, mate, across, _ = cp_places()
     meet([pair] + z_peer[1:], [mate, across])
-
-    def columns(which):
-        return pl.ds(pl.multiple_of(which * half, half), half)
-
-    first = remote(wo_part.at[:, :, columns(1 - core)], wo_in, w_sem, (0,), 'cp', mate)
-    first.start()
-    swaps = [remote(halves[i], mates[i], sem, (i,), 'cp', mate) for i in range(n)]
-    for copy in swaps:
-        copy.start()
-    first.wait()
-    wo_sum[:] = wo_part[:, :, columns(core)] + wo_in[:]
-    second = remote(wo_sum.at[1 - chip], wo_x, w_sem, (1,), 'cp', across)
-    second.start()
     mine = small
     for k, (axis, peer) in enumerate((('cp', mate), ('cp', across), ('tp', pair))):
-        copy = remote(mine, stage.at[2 * k], s_sem, (k,), axis, peer)
+        copy = remote(mine, stage.at[2 * k], sem, (k,), axis, peer)
         copy.start()
         copy.wait()
         if k < 2:
@@ -862,41 +901,34 @@
             mine = stage.at[2 * k + 1]
         else:
             by_z[z] = mine[:] + stage[2 * k]
-    copies = [remote(by_z.at[z], by_z.at[z], s_sem, (2 + j,), 'tp', z_peer[j]) for j in (1, 2, 3)]
+    copies = [remote(by_z.at[z], by_z.at[z], sem, (2 + j,), 'tp', z_peer[j]) for j in (1, 2, 3)]
     for copy in copies:
         copy.start()
-    second.wait()
-    wo_own[chip] = (wo_sum[chip] + wo_x[:]).astype(BF16)
-    third = remote(wo_own.at[chip], wo_own.at[chip], w_sem, (2,), 'cp', across)
-    third.start()
     for copy in copies:
         copy.wait()
-    total[:] = by_z[0] + by_z[1] + by_z[2] + by_z[3]
-    third.wait()
-    last = remote(wo_own, wo_mate, w_sem, (3,), 'cp', mate)
-    last.start()
-    for copy in swaps + [last]:
-        copy.wait()
-
-
-def swap(halves, wo_part, small, cid):
-    n = len(halves)
-    layers, width, d_model = wo_part.shape
-    half = d_model // 2
-    any_spec = pl.BlockSpec(memory_space=pl.ANY)
-    dma = pltpu.SemaphoreType.DMA
-    wo_shape = jax.ShapeDtypeStruct((layers, width, half), BF16)
-    result = pl.pallas_call(
-        functools.partial(swap_kernel, n),
-        out_shape=tuple(jax.ShapeDtypeStruct(h.shape, h.dtype) for h in halves) + (wo_shape, wo_shape, jax.ShapeDtypeStruct(small.shape, F32)),
-        in_specs=[any_spec] * n + [VMEM_SPEC] * 2,
-        out_specs=tuple([any_spec] * n + [VMEM_SPEC] * 3),
-        scratch_shapes=[pltpu.VMEM((layers, width, half), F32), pltpu.VMEM((layers, width, half), F32), pltpu.VMEM((width, half), F32),
-                        pltpu.VMEM((5,) + small.shape, F32), pltpu.VMEM((4,) + small.shape, F32), dma((2, n)), dma((2, 6)), dma((2, 4))],
-        compiler_params=comm_params(cid, 24),
-        name='swap',
-    )(*halves, wo_part, small)
-    return list(result[:n]), result[n], result[n + 1], result[n + 2]
+    total = by_z[0] + by_z[1] + by_z[2] + by_z[3]
+    lanes = total.shape[1]
+    n_lines = g_attn.shape[1] // lanes
+    for i, ref in enumerate((g_attn, g_mlp)):
+        for l in range(2):
+            for k in range(n_lines):
+                first = (2 * i + l) * n_lines + k
+                ref[l:l + 1, k * lanes:(k + 1) * lanes] = total[first:first + 1]
+    own = lax.broadcasted_iota(jnp.int32, (8, lanes), 0) == lax.axis_index('tp')
+    g_bias[:] = jnp.sum(jnp.where(own, total[4 * n_lines:], 0.0), axis=0, keepdims=True)
+
+
+def sums(small, d_model, cid):
+    return pl.pallas_call(
+        sums_kernel,
+        out_shape=(jax.ShapeDtypeStruct((2, d_model), F32), jax.ShapeDtypeStruct((2, d_model), F32), jax.ShapeDtypeStruct((1, 128), F32)),
+        in_specs=[VMEM_SPEC],
+        out_specs=(VMEM_SPEC,) * 3,
+        scratch_shapes=[pltpu.VMEM((5,) + small.shape, F32), pltpu.VMEM((4,) + small.shape, F32), pltpu.SemaphoreType.DMA((2, 6))],
+        compiler_params=comm_params(cid, 4),
+        cost_estimate=cost(10),
+        name='sums',
+    )(small)
 
 
 def place_kernel(plan, n_out, *refs):
@@ -904,7 +936,11 @@
     owns, mates, outs = refs[:n], refs[n:2 * n], refs[2 * n:2 * n + n_out]
     bufs, in_sem, out_sem = refs[2 * n + n_out:4 * n + n_out], refs[4 * n + n_out], refs[4 * n + n_out + 1]
     core = lax.rem(lax.axis_index('cp'), 2)
-    loads = [pltpu.make_async_copy(src, buf, in_sem.at[i]) for i, (src, buf) in enumerate(zip(owns + mates, bufs))]
+    loads = []
+    for src, buf in zip(owns + mates, bufs):
+        if len(src.shape) > len(buf.shape):
+            src = src.at[plan[len(loads) % n][0]]
+        loads.append(pltpu.make_async_copy(src, buf, in_sem.at[len(loads)]))
     for load in loads:
         load.start()
     stores = []
@@ -935,7 +971,7 @@
         out_shape=tuple(jax.ShapeDtypeStruct(s, BF16) for s in out_shapes),
         in_specs=[any_spec] * (2 * n),
         out_specs=tuple([any_spec] * len(out_shapes)),
-        scratch_shapes=[pltpu.VMEM(a.shape, BF16) for a in list(owns) + list(mates)] + [pltpu.SemaphoreType.DMA((2 * n,)), pltpu.SemaphoreType.DMA((n_stores,))],
+        scratch_shapes=[pltpu.VMEM(a.shape[-2:], BF16) for a in list(owns) + list(mates)] + [pltpu.SemaphoreType.DMA((2 * n,)), pltpu.SemaphoreType.DMA((n_stores,))],
         compiler_params=pltpu.CompilerParams(vmem_limit_bytes=40 * MIB),
         name='place',
     )(*owns, *mates)
@@ -952,7 +988,6 @@
         tokens = batch * rows
         n_layers = w_q.shape[0]
         n_buckets, heads = rel_bias.shape
-        tp_index = lax.axis_index('tp')
         core = lax.rem(lax.axis_index('cp'), 2)
         half = d_model // 2
 
@@ -971,18 +1006,11 @@
             return (dot_tn(a, b) + dot_tn(a_g, b_g)).astype(BF16)
 
         owns = [grad('h0', 'qkv0', True), grad('h1', 'qkv1', True), grad('m0', 'gl0', True), grad('m1', 'gl1', True), grad('u0', 'd0', False), grad('u1', 'dy', False)]
-        wo_part = jnp.stack([dot_tn(flat(m['out_o%d' % l]), m['out_dm%d' % l].reshape(tokens, d_model)) for l in range(n_layers)])
-        slots = jnp.zeros((8, n_buckets * heads), F32)
-        slots = lax.dynamic_update_slice(slots, jnp.sum(m['bias_sum'], axis=-1).reshape(1, -1), (tp_index, jnp.int32(0)))
-        small = jnp.concatenate([part.reshape(-1, 128) for part in (m['dga0'], m['dga1'], m['dgm0'], m['dgm1'], slots)], axis=0)
-        mates, wo_own, wo_mate, small = swap(owns, wo_part, small, 1)
-        n_gain = n_layers * d_model // 128
-        d_g_attn = small[:n_gain].reshape(n_layers, d_model)
-        d_g_mlp = small[n_gain:2 * n_gain].reshape(n_layers, d_model)
-        d_rel = lax.dynamic_slice(small[2 * n_gain:], (tp_index, jnp.int32(0)), (1, n_buckets * heads)).reshape(n_buckets, heads)
+        owns += [m['wo_half'].reshape(n_layers, -1, half)]
+        mates = [lax.ppermute(part, 'cp', [(0, 1), (1, 0), (2, 3), (3, 2)]) for part in owns]
+        d_g_attn, d_g_mlp, d_rel = sums(m['small'], d_model, 1)
         plan = tuple((layer, by_rows, first, n) for by_rows, first, n in ((True, 0, 3), (True, 4, 2), (False, 6, 1), (False, 3, 1)) for layer in range(n_layers))
-        wo_halves = [[w[l] for l in range(n_layers)] for w in (wo_own, wo_mate)]
-        grads = place(plan, owns + wo_halves[0], mates + wo_halves[1], [w.shape for w in (w_q, w_k, w_v, w_o, w_gate, w_lin, w_out)])
-        return (m['out_dx'].reshape(batch, rows, d_model), d_rel, d_g_attn, d_g_mlp) + tuple(grads)
+        grads = place(plan, owns + owns[-1:], mates + mates[-1:], [w.shape for w in (w_q, w_k, w_v, w_o, w_gate, w_lin, w_out)])
+        return (m['out_dx'].reshape(batch, rows, d_model), d_rel.reshape(n_buckets, heads), d_g_attn, d_g_mlp) + tuple(grads)
 
     return jax.shard_map(local_program, mesh=mesh, in_specs=(seq_spec, seq_spec, P(None, 'cp'), P(None, 'tp')) + weight_specs, out_specs=(seq_spec, P(None, 'tp')) + weight_specs, check_vma=False)

time: 700 us -> 655 us (0.936)
  Pallas kernels: 633 us -> 599 us
  local copies, waits for them, and re-layouts: 21.1 us -> 12.5 us
    pallas_call x1, Pallas kernels: 55.5 us -> 16.5 us  [sums(): pl.pallas_call(sums_kernel, out_shape=(jax.ShapeDtypeStruct((2, d_model),...]
    unnamed x73 -> x65, local copies, waits for them, and re-layouts: 19.3 us -> 11.9 us
    dot_general x14 -> x12, matrix products: 30 us -> 32.9 us  [dot_tn(): lax.dot_general(a, b, (((0,), (0,)), ((), ())), preferred_element_type=F32)]
  transfers between devices with their start and end apart: 0 -> 7, of which waited for: 0 -> 0; matrix products, arithmetic and copies ran while one was open for 0% -> 4% of each run, Pallas kernels for 0% -> 3%
where the time goes in v6:
time: 655 us; the launch traced here: 648 us
  Pallas kernels  599 us (91%)
  matrix products  32.9 us (5%)
  local copies, waits for them, and re-layouts  12.5 us (2%)
    pallas_call x1, Pallas kernels, mega(): pl.pallas_call(functools.partial(mega_kernel, list(ins) + list(outs) + li...  567 us
    dot_general x12, matrix products, dot_tn(): lax.dot_general(a, b, (((0,), (0,)), ((), ())), preferred_element_type=F32)  32.9 us
    pallas_call x1, Pallas kernels, sums(): pl.pallas_call(sums_kernel, out_shape=(jax.ShapeDtypeStruct((2, d_model),...  16.5 us
    pallas_call x1, Pallas kernels, place(): pl.pallas_call(functools.partial(place_kernel, plan, len(out_shapes)), ou...  15 us
  transfers between devices with their start and end apart: 7, of which 0 were waited for; matrix products, arithmetic and copies ran while one was open for 4% of the time, Pallas kernels for 3%

profile of v6, /device:TPU:0, one launch (start us, length us, event | category | flops | bytes accessed | tf_op | source)
XLA Modules:
  0.0 647.8 jit_solution(7181023088793088949)
XLA Ops:
  0.6 1.4 copy.31.refs_13_
  2.0 567.0 %mega.1 = (bf16[4,128,2048]{2,1,0:T(8,128)(2,1)}, bf16[4,128,2048]{2,1,0:T(8,128)(2,1)}, bf16[4,128,2048]{2,1,0:T(8,128)(2,1)}, bf16[4,128,2048]{2,1,0:T(8,128)(...) custom-call(bf16[4,8,16,2048]{3,2,1,0:T(8,128)(2,1)} %bitcast.80, ...), custom_call_target="tpu_custom_call" | custom-call | flops 314572800000 | bytes 8388608 | tf_op jit(solution)/shard_map/mega/pallas_call | solution.py:877
  569.0 0.0 copy-start.27
  569.0 0.0 copy-start.29
  569.0 2.6 fusion.12
  571.6 0.0 copy-done.27
  571.6 0.5 copy-done.29
  572.2 3.9 fusion.3.refs_0_
  576.1 0.0 collective-permute-start
  576.1 0.0 copy-done.23
  576.1 0.0 copy-done.25
  576.1 0.0 copy-start.11
  576.1 0.0 copy-start.16
  576.1 4.3 fusion.20
  580.5 0.0 copy-done.11
  580.5 0.0 copy-done.16
  580.5 0.0 copy-start.22
  580.5 0.0 copy-start.24
  580.5 3.1 fusion.1.refs_2_
  583.6 0.5 collective-permute-start.2
  584.1 0.0 copy-done.22
  584.1 0.4 copy-done.24
  584.5 4.3 fusion.21
  588.9 3.3 fusion.refs_3_
  592.2 0.5 collective-permute-start.3
  592.7 0.0 copy-done.18
  592.7 2.3 fusion.22
  595.0 0.9 add_convert_fusion.refs_4_
  595.9 0.1 collective-permute-start.4
  596.0 0.2 copy-done
  596.2 0.3 collective-permute-start.6
  596.5 0.4 copy-done.19
  596.9 0.2 copy-done.21
  597.0 1.0 fusion.10
  598.1 0.0 copy-start.26
  598.1 0.0 copy-done.12
  598.1 0.7 copy-done.14
  598.9 0.9 fusion.5
  599.7 1.0 copy-done.26
  600.7 4.0 fusion.2.refs_1_
  604.6 0.0 collective-permute-done.6.refs_14_.refs_15_
  604.6 0.0 collective-permute-start.1
  604.7 0.0 copy-done.9
  604.7 2.3 fusion.4.refs_5_
  607.0 0.0 collective-permute-done.4.refs_12_
  607.0 0.0 copy-start.4
  607.1 0.5 collective-permute-start.5
  607.6 16.5 %sums.1 = (f32[2,2048]{1,0:T(2,128)S(1)}, f32[2,2048]{1,0:T(2,128)S(1)}, f32[1,128]{1,0:T(1,128)S(1)}) custom-call(f32[72,128]{1,0:T(8,128)S(1)} %copy-done.6), custom_call_target="tpu_custom_call" | custom-call | flops 10485760000 | bytes 8388608 | tf_op jit(solution)/shard_map/sums/pallas_call | solution.py:922
  624.2 0.5 broadcast.4
  624.7 0.7 reduce.3
  625.3 0.1 reshape.96
  625.4 0.7 copy.37
  626.1 0.0 collective-permute-done.5.refs_13_
  626.1 0.0 collective-permute-done.refs_8_
  626.1 0.0 collective-permute-done.1.refs_9_
  626.1 0.0 collective-permute-done.2.refs_10_
  626.1 0.0 collective-permute-done.3.refs_11_
  626.1 1.2 copy-done.1
  627.4 1.2 copy-done.3
  628.6 1.3 copy-done.5
  629.9 15.0 %place.1 = (bf16[2,2048,256]{2,1,0:T(8,128)(2,1)}, bf16[2,2048,256]{2,1,0:T(8,128)(2,1)}, bf16[2,2048,256]{2,1,0:T(8,128)(2,1)}, bf16[2,256,2048]{2,1,0:T(8,128)...) custom-call(bf16[1024,768]{1,0:T(8,128)(2,1)} %fusion.3.refs_0_, ...), custom_call_target="tpu_custom_call" | custom-call | tf_op jit(solution)/shard_map/place/pallas_call | solution.py:969
  644.9 1.3 copy.51
  646.3 0.6 copy.52
  646.9 0.6 copy.53
  (33 shorter events, 0.1 us)
Async XLA Ops:
  569.0 2.7 copy-start.27
  569.0 3.2 copy-start.29
  572.2 3.9 copy-start.23
  572.2 3.9 copy-start.25
  576.1 50.0 %collective-permute-start = (bf16[1024,768]{1,0:T(8,128)(2,1)}, bf16[1024,768]{1,0:T(8,128)(2,1)}, u32[]{:S(2)}, u32[]{:S(2)}) collective-permute-start(bf16[1024,768]{1,0:T(8,128)(2,1)} %fusion.3.refs_0_), channel_id=1, source_target_pairs={{0,1},{1,0},{2,3},{3,2},{4,5},{5,4},{6,7},{7,6},{8,9},{9,8},{10,11... | collective-permute-start | bytes 4718600 | tf_op jit(solution)/shard_map/ppermute | solution.py:1010
  576.1 4.4 copy-start.11
  576.1 4.4 copy-start.16
  580.5 3.6 copy-start.22
  580.5 4.0 copy-start.24
  583.6 42.5 %collective-permute-start.2 = (bf16[1024,1280]{1,0:T(8,128)(2,1)}, bf16[1024,1280]{1,0:T(8,128)(2,1)}, u32[]{:S(2)}, u32[]{:S(2)}) collective-permute-start(bf16[1024,1280]{1,0:T(8,128)(2,1)} %fusion.1.refs_2_), channel_id=1, source_target_pairs={{0,1},{1,0},{2,3},{3,2},{4,5},{5,4},{6,7},{7,6},{8,9},{9,8},{10,11... | collective-permute-start | bytes 7864328 | tf_op jit(solution)/shard_map/ppermute | solution.py:1010
  584.5 4.4 copy-start.10
  584.5 4.4 copy-start.15
  588.9 3.8 copy-start.18
  588.9 3.8 copy-start.20
  592.2 34.0 %collective-permute-start.3 = (bf16[1024,1280]{1,0:T(8,128)(2,1)}, bf16[1024,1280]{1,0:T(8,128)(2,1)}, u32[]{:S(2)}, u32[]{:S(2)}) collective-permute-start(bf16[1024,1280]{1,0:T(8,128)(2,1)} %fusion.refs_3_), channel_id=1, source_target_pairs={{0,1},{1,0},{2,3},{3,2},{4,5},{5,4},{6,7},{7,6},{8,9},{9,8},{10,11... | collective-permute-start | bytes 7864328 | tf_op jit(solution)/shard_map/ppermute | solution.py:1010
  592.7 2.3 copy-start.13
  592.7 2.3 copy-start.17
  595.0 1.2 copy-start
  595.0 1.9 copy-start.19
  595.0 2.1 copy-start.21
  595.9 11.2 %collective-permute-start.4 = (bf16[640,1024]{1,0:T(8,128)(2,1)S(1)}, bf16[640,1024]{1,0:T(8,128)(2,1)S(1)}, u32[]{:S(2)}, u32[]{:S(2)}) collective-permute-start(bf16[640,1024]{1,0:T(8,128)(2,1)S(1)} %add_convert_fusion.refs_4_), channel_id=1, source_target_pairs={{0,1},{1,0},{2,3},{3,2},{4,5},{5,4},{6,7},{7,6},{8,9},{9,8},{10,11... | collective-permute-start | bytes 3932168 | tf_op jit(solution)/shard_map/ppermute | solution.py:1010
  596.2 8.5 %collective-permute-start.6 = (bf16[2,256,1024]{2,1,0:T(8,128)(2,1)S(1)}, bf16[2,256,1024]{2,1,0:T(8,128)(2,1)S(1)}, u32[]{:S(2)}, u32[]{:S(2)}) collective-permute-start(bf16[2,256,1024]{2,1,0:T(8,128)(2,1)S(1)} %bitcast.67), channel_id=1, source_target_pairs={{0,1},{1,0},{2,3},{3,2},{4,5},{5,4},{6,7},{7,6},{8,9},{9,8},{10,11... | collective-permute-start | bytes 3145736 | tf_op jit(solution)/shard_map/ppermute | solution.py:1010
  597.0 1.1 copy-start.12
  597.0 1.8 copy-start.14
  597.0 2.7 copy-start.28
  598.1 2.6 copy-start.26
  600.7 4.0 copy-start.7
  600.7 4.0 copy-start.9
  604.6 2.4 copy-start.2
  604.6 21.5 %collective-permute-start.1 = (bf16[1024,768]{1,0:T(8,128)(2,1)}, bf16[1024,768]{1,0:T(8,128)(2,1)}, u32[]{:S(2)}, u32[]{:S(2)}) collective-permute-start(bf16[1024,768]{1,0:T(8,128)(2,1)} %fusion.2.refs_1_), channel_id=1, source_target_pairs={{0,1},{1,0},{2,3},{3,2},{4,5},{5,4},{6,7},{7,6},{8,9},{9,8},{10,11... | collective-permute-start | bytes 4718600 | tf_op jit(solution)/shard_map/ppermute | solution.py:1010
  604.7 2.9 copy-start.6
  607.0 17.1 %copy-start.4 = (bf16[640,1024]{1,0:T(8,128)(2,1)}, bf16[640,1024]{1,0:T(8,128)(2,1)S(1)}, u32[]{:S(2)}) copy-start(bf16[640,1024]{1,0:T(8,128)(2,1)S(1)} %collective-permute-done.4.refs_12_) | copy-start | bytes 3932164
  607.1 19.1 %collective-permute-start.5 = (bf16[640,1024]{1,0:T(8,128)(2,1)S(1)}, bf16[640,1024]{1,0:T(8,128)(2,1)}, u32[]{:S(2)}, u32[]{:S(2)}) collective-permute-start(bf16[640,1024]{1,0:T(8,128)(2,1)S(1)} %fusion.4.refs_5_), channel_id=1, source_target_pairs={{0,1},{1,0},{2,3},{3,2},{4,5},{5,4},{6,7},{7,6},{8,9},{9,8},{10,11... | collective-permute-start | bytes 3932168 | tf_op jit(solution)/shard_map/ppermute | solution.py:1010
  626.1 1.2 copy-start.1
  627.4 1.2 copy-start.3
  628.6 1.3 copy-start.5
  629.9 15.0 %copy-start.8 = (bf16[4,8,16,2048]{3,2,1,0:T(8,128)(2,1)S(1)}, bf16[4,8,16,2048]{3,2,1,0:T(8,128)(2,1)}, u32[]{:S(2)}) copy-start(bf16[4,8,16,2048]{3,2,1,0:T(8,128)(2,1)} %get-tuple-element.47) | copy-start | bytes 6291460

commit v7 on v6

--- a/solution.py
+++ b/solution.py
@@ -268,8 +268,8 @@
 
 
 class Narrow:
-    def __init__(self, src, dst, sem, index):
-        self.src, self.dst, self.sem, self.index = src, dst, sem, index
+    def __init__(self, dst, sem, index):
+        self.src, self.dst, self.sem, self.index = dst.at[3], dst, sem, index
         _, self.mate, self.across, _ = cp_places()
 
     def copy(self, r, window):
@@ -293,16 +293,25 @@
 
 
 class Spill:
-    def __init__(self, slots, sem):
-        self.slots, self.sem = slots, sem
-
-    def copy(self, out, b):
+    def __init__(self, slots, sem, columns=None):
+        self.slots, self.sem, self.columns = slots, sem, columns
+
+    def copies(self, out, own, b):
         slot = lax.rem(b, 2)
-        return pltpu.make_async_copy(self.slots.at[slot], out.at[b], self.sem.at[slot])
-
-    def put(self, out, b, value):
+        src = self.slots.at[slot]
+        copies = [] if out is None else [pltpu.make_async_copy(src, out.at[b], self.sem.at[1, slot])]
+        if self.columns is not None:
+            src = src.at[:, self.columns]
+        return copies + [pltpu.make_async_copy(src, own.at[3, b], self.sem.at[0, slot])]
+
+    def put(self, out, own, b, value):
         self.slots[lax.rem(b, 2)] = value
-        self.copy(out, b).start()
+        for copy in self.copies(out, own, b):
+            copy.start()
+
+    def wait(self, out, own, b):
+        for copy in self.copies(out, own, b):
+            copy.wait()
 
 
 def norm_rows(rows, gain):
@@ -314,7 +323,7 @@
     x_f = x_shard.astype(F32)
     inv_rms = lax.rsqrt(jnp.mean(x_f * x_f, axis=-1, keepdims=True) + NORM_EPS)
     normed = x_f * inv_rms
-    d_gain_ref[:] += jnp.sum(d_norm * normed, axis=0, keepdims=True)
+    d_gain_ref[:] += col_sum(d_norm * normed)
     d_normed = d_norm * gain
     d_x = inv_rms * (d_normed - normed * jnp.mean(d_normed * normed, axis=-1, keepdims=True))
     return (res.astype(F32) + d_x).astype(BF16)
@@ -328,6 +337,10 @@
 
 def row_sum(x):
     return jnp.sum(x, axis=1, keepdims=True)
+
+
+def col_sum(x):
+    return jnp.sum(x, axis=0, keepdims=True)
 
 
 def row_max(x):
@@ -398,38 +411,38 @@
     seq = rows_ref.shape[1]
 
     def strip(i, carry):
-        first = pl.multiple_of(i * 8, 8)
-        rel = lax.broadcasted_iota(jnp.int32, (8, seq), 1) - lax.broadcasted_iota(jnp.int32, (8, seq), 0) - me * rows - first
+        first = pl.multiple_of(i * SUBLANES, SUBLANES)
+        rel = lax.broadcasted_iota(jnp.int32, (SUBLANES, seq), 1) - lax.broadcasted_iota(jnp.int32, (SUBLANES, seq), 0) - me * rows - first
         for is_col in (False, True):
             buckets = rel_bucket(-rel if is_col else rel)
-            vals = [jnp.zeros((8, seq), F32) for _ in range(heads)]
+            vals = [jnp.zeros((SUBLANES, seq), F32) for _ in range(heads)]
             for k in range(n_buckets):
                 hit = buckets == k
                 vals = [jnp.where(hit, table_ref[k, h], v) for h, v in enumerate(vals)]
             for h, v in enumerate(vals):
                 if is_col:
                     for q in range(seq // rows):
-                        cols_ref[q, pl.ds(first, 8), h * rows:(h + 1) * rows] = v[:, q * rows:(q + 1) * rows]
+                        cols_ref[q, pl.ds(first, SUBLANES), h * rows:(h + 1) * rows] = v[:, q * rows:(q + 1) * rows]
                 else:
-                    rows_ref[pl.ds(pl.multiple_of(h * rows + first, 8), 8), :] = v
+                    rows_ref[pl.ds(pl.multiple_of(h * rows + first, SUBLANES), SUBLANES), :] = v
         return carry
 
-    lax.fori_loop(0, rows // 8, strip, 0)
-
-
-def bucket_sums(ds_ref, heads, n_buckets, me):
+    lax.fori_loop(0, rows // SUBLANES, strip, 0)
+
+
+def bucket_sums(ds_ref, heads, lines_ref, me):
     rows, seq = ds_ref.shape[0] // heads, ds_ref.shape[1]
     rel = lax.broadcasted_iota(jnp.int32, (rows, seq), 1) - lax.broadcasted_iota(jnp.int32, (rows, seq), 0) - me * rows
-    lane = lax.broadcasted_iota(jnp.int32, (1, n_buckets * heads), 1)
-
-    def step(k, acc):
-        hit = rel_bucket(rel) == k
-        for h in range(heads):
-            total = jnp.sum(row_sum(jnp.where(hit, ds_ref[h * rows:(h + 1) * rows], 0.0)), axis=0, keepdims=True)
-            acc = jnp.where(lane == k * heads + h, total, acc)
-        return acc
-
-    return lax.fori_loop(0, n_buckets, step, jnp.zeros(lane.shape, F32))
+    buckets = rel_bucket(rel)
+
+    def step(k, carry):
+        hit = buckets == k
+        lines_ref[k] = jnp.concatenate([col_sum(jnp.where(hit, ds_ref[h * rows:(h + 1) * rows], 0.0)) for h in range(heads)], axis=0)
+        return carry
+
+    lax.fori_loop(0, lines_ref.shape[0], step, 0)
+    totals = row_sum(jnp.concatenate([lines_ref[k] for k in range(lines_ref.shape[0])], axis=0))
+    return jnp.transpose(jnp.broadcast_to(totals, (totals.shape[0],) * 2))[:1]
 
 
 class Refs:
@@ -438,11 +451,12 @@
 
 WIDE = ('h0', 'h1', 'm0', 'm1', 'dy', 'd0')
 NARROW = ('u0', 'u1', 'gl0', 'gl1', 'qkv0', 'qkv1')
+LANES = 128
+SUBLANES = 8
 LETTERS = string.ascii_letters
-STEPS = '0303221222210111101101010101101101123'
-ORDER = 'FaKGeCtbdqpHlkExvozmjiwshfuBJnDIcAgyr'
-PASS_FROM = 34
-GIVES = tuple(zip(('h0', 'dy', 'u0', 'm0', 'h1', 'u1', 'm1', 'gl1', 'd0', 'qkv1', 'gl0', 'qkv0'), map(LETTERS.index, 'ddmvxzABDHHJ')))
+STEPS = '0302321222210111101101010101101101123'
+ORDER = 'FaKGeCtbdqpHlkExvozmjiwshfuBJynDIcAgr'
+GIVES = tuple(zip(('h0', 'dy', 'u0', 'm0', 'h1', 'u1', 'm1', 'gl1', 'd0', 'qkv1', 'gl0', 'qkv0'), map(LETTERS.index, 'demvxzABDGHJ')))
 
 
 def mega_kernel(names, heads, *refs):
@@ -492,7 +506,7 @@
     def wo_send(l, step):
         src, dst, peer = (
             (r.wo_acc.at[:, half_of(1 - core)], r.wo_in.at[l], mate),
-            (r.wo_in.at[l, pl.ds(pl.multiple_of((1 - chip) * (width // 2), 8), width // 2)], r.wo_x.at[l], across),
+            (r.wo_in.at[l, pl.ds(pl.multiple_of((1 - chip) * (width // 2), SUBLANES), width // 2)], r.wo_x.at[l], across),
             (r.wo_half.at[l, chip], r.wo_half.at[l, chip], across))[step]
         return remote(src, dst, r.sem_wo, (l, step), 'cp', peer)
 
@@ -509,7 +523,7 @@
     def wo_third(l):
         def go():
             wo_send(l, 1).wait()
-            mine = r.wo_in[l, pl.ds(pl.multiple_of(chip * (width // 2), 8), width // 2)]
+            mine = r.wo_in[l, pl.ds(pl.multiple_of(chip * (width // 2), SUBLANES), width // 2)]
             r.wo_half[l, chip] = (mine + r.wo_x[l]).astype(BF16)
             wo_send(l, 2).start()
         return go
@@ -569,17 +583,16 @@
 
     for ref in (r.ds_sum, r.dga0, r.dga1, r.dgm0, r.dgm1):
         ref[:] = jnp.zeros_like(ref)
-    bias_tables(r.rel_bias, me, r.bias_rows, r.bias_cols)
     for copy in rows_in + shards_in:
         copy.wait()
     loaded('qkv', 0)()
 
-    hold = dict(h=Spill(r.hbuf, r.sem_h), u=Spill(r.ubuf, r.sem_u), gl=Spill(r.gbuf, r.sem_g), qkv=Spill(r.qbuf, r.sem_q))
+    hold = dict(h=Spill(r.hbuf, r.sem_h, half_of(core)), u=Spill(r.ubuf, r.sem_u), gl=Spill(r.gbuf, r.sem_g), qkv=Spill(r.qbuf, r.sem_q))
     moves = {}
     for i, key in enumerate(WIDE):
         moves[key] = Wide(r.dy_rows if key == 'dy' else getattr(r, 'out_' + key), getattr(r, 'got_' + key), r.sem_wide, i)
     for i, key in enumerate(NARROW):
-        moves[key] = Narrow(getattr(r, 'out_' + key), getattr(r, 'got_' + key), r.sem_narrow, i)
+        moves[key] = Narrow(getattr(r, 'got_' + key), r.sem_narrow, i)
     kv = [Trade(store, r.sem_kv, l) for l, store in enumerate((r.kv0, r.kv1))]
     qdo = [Trade(store, r.sem_qdo, l) for l, store in enumerate((r.qdo0, r.qdo1))]
     q_own = (r.q0, r.q1)
@@ -589,12 +602,13 @@
         ref = stats[l].at[b, me]
         return remote(ref, ref, r.sem_stats, (l, i, b), 'cp', others[i])
 
-    def out(key, l):
-        return getattr(r, 'out_%s%d' % (key, l))
+    def places(key, l):
+        tag = '%s%d' % (key, l)
+        return getattr(r, 'out_' + tag, None), getattr(r, 'got_' + tag)
 
     def project(l, b, flat):
         h = norm_rows(flat, r.g_attn[l:l + 1])
-        hold['h'].put(out('h', l), b, h)
+        hold['h'].put(*places('h', l), b, h)
         qkv = dot_nn(h, r.wqkv[:]).astype(BF16)
         q_own[l][b] = qkv[:, :width]
         kv[l].store[b, me] = qkv[:, width:]
@@ -640,11 +654,11 @@
         window = pl.ds(pl.multiple_of(ring.seg * seg, seg), seg)
         shard[b] = jnp.concatenate([r.x_all[b, t, window] for t in range(n_seg)], axis=1)
         h2 = norm_rows(gather_x.rows(b), r.g_mlp[l:l + 1])
-        hold['h'].put(out('m', l), b, h2)
+        hold['h'].put(*places('m', l), b, h2)
         both = dot_nn(h2, r.wgl[:])
         gate, lin = both[:, :ff], both[:, ff:]
         u = (gelu_parts(gate)[0] * lin).astype(BF16)
-        hold['u'].put(out('u', l), b, u)
+        hold['u'].put(*places('u', l), b, u)
         return gate, lin, u
 
     def stage_mlp0(b):
@@ -662,16 +676,21 @@
         slot = lax.rem(b, 2)
         return pltpu.make_async_copy(r.dy_rows.at[b], r.dybuf.at[slot], r.sem_dy.at[slot])
 
-    def mlp_backward(l, b, d, gate, lin, copy=None):
+    def dy_own(b):
+        slot = lax.rem(b, 2)
+        return pltpu.make_async_copy(r.dybuf.at[slot, :, half_of(core)], r.got_dy.at[3, b], r.sem_dy_own.at[slot])
+
+    def mlp_backward(l, b, d, gate, lin, copies=()):
         dgl = mlp_pull(dot_nt(d, r.wout[:]), gate, lin)
-        hold['gl'].put(out('gl', l), b, dgl)
-        if copy is not None:
+        hold['gl'].put(*places('gl', l), b, dgl)
+        for copy in copies:
             copy.wait()
         ring.send_partial(b, dot_nt(dgl, r.wgl[:]))
 
     def stage_mlp1(b):
         gate, lin, _ = mlp_forward(1, b, r.x1s1)
         dy_in(b).wait()
+        dy_own(b).start()
         mlp_backward(1, b, r.dybuf[lax.rem(b, 2)], gate, lin)
 
     def keep(dst, b):
@@ -712,14 +731,15 @@
             mask_col = jnp.transpose(jnp.broadcast_to(r.key_add[b], (rows, rows)))[:, :1]
             d_kv = attend_cols_back(heads, kv[l].store[b, me], mask_col, r.bias_cols, lambda s: qdo[l].store[b, s], lambda s: stats[l][b, s])
             d_qkv = jnp.concatenate([r.dq[b], d_kv], axis=1)
-            hold['qkv'].put(out('qkv', l), b, d_qkv)
+            hold['qkv'].put(*places('qkv', l), b, d_qkv)
             ring.send_partial(b, dot_nt(d_qkv, r.wqkv[:]))
         return go
 
     def stage_mlp_back0(b):
         ring.arrive(b)
-        copy = keep(r.out_d0, b)
-        mlp_backward(0, b, ring.rows(b), r.gate[b], r.lin[b], copy)
+        copies = [keep(r.out_d0, b), pltpu.make_async_copy(ring.full.at[b, :, :, half_of(core)], r.got_d0.at[3, b], r.sem_d0.at[b])]
+        copies[1].start()
+        mlp_backward(0, b, ring.rows(b), r.gate[b], r.lin[b], copies)
 
     def stage_last(b):
         ring.arrive(b)
@@ -729,7 +749,7 @@
         return [('at' + tag, stage_attend(l)), ('', gather_o.forward), ('col' + tag, stage_columns(l)), ('', gather_x.forward)]
 
     def by_sum(tag, start, finish):
-        return [(tag, start), ('', ring.reduce_pair), ('', finish), ('', ring.forward)]
+        return [(tag, start), ('', ring.reduce_pair), ('sum' + tag[-1], finish), ('', ring.forward)]
 
     stages = (
         [('first', stage_first), ('', kv[0].pass_on)] + by_columns('0', 0)
@@ -748,30 +768,75 @@
     use = lambda tag: lag_of[tag]
     after = lambda tag: lag_of[tag] + batch
 
-    def masked():
+    def tables():
+        bias_tables(r.rel_bias, me, r.bias_rows, r.bias_cols)
         for copy in masks:
             copy.wait()
 
+    n_lines = d_model // LANES
+
     def count_buckets():
-        r.small[-n_seg:] = jnp.where(lax.broadcasted_iota(jnp.int32, (n_seg, 128), 0) == tp_me, bucket_sums(r.ds_sum, heads, r.rel_bias.shape[0], me), 0.0)
+        r.by_z[ring.z, 4 * n_lines:] = jnp.where(lax.broadcasted_iota(jnp.int32, (n_seg, LANES), 0) == tp_me, bucket_sums(r.ds_sum, heads, r.lines, me), 0.0)
+
+    def all_gather_z(j):
+        ref = r.by_z.at[ring.z]
+        return remote(ref, ref, r.sem_all, (j,), 'tp', ring.z_peer[j])
+
+    def all_start():
+        for i, ref in enumerate((r.dga0, r.dga1, r.dgm0, r.dgm1)):
+            for k in range(n_lines):
+                r.by_z[ring.z, i * n_lines + k:i * n_lines + k + 1] = ref[:, k * LANES:(k + 1) * LANES]
+        for j in Z_STEPS:
+            all_gather_z(j).start()
+
+    def all_step(k):
+        axis, peer = (('tp', ring.pair), ('cp', mate), ('cp', across))[k]
+        return remote(r.stage.at[k], r.stage_in.at[k], r.sem_all, (4 + k,), axis, peer)
+
+    def all_sum(k):
+        all_step(k).wait()
+        return r.stage[k] + r.stage_in[k]
+
+    def all_next(k):
+        def go():
+            if k == 0:
+                for j in Z_STEPS:
+                    all_gather_z(j).wait()
+                r.stage[k] = r.by_z[0] + r.by_z[1] + r.by_z[2] + r.by_z[3]
+            else:
+                r.stage[k] = all_sum(k - 1)
+            all_step(k).start()
+        return go
+
+    def all_end():
+        total = all_sum(2)
+        for i, ref in enumerate((r.g_attn_out, r.g_mlp_out)):
+            for l in range(2):
+                for k in range(n_lines):
+                    first = (2 * i + l) * n_lines + k
+                    ref[l:l + 1, k * LANES:(k + 1) * LANES] = total[first:first + 1]
+        own = lax.broadcasted_iota(jnp.int32, (n_seg, LANES), 0) == tp_me
+        r.g_bias[:] = col_sum(jnp.where(own, total[4 * n_lines:], 0.0))
 
     once = [
-        (use('at0'), masked), (use('mlp0'), loaded('gl', 0)), (use('mlp0'), loaded('out', 0)),
-        (batch, share_start(0)), (batch + 1, share_pass(0)), (use('col0'), shared(0)), (batch, share_start(1)), (after('col0'), share_pass(1)), (use('col1'), shared(1)),
+        (use('at0'), tables), (use('mlp0'), loaded('gl', 0)), (use('mlp0'), loaded('out', 0)),
+        (batch - 1, share_start(0)), (batch - 1, share_start(1)), (batch + 1, share_pass(0)), (use('col0'), shared(0)), (use('col0'), share_pass(1)), (use('col1'), shared(1)),
         (after('first'), load('qkv', 1)), (use('next'), loaded('qkv', 1)),
         (after('mlp0'), load('gl', 1)), (after('mlp0'), load('out', 1)), (use('mlp1'), loaded('gl', 1)), (use('mlp1'), loaded('out', 1)),
         (after('mlp1'), load('gl', 0)), (after('mlp1'), load('out', 0)), (use('back0'), loaded('gl', 0)), (use('back0'), loaded('out', 0)),
         (use('rows1'), loaded('o', 1)), (after('rows1'), load('o', 0)), (use('rows0'), loaded('o', 0)),
         (after('cols1'), load('qkv', 0)), (use('cols0'), loaded('qkv', 0)),
-        (after('rows1'), wo_first(1)), (after('rows1') + 1, wo_second(1)), (after('rows1') + 4, wo_third(1)),
-        (after('rows0'), wo_first(0)), (after('rows0') + 1, wo_second(0)),
+        (after('rows1'), wo_first(1)), (after('rows1') + 1, wo_second(1)), (after('rows0'), wo_third(1)),
+        (after('rows0'), wo_first(0)), (after('rows0'), count_buckets), (after('rows0') + 1, wo_second(0)),
+        (after('sum0'), all_start), (after('sum0') + 1, all_next(0)), (after('sum0') + 2, all_next(1)), (after('sum0') + 3, all_next(2)),
+        (len(lags) * batch, wo_third(0)), (len(lags) * batch, all_end),
     ]
-    early = [(use(tag) + 1, hold[key], ref) for tag, key, ref in (
-        ('first', 'h', r.out_h0), ('mlp0', 'h', r.out_m0), ('mlp0', 'u', r.out_u0), ('next', 'h', r.out_h1),
-        ('mlp1', 'h', r.out_m1), ('mlp1', 'u', r.out_u1), ('mlp1', 'gl', r.out_gl1), ('cols1', 'qkv', r.out_qkv1), ('back0', 'gl', r.out_gl0), ('cols0', 'qkv', r.out_qkv0))]
+    early = [(use(tag) + 1, hold[key], places(name, l)) for tag, key, name, l in (
+        ('first', 'h', 'h', 0), ('mlp0', 'h', 'm', 0), ('mlp0', 'u', 'u', 0), ('next', 'h', 'h', 1), ('mlp1', 'h', 'm', 1), ('mlp1', 'u', 'u', 1), ('mlp1', 'gl', 'gl', 1),
+        ('cols1', 'qkv', 'qkv', 1), ('back0', 'gl', 'gl', 0), ('cols0', 'qkv', 'qkv', 0))]
     gives = dict(GIVES)
-    passes = [(max(gives[key] + 2 * batch, PASS_FROM), moves[key].pass_on) for key in NARROW]
     n_slots = batch + lags[-1]
+    passes = [(n_slots - 3 if gives[key] + 2 * batch < n_slots else n_slots, moves[key].pass_on) for key in NARROW]
 
     def chunk_at(slot, lag, work):
         @pl.when(jnp.logical_and(slot >= lag, slot < batch + lag))
@@ -782,25 +847,20 @@
         for at, work in once + passes:
             if at < n_slots:
                 pl.when(slot == at)(work)
-        for lag, spill, ref in early:
-            chunk_at(slot, lag, lambda b: spill.copy(ref, b).wait())
+        for lag, spill, where in early:
+            chunk_at(slot, lag, lambda b: spill.wait(*where, b))
+        chunk_at(slot, use('mlp1') + 1, lambda b: dy_own(b).wait())
         chunk_at(slot, use('mlp1') - 1, lambda b: dy_in(b).start())
         for k in order:
             chunk_at(slot, lags[k], stages[k][1])
         for key, lag in GIVES:
             chunk_at(slot, lag, moves[key].give)
-        pl.when(slot == n_slots - batch)(count_buckets)
         return carry
 
     lax.fori_loop(0, n_slots, slot_step, 0)
-    wo_third(0)()
-    for at, work in passes:
+    for at, work in sorted(passes + once, key=lambda entry: entry[0]):
         if at >= n_slots:
             work()
-    n_lines = d_model // 128
-    for i, ref in enumerate((r.dga0, r.dga1, r.dgm0, r.dgm1)):
-        for k in range(n_lines):
-            r.small[i * n_lines + k:i * n_lines + k + 1] = ref[:, k * 128:(k + 1) * 128]
 
     def finish(b, carry):
         for l in range(2):
@@ -830,20 +890,20 @@
     in_hbm = dict(x=by_seg(x), x_rows=x, dy=by_seg(dy), dy_rows=dy, w_q=w_q, w_k=w_k, w_v=w_v, w_o=w_o, w_deal=w_o.reshape(-1, n_cp, quarter, d_model), w_gate=w_gate, w_lin=w_lin, w_out=w_out)
     ins = {key: (value, any_spec) for key, value in in_hbm.items()}
     ins.update(key_mask=(key_mask, VMEM_SPEC), rel_bias=(rel_bias, SMEM_SPEC), g_attn=(g_attn, VMEM_SPEC), g_mlp=(g_mlp, VMEM_SPEC))
-    size = dict(h=d_model, m=d_model, u=ff, gl=2 * ff, qkv=3 * width)
+    size = dict(u=ff, gl=2 * ff, qkv=3 * width)
     outs = {}
-    for key, n in size.items():
-        for l in range(2):
-            outs['out_%s%d' % (key, l)] = ((batch, rows, n), BF16)
+    for key in ('h0', 'h1', 'm0', 'm1'):
+        outs['out_' + key] = (x.shape, BF16)
     for key in ('d0', 'dx'):
         outs['out_' + key] = ((batch, n_tp, seg, d_model), BF16)
     for key in WIDE:
         shape = outs['out_' + key][0] if key != 'dy' else x.shape
-        outs['got_' + key] = ((3,) + shape[:-1] + (d_model // 2,), BF16)
+        outs['got_' + key] = ((4,) + shape[:-1] + (d_model // 2,), BF16)
     for key in NARROW:
-        outs['got_' + key] = ((3,) + outs['out_' + key][0], BF16)
+        outs['got_' + key] = ((4, batch, rows, size[key[:-1]]), BF16)
     n_any = len(outs)
-    outs['small'] = ((4 * d_model // 128 + n_tp, 128), F32)
+    outs['g_attn_out'] = outs['g_mlp_out'] = (g_attn.shape, F32)
+    outs['g_bias'] = ((1, LANES), F32)
     outs['wo_half'] = ((2, 2, width // 2, d_model // 2), BF16)
     vmem = lambda *shape: pltpu.VMEM(shape, BF16)
     wide = lambda *shape: pltpu.VMEM(shape, F32)
@@ -863,15 +923,19 @@
     scratch.update(o_own=vmem(2, batch, rows, width), wo_acc=wide(width, d_model), wo_in=wide(2, width, d_model // 2), wo_x=wide(2, width // 2, d_model // 2), sem_wo=dma((2, 2, 3)))
     for key, n in (('hbuf', d_model), ('ubuf', ff), ('gbuf', 2 * ff), ('qbuf', 3 * width), ('dybuf', d_model)):
         scratch[key] = vmem(2, rows, n)
-    for key in ('o', 'out', 'gl', 'h', 'u', 'g', 'q', 'dy', 'deal_in'):
+    for key in ('o', 'out', 'gl', 'dy', 'dy_own', 'deal_in'):
         scratch['sem_' + key] = dma((2,))
-    scratch.update(sem_qkv=dma((3,)), sem_in=dma((batch + 3,)), sem_keep=dma((batch,)), sem_mask=dma((2, 3)), sem_deal=dma((2, 2, n_tp)), sem_share=dma((2, 2, 3)),
+    for key in 'hugq':
+        scratch['sem_' + key] = dma((2, 2))
+    scratch.update(sem_qkv=dma((3,)), sem_in=dma((batch + 3,)), sem_keep=dma((batch,)), sem_d0=dma((batch,)), sem_mask=dma((2, 3)), sem_deal=dma((2, 2, n_tp)), sem_share=dma((2, 2, 3)),
                    sem_wide=dma((2, len(WIDE), 3)), sem_narrow=dma((2, len(NARROW), 3)))
     for key in ('kv', 'qdo', 'stats'):
         scratch['sem_' + key] = dma((2, 2, 3, batch))
     for key in ('o', 'x'):
         scratch['sem_%sz' % key] = dma((2, batch, 3))
         scratch['sem_%sy' % key] = dma((2, batch, 4))
+    n_small = 4 * d_model // LANES + n_tp
+    scratch.update(by_z=wide(4, n_small, LANES), stage=wide(3, n_small, LANES), stage_in=wide(3, n_small, LANES), sem_all=dma((2, 7)), lines=wide(rel_bias.shape[0], heads, n_cp * rows))
     for i, piece in enumerate(Ring.scratch(batch, seg, d_model)):
         scratch['ring_%d' % i] = piece
     result = pl.pallas_call(
@@ -885,50 +949,6 @@
         name='mega',
     )(*[v[0] for v in ins.values()])
     return dict(zip(outs, result))
-
-
-def sums_kernel(small, g_attn, g_mlp, g_bias, stage, by_z, sem):
-    _, z, y, pair, z_peer = tp_places()
-    _, mate, across, _ = cp_places()
-    meet([pair] + z_peer[1:], [mate, across])
-    mine = small
-    for k, (axis, peer) in enumerate((('cp', mate), ('cp', across), ('tp', pair))):
-        copy = remote(mine, stage.at[2 * k], sem, (k,), axis, peer)
-        copy.start()
-        copy.wait()
-        if k < 2:
-            stage[2 * k + 1] = mine[:] + stage[2 * k]
-            mine = stage.at[2 * k + 1]
-        else:
-            by_z[z] = mine[:] + stage[2 * k]
-    copies = [remote(by_z.at[z], by_z.at[z], sem, (2 + j,), 'tp', z_peer[j]) for j in (1, 2, 3)]
-    for copy in copies:
-        copy.start()
-    for copy in copies:
-        copy.wait()
-    total = by_z[0] + by_z[1] + by_z[2] + by_z[3]
-    lanes = total.shape[1]
-    n_lines = g_attn.shape[1] // lanes
-    for i, ref in enumerate((g_attn, g_mlp)):
-        for l in range(2):
-            for k in range(n_lines):
-                first = (2 * i + l) * n_lines + k
-                ref[l:l + 1, k * lanes:(k + 1) * lanes] = total[first:first + 1]
-    own = lax.broadcasted_iota(jnp.int32, (8, lanes), 0) == lax.axis_index('tp')
-    g_bias[:] = jnp.sum(jnp.where(own, total[4 * n_lines:], 0.0), axis=0, keepdims=True)
-
-
-def sums(small, d_model, cid):
-    return pl.pallas_call(
-        sums_kernel,
-        out_shape=(jax.ShapeDtypeStruct((2, d_model), F32), jax.ShapeDtypeStruct((2, d_model), F32), jax.ShapeDtypeStruct((1, 128), F32)),
-        in_specs=[VMEM_SPEC],
-        out_specs=(VMEM_SPEC,) * 3,
-        scratch_shapes=[pltpu.VMEM((5,) + small.shape, F32), pltpu.VMEM((4,) + small.shape, F32), pltpu.SemaphoreType.DMA((2, 6))],
-        compiler_params=comm_params(cid, 4),
-        cost_estimate=cost(10),
-        name='sums',
-    )(small)
 
 
 def place_kernel(plan, n_out, *refs):
@@ -985,32 +1005,20 @@
 
     def local_program(x_in, d_y, key_mask, rel_bias, g_attn, g_mlp, w_q, w_k, w_v, w_o, w_gate, w_lin, w_out):
         batch, rows, d_model = x_in.shape
-        tokens = batch * rows
         n_layers = w_q.shape[0]
         n_buckets, heads = rel_bias.shape
-        core = lax.rem(lax.axis_index('cp'), 2)
         half = d_model // 2
-
         m = mega(x_in, d_y, key_mask, rel_bias, g_attn, g_mlp, w_q, w_k, w_v, w_o, w_gate, w_lin, w_out, 0)
 
-        def flat(array):
+        def flat(key):
+            array = m['got_' + key]
             return array.reshape(-1, array.shape[-1])
 
-        def own_half(array):
-            return lax.dynamic_slice_in_dim(array.reshape(tokens, d_model), core * half, half, axis=1)
-
-        def grad(left, right, left_wide):
-            a, b = [d_y if key == 'dy' else m['out_' + key] for key in (left, right)]
-            a_g, b_g = flat(m['got_' + left]), flat(m['got_' + right])
-            a, b = (own_half(a), flat(b)) if left_wide else (flat(a), own_half(b))
-            return (dot_tn(a, b) + dot_tn(a_g, b_g)).astype(BF16)
-
-        owns = [grad('h0', 'qkv0', True), grad('h1', 'qkv1', True), grad('m0', 'gl0', True), grad('m1', 'gl1', True), grad('u0', 'd0', False), grad('u1', 'dy', False)]
+        owns = [dot_tn(flat(a), flat(b)).astype(BF16) for a, b in (('h0', 'qkv0'), ('h1', 'qkv1'), ('m0', 'gl0'), ('m1', 'gl1'), ('u0', 'd0'), ('u1', 'dy'))]
         owns += [m['wo_half'].reshape(n_layers, -1, half)]
         mates = [lax.ppermute(part, 'cp', [(0, 1), (1, 0), (2, 3), (3, 2)]) for part in owns]
-        d_g_attn, d_g_mlp, d_rel = sums(m['small'], d_model, 1)
         plan = tuple((layer, by_rows, first, n) for by_rows, first, n in ((True, 0, 3), (True, 4, 2), (False, 6, 1), (False, 3, 1)) for layer in range(n_layers))
         grads = place(plan, owns + owns[-1:], mates + mates[-1:], [w.shape for w in (w_q, w_k, w_v, w_o, w_gate, w_lin, w_out)])
-        return (m['out_dx'].reshape(batch, rows, d_model), d_rel.reshape(n_buckets, heads), d_g_attn, d_g_mlp) + tuple(grads)
+        return (m['out_dx'].reshape(batch, rows, d_model), m['g_bias'].reshape(n_buckets, heads), m['g_attn_out'], m['g_mlp_out']) + tuple(grads)
 
     return jax.shard_map(local_program, mesh=mesh, in_specs=(seq_spec, seq_spec, P(None, 'cp'), P(None, 'tp')) + weight_specs, out_specs=(seq_spec, P(None, 'tp')) + weight_specs, check_vma=False)

time: 655 us -> 602 us (0.919); the launches traced: 648 us -> 602 us
  Pallas kernels: 599 us -> 555 us
    pallas_call x1, Pallas kernels: 567 us -> 540 us  [mega(): pl.pallas_call(functools.partial(mega_kernel, list(ins) + list(outs) + li...]
    pallas_call x1 -> x0, Pallas kernels: 16.5 us -> none  [sums(): pl.pallas_call(sums_kernel, out_shape=(jax.ShapeDtypeStruct((2, d_model),...]
    dot_general x12 -> x6, matrix products: 32.9 us -> 35.5 us  [dot_tn(): lax.dot_general(a, b, (((0,), (0,)), ((), ())), preferred_element_type=F32)]
  transfers between devices with their start and end apart: 7 -> 7, of which waited for: 0 -> 1; matrix products, arithmetic and copies ran while one was open for 4% -> 5% of each run, Pallas kernels for 3% -> 0%
where the time goes in v7:
time: 602 us
  Pallas kernels  555 us (92%)
  matrix products  35.5 us (6%)
  local copies, waits for them, and re-layouts  7.59 us (1%)
    pallas_call x1, Pallas kernels, mega(): pl.pallas_call(functools.partial(mega_kernel, list(ins) + list(outs) + li...  540 us
    dot_general x6, matrix products, dot_tn(): lax.dot_general(a, b, (((0,), (0,)), ((), ())), preferred_element_type=F32)  35.5 us
    pallas_call x1, Pallas kernels, place(): pl.pallas_call(functools.partial(place_kernel, plan, len(out_shapes)), ou...  14.9 us
  transfers between devices with their start and end apart: 7, of which 1 were waited for; matrix products, arithmetic and copies ran while one was open for 5% of the time, Pallas kernels for 0%

profile of v7, /device:TPU:0, one launch (start us, length us, event | category | flops | bytes accessed | tf_op | source)
XLA Modules:
  0.0 602.0 jit_solution(10477405891863436572)
XLA Ops:
  0.6 1.4 copy.31.refs_13_
  2.0 539.9 %mega.1 = (bf16[4,128,2048]{2,1,0:T(8,128)(2,1)}, bf16[4,128,2048]{2,1,0:T(8,128)(2,1)}, bf16[4,128,2048]{2,1,0:T(8,128)(2,1)}, bf16[4,128,2048]{2,1,0:T(8,128)(...) custom-call(bf16[4,8,16,2048]{3,2,1,0:T(8,128)(2,1)} %bitcast.43, ...), custom_call_target="tpu_custom_call" | custom-call | flops 314572800000 | bytes 8388608 | tf_op jit(solution)/shard_map/mega/pallas_call | solution.py:941
  541.9 0.0 copy-start.13
  541.9 0.0 slice-start
  542.0 6.0 %bitcast_convert_fusion.4.refs_5_ = bf16[640,1024]{1,0:T(8,128)(2,1)S(1)} fusion(bf16[4,4,128,640]{3,2,1,0:T(8,128)(2,1)} %get-tuple-element.49, bf16[4,4,128,1024]{3,2,1,0:T(8,128)(2,1)} %get-tuple-element.50), kind=kOutput, calls=%fused_computation.4 | convolution fusion | flops 2685009920 | bytes 8126464 | tf_op jit(solution)/shard_map/dot_general | solution.py:48
  548.0 0.1 collective-permute-start.5
  548.1 0.0 copy-done.13
  548.1 0.0 slice-start.1
  548.1 0.0 copy-start.14
  548.1 8.7 %bitcast_convert_fusion.refs_3_ = bf16[1024,1280]{1,0:T(8,128)(2,1)} fusion(bf16[4,4,128,1024]{3,2,1,0:T(8,128)(2,1)} %get-tuple-element.45, bf16[4,4,128,1280]{3,2,1,0:T(8,128)(2,1)S(1)} %copy-done.13), kind=kOutput, calls=%fused_computation | convolution fusion | flops 5370019840 | bytes 12058624 | tf_op jit(solution)/shard_map/dot_general | solution.py:48
  556.8 0.5 collective-permute-start.3
  557.3 0.0 slice-done
  557.3 0.0 slice-done.1
  557.3 0.0 copy-done.14
  557.3 0.0 copy-start
  557.3 0.0 copy-start.10
  557.3 0.0 copy-start.12
  557.3 7.1 %bitcast_convert_fusion.1.refs_2_ = bf16[1024,1280]{1,0:T(8,128)(2,1)} fusion(bf16[4,4,128,1024]{3,2,1,0:T(8,128)(2,1)S(1)} %copy-done.14, bf16[4,4,128,1280]{3,2,1,0:T(8,128)(2,1)S(1)} %bitcast.49), kind=kOutput, calls=%fused_computation.1 | convolution fusion | flops 5370019840 | bytes 12058624 | tf_op jit(solution)/shard_map/dot_general | solution.py:48
  564.5 0.0 collective-permute-start.2
  564.5 0.0 copy-done
  564.5 0.5 collective-permute-start.6
  565.0 0.0 copy-done.10
  565.0 0.0 copy-done.12
  565.0 0.0 copy-start.9
  565.0 0.0 copy-start.11
  565.0 4.7 bitcast_convert_fusion.2.refs_1_
  569.7 0.1 collective-permute-start.1
  569.7 0.0 copy-done.9
  569.7 0.0 copy-done.11
  569.7 0.0 copy-start.6
  569.7 0.0 copy-start.7
  569.7 4.9 bitcast_convert_fusion.3.refs_0_
  574.6 0.0 collective-permute-done.6.refs_14_.refs_15_
  574.6 0.5 collective-permute-start
  575.1 0.0 copy-done.6
  575.1 0.0 copy-done.7
  575.1 0.0 copy-start.8
  575.1 4.1 convolution_convert_fusion.refs_4_
  579.2 0.0 collective-permute-done.5.refs_13_
  579.2 0.0 copy-start.1
  579.2 1.1 copy-done.1
  580.2 0.1 collective-permute-start.4
  580.3 0.5 broadcast.3
  580.8 0.0 copy-done.8
  580.8 0.7 reduce.3
  581.4 0.1 reshape.60
  581.5 0.7 copy.37
  582.2 1.0 collective-permute-done.4.refs_12_
  583.2 0.0 collective-permute-done.1.refs_9_
  583.2 0.0 collective-permute-done.refs_8_
  583.2 0.0 collective-permute-done.3.refs_11_
  583.2 0.0 collective-permute-done.2.refs_10_
  583.2 0.0 copy-start.2
  583.2 1.3 copy-done.2
  584.5 0.0 copy-start.3
  584.5 14.9 %place.1 = (bf16[2,2048,256]{2,1,0:T(8,128)(2,1)}, bf16[2,2048,256]{2,1,0:T(8,128)(2,1)}, bf16[2,2048,256]{2,1,0:T(8,128)(2,1)}, bf16[2,256,2048]{2,1,0:T(8,128)...) custom-call(bf16[1024,768]{1,0:T(8,128)(2,1)} %bitcast_convert_fusion.3.refs_0_, ...), custom_call_target="tpu_custom_call" | custom-call | tf_op jit(solution)/shard_map/place/pallas_call | solution.py:989
  599.5 0.0 copy-start.5
  599.5 0.0 copy-start.4
  599.5 0.0 copy-done.3
  599.5 1.3 copy.51
  600.8 0.0 copy-done.5
  600.8 0.6 copy.52
  601.4 0.0 copy-done.4
  601.4 0.6 copy.53
  (1 shorter events, 0.0 us)
Async XLA Ops:
  541.9 6.1 %copy-start.13 = (bf16[4,4,128,1280]{3,2,1,0:T(8,128)(2,1)S(1)}, bf16[4,4,128,1280]{3,2,1,0:T(8,128)(2,1)}, u32[]{:S(2)}) copy-start(bf16[4,4,128,1280]{3,2,1,0:T(8,128)(2,1)} %get-tuple-element.46) | copy-start | bytes 15728644
  541.9 15.3 %slice-start = ((s8[5242880]{0:T(1024)(128)(4,1)}), s8[4194304]{0:T(1024)(128)(4,1)S(1)}, s32[]{:S(2)}) async-start(s8[5242880]{0:T(1024)(128)(4,1)} %bitcast.48), calls=%async_computation | async-start | bytes 8388608
  548.0 31.2 %collective-permute-start.5 = (bf16[640,1024]{1,0:T(8,128)(2,1)S(1)}, bf16[640,1024]{1,0:T(8,128)(2,1)S(1)}, u32[]{:S(2)}, u32[]{:S(2)}) collective-permute-start(bf16[640,1024]{1,0:T(8,128)(2,1)S(1)} %bitcast_convert_fusion.4.refs_5_), channel_id=1, source_target_pairs={{0,1},{1,0},{2,3},{3,2},{4,5},{5,4},{6,7},{7,6},{8,9},{9,8},{10,11... | collective-permute-start | bytes 3932168 | tf_op jit(solution)/shard_map/ppermute | solution.py:1019
  548.1 9.2 %slice-start.1 = ((s8[5242880]{0:T(1024)(128)(4,1)}), s8[1048576]{0:T(1024)(128)(4,1)S(1)}, s32[]{:S(2)}) async-start(s8[5242880]{0:T(1024)(128)(4,1)} %bitcast.48), calls=%async_computation.1 | async-start | bytes 2097152
  548.1 9.2 %copy-start.14 = (bf16[4,4,128,1024]{3,2,1,0:T(8,128)(2,1)S(1)}, bf16[4,4,128,1024]{3,2,1,0:T(8,128)(2,1)}, u32[]{:S(2)}) copy-start(bf16[4,4,128,1024]{3,2,1,0:T(8,128)(2,1)} %get-tuple-element.43) | copy-start | bytes 12582916
  556.8 26.4 %collective-permute-start.3 = (bf16[1024,1280]{1,0:T(8,128)(2,1)}, bf16[1024,1280]{1,0:T(8,128)(2,1)}, u32[]{:S(2)}, u32[]{:S(2)}) collective-permute-start(bf16[1024,1280]{1,0:T(8,128)(2,1)} %bitcast_convert_fusion.refs_3_), channel_id=1, source_target_pairs={{0,1},{1,0},{2,3},{3,2},{4,5},{5,4},{6,7},{7,6},{8,9},{9,8},{10,11... | collective-permute-start | bytes 7864328 | tf_op jit(solution)/shard_map/ppermute | solution.py:1019
  557.3 7.2 %copy-start = (bf16[2,2,128,1024]{3,2,1,0:T(8,128)(2,1)S(1)}, bf16[2,2,128,1024]{3,2,1,0:T(8,128)(2,1)}, u32[]{:S(2)}) copy-start(bf16[2,2,128,1024]{3,2,1,0:T(8,128)(2,1)} %get-tuple-element.51) | copy-start | bytes 3145732
  557.3 7.7 %copy-start.10 = (bf16[4,4,128,1024]{3,2,1,0:T(8,128)(2,1)S(1)}, bf16[4,4,128,1024]{3,2,1,0:T(8,128)(2,1)}, u32[]{:S(2)}) copy-start(bf16[4,4,128,1024]{3,2,1,0:T(8,128)(2,1)} %get-tuple-element.41) | copy-start | bytes 12582916
  557.3 7.7 %copy-start.12 = (bf16[4,4,128,768]{3,2,1,0:T(8,128)(2,1)S(1)}, bf16[4,4,128,768]{3,2,1,0:T(8,128)(2,1)}, u32[]{:S(2)}) copy-start(bf16[4,4,128,768]{3,2,1,0:T(8,128)(2,1)} %get-tuple-element.42) | copy-start | bytes 9437188
  564.5 18.7 %collective-permute-start.2 = (bf16[1024,1280]{1,0:T(8,128)(2,1)}, bf16[1024,1280]{1,0:T(8,128)(2,1)}, u32[]{:S(2)}, u32[]{:S(2)}) collective-permute-start(bf16[1024,1280]{1,0:T(8,128)(2,1)} %bitcast_convert_fusion.1.refs_2_), channel_id=1, source_target_pairs={{0,1},{1,0},{2,3},{3,2},{4,5},{5,4},{6,7},{7,6},{8,9},{9,8},{10,11... | collective-permute-start | bytes 7864328 | tf_op jit(solution)/shard_map/ppermute | solution.py:1019
  564.5 10.1 %collective-permute-start.6 = (bf16[2,256,1024]{2,1,0:T(8,128)(2,1)S(1)}, bf16[2,256,1024]{2,1,0:T(8,128)(2,1)S(1)}, u32[]{:S(2)}, u32[]{:S(2)}) collective-permute-start(bf16[2,256,1024]{2,1,0:T(8,128)(2,1)S(1)} %bitcast.39), channel_id=1, source_target_pairs={{0,1},{1,0},{2,3},{3,2},{4,5},{5,4},{6,7},{7,6},{8,9},{9,8},{10,11... | collective-permute-start | bytes 3145736 | tf_op jit(solution)/shard_map/ppermute | solution.py:1019
  565.0 4.7 copy-start.9
  565.0 4.7 copy-start.11
  569.7 13.5 %collective-permute-start.1 = (bf16[1024,768]{1,0:T(8,128)(2,1)}, bf16[1024,768]{1,0:T(8,128)(2,1)}, u32[]{:S(2)}, u32[]{:S(2)}) collective-permute-start(bf16[1024,768]{1,0:T(8,128)(2,1)} %bitcast_convert_fusion.2.refs_1_), channel_id=1, source_target_pairs={{0,1},{1,0},{2,3},{3,2},{4,5},{5,4},{6,7},{7,6},{8,9},{9,8},{10,11... | collective-permute-start | bytes 4718600 | tf_op jit(solution)/shard_map/ppermute | solution.py:1019
  569.7 5.4 copy-start.6
  569.7 5.4 copy-start.7
  574.6 8.6 %collective-permute-start = (bf16[1024,768]{1,0:T(8,128)(2,1)}, bf16[1024,768]{1,0:T(8,128)(2,1)}, u32[]{:S(2)}, u32[]{:S(2)}) collective-permute-start(bf16[1024,768]{1,0:T(8,128)(2,1)} %bitcast_convert_fusion.3.refs_0_), channel_id=1, source_target_pairs={{0,1},{1,0},{2,3},{3,2},{4,5},{5,4},{6,7},{7,6},{8,9},{9,8},{10,11... | collective-permute-start | bytes 4718600 | tf_op jit(solution)/shard_map/ppermute | solution.py:1019
  575.1 5.7 copy-start.8
  579.2 1.1 copy-start.1
  580.2 3.0 collective-permute-start.4
  583.2 1.3 copy-start.2
  584.5 15.0 %copy-start.3 = (bf16[4,8,16,2048]{3,2,1,0:T(8,128)(2,1)S(1)}, bf16[4,8,16,2048]{3,2,1,0:T(8,128)(2,1)}, u32[]{:S(2)}) copy-start(bf16[4,8,16,2048]{3,2,1,0:T(8,128)(2,1)} %get-tuple-element.35) | copy-start | bytes 6291460
  599.5 1.4 copy-start.5
  599.5 2.0 copy-start.4

commit v8 on v7

--- a/solution.py
+++ b/solution.py
@@ -99,12 +99,24 @@
     return me, z, y, pair, [2 * lax.rem(z + j, 4) + y for j in range(4)]
 
 
-def meet(tp_peers, cp_peers):
+def core_of(place):
+    return lax.rem(place, 2)
+
+
+def chip_of(place):
+    return place // 2
+
+
+def window_of(which, size):
+    return pl.ds(pl.multiple_of(which * size, size), size)
+
+
+def arrive_at(tp_peers, cp_peers):
     barrier = pltpu.get_barrier_semaphore()
     for axis, peers in (('tp', tp_peers), ('cp', cp_peers)):
         for peer in peers:
             pl.semaphore_signal(barrier, inc=1, device_id={axis: peer}, device_id_type=MESH)
-    pl.semaphore_wait(barrier, len(tp_peers) + len(cp_peers))
+    return barrier, len(tp_peers) + len(cp_peers)
 
 
 class Ring:
@@ -244,15 +256,17 @@
 class Wide:
     def __init__(self, src, dst, sem, index):
         self.src, self.dst, self.sem, self.index = src, dst, sem, index
-        me, *self.peers = cp_places()
-        mate, across, diagonal = self.peers
-        self.peers = (mate, across, diagonal)
-        self.core = lax.rem(me, 2)
+        me, mate, across, diagonal = cp_places()
+        self.peers = (mate, across, diagonal, me)
+
+    def columns(self, r):
+        n = self.dst.shape[-1]
+        core, chip = core_of(self.peers[r]), chip_of(self.peers[r])
+        first = core * n if 2 * n == self.src.shape[-1] else (2 * core + chip) * n
+        return pl.ds(pl.multiple_of(first, n), n)
 
     def copy(self, r, window):
-        n = self.dst.shape[-1]
-        want = self.core if r == 1 else 1 - self.core
-        columns = pl.ds(pl.multiple_of(want * n, n), n)
+        columns = self.columns(r)
         return remote(self.src.at[window].at[..., columns], self.dst.at[r].at[window], self.sem, (self.index, r), 'cp', self.peers[r])
 
     def give(self, b):
@@ -452,11 +466,12 @@
 WIDE = ('h0', 'h1', 'm0', 'm1', 'dy', 'd0')
 NARROW = ('u0', 'u1', 'gl0', 'gl1', 'qkv0', 'qkv1')
 LANES = 128
+LAYERS = (0, 1)
 SUBLANES = 8
 LETTERS = string.ascii_letters
-STEPS = '0302321222210111101101010101101101123'
-ORDER = 'FaKGeCtbdqpHlkExvozmjiwshfuBJynDIcAgr'
-GIVES = tuple(zip(('h0', 'dy', 'u0', 'm0', 'h1', 'u1', 'm1', 'gl1', 'd0', 'qkv1', 'gl0', 'qkv0'), map(LETTERS.index, 'demvxzABDGHJ')))
+STEPS = '0203322112010111110101012111110101212'
+ORDER = 'byrvzgxDtqIajpoKlhFAGCwBfHeJnkdsEmuic'
+GIVES = tuple(zip(('dy', 'h0', 'u0', 'h1', 'm0', 'm1', 'u1', 'qkv1', 'gl1', 'gl0', 'd0', 'qkv0'), map(LETTERS.index, 'flnruxyBDFHK')))
 
 
 def mega_kernel(names, heads, *refs):
@@ -473,7 +488,7 @@
     me, mate, across, diagonal = cp_places()
     tp_me = gather_o.me
     others = (mate, across, diagonal)
-    my_columns = pl.ds(pl.multiple_of(tp_me * width, width), width)
+    my_columns = window_of(tp_me, width)
 
     def weight(buf, sem, sources, layer):
         out, col = [], 0
@@ -497,16 +512,16 @@
                 copy.wait()
         return go
 
-    chip, core = me // 2, lax.rem(me, 2)
+    chip, core = chip_of(me), core_of(me)
     half = d_model // 2
 
     def half_of(which):
-        return pl.ds(pl.multiple_of(which * half, half), half)
+        return window_of(which, half)
 
     def wo_send(l, step):
         src, dst, peer = (
             (r.wo_acc.at[:, half_of(1 - core)], r.wo_in.at[l], mate),
-            (r.wo_in.at[l, pl.ds(pl.multiple_of((1 - chip) * (width // 2), SUBLANES), width // 2)], r.wo_x.at[l], across),
+            (r.wo_in.at[l, window_of(1 - chip, width // 2)], r.wo_x.at[l], across),
             (r.wo_half.at[l, chip], r.wo_half.at[l, chip], across))[step]
         return remote(src, dst, r.sem_wo, (l, step), 'cp', peer)
 
@@ -523,36 +538,41 @@
     def wo_third(l):
         def go():
             wo_send(l, 1).wait()
-            mine = r.wo_in[l, pl.ds(pl.multiple_of(chip * (width // 2), SUBLANES), width // 2)]
+            mine = r.wo_in[l, window_of(chip, width // 2)]
             r.wo_half[l, chip] = (mine + r.wo_x[l]).astype(BF16)
             wo_send(l, 2).start()
         return go
 
-    for key, layer in (('qkv', 0), ('o', 1), ('gl', 0), ('out', 0)):
-        load(key, layer)()
+    peers = [lax.rem(tp_me + j, n_seg) for j in range(n_seg)]
+    barrier, n_peers = arrive_at(peers[1:], others)
+    load('qkv', 0)()
     rows_in = [pltpu.make_async_copy(r.x.at[b], ring.full.at[b], r.sem_in.at[b]) for b in range(batch)]
     shards_in = [(r.x.at[:, ring.seg], r.xs0), (r.dy.at[:, ring.seg], r.ds1), (r.x_rows.at[:, :, my_columns], r.x_col)]
     shards_in = [pltpu.make_async_copy(src, dst, r.sem_in.at[batch + i]) for i, (src, dst) in enumerate(shards_in)]
-    deal_own = [pltpu.make_async_copy(r.w_deal.at[l, me, :, my_columns], r.w_cols.at[l, me, tp_me], r.sem_deal_in.at[l]) for l in range(2)]
+    deal_own = [pltpu.make_async_copy(r.w_deal.at[l, me, :, my_columns], r.w_cols.at[l, me, tp_me], r.sem_deal_in.at[l]) for l in LAYERS]
     for copy in rows_in + shards_in + deal_own:
         copy.start()
+    for key, layer in (('o', 1), ('gl', 0), ('out', 0)):
+        load(key, layer)()
     r.key_add[:] = jnp.where(r.key_mask[:] > 0, 0.0, MASK_NEG).astype(F32)[:, None, :]
-    peers = [lax.rem(tp_me + j, n_seg) for j in range(n_seg)]
-    meet(peers[1:], others)
+    for ref in (r.ds_sum, r.dga0, r.dga1, r.dgm0, r.dgm1):
+        ref[:] = jnp.zeros_like(ref)
+    bias_tables(r.rel_bias, me, r.bias_rows, r.bias_cols)
+    pl.semaphore_wait(barrier, n_peers)
     masks = [remote(r.key_add, r.mask_all.at[me], r.sem_mask, (i,), 'cp', peer) for i, peer in enumerate(others)]
     for copy in masks:
         copy.start()
     r.mask_all[me] = r.key_add[:]
 
     def deal(l, j):
-        window = pl.ds(pl.multiple_of(peers[j] * width, width), width)
+        window = window_of(peers[j], width)
         return remote(r.w_deal.at[l, me, :, window], r.w_cols.at[l, me, tp_me], r.sem_deal, (l, j), 'tp', peers[j])
 
     def share(l, i):
         ref = r.w_cols.at[l, across if i == 2 else me]
         return remote(ref, ref, r.sem_share, (l, i), 'cp', across if i == 1 else mate)
 
-    for l in range(2):
+    for l in LAYERS:
         for j in range(1, n_seg):
             deal(l, j).start()
 
@@ -581,8 +601,6 @@
                     r.w_now[t, c] = r.w_cols[l, c, t]
         return go
 
-    for ref in (r.ds_sum, r.dga0, r.dga1, r.dgm0, r.dgm1):
-        ref[:] = jnp.zeros_like(ref)
     for copy in rows_in + shards_in:
         copy.wait()
     loaded('qkv', 0)()
@@ -651,7 +669,7 @@
 
     def mlp_forward(l, b, shard):
         gather_x.arrive(b)
-        window = pl.ds(pl.multiple_of(ring.seg * seg, seg), seg)
+        window = window_of(ring.seg, seg)
         shard[b] = jnp.concatenate([r.x_all[b, t, window] for t in range(n_seg)], axis=1)
         h2 = norm_rows(gather_x.rows(b), r.g_mlp[l:l + 1])
         hold['h'].put(*places('m', l), b, h2)
@@ -678,7 +696,7 @@
 
     def dy_own(b):
         slot = lax.rem(b, 2)
-        return pltpu.make_async_copy(r.dybuf.at[slot, :, half_of(core)], r.got_dy.at[3, b], r.sem_dy_own.at[slot])
+        return pltpu.make_async_copy(r.dybuf.at[slot, :, moves['dy'].columns(3)], r.got_dy.at[3, b], r.sem_dy_own.at[slot])
 
     def mlp_backward(l, b, d, gate, lin, copies=()):
         dgl = mlp_pull(dot_nt(d, r.wout[:]), gate, lin)
@@ -737,7 +755,7 @@
 
     def stage_mlp_back0(b):
         ring.arrive(b)
-        copies = [keep(r.out_d0, b), pltpu.make_async_copy(ring.full.at[b, :, :, half_of(core)], r.got_d0.at[3, b], r.sem_d0.at[b])]
+        copies = [keep(r.out_d0, b), pltpu.make_async_copy(ring.full.at[b, :, :, moves['d0'].columns(3)], r.got_d0.at[3, b], r.sem_d0.at[b])]
         copies[1].start()
         mlp_backward(0, b, ring.rows(b), r.gate[b], r.lin[b], copies)
 
@@ -768,8 +786,7 @@
     use = lambda tag: lag_of[tag]
     after = lambda tag: lag_of[tag] + batch
 
-    def tables():
-        bias_tables(r.rel_bias, me, r.bias_rows, r.bias_cols)
+    def masked():
         for copy in masks:
             copy.wait()
 
@@ -811,7 +828,7 @@
     def all_end():
         total = all_sum(2)
         for i, ref in enumerate((r.g_attn_out, r.g_mlp_out)):
-            for l in range(2):
+            for l in LAYERS:
                 for k in range(n_lines):
                     first = (2 * i + l) * n_lines + k
                     ref[l:l + 1, k * LANES:(k + 1) * LANES] = total[first:first + 1]
@@ -819,8 +836,8 @@
         r.g_bias[:] = col_sum(jnp.where(own, total[4 * n_lines:], 0.0))
 
     once = [
-        (use('at0'), tables), (use('mlp0'), loaded('gl', 0)), (use('mlp0'), loaded('out', 0)),
-        (batch - 1, share_start(0)), (batch - 1, share_start(1)), (batch + 1, share_pass(0)), (use('col0'), shared(0)), (use('col0'), share_pass(1)), (use('col1'), shared(1)),
+        (use('at0'), masked), (use('mlp0'), loaded('gl', 0)), (use('mlp0'), loaded('out', 0)),
+        (batch + 1, share_start(0)), (batch + 1, share_start(1)), (batch + 3, share_pass(0)), (use('col0'), shared(0)), (after('col0'), share_pass(1)), (use('col1'), shared(1)),
         (after('first'), load('qkv', 1)), (use('next'), loaded('qkv', 1)),
         (after('mlp0'), load('gl', 1)), (after('mlp0'), load('out', 1)), (use('mlp1'), loaded('gl', 1)), (use('mlp1'), loaded('out', 1)),
         (after('mlp1'), load('gl', 0)), (after('mlp1'), load('out', 0)), (use('back0'), loaded('gl', 0)), (use('back0'), loaded('out', 0)),
@@ -863,7 +880,7 @@
             work()
 
     def finish(b, carry):
-        for l in range(2):
+        for l in LAYERS:
             kv[l].finish(b)
             qdo[l].finish(b)
             for i in range(3):
@@ -898,7 +915,7 @@
         outs['out_' + key] = ((batch, n_tp, seg, d_model), BF16)
     for key in WIDE:
         shape = outs['out_' + key][0] if key != 'dy' else x.shape
-        outs['got_' + key] = ((4,) + shape[:-1] + (d_model // 2,), BF16)
+        outs['got_' + key] = ((4,) + shape[:-1] + (d_model // (4 if key[0] == 'd' else 2),), BF16)
     for key in NARROW:
         outs['got_' + key] = ((4, batch, rows, size[key[:-1]]), BF16)
     n_any = len(outs)
@@ -953,48 +970,46 @@
 
 def place_kernel(plan, n_out, *refs):
     n = len(plan)
-    owns, mates, outs = refs[:n], refs[n:2 * n], refs[2 * n:2 * n + n_out]
-    bufs, in_sem, out_sem = refs[2 * n + n_out:4 * n + n_out], refs[4 * n + n_out], refs[4 * n + n_out + 1]
-    core = lax.rem(lax.axis_index('cp'), 2)
+    srcs, outs, bufs, in_sem, out_sem = refs[:n], refs[n:n + n_out], refs[n + n_out:2 * n + n_out], refs[2 * n + n_out], refs[2 * n + n_out + 1]
+    me = lax.axis_index('cp')
     loads = []
-    for src, buf in zip(owns + mates, bufs):
+    for src, buf, (_, layer, _, _, _) in zip(srcs, bufs, plan):
         if len(src.shape) > len(buf.shape):
-            src = src.at[plan[len(loads) % n][0]]
+            src = src.at[layer]
         loads.append(pltpu.make_async_copy(src, buf, in_sem.at[len(loads)]))
     for load in loads:
         load.start()
     stores = []
-    for i, load in enumerate(loads):
-        layer, by_rows, first_out, n_pieces = plan[i % n]
-        which = core if i < n else 1 - core
-        buf = bufs[i]
+    for load, buf, (first_out, layer, flip, by_rows, n_pieces) in zip(loads, bufs, plan):
         load.wait()
         width = buf.shape[1] // n_pieces
+        size = buf.shape[0] if by_rows else width
+        owner = me + flip - 2 * core_of(me) * core_of(flip) - 4 * chip_of(me) * chip_of(flip)
+        core, chip = core_of(owner), chip_of(owner)
+        parts = outs[first_out].shape[1 if by_rows else 2] // size
+        which = core if parts == 2 else 2 * core + chip
+        window = window_of(which, size)
         for p in range(n_pieces):
             src = buf if n_pieces == 1 else buf.at[:, pl.ds(p * width, width)]
-            size = buf.shape[0] if by_rows else width
-            window = pl.ds(pl.multiple_of(which * size, size), size)
             out = outs[first_out + p].at[layer]
-            dst = out.at[window, :] if by_rows else out.at[:, window]
-            stores.append(pltpu.make_async_copy(src, dst, out_sem.at[len(stores)]))
+            stores.append(pltpu.make_async_copy(src, out.at[window, :] if by_rows else out.at[:, window], out_sem.at[len(stores)]))
             stores[-1].start()
     for store in stores:
         store.wait()
 
 
-def place(plan, owns, mates, out_shapes):
-    n = len(plan)
+def place(plan, srcs, out_shapes):
     any_spec = pl.BlockSpec(memory_space=pl.ANY)
-    n_stores = 2 * sum(p[3] for p in plan)
+    dma = pltpu.SemaphoreType.DMA
     return pl.pallas_call(
         functools.partial(place_kernel, plan, len(out_shapes)),
         out_shape=tuple(jax.ShapeDtypeStruct(s, BF16) for s in out_shapes),
-        in_specs=[any_spec] * (2 * n),
+        in_specs=[any_spec] * len(srcs),
         out_specs=tuple([any_spec] * len(out_shapes)),
-        scratch_shapes=[pltpu.VMEM(a.shape[-2:], BF16) for a in list(owns) + list(mates)] + [pltpu.SemaphoreType.DMA((2 * n,)), pltpu.SemaphoreType.DMA((n_stores,))],
+        scratch_shapes=[pltpu.VMEM(a.shape[-2:], BF16) for a in srcs] + [dma((len(srcs),)), dma((sum(p[-1] for p in plan),))],
         compiler_params=pltpu.CompilerParams(vmem_limit_bytes=40 * MIB),
         name='place',
-    )(*owns, *mates)
+    )(*srcs)
 
 
 def solution(mesh):
@@ -1014,11 +1029,32 @@
             array = m['got_' + key]
             return array.reshape(-1, array.shape[-1])
 
-        owns = [dot_tn(flat(a), flat(b)).astype(BF16) for a, b in (('h0', 'qkv0'), ('h1', 'qkv1'), ('m0', 'gl0'), ('m1', 'gl1'), ('u0', 'd0'), ('u1', 'dy'))]
-        owns += [m['wo_half'].reshape(n_layers, -1, half)]
-        mates = [lax.ppermute(part, 'cp', [(0, 1), (1, 0), (2, 3), (3, 2)]) for part in owns]
-        plan = tuple((layer, by_rows, first, n) for by_rows, first, n in ((True, 0, 3), (True, 4, 2), (False, 6, 1), (False, 3, 1)) for layer in range(n_layers))
-        grads = place(plan, owns + owns[-1:], mates + mates[-1:], [w.shape for w in (w_q, w_k, w_v, w_o, w_gate, w_lin, w_out)])
+        def grad(left, right):
+            return dot_tn(flat(left), flat(right)).astype(BF16)
+
+        def swap(part, flip):
+            return lax.ppermute(part, 'cp', [(c, c ^ flip) for c in range(4)])
+
+        plan, srcs = [], []
+
+        def put(result, layer, by_rows, pieces, part, across=False):
+            held = [(0, part)] + ([(2, swap(part, 2))] if across else [])
+            for flip, piece in held + [(flip + 1, swap(piece, 1)) for flip, piece in held]:
+                plan.append((result, layer, flip, by_rows, pieces))
+                srcs.append(piece)
+
+        put(6, 1, False, 1, grad('u1', 'dy'), True)
+        put(6, 0, False, 1, grad('u0', 'd0'), True)
+        for layer in range(n_layers):
+            put(4, layer, True, 2, grad('m%d' % layer, 'gl%d' % layer))
+        for layer in range(n_layers):
+            put(0, layer, True, 3, grad('h%d' % layer, 'qkv%d' % layer))
+        wo = m['wo_half'].reshape(n_layers, -1, half)
+        for flip, part in ((0, wo), (1, swap(wo, 1))):
+            for layer in range(n_layers):
+                plan.append((3, layer, flip, False, 1))
+                srcs.append(part)
+        grads = place(tuple(plan), srcs, [w.shape for w in (w_q, w_k, w_v, w_o, w_gate, w_lin, w_out)])
         return (m['out_dx'].reshape(batch, rows, d_model), m['g_bias'].reshape(n_buckets, heads), m['g_attn_out'], m['g_mlp_out']) + tuple(grads)
 
     return jax.shard_map(local_program, mesh=mesh, in_specs=(seq_spec, seq_spec, P(None, 'cp'), P(None, 'tp')) + weight_specs, out_specs=(seq_spec, P(None, 'tp')) + weight_specs, check_vma=False)

time: 602 us -> 598 us (level)
  Pallas kernels: 555 us -> 538 us
  waiting for transfers between devices: 1 us -> 10.4 us
    pallas_call x1, Pallas kernels: 540 us -> 522 us  [mega(): pl.pallas_call(functools.partial(mega_kernel, list(ins) + list(outs) + li...]
    ppermute x7 -> x11, waiting for transfers between devices: 1 us -> 10.4 us  [swap(): return lax.ppermute(part, 'cp', [(c, c ^ flip) for c in range(4)])]
  transfers between devices with their start and end apart: 7 -> 11, of which waited for: 1 -> 2; matrix products, arithmetic and copies ran while one was open for 5% -> 5% of each run, Pallas kernels for 0% -> 0%
where the time goes in v8:
time: 598 us; the launch traced here: 597 us
  Pallas kernels  538 us (90%)
  matrix products  31 us (5%)
  local copies, waits for them, and re-layouts  12.1 us (2%)
  waiting for transfers between devices  10.4 us (2%)
    pallas_call x1, Pallas kernels, mega(): pl.pallas_call(functools.partial(mega_kernel, list(ins) + list(outs) + li...  522 us
    dot_general x6, matrix products, dot_tn(): lax.dot_general(a, b, (((0,), (0,)), ((), ())), preferred_element_type=F32)  31 us
    pallas_call x1, Pallas kernels, place(): pl.pallas_call(functools.partial(place_kernel, plan, len(out_shapes)), ou...  16.2 us
  transfers between devices with their start and end apart: 11, of which 2 were waited for; matrix products, arithmetic and copies ran while one was open for 5% of the time, Pallas kernels for 0%

profile of v8, /device:TPU:0, one launch (start us, length us, event | category | flops | bytes accessed | tf_op | source)
XLA Modules:
  0.0 597.4 jit_solution(9322961513318380912)
XLA Ops:
  0.6 1.4 copy.31.refs_13_
  2.0 522.0 %mega.1 = (bf16[4,128,2048]{2,1,0:T(8,128)(2,1)}, bf16[4,128,2048]{2,1,0:T(8,128)(2,1)}, bf16[4,128,2048]{2,1,0:T(8,128)(2,1)}, bf16[4,128,2048]{2,1,0:T(8,128)(...) custom-call(bf16[4,8,16,2048]{3,2,1,0:T(8,128)(2,1)} %bitcast.47, ...), custom_call_target="tpu_custom_call" | custom-call | flops 314572800000 | bytes 8388608 | tf_op jit(solution)/shard_map/mega/pallas_call | solution.py:958
  524.0 0.0 copy-start.9
  524.0 0.0 copy-start.11
  524.0 0.0 copy-start.19
  524.0 4.1 convolution_convert_fusion.refs_4_
  528.1 0.1 collective-permute-start.3
  528.2 0.1 collective-permute-start.4
  528.3 0.0 copy-done.9
  528.3 0.0 copy-done.11
  528.3 0.0 slice-start
  528.3 1.5 fusion.refs_0_
  529.8 2.0 collective-permute-start
  531.8 0.0 copy-done.19
  531.8 8.7 %bitcast_convert_fusion.refs_10_ = bf16[1024,1280]{1,0:T(8,128)(2,1)} fusion(bf16[4,4,128,1024]{3,2,1,0:T(8,128)(2,1)} %get-tuple-element.45, bf16[4,4,128,1280]{3,2,1,0:T(8,128)(2,1)S(1)} %copy-done.19), kind=kOutput, calls=%fused_computation | convolution fusion | flops 5370019840 | bytes 12058624 | tf_op jit(solution)/shard_map/dot_general | solution.py:48
  540.6 0.2 collective-permute-start.7
  540.8 0.0 slice-done
  540.8 0.0 slice-done.1
  540.8 0.0 copy-done.20
  540.8 0.0 copy-start.16
  540.8 0.0 copy-start.18
  540.8 7.1 %bitcast_convert_fusion.1.refs_8_ = bf16[1024,1280]{1,0:T(8,128)(2,1)} fusion(bf16[4,4,128,1024]{3,2,1,0:T(8,128)(2,1)S(1)} %copy-done.20, bf16[4,4,128,1280]{3,2,1,0:T(8,128)(2,1)S(1)} %bitcast.51), kind=kOutput, calls=%fused_computation.1 | convolution fusion | flops 5370019840 | bytes 12058624 | tf_op jit(solution)/shard_map/dot_general | solution.py:48
  547.9 0.3 collective-permute-start.6
  548.2 0.0 copy-done.16
  548.2 0.0 copy-done.18
  548.2 0.0 copy-start.17
  548.2 4.7 bitcast_convert_fusion.2.refs_14_
  552.9 0.0 collective-permute-done.3.refs_5_
  552.9 0.2 collective-permute-start.1
  553.1 5.5 collective-permute-done.refs_1_
  558.6 0.0 copy-done
  558.6 0.0 collective-permute-start.10
  558.6 0.0 copy-done.15
  558.6 0.0 copy-done.17
  558.7 4.9 bitcast_convert_fusion.3.refs_12_
  563.5 0.0 collective-permute-done.4.refs_6_
  563.5 0.8 copy-done.3
  564.4 0.5 collective-permute-start.9
  564.9 0.0 collective-permute-done.1.refs_2_
  564.9 0.8 copy-done.5
  565.7 0.0 collective-permute-start.8
  565.7 0.0 collective-permute-done.10.refs_18_.refs_19_
  565.7 0.5 collective-permute-start.5
  566.2 4.9 collective-permute-done.5.refs_7_
  571.1 0.8 copy-done.7
  571.9 0.4 collective-permute-start.2
  572.3 0.5 broadcast.3
  572.8 0.7 reduce.3
  573.5 0.1 reshape.60
  573.6 0.7 copy.37
  574.2 0.0 collective-permute-done.2.refs_3_
  574.2 0.0 collective-permute-done.9.refs_15_
  574.3 0.0 collective-permute-done.8.refs_13_
  574.3 0.0 collective-permute-done.7.refs_11_
  574.3 0.0 collective-permute-done.6.refs_9_
  574.3 0.0 copy-start.2
  574.3 1.1 copy-done.2
  575.4 1.1 copy-done.4
  576.5 1.1 copy-done.6
  577.5 1.1 copy-done.8
  578.6 16.2 %place.1 = (bf16[2,2048,256]{2,1,0:T(8,128)(2,1)}, bf16[2,2048,256]{2,1,0:T(8,128)(2,1)}, bf16[2,2048,256]{2,1,0:T(8,128)(2,1)}, bf16[2,256,2048]{2,1,0:T(8,128)...) custom-call(bf16[640,512]{1,0:T(8,128)(2,1)S(1)} %fusion.refs_0_, ...), custom_call_target="tpu_custom_call" | custom-call | tf_op jit(solution)/shard_map/place/pallas_call | solution.py:1004
  594.9 1.3 copy.51
  596.2 0.6 copy.52
  596.8 0.6 copy.53
  (21 shorter events, 0.0 us)
Async XLA Ops:
  524.0 4.3 copy-start.9
  524.0 4.3 copy-start.11
  524.0 7.8 %copy-start.19 = (bf16[4,4,128,1280]{3,2,1,0:T(8,128)(2,1)S(1)}, bf16[4,4,128,1280]{3,2,1,0:T(8,128)(2,1)}, u32[]{:S(2)}) copy-start(bf16[4,4,128,1280]{3,2,1,0:T(8,128)(2,1)} %get-tuple-element.46) | copy-start | bytes 15728644
  528.1 24.8 %collective-permute-start.3 = (bf16[640,512]{1,0:T(8,128)(2,1)S(1)}, bf16[640,512]{1,0:T(8,128)(2,1)S(1)}, u32[]{:S(2)}, u32[]{:S(2)}) collective-permute-start(bf16[640,512]{1,0:T(8,128)(2,1)S(1)} %convolution_convert_fusion.refs_4_), channel_id=1, source_target_pairs={{0,2},{1,3},{2,0},{3,1},{4,6},{5,7},{6,4},{7,5},{8,10},{9,11},{10,... | collective-permute-start | bytes 1966088 | tf_op jit(solution)/shard_map/ppermute | solution.py:1036
  528.2 35.4 %collective-permute-start.4 = (bf16[640,512]{1,0:T(8,128)(2,1)S(1)}, bf16[640,512]{1,0:T(8,128)(2,1)S(1)}, u32[]{:S(2)}, u32[]{:S(2)}) collective-permute-start(bf16[640,512]{1,0:T(8,128)(2,1)S(1)} %convolution_convert_fusion.refs_4_), channel_id=1, source_target_pairs={{0,1},{1,0},{2,3},{3,2},{4,5},{5,4},{6,7},{7,6},{8,9},{9,8},{10,11... | collective-permute-start | bytes 1966088 | tf_op jit(solution)/shard_map/ppermute | solution.py:1036
  528.3 12.5 %slice-start = ((s8[5242880]{0:T(1024)(128)(4,1)}), s8[4194304]{0:T(1024)(128)(4,1)S(1)}, s32[]{:S(2)}) async-start(s8[5242880]{0:T(1024)(128)(4,1)} %bitcast.50), calls=%async_computation | async-start | bytes 8388608
  529.8 28.8 %collective-permute-start = (bf16[640,512]{1,0:T(8,128)(2,1)S(1)}, bf16[640,512]{1,0:T(8,128)(2,1)}, u32[]{:S(2)}, u32[]{:S(2)}) collective-permute-start(bf16[640,512]{1,0:T(8,128)(2,1)S(1)} %fusion.refs_0_), channel_id=1, source_target_pairs={{0,2},{1,3},{2,0},{3,1},{4,6},{5,7},{6,4},{7,5},{8,10},{9,11},{10,... | collective-permute-start | bytes 1966088 | tf_op jit(solution)/shard_map/ppermute | solution.py:1036
  531.8 8.9 %slice-start.1 = ((s8[5242880]{0:T(1024)(128)(4,1)}), s8[1048576]{0:T(1024)(128)(4,1)S(1)}, s32[]{:S(2)}) async-start(s8[5242880]{0:T(1024)(128)(4,1)} %bitcast.50), calls=%async_computation.1 | async-start | bytes 2097152
  531.8 8.9 %copy-start.20 = (bf16[4,4,128,1024]{3,2,1,0:T(8,128)(2,1)S(1)}, bf16[4,4,128,1024]{3,2,1,0:T(8,128)(2,1)}, u32[]{:S(2)}) copy-start(bf16[4,4,128,1024]{3,2,1,0:T(8,128)(2,1)} %get-tuple-element.43) | copy-start | bytes 12582916
  540.6 33.7 %collective-permute-start.7 = (bf16[1024,1280]{1,0:T(8,128)(2,1)}, bf16[1024,1280]{1,0:T(8,128)(2,1)}, u32[]{:S(2)}, u32[]{:S(2)}) collective-permute-start(bf16[1024,1280]{1,0:T(8,128)(2,1)} %bitcast_convert_fusion.refs_10_), channel_id=1, source_target_pairs={{0,1},{1,0},{2,3},{3,2},{4,5},{5,4},{6,7},{7,6},{8,9},{9,8},{10,11... | collective-permute-start | bytes 7864328 | tf_op jit(solution)/shard_map/ppermute | solution.py:1036
  540.8 7.4 %copy-start.16 = (bf16[4,4,128,1024]{3,2,1,0:T(8,128)(2,1)S(1)}, bf16[4,4,128,1024]{3,2,1,0:T(8,128)(2,1)}, u32[]{:S(2)}) copy-start(bf16[4,4,128,1024]{3,2,1,0:T(8,128)(2,1)} %get-tuple-element.49) | copy-start | bytes 12582916
  540.8 7.4 %copy-start.18 = (bf16[4,4,128,768]{3,2,1,0:T(8,128)(2,1)S(1)}, bf16[4,4,128,768]{3,2,1,0:T(8,128)(2,1)}, u32[]{:S(2)}) copy-start(bf16[4,4,128,768]{3,2,1,0:T(8,128)(2,1)} %get-tuple-element.50) | copy-start | bytes 9437188
  547.9 26.4 %collective-permute-start.6 = (bf16[1024,1280]{1,0:T(8,128)(2,1)}, bf16[1024,1280]{1,0:T(8,128)(2,1)}, u32[]{:S(2)}, u32[]{:S(2)}) collective-permute-start(bf16[1024,1280]{1,0:T(8,128)(2,1)} %bitcast_convert_fusion.1.refs_8_), channel_id=1, source_target_pairs={{0,1},{1,0},{2,3},{3,2},{4,5},{5,4},{6,7},{7,6},{8,9},{9,8},{10,11... | collective-permute-start | bytes 7864328 | tf_op jit(solution)/shard_map/ppermute | solution.py:1036
  548.2 10.4 %copy-start = (bf16[2,2,128,1024]{3,2,1,0:T(8,128)(2,1)S(1)}, bf16[2,2,128,1024]{3,2,1,0:T(8,128)(2,1)}, u32[]{:S(2)}) copy-start(bf16[2,2,128,1024]{3,2,1,0:T(8,128)(2,1)} %get-tuple-element.51) | copy-start | bytes 3145732
  548.2 10.4 %copy-start.15 = (bf16[4,4,128,1024]{3,2,1,0:T(8,128)(2,1)S(1)}, bf16[4,4,128,1024]{3,2,1,0:T(8,128)(2,1)}, u32[]{:S(2)}) copy-start(bf16[4,4,128,1024]{3,2,1,0:T(8,128)(2,1)} %get-tuple-element.47) | copy-start | bytes 12582916
  548.2 10.4 %copy-start.17 = (bf16[4,4,128,768]{3,2,1,0:T(8,128)(2,1)S(1)}, bf16[4,4,128,768]{3,2,1,0:T(8,128)(2,1)}, u32[]{:S(2)}) copy-start(bf16[4,4,128,768]{3,2,1,0:T(8,128)(2,1)} %get-tuple-element.48) | copy-start | bytes 9437188
  552.9 12.8 %copy-start.1 = (bf16[640,512]{1,0:T(8,128)(2,1)}, bf16[640,512]{1,0:T(8,128)(2,1)S(1)}, u32[]{:S(2)}) copy-start(bf16[640,512]{1,0:T(8,128)(2,1)S(1)} %collective-permute-done.3.refs_5_) | copy-start | bytes 1966084
  552.9 12.0 %collective-permute-start.1 = (bf16[640,512]{1,0:T(8,128)(2,1)S(1)}, bf16[640,512]{1,0:T(8,128)(2,1)S(1)}, u32[]{:S(2)}, u32[]{:S(2)}) collective-permute-start(bf16[640,512]{1,0:T(8,128)(2,1)S(1)} %fusion.refs_0_), channel_id=1, source_target_pairs={{0,1},{1,0},{2,3},{3,2},{4,5},{5,4},{6,7},{7,6},{8,9},{9,8},{10,11... | collective-permute-start | bytes 1966088 | tf_op jit(solution)/shard_map/ppermute | solution.py:1036
  558.6 7.1 %collective-permute-start.10 = (bf16[2,256,1024]{2,1,0:T(8,128)(2,1)S(1)}, bf16[2,256,1024]{2,1,0:T(8,128)(2,1)S(1)}, u32[]{:S(2)}, u32[]{:S(2)}) collective-permute-start(bf16[2,256,1024]{2,1,0:T(8,128)(2,1)S(1)} %bitcast.41), channel_id=1, source_target_pairs={{0,1},{1,0},{2,3},{3,2},{4,5},{5,4},{6,7},{7,6},{8,9},{9,8},{10,11... | collective-permute-start | bytes 3145736 | tf_op jit(solution)/shard_map/ppermute | solution.py:1036
  558.7 14.2 %copy-start.14 = (f32[1,128]{1,0:T(1,128)S(1)}, f32[1,128]{1,0:T(1,128)}, u32[]{:S(2)}) copy-start(f32[1,128]{1,0:T(1,128)} %get-tuple-element.36) | copy-start | bytes 1540
  563.5 0.8 copy-start.3
  564.4 9.9 %collective-permute-start.9 = (bf16[1024,768]{1,0:T(8,128)(2,1)}, bf16[1024,768]{1,0:T(8,128)(2,1)}, u32[]{:S(2)}, u32[]{:S(2)}) collective-permute-start(bf16[1024,768]{1,0:T(8,128)(2,1)} %bitcast_convert_fusion.2.refs_14_), channel_id=1, source_target_pairs={{0,1},{1,0},{2,3},{3,2},{4,5},{5,4},{6,7},{7,6},{8,9},{9,8},{10,11... | collective-permute-start | bytes 4718600 | tf_op jit(solution)/shard_map/ppermute | solution.py:1036
  564.9 0.8 copy-start.5
  565.7 8.5 %collective-permute-start.8 = (bf16[1024,768]{1,0:T(8,128)(2,1)}, bf16[1024,768]{1,0:T(8,128)(2,1)}, u32[]{:S(2)}, u32[]{:S(2)}) collective-permute-start(bf16[1024,768]{1,0:T(8,128)(2,1)} %bitcast_convert_fusion.3.refs_12_), channel_id=1, source_target_pairs={{0,1},{1,0},{2,3},{3,2},{4,5},{5,4},{6,7},{7,6},{8,9},{9,8},{10,11... | collective-permute-start | bytes 4718600 | tf_op jit(solution)/shard_map/ppermute | solution.py:1036
  565.7 5.3 collective-permute-start.5
  571.1 0.8 copy-start.7
  571.9 2.3 collective-permute-start.2
  574.3 1.1 copy-start.2
  575.4 1.1 copy-start.4
  576.5 1.1 copy-start.6
  577.5 1.1 copy-start.8
  578.6 16.3 %copy-start.10 = (bf16[4,8,16,2048]{3,2,1,0:T(8,128)(2,1)S(1)}, bf16[4,8,16,2048]{3,2,1,0:T(8,128)(2,1)}, u32[]{:S(2)}) copy-start(bf16[4,8,16,2048]{3,2,1,0:T(8,128)(2,1)} %get-tuple-element.35) | copy-start | bytes 6291460
  594.9 1.4 copy-start.13
  594.9 2.0 copy-start.12
